TPU v7x, 32 devices: a whole 2x2x4 slice. The times are simulated.
32 devices in a mesh: dp: 4 (over y, x), fsdp: 8 (over z, core).
Axes of the slice: x: 2, y: 2, z: 4, core: 2. Of those that a mesh axis runs over, the one named last changes fastest.
Arguments:
- token_ids: int32 [2, 4, 1024], P(None, 'dp'), may hold values from 0 to 50287
- target_ids: int32 [2, 4, 1024], P(None, 'dp'), may hold values from 0 to 50287
- seq_lengths: int32 [2, 4], replicated, may hold values from 512 to 1024, as said below
- embedding: float32 [50288, 1024], P('fsdp', 'dp'), may hold values from -0.5625 to 0.5625
- embedding_mom: float32 [50288, 1024], P('fsdp', 'dp'), may hold values from -0.00036621094 to 0.00036621094
- embedding_avg: float32 [50288, 1024], P('fsdp', 'dp'), may hold values from -1 to 1
- in_proj: float32 [2, 1024, 4384], P(None, ('dp', 'fsdp')), may hold values from -0.1875 to 0.1875
- in_proj_mom: float32 [2, 1024, 4384], P(None, ('dp', 'fsdp')), may hold values from -0.00036621094 to 0.00036621094
- in_proj_avg: float32 [2, 1024, 4384], P(None, ('dp', 'fsdp')), may hold values from -0.1875 to 0.1875
- out_proj: float32 [2, 2048, 1024], P(None, ('dp', 'fsdp')), may hold values from -0.125 to 0.125
- out_proj_mom: float32 [2, 2048, 1024], P(None, ('dp', 'fsdp')), may hold values from -0.00036621094 to 0.00036621094
- out_proj_avg: float32 [2, 2048, 1024], P(None, ('dp', 'fsdp')), may hold values from -0.125 to 0.125
- vector_params: float32 [30400], replicated, may hold values from -8 to 1.5, as said below
- vector_mom: float32 [30400], replicated, may hold values from -0.0014648438 to 0.0014648438
- vector_avg: float32 [30400], replicated, may hold values from -8 to 1.5, as said below
Outputs:
- loss_value: float32 [], replicated
- grad_norm: float32 [], replicated
- embedding_new: float32 [50288, 1024], P('fsdp', 'dp')
- embedding_mom_new: float32 [50288, 1024], P('fsdp', 'dp')
- embedding_avg_new: float32 [50288, 1024], P('fsdp', 'dp')
- embedding_bf16: bfloat16 [50288, 1024], P('fsdp', 'dp')
- in_proj_new: float32 [2, 1024, 4384], P(None, ('dp', 'fsdp'))
- in_proj_mom_new: float32 [2, 1024, 4384], P(None, ('dp', 'fsdp'))
- in_proj_avg_new: float32 [2, 1024, 4384], P(None, ('dp', 'fsdp'))
- in_proj_bf16: bfloat16 [2, 1024, 4384], P(None, ('dp', 'fsdp'))
- out_proj_new: float32 [2, 2048, 1024], P(None, ('dp', 'fsdp'))
- out_proj_mom_new: float32 [2, 2048, 1024], P(None, ('dp', 'fsdp'))
- out_proj_avg_new: float32 [2, 2048, 1024], P(None, ('dp', 'fsdp'))
- out_proj_bf16: bfloat16 [2, 2048, 1024], P(None, ('dp', 'fsdp'))
- vector_new: float32 [30400], replicated
- vector_mom_new: float32 [30400], replicated
- vector_avg_new: float32 [30400], replicated
- vector_bf16: bfloat16 [30400], replicated
Inputs may be any that keep to these rules, and one draw needn't show every extreme that they name: `seq_lengths`: positions from a sequence's length on are padding. `vector_params`: laid out as the steps say. `vector_avg`: laid out as vector_params.
All inputs are finite; a program needn't handle non-finite values.
Results may differ from a plain program's by a relative error of at most 0.018.
Values may be sent and summed in bfloat16 or wider, within the bound.
A program may use at most 384 MiB of HBM per device.

v0:
```python
import math

import jax
import jax.numpy as jnp
from jax import lax
from jax.sharding import PartitionSpec as P

D = 1024
HEADS = 32
HDIM = 64
NSTATE = 128
CONV = 4
VOCAB = 50288
LAYERS = 2
MB = 2
DI = 2048
XBC = 2304
PER = 14688


epsilon = 1e-05
z_weight = 0.001
clip_limit = 0.2
step_rate = 1000.0
highest = lax.Precision.HIGHEST


def from_behind(block, axis, distance):
    devices = range(lax.axis_size(axis))
    route = [(i - distance, i) for i in devices if i - distance in devices]
    return lax.ppermute(block, axis, route)


def carried_in(shard, axis, join, neutral):
    place = lax.axis_index(axis)
    gathered = jax.tree.map(
        lambda a, kind: lax.all_gather(a.astype(kind), axis), shard, (jnp.bfloat16, jnp.bfloat16)
    )
    state = jax.tree.map(lambda a, e: jnp.zeros_like(a) + jnp.asarray(e, a.dtype), shard, neutral)

    def one(step, state):
        return join(
            state,
            jax.tree.map(
                lambda a, own: lax.dynamic_index_in_dim(a, step, 0, False).astype(own.dtype),
                gathered,
                shard,
            ),
        )

    return lax.fori_loop(0, place, one, state)


def carried_in_2(shard, axis, combine, identity):
    size, place = (lax.axis_size(axis), lax.axis_index(axis))
    everything = jax.tree.map(
        lambda part, kind: lax.all_gather(part.astype(kind), axis),
        shard,
        jax.tree.map(lambda a: jnp.bfloat16 if a.dtype == jnp.float32 else a.dtype, shard),
    )
    start = jax.tree.map(
        lambda part, zero: jnp.broadcast_to(jnp.asarray(zero, part.dtype), part.shape),
        shard,
        identity,
    )

    def step(k, before):
        at = size - 1 - k
        reached = at > place
        new = combine(
            before, jax.tree.map(lambda part, own: part[at].astype(own.dtype), everything, shard)
        )
        return jax.tree.map(lambda a, b: jnp.where(reached, a, b), new, before)

    return lax.fori_loop(0, size, step, start)


def merged(shard, axis, combine):
    everything = jax.tree.map(lambda part: lax.all_gather(part, axis), shard)
    leading = jax.tree.map(lambda part: part[0], everything)

    def step(k, so_far):
        return combine(so_far, jax.tree.map(lambda part: part[k], everything))

    return lax.fori_loop(1, lax.axis_size(axis), step, leading)


def rms_scale(values, gain):
    return values * lax.rsqrt(jnp.mean(values * values, axis=-1, keepdims=True) + epsilon) * gain


def layer_vectors(vector_params, layer_index):
    offset = layer_index * PER
    conv_weight = vector_params[offset : offset + CONV * XBC].reshape(CONV, XBC)
    offset = offset + CONV * XBC
    conv_bias = vector_params[offset : offset + XBC]
    offset = offset + XBC
    dt_bias = vector_params[offset : offset + HEADS]
    offset = offset + HEADS
    decay_log = vector_params[offset : offset + HEADS]
    offset = offset + HEADS
    skip_gain = vector_params[offset : offset + HEADS]
    offset = offset + HEADS
    pre_gain = vector_params[offset : offset + D]
    offset = offset + D
    gate_gain = vector_params[offset : offset + DI]
    return (conv_weight, conv_bias, dt_bias, decay_log, skip_gain, pre_gain, gate_gain)


def conv_inputs(projected, before, vector_params, layer_index):
    conv_weight, conv_bias, dt_bias, decay_log, skip_gain, pre_gain, gate_gain = layer_vectors(
        vector_params, layer_index
    )
    rows_here = projected.shape[0]
    padded = jnp.concatenate([before, projected[:, DI : DI + XBC]], axis=0)
    convolved = conv_bias + sum(
        (conv_weight[tap] * padded[tap : tap + rows_here] for tap in range(CONV))
    )
    activated = jax.nn.silu(convolved)
    values = activated[:, :DI].reshape(rows_here, HEADS, HDIM)
    in_map = activated[:, DI : DI + NSTATE]
    out_map = activated[:, DI + NSTATE :]
    step_size = jax.nn.softplus(projected[:, DI + XBC :] + dt_bias)
    log_decay = jnp.cumsum(step_size * (-jnp.exp(decay_log))[None, :], axis=0)
    return (values, in_map, out_map, step_size, log_decay)


def local_state(projected, before, vector_params, layer_index):
    values, in_map, out_map, step_size, log_decay = conv_inputs(
        projected, before, vector_params, layer_index
    )
    tail = jnp.exp(log_decay[-1][None, :] - log_decay) * step_size
    state_part = jnp.einsum("sh,shp,sn->hpn", tail, values, in_map, precision=highest)
    return (jnp.exp(log_decay[-1]), state_part)


def mixer_output(projected, before, vector_params, entering, layer_index):
    values, in_map, out_map, step_size, log_decay = conv_inputs(
        projected, before, vector_params, layer_index
    )
    skip_gain = layer_vectors(vector_params, layer_index)[4]
    gate_gain = layer_vectors(vector_params, layer_index)[6]
    rows_here = projected.shape[0]
    causal = jnp.arange(rows_here)[:, None] >= jnp.arange(rows_here)[None, :]
    spread = log_decay.T[:, :, None] - log_decay.T[:, None, :]
    weights = jnp.where(causal[None], jnp.exp(jnp.where(causal[None], spread, 0.0)), 0.0)
    inner = jnp.dot(out_map, in_map.T, precision=highest, preferred_element_type=jnp.float32)
    scaled = values * step_size[:, :, None]
    result = jnp.einsum("hts,shp->thp", weights * inner[None], scaled, precision=highest)
    result = result + jnp.exp(log_decay)[:, :, None] * jnp.einsum(
        "tn,hpn->thp", out_map, entering, precision=highest
    )
    result = result + skip_gain[None, :, None] * values
    gated = result.reshape(rows_here, DI) * jax.nn.silu(projected[:, :DI])
    return rms_scale(gated, gate_gain)


def chain_join(earlier, later):
    return (earlier[0] * later[0], later[0][:, None, None] * earlier[1] + later[1])


def stats_join(first, second):
    row_top = jnp.maximum(first[0], second[0])
    summed = first[1] * jnp.exp(first[0] - row_top) + second[1] * jnp.exp(second[0] - row_top)
    return (row_top, summed, first[2] + second[2], first[3] + second[3])


def fetch_layer(in_low, out_low, layer_index):
    return (
        lax.all_gather(in_low[layer_index], ("dp", "fsdp"), axis=0, tiled=True),
        lax.all_gather(out_low[layer_index], ("dp", "fsdp"), axis=0, tiled=True),
    )


def fetch_table(embed_low):
    return lax.all_gather(embed_low, "dp", axis=1, tiled=True)


def send_layer(grad_in, grad_out):
    return (
        lax.psum_scatter(grad_in, ("dp", "fsdp"), scatter_dimension=0, tiled=True),
        lax.psum_scatter(grad_out, ("dp", "fsdp"), scatter_dimension=0, tiled=True),
    )


def send_table(table_grad):
    return lax.psum_scatter(
        table_grad.astype(jnp.bfloat16), "dp", scatter_dimension=1, tiled=True
    ).astype(jnp.float32)


def layer_forward(hidden, weights_pair, vector_params, layer_index):
    in_full, out_full = weights_pair
    normed, norm_back = jax.vjp(
        lambda rows_in, vec_in: rms_scale(rows_in, layer_vectors(vec_in, layer_index)[5]),
        hidden,
        vector_params,
    )
    normed_low = normed.astype(jnp.bfloat16)
    projected = jnp.dot(normed_low, in_full, preferred_element_type=jnp.float32)
    rim = from_behind(projected[-(CONV - 1) :, DI : DI + XBC], "fsdp", 1)
    carried, state_back = jax.vjp(
        lambda proj_in, rim_in, vec_in: local_state(proj_in, rim_in, vec_in, layer_index),
        projected,
        rim,
        vector_params,
    )
    carry_decay, carry_state = carried
    entering = carried_in(
        (carry_decay, carry_state),
        "fsdp",
        chain_join,
        (jnp.ones_like(carry_decay), jnp.zeros_like(carry_state)),
    )[1]
    mixed, mixer_back = jax.vjp(
        lambda proj_in, rim_in, vec_in, enter_in: mixer_output(
            proj_in, rim_in, vec_in, enter_in, layer_index
        ),
        projected,
        rim,
        vector_params,
        entering,
    )
    mixed_low = mixed.astype(jnp.bfloat16)
    branch = jnp.dot(mixed_low, out_full, preferred_element_type=jnp.float32)
    record = (norm_back, normed_low, state_back, mixer_back, mixed_low, carry_decay, entering)
    return (hidden + branch, record)


def layer_backward(grad_hidden, weights_pair, record):
    in_full, out_full = weights_pair
    norm_back, normed_low, state_back, mixer_back, mixed_low, carry_decay, entering = record
    grad_branch = grad_hidden.astype(jnp.bfloat16)
    grad_out = jnp.einsum("td,te->de", mixed_low, grad_branch, preferred_element_type=jnp.float32)
    grad_mixed = jnp.einsum("te,de->td", grad_branch, out_full, preferred_element_type=jnp.float32)
    grad_proj_mix, grad_rim_mix, grad_vec_mix, grad_enter = mixer_back(grad_mixed)
    later = carried_in_2(
        (carry_decay, grad_enter),
        "fsdp",
        chain_join,
        (jnp.ones_like(carry_decay), jnp.zeros_like(grad_enter)),
    )[1]
    grad_decay = jnp.sum(later * entering, axis=(1, 2))
    grad_proj_state, grad_rim_state, grad_vec_state = state_back((grad_decay, later))
    from_next = from_behind(grad_rim_mix + grad_rim_state, "fsdp", -1)
    grad_proj = grad_proj_mix + grad_proj_state
    grad_proj = grad_proj.at[-(CONV - 1) :, DI : DI + XBC].add(from_next)
    grad_proj_low = grad_proj.astype(jnp.bfloat16)
    grad_in = jnp.einsum("td,tz->dz", normed_low, grad_proj_low, preferred_element_type=jnp.float32)
    grad_normed = jnp.einsum(
        "tz,dz->td", grad_proj_low, in_full, preferred_element_type=jnp.float32
    )
    grad_prev, grad_vec_norm = norm_back(grad_normed)
    return (
        grad_hidden + grad_prev,
        grad_in,
        grad_out,
        grad_vec_mix + grad_vec_state + grad_vec_norm,
    )


def advance(weight, moment, average, grad, factor):
    scaled = grad * factor
    moment_new = 0.5 * moment + scaled
    weight_new = weight - step_rate * (scaled + 0.5 * moment_new)
    average_new = 0.5 * average + 0.5 * weight_new
    return (weight_new, moment_new, average_new, weight_new.astype(jnp.bfloat16))


def body(
    token_ids,
    target_ids,
    seq_lengths,
    embedding,
    embedding_mom,
    embedding_avg,
    in_proj,
    in_proj_mom,
    in_proj_avg,
    out_proj,
    out_proj_mom,
    out_proj_avg,
    vector_params,
    vector_mom,
    vector_avg,
):
    group_index = lax.axis_index("dp")
    shard_index = lax.axis_index("fsdp")
    seq_rows = token_ids.shape[2]
    own_rows = seq_rows // lax.axis_size("fsdp")
    vocab_rows = embedding.shape[0]
    total_count = jnp.sum(seq_lengths).astype(jnp.float32)
    embed_low = embedding.astype(jnp.bfloat16)
    in_low = in_proj.astype(jnp.bfloat16)
    out_low = out_proj.astype(jnp.bfloat16)
    positions = jnp.arange(seq_rows)
    own_mask = positions // own_rows == shard_index
    block_rows = math.gcd(seq_rows, 512)
    count_blocks = seq_rows // block_rows
    vocab_iota = jnp.arange(vocab_rows)
    in_parts = [jnp.zeros(in_proj.shape[1:], jnp.float32) for section in range(LAYERS)]
    out_parts = [jnp.zeros(out_proj.shape[1:], jnp.float32) for section in range(LAYERS)]
    table_part = jnp.zeros(embedding.shape, jnp.float32)
    vector_grad = jnp.zeros(vector_params.shape, jnp.float32)
    loss_sum = jnp.zeros((), jnp.float32)
    for micro in range(MB):
        ids_here = token_ids[micro, 0]
        labels_here = target_ids[micro, 0]
        length_here = lax.dynamic_index_in_dim(seq_lengths[micro], group_index, keepdims=False)
        valid = (positions < length_here).astype(jnp.float32)
        row_weight = valid / total_count
        table_full = fetch_table(embed_low)
        local_ids = ids_here - shard_index * vocab_rows
        inside = (local_ids >= 0) & (local_ids < vocab_rows)
        looked = jnp.where(
            inside[:, None],
            table_full[jnp.clip(local_ids, 0, vocab_rows - 1)],
            jnp.zeros((), jnp.bfloat16),
        )
        hidden = lax.psum_scatter(
            looked.astype(jnp.float32).astype(jnp.bfloat16), "fsdp", scatter_dimension=0, tiled=True
        ).astype(jnp.float32)
        records = []
        for layer_index in range(LAYERS):
            weights_pair = fetch_layer(in_low, out_low, layer_index)
            hidden, record = layer_forward(hidden, weights_pair, vector_params, layer_index)
            records.append(record)
        final_out, final_back = jax.vjp(
            lambda rows_in, vec_in: rms_scale(rows_in, vec_in[LAYERS * PER :]),
            hidden,
            vector_params,
        )
        group_hidden = lax.all_gather(final_out.astype(jnp.bfloat16), "fsdp", axis=0, tiled=True)
        hidden_blocks = group_hidden.reshape(count_blocks, block_rows, D)
        label_blocks = (labels_here - shard_index * vocab_rows).reshape(count_blocks, block_rows)

        def block_stats(packed):
            rows_block, labels_block = packed
            logits = jnp.einsum(
                "rd,vd->rv", rows_block, table_full, preferred_element_type=jnp.float32
            )
            row_top = jnp.max(logits, axis=1)
            expsum = jnp.sum(jnp.exp(logits - row_top[:, None]), axis=1)
            matches = vocab_iota[None, :] == labels_block[:, None]
            target = jnp.sum(jnp.where(matches, logits, 0.0), axis=1)
            return (row_top, expsum, target, jnp.sum(logits, axis=1))

        stats = lax.map(block_stats, (hidden_blocks, label_blocks))
        stats = tuple((piece.reshape(seq_rows) for piece in stats))
        row_top, expsum, target, logit_sum = merged(stats, "fsdp", stats_join)
        log_total = row_top + jnp.log(expsum)
        per_row = (
            log_total - 0.9 * target - 0.1 * logit_sum / VOCAB + z_weight * log_total * log_total
        )
        loss_sum = loss_sum + jnp.sum(jnp.where(own_mask, per_row * valid, 0.0))
        prob_scale = row_weight * (1.0 + 2.0 * z_weight * log_total)

        def block_back(table_grad, packed):
            rows_block, labels_block, lse_block, scale_block, weight_block = packed
            logits = jnp.einsum(
                "rd,vd->rv", rows_block, table_full, preferred_element_type=jnp.float32
            )
            probs = jnp.exp(logits - lse_block[:, None])
            matches = (vocab_iota[None, :] == labels_block[:, None]).astype(jnp.float32)
            grad_logits = scale_block[:, None] * probs - weight_block[:, None] * (
                0.9 * matches + 0.1 / VOCAB
            )
            grad_low = grad_logits.astype(jnp.bfloat16)
            rows_grad = jnp.dot(grad_low, table_full, preferred_element_type=jnp.float32)
            table_grad = table_grad + jnp.einsum(
                "rv,rd->vd", grad_low, rows_block, preferred_element_type=jnp.float32
            )
            return (table_grad, rows_grad)

        packed = (
            hidden_blocks,
            label_blocks,
            log_total.reshape(count_blocks, block_rows),
            prob_scale.reshape(count_blocks, block_rows),
            row_weight.reshape(count_blocks, block_rows),
        )
        table_grad, hidden_grad = lax.scan(
            block_back, jnp.zeros((vocab_rows, D), jnp.float32), packed
        )
        own_grad = lax.psum_scatter(
            hidden_grad.reshape(seq_rows, D).astype(jnp.bfloat16),
            "fsdp",
            scatter_dimension=0,
            tiled=True,
        ).astype(jnp.float32)
        grad_hidden, grad_vec = final_back(own_grad)
        vector_grad = vector_grad + grad_vec
        for layer_index in reversed(range(LAYERS)):
            weights_pair = fetch_layer(in_low, out_low, layer_index)
            grad_hidden, grad_in, grad_out, grad_vec = layer_backward(
                grad_hidden, weights_pair, records[layer_index]
            )
            vector_grad = vector_grad + grad_vec
            owned_in, owned_out = send_layer(grad_in, grad_out)
            in_parts[layer_index] = in_parts[layer_index] + owned_in
            out_parts[layer_index] = out_parts[layer_index] + owned_out
        embed_back = lax.all_gather(grad_hidden.astype(jnp.bfloat16), "fsdp", axis=0, tiled=True)
        table_grad = table_grad.at[jnp.where(inside, local_ids, vocab_rows)].add(
            embed_back.astype(jnp.float32), mode="drop"
        )
        table_part = table_part + send_table(table_grad)
    grad_in_all = jnp.stack(in_parts)
    grad_out_all = jnp.stack(out_parts)
    owner_squares = (
        jnp.sum(grad_in_all * grad_in_all)
        + jnp.sum(grad_out_all * grad_out_all)
        + jnp.sum(table_part * table_part)
    )
    vector_total, squares_total, loss_total = lax.psum(
        (vector_grad, owner_squares, loss_sum), ("dp", "fsdp")
    )
    grad_norm = jnp.sqrt(squares_total + jnp.sum(vector_total * vector_total))
    factor = jnp.minimum(1.0, clip_limit / grad_norm)
    loss_value = loss_total / total_count
    table_new, table_mom_new, table_avg_new, table_bf16 = advance(
        embedding, embedding_mom, embedding_avg, table_part, factor
    )
    in_new, in_mom_new, in_avg_new, in_bf16 = advance(
        in_proj, in_proj_mom, in_proj_avg, grad_in_all, factor
    )
    out_new, out_mom_new, out_avg_new, out_bf16 = advance(
        out_proj, out_proj_mom, out_proj_avg, grad_out_all, factor
    )
    vec_new, vec_mom_new, vec_avg_new, vec_bf16 = advance(
        vector_params, vector_mom, vector_avg, vector_total, factor
    )
    return (
        loss_value,
        grad_norm,
        table_new,
        table_mom_new,
        table_avg_new,
        table_bf16,
        in_new,
        in_mom_new,
        in_avg_new,
        in_bf16,
        out_new,
        out_mom_new,
        out_avg_new,
        out_bf16,
        vec_new,
        vec_mom_new,
        vec_avg_new,
        vec_bf16,
    )


def solution(mesh):
    return jax.shard_map(
        body,
        mesh=mesh,
        in_specs=(
            P(None, "dp", None),
            P(None, "dp", None),
            P(),
            P("fsdp", "dp"),
            P("fsdp", "dp"),
            P("fsdp", "dp"),
            P(None, ("dp", "fsdp"), None),
            P(None, ("dp", "fsdp"), None),
            P(None, ("dp", "fsdp"), None),
            P(None, ("dp", "fsdp"), None),
            P(None, ("dp", "fsdp"), None),
            P(None, ("dp", "fsdp"), None),
            P(),
            P(),
            P(),
        ),
        out_specs=(
            P(),
            P(),
            P("fsdp", "dp"),
            P("fsdp", "dp"),
            P("fsdp", "dp"),
            P("fsdp", "dp"),
            P(None, ("dp", "fsdp"), None),
            P(None, ("dp", "fsdp"), None),
            P(None, ("dp", "fsdp"), None),
            P(None, ("dp", "fsdp"), None),
            P(None, ("dp", "fsdp"), None),
            P(None, ("dp", "fsdp"), None),
            P(None, ("dp", "fsdp"), None),
            P(None, ("dp", "fsdp"), None),
            P(),
            P(),
            P(),
            P(),
        ),
        check_vma=False,
    )
```

profile of v0, /device:TPU:12, one launch (start us, length us, event | category | flops | bytes accessed | tf_op | source)
XLA Modules:
  0.0 2780.9 jit_solution(12047751130583067095)
XLA Ops:
  14.3 124.6 %all-gather.42.cloned.1.call-done = bf16[6286,1024]{1,0:T(8,128)(2,1)} async-done(((bf16[6286,256]{1,0:T(8,128)(2,1)}), bf16[6286,1024]{1,0:T(8,128)(2,1)}) %all-gather.42.cloned.1.call-update) | async-done | bytes 12873744 | tf_op jit(solution)/shard_map/all_gather | solution.py:176
  168.4 16.5 reduce-scatter.11.cloned.1.call-done
  186.0 58.4 %reduce-scatter.13.cloned.1.call-done = bf16[128,1024]{1,0:T(8,128)(2,1)} async-done(((bf16[1024,1024]{1,0:T(8,128)(2,1)}), bf16[128,1024]{1,0:T(8,128)(2,1)}) %reduce-scatter.13.cloned.1.call-update) | async-done | bytes 262160 | tf_op jit(solution)/shard_map/reduce_scatter | solution.py:320
  362.2 36.3 %all-gather.64.cloned.1.call-done = bf16[256,64,128]{2,1,0:T(8,128)(2,1)} async-done(((bf16[32,64,128]{2,1,0:T(8,128)(2,1)}), bf16[256,64,128]{2,1,0:T(8,128)(2,1)}) %all-gather.64.cloned.1.call-update) | async-done | bytes 4194320 | tf_op jit(solution)/shard_map/all_gather | solution.py:37
  419.3 44.3 %all-gather.56.cloned.1.call-done = bf16[1,2048,1024]{2,1,0:T(8,128)(2,1)} async-done(((bf16[1,64,1024]{2,1,0:T(8,128)(2,1)}), bf16[1,2048,1024]{2,1,0:T(8,128)(2,1)}) %all-gather.56.cloned.1.call-update) | async-done | bytes 4194320 | tf_op jit(solution)/shard_map/all_gather | solution.py:171
  469.5 76.6 %all-gather.58.cloned.1.call-done = bf16[1,1024,4384]{2,1,0:T(8,128)(2,1)} async-done(((bf16[1,32,4384]{2,1,0:T(8,128)(2,1)}), bf16[1,1024,4384]{2,1,0:T(8,128)(2,1)}) %all-gather.58.cloned.1.call-update) | async-done | bytes 8978448 | tf_op jit(solution)/shard_map/all_gather | solution.py:170
  606.2 32.6 %all-gather.60.cloned.1.call-done = bf16[256,64,128]{2,1,0:T(8,128)(2,1)} async-done(((bf16[32,64,128]{2,1,0:T(8,128)(2,1)}), bf16[256,64,128]{2,1,0:T(8,128)(2,1)}) %all-gather.60.cloned.1.call-update) | async-done | bytes 4194320 | tf_op jit(solution)/shard_map/all_gather | solution.py:37
  651.1 53.0 %all-gather.62.cloned.1.call-done = bf16[1,2048,1024]{2,1,0:T(8,128)(2,1)} async-done(((bf16[1,64,1024]{2,1,0:T(8,128)(2,1)}), bf16[1,2048,1024]{2,1,0:T(8,128)(2,1)}) %all-gather.62.cloned.1.call-update) | async-done | bytes 4194320 | tf_op jit(solution)/shard_map/all_gather | solution.py:171
  717.2 20.3 all-gather.44.cloned.1.call-done
  737.5 40.4 %while.224 = (s32[]{:T(128)}, f32[2,512]{1,0:T(2,128)S(1)}, f32[2,512]{1,0:T(2,128)S(1)}, f32[2,512]{1,0:T(2,128)S(1)}, f32[2,512]{1,0:T(2,128)S(1)}, /*index=5*...) while((s32[]{:T(128)}, f32[2,512]{1,0:T(2,128)S(1)}, ...), condition=%wide.region_17.19_spmd.clone, body=%wide.region_12.18_spmd.clone.sunk | while | flops 6613875712 | bytes 39706756 | solution.py:348
  836.2 90.6 %while.226 = (s32[]{:T(128)}, f32[6286,1024]{1,0:T(8,128)}, bf16[2,512,1024]{2,1,0:T(8,128)(2,1)}, f32[2,512]{1,0:T(2,128)S(1)}, bf16[2,512,1024]{2,1,0:T(8,128)...) while((s32[]{:T(128)}, f32[6286,1024]{1,0:T(8,128)}, ...), condition=%wide.region_45.47_spmd.clone, body=%wide.region_44.46_spmd.clone.sunk | while | flops 19812667392 | bytes 100778128 | solution.py:382
  836.3 15.9 subtract_convert_fusion.4
  895.6 18.5 select_add_fusion.4
  963.3 31.1 %all-gather.46.cloned.1.call-done = bf16[1024,1024]{1,0:T(8,128)(2,1)} async-done(((bf16[128,1024]{1,0:T(8,128)(2,1)}), bf16[1024,1024]{1,0:T(8,128)(2,1)}) %all-gather.46.cloned.1.call-update) | async-done | bytes 2097168 | tf_op jit(solution)/shard_map/all_gather | solution.py:333
  994.4 40.2 %while.225 = (s32[]{:T(128)}, f32[2,512]{1,0:T(2,128)S(1)}, f32[2,512]{1,0:T(2,128)S(1)}, f32[2,512]{1,0:T(2,128)S(1)}, f32[2,512]{1,0:T(2,128)S(1)}, /*index=5*...) while((s32[]{:T(128)}, f32[2,512]{1,0:T(2,128)S(1)}, ...), condition=%wide.region_38.40_spmd.clone, body=%wide.region_33.39_spmd.clone.sunk | while | flops 6613875712 | bytes 39706756 | solution.py:348
  1092.9 90.8 %while.229 = (s32[]{:T(128)}, f32[6286,1024]{1,0:T(8,128)}, bf16[2,512,1024]{2,1,0:T(8,128)(2,1)}, f32[2,512]{1,0:T(2,128)S(1)}, bf16[2,512,1024]{2,1,0:T(8,128)...) while((s32[]{:T(128)}, f32[6286,1024]{1,0:T(8,128)}, ...), condition=%wide.region_75.77_spmd.clone, body=%wide.region_74.76_spmd.clone.sunk | while | flops 19812667392 | bytes 100778128 | solution.py:382
  1093.0 15.9 subtract_convert_fusion.5
  1136.5 15.9 subtract_convert_fusion.5
  1152.4 18.6 select_add_fusion.5
  1184.4 32.4 %reduce-scatter.17.cloned.1.call-done = bf16[128,1024]{1,0:T(8,128)(2,1)} async-done(((bf16[1024,1024]{1,0:T(8,128)(2,1)}), bf16[128,1024]{1,0:T(8,128)(2,1)}) %reduce-scatter.17.cloned.1.call-update) | async-done | bytes 262160 | tf_op jit(solution)/shard_map/reduce_scatter | solution.py:385
  1280.1 26.0 while.230
  1507.1 25.5 while.231
  1554.2 16.2 while.228
  1720.5 16.6 all-gather.50.cloned.1.call-done
  1737.2 27.0 scatter_custom_fusion.1
  1778.2 26.8 scatter_custom_fusion
  1878.5 153.9 %reduce-scatter.27.cloned.1.call-done = f32[64,1024]{1,0:T(8,128)} async-done(((f32[2048,1024]{1,0:T(8,128)}), f32[64,1024]{1,0:T(8,128)}) %reduce-scatter.27.cloned.1.call-update) | async-done | bytes 262160 | tf_op jit(solution)/shard_map/reduce_scatter | solution.py:182
  2034.2 129.5 %reduce-scatter.21.cloned.1.call-done = bf16[6286,256]{1,0:T(8,128)(2,1)} async-done(((bf16[6286,1024]{1,0:T(8,128)(2,1)}), bf16[6286,256]{1,0:T(8,128)(2,1)}) %reduce-scatter.21.cloned.1.call-update) | async-done | bytes 3218448 | tf_op jit(solution)/shard_map/reduce_scatter | solution.py:187
  2163.6 126.7 %reduce-scatter.19.cloned.1.call-done = bf16[6286,256]{1,0:T(8,128)(2,1)} async-done(((bf16[6286,1024]{1,0:T(8,128)(2,1)}), bf16[6286,256]{1,0:T(8,128)(2,1)}) %reduce-scatter.19.cloned.1.call-update) | async-done | bytes 3218448 | tf_op jit(solution)/shard_map/reduce_scatter | solution.py:187
  2295.6 194.6 %reduce-scatter.25.cloned.1.call-done = f32[32,4384]{1,0:T(8,128)} async-done(((f32[1024,4384]{1,0:T(8,128)}), f32[32,4384]{1,0:T(8,128)}) %reduce-scatter.25.cloned.1.call-update) | async-done | bytes 561168 | tf_op jit(solution)/shard_map/reduce_scatter | solution.py:181
  2490.2 202.3 %reduce-scatter.23.cloned.1.call-done = f32[32,4384]{1,0:T(8,128)} async-done(((f32[1024,4384]{1,0:T(8,128)}), f32[32,4384]{1,0:T(8,128)}) %reduce-scatter.23.cloned.1.call-update) | async-done | bytes 561168 | tf_op jit(solution)/shard_map/reduce_scatter | solution.py:181
  2698.1 44.5 %all-reduce.158 = (f32[]{:T(128)}, f32[]{:T(128)}) all-reduce(f32[]{:T(128)S(6)} %add.1330, f32[]{:T(128)S(6)} %add.1357), channel_id=1, replica_groups=mesh['dp'=4,'fsdp'=8] {'dp','fsdp'}, use_global_device_ids=true, to_apply=%region_42.44 | all-reduce | flops 2 | bytes 16 | tf_op jit(solution)/shard_map/psum | solution.py:414
  (1502 shorter events, 1246.8 us)
Async XLA Ops:
  8.0 130.9 %all-gather.42.cloned.1.call-start = ((), (), s32[]{:S(2)}) async-start(), calls=%async_computation.10 | async-start | bytes 16097280 | tf_op jit(solution)/shard_map/all_gather | solution.py:176
  12.9 172.0 %reduce-scatter.11.cloned.1.call-start = ((), (), s32[]{:S(2)}) async-start(), calls=%async_computation.11 | async-start | bytes 2359296 | tf_op jit(solution)/shard_map/reduce_scatter | solution.py:320
  151.8 92.6 %reduce-scatter.13.cloned.1.call-start = ((), (), s32[]{:S(2)}) async-start(), calls=%async_computation.13 | async-start | bytes 2359296 | tf_op jit(solution)/shard_map/reduce_scatter | solution.py:320
  164.7 93.8 %all-gather.52.cloned.1.call-start = ((), (), s32[]{:S(2)}) async-start(), calls=%async_computation.22 | async-start | bytes 9461760 | tf_op jit(solution)/shard_map/all_gather | solution.py:170
  166.9 183.8 %all-gather.54.cloned.1.call-start = ((), (), s32[]{:S(2)}) async-start(), calls=%async_computation.23 | async-start | bytes 4718592 | tf_op jit(solution)/shard_map/all_gather | solution.py:37
  268.0 21.7 collective-permute-start.2
  305.2 93.3 %all-gather.64.cloned.1.call-start = ((), (), s32[]{:S(2)}) async-start(), calls=%async_computation.28 | async-start | bytes 4718592 | tf_op jit(solution)/shard_map/all_gather | solution.py:37
  310.6 153.0 %all-gather.56.cloned.1.call-start = ((), (), s32[]{:S(2)}) async-start(), calls=%async_computation.24 | async-start | bytes 4325376 | tf_op jit(solution)/shard_map/all_gather | solution.py:171
  311.5 234.6 %all-gather.58.cloned.1.call-start = ((), (), s32[]{:S(2)}) async-start(), calls=%async_computation.25 | async-start | bytes 9461760 | tf_op jit(solution)/shard_map/all_gather | solution.py:170
  312.2 326.6 %all-gather.60.cloned.1.call-start = ((), (), s32[]{:S(2)}) async-start(), calls=%async_computation.26 | async-start | bytes 4718592 | tf_op jit(solution)/shard_map/all_gather | solution.py:37
  594.9 109.3 %all-gather.62.cloned.1.call-start = ((), (), s32[]{:S(2)}) async-start(), calls=%async_computation.27 | async-start | bytes 4325376 | tf_op jit(solution)/shard_map/all_gather | solution.py:171
  595.6 141.9 %all-gather.44.cloned.1.call-start = ((), (), s32[]{:S(2)}) async-start(), calls=%async_computation.12 | async-start | bytes 2359296 | tf_op jit(solution)/shard_map/all_gather | solution.py:333
  709.3 230.4 %all-gather.66.cloned.1.call-start = ((), (), s32[]{:S(2)}) async-start(), calls=%async_computation.29 | async-start | bytes 4718592 | tf_op jit(solution)/shard_map/all_gather | solution.py:37
  716.7 243.4 %reduce-scatter.15.cloned.1.call-start = ((), (), s32[]{:S(2)}) async-start(), calls=%async_computation.15 | async-start | bytes 2359296 | tf_op jit(solution)/shard_map/reduce_scatter | solution.py:385
  926.8 67.6 %all-gather.46.cloned.1.call-start = ((), (), s32[]{:S(2)}) async-start(), calls=%async_computation.14 | async-start | bytes 2359296 | tf_op jit(solution)/shard_map/all_gather | solution.py:333
  962.5 254.2 %reduce-scatter.17.cloned.1.call-start = ((), (), s32[]{:S(2)}) async-start(), calls=%async_computation.16 | async-start | bytes 2359296 | tf_op jit(solution)/shard_map/reduce_scatter | solution.py:385
  1183.8 96.3 %all-gather.72.cloned.1.call-start = ((), (), s32[]{:S(2)}) async-start(), calls=%async_computation.32 | async-start | bytes 4718592 | tf_op jit(solution)/shard_map/all_gather | solution.py:57
  1231.7 95.5 %all-gather.68.cloned.1.call-start = ((), (), s32[]{:S(2)}) async-start(), calls=%async_computation.30 | async-start | bytes 4718592 | tf_op jit(solution)/shard_map/all_gather | solution.py:57
  1234.3 272.8 %all-gather.74.cloned.1.call-start = ((), (), s32[]{:S(2)}) async-start(), calls=%async_computation.33 | async-start | bytes 4718592 | tf_op jit(solution)/shard_map/all_gather | solution.py:57
  1388.5 24.2 collective-permute-start.6
  1461.6 92.7 %all-gather.70.cloned.1.call-start = ((), (), s32[]{:S(2)}) async-start(), calls=%async_computation.31 | async-start | bytes 4718592 | tf_op jit(solution)/shard_map/all_gather | solution.py:57
  1463.4 273.7 %all-gather.50.cloned.1.call-start = ((), (), s32[]{:S(2)}) async-start(), calls=%async_computation.19 | async-start | bytes 2359296 | tf_op jit(solution)/shard_map/all_gather | solution.py:402
  1628.5 37.0 %collective-permute-start.7 = (f32[3,2304]{1,0:T(4,128)}, f32[3,2304]{1,0:T(4,128)}, u32[]{:S(2)}, u32[]{:S(2)}) collective-permute-start(f32[3,2304]{1,0:T(4,128)} %copy.582), channel_id=1, source_target_pairs={{1,0},{2,1},{3,2},{4,3},{5,4},{6,5},{7,6},{9,8},{10,9},{11,10},{12... | collective-permute-start | bytes 82952 | tf_op jit(solution)/shard_map/ppermute | solution.py:31
  1651.1 24.3 collective-permute-start.5
  1703.7 74.5 %all-gather.48.cloned.1.call-start = ((), (), s32[]{:S(2)}) async-start(), calls=%async_computation.17 | async-start | bytes 2359296 | tf_op jit(solution)/shard_map/all_gather | solution.py:402
  1704.3 174.1 %reduce-scatter.29.cloned.1.call-start = ((), (), s32[]{:S(2)}) async-start(), calls=%async_computation.37 | async-start | bytes 8650752 | tf_op jit(solution)/shard_map/reduce_scatter | solution.py:182
  1712.1 320.3 %reduce-scatter.27.cloned.1.call-start = ((), (), s32[]{:S(2)}) async-start(), calls=%async_computation.36 | async-start | bytes 8650752 | tf_op jit(solution)/shard_map/reduce_scatter | solution.py:182
  1720.5 443.2 %reduce-scatter.21.cloned.1.call-start = ((), (), s32[]{:S(2)}) async-start(), calls=%async_computation.20 | async-start | bytes 16097280 | tf_op jit(solution)/shard_map/reduce_scatter | solution.py:187
  1777.9 512.4 %reduce-scatter.19.cloned.1.call-start = ((), (), s32[]{:S(2)}) async-start(), calls=%async_computation.18 | async-start | bytes 16097280 | tf_op jit(solution)/shard_map/reduce_scatter | solution.py:187
  1818.7 671.5 %reduce-scatter.25.cloned.1.call-start = ((), (), s32[]{:S(2)}) async-start(), calls=%async_computation.35 | async-start | bytes 18923520 | tf_op jit(solution)/shard_map/reduce_scatter | solution.py:181
  1841.3 851.1 %reduce-scatter.23.cloned.1.call-start = ((), (), s32[]{:S(2)}) async-start(), calls=%async_computation.34 | async-start | bytes 18923520 | tf_op jit(solution)/shard_map/reduce_scatter | solution.py:181
  1863.9 832.7 %all-reduce.161.cloned.1.call-start = ((), (), s32[]{:S(2)}) async-start(), calls=%async_computation.21 | async-start | bytes 245760 | tf_op jit(solution)/shard_map/psum | solution.py:414
  (395 other events, 8113.4 us)
Sparse Core Ops, SparseCore 0:
  13.0 125.8 all-gather.41
  151.9 32.9 reduce-scatter.10
  187.8 56.5 reduce-scatter.12
  305.3 45.3 all-gather.53
  352.7 45.7 all-gather.63
  401.9 61.6 all-gather.55
  467.0 78.9 all-gather.57
  595.0 43.8 all-gather.59
  642.4 61.6 all-gather.61
  709.5 27.9 all-gather.43
  739.6 45.0 all-gather.65
  926.9 33.0 reduce-scatter.14
  962.7 31.6 all-gather.45
  1183.9 32.7 reduce-scatter.16
  1231.8 48.1 all-gather.71
  1281.5 45.6 all-gather.67
  1461.7 45.3 all-gather.73
  1508.5 45.6 all-gather.69
  1703.9 33.2 all-gather.49
  1739.2 36.2 all-gather.47
  1877.1 130.4 all-reduce.160
Sparse Core Ops, SparseCore 1:
  168.6 89.8 all-gather.51
  1712.1 166.3 reduce-scatter.28
  1880.6 151.7 reduce-scatter.26
  2035.5 128.0 reduce-scatter.20
  2166.8 123.4 reduce-scatter.18
  2292.7 197.5 reduce-scatter.24
  2492.4 200.0 reduce-scatter.22
where the time goes:
time: 2800 us; the launch traced here: 2780 us
  waiting for transfers between devices  1440 us (51%)
  matrix products  493 us (18%)
  other arithmetic  422 us (15%)
  blocking collectives  195 us (7%)
  local copies, waits for them, and re-layouts  169 us (6%)
  between operations  30.1 us (1%)
    reduce_scatter x2, waiting for transfers between devices, send_layer(): lax.psum_scatter(grad_in, ('dp', 'fsdp'), scatter_dimension=0, tiled=True)  397 us
    reduce_scatter x2, waiting for transfers between devices, send_table(): lax.psum_scatter(table_grad.astype(jnp.bfloat16), 'dp', scatter_dimension...  256 us
    reduce_scatter x2, waiting for transfers between devices, send_layer(): lax.psum_scatter(grad_out, ('dp', 'fsdp'), scatter_dimension=0, tiled=True)  155 us
    all_gather x1, waiting for transfers between devices, fetch_table(): return lax.all_gather(embed_low, 'dp', axis=1, tiled=True)  125 us
    all_gather x8, blocking collectives, merged(): everything = jax.tree.map(lambda part: lax.all_gather(part, axis), shard)  110 us
    all_gather x2, waiting for transfers between devices, fetch_layer(): lax.all_gather(out_low[layer_index], ('dp', 'fsdp'), axis=0, tiled=True)  97.3 us
    all_gather x2, waiting for transfers between devices, fetch_layer(): lax.all_gather(in_low[layer_index], ('dp', 'fsdp'), axis=0, tiled=True)  89.5 us
    all_gather x4, waiting for transfers between devices, carried_in(): lax.all_gather(a.astype(kind), axis)  81.9 us
  transfers between devices with their start and end apart: 36, of which 25 were waited for; matrix products, arithmetic and copies ran while one was open for 22% of the time, Pallas kernels for 0%

commit v1 on v0

v1 whole, which is shorter than its diff:
```python
import functools

import jax
import jax.numpy as jnp
from jax import lax
from jax.experimental import pallas as pl
from jax.experimental.pallas import tpu as pltpu
from jax.sharding import PartitionSpec as P


D = 1024
HEADS = 32
HDIM = 64
NSTATE = 128
CONV = 4
VOCAB = 50288
LAYERS = 2
MB = 2
DI = 2048
XBC = 2304
PER = 14688
LANES = 128
PAIRS = DI // LANES

epsilon = 1e-05
z_weight = 0.001
clip_limit = 0.2
step_rate = 1000.0
highest = lax.Precision.HIGHEST
bf16 = jnp.bfloat16
f32 = jnp.float32
VMEM_LIMIT = 62 * 1024 * 1024
OFF = -1e30


def dot_nn(a, b, precision=None):
    return lax.dot_general(
        a, b, (((1,), (0,)), ((), ())), precision=precision, preferred_element_type=f32
    )


def dot_nt(a, b, precision=None):
    return lax.dot_general(
        a, b, (((1,), (1,)), ((), ())), precision=precision, preferred_element_type=f32
    )


def dot_tn(a, b, precision=None):
    return lax.dot_general(
        a, b, (((0,), (0,)), ((), ())), precision=precision, preferred_element_type=f32
    )


def silu(v):
    return v * lax.logistic(v)


def silu_grad(v):
    s = lax.logistic(v)
    return s * (1.0 + v * (1.0 - s))


def local_call(kernel, ins, outs, scratch=(), in_smem=(), flops=0):
    total = sum(a.size * a.dtype.itemsize for a in ins)
    return pl.pallas_call(
        kernel,
        out_shape=[jax.ShapeDtypeStruct(shape, kind) for shape, kind in outs],
        in_specs=[
            pl.BlockSpec(memory_space=pltpu.SMEM if i in in_smem else pltpu.VMEM)
            for i in range(len(ins))
        ],
        out_specs=[pl.BlockSpec(memory_space=pltpu.VMEM) for _ in outs],
        scratch_shapes=list(scratch),
        compiler_params=pltpu.CompilerParams(vmem_limit_bytes=VMEM_LIMIT),
        cost_estimate=pl.CostEstimate(
            flops=flops or total, transcendentals=0, bytes_accessed=2 * total
        ),
    )(*ins)


def lookup_kernel(count_ref, row_ref, tok_ref, table_ref, out_ref, held):
    tokens = out_ref.shape[0]
    step = 512

    def clear(i, _):
        held[pl.ds(pl.multiple_of(i * step, step), step), :] = jnp.zeros(
            (step, held.shape[1]), f32
        )
        return 0

    lax.fori_loop(0, tokens // step, clear, 0)

    def move(i, _):
        for k in range(8):
            row = row_ref[i * 8 + k]
            tok = tok_ref[i * 8 + k]
            held[pl.ds(tok, 1), :] = table_ref[pl.ds(row, 1), :]
        return 0

    lax.fori_loop(0, (count_ref[0] + 7) // 8, move, 0)

    def put(i, _):
        rows = pl.ds(pl.multiple_of(i * step, step), step)
        out_ref[rows, :] = held[rows, :].astype(bf16)
        return 0

    lax.fori_loop(0, tokens // step, put, 0)


def spread_kernel(count_ref, row_ref, tok_ref, grad_ref, base_ref, out_ref, held):
    tokens = grad_ref.shape[0]
    step = 512
    rows_all = out_ref.shape[0]

    def take(i, _):
        rows = pl.ds(pl.multiple_of(i * step, step), step)
        held[rows, :] = grad_ref[rows, :].astype(f32)
        return 0

    lax.fori_loop(0, tokens // step, take, 0)
    held[pl.ds(tokens, 8), :] = jnp.zeros((8, held.shape[1]), f32)

    whole = rows_all // step

    def start(i, _):
        rows = pl.ds(pl.multiple_of(i * step, step), step)
        out_ref[rows, :] = base_ref[rows, :].astype(f32)
        return 0

    lax.fori_loop(0, whole, start, 0)
    if rows_all > whole * step:
        out_ref[whole * step :, :] = base_ref[whole * step :, :].astype(f32)

    def move(i, _):
        for k in range(8):
            row = row_ref[i * 8 + k]
            tok = tok_ref[i * 8 + k]
            out_ref[pl.ds(row, 1), :] = out_ref[pl.ds(row, 1), :] + held[pl.ds(tok, 1), :]
        return 0

    lax.fori_loop(0, (count_ref[0] + 7) // 8, move, 0)


MESH = pl.DeviceIdType.MESH


def remote(src, dst, send, recv, dp, fsdp):
    return pltpu.make_async_remote_copy(
        src_ref=src,
        dst_ref=dst,
        send_sem=send,
        recv_sem=recv,
        device_id=(dp, fsdp),
        device_id_type=MESH,
    )


def comm_call(kernel, number, ins, outs, scratch, in_spaces, out_spaces, sent):
    return pl.pallas_call(
        kernel,
        out_shape=[jax.ShapeDtypeStruct(shape, kind) for shape, kind in outs],
        in_specs=[pl.BlockSpec(memory_space=space) for space in in_spaces],
        out_specs=[pl.BlockSpec(memory_space=space) for space in out_spaces],
        scratch_shapes=list(scratch),
        compiler_params=pltpu.CompilerParams(
            collective_id=number, has_side_effects=True, vmem_limit_bytes=VMEM_LIMIT
        ),
        cost_estimate=pl.CostEstimate(flops=sent, transcendentals=0, bytes_accessed=2 * sent),
    )(*ins)


def chain_kernel(direction, steps, decay_ref, local_ref, out_ref, got, give, send, recv):
    dp = lax.axis_index("dp")
    me = lax.axis_index("fsdp")
    place = me // MB
    count = lax.axis_size("fsdp") // MB
    first = place == (0 if direction > 0 else count - 1)
    final = place == (count - 1 if direction > 0 else 0)
    part = DI // steps
    heads = part // HDIM
    barrier = pltpu.get_barrier_semaphore()

    @pl.when(jnp.logical_not(first))
    def _():
        pl.semaphore_signal(
            barrier, inc=1, device_id=(dp, me - MB * direction), device_id_type=MESH
        )

    @pl.when(jnp.logical_not(final))
    def _():
        pl.semaphore_wait(barrier, 1)

    @pl.when(first)
    def _():
        got[...] = jnp.zeros(got.shape, bf16)

    def copy(g):
        rows = pl.ds(g * part, part)
        return remote(
            give.at[rows], got.at[rows], send.at[g], recv.at[g], dp, me + MB * direction
        )

    for g in range(steps):
        rows = pl.ds(g * part, part)

        @pl.when(jnp.logical_not(first))
        def _():
            copy(g).wait_recv()

        @pl.when(jnp.logical_not(final))
        def _():
            for i in range(heads):
                h = pl.ds(g * part + i * HDIM, HDIM)
                give[h, :] = (
                    decay_ref[g * heads + i] * got[h, :].astype(f32) + local_ref[h, :]
                ).astype(bf16)
            copy(g).start()

        out_ref[rows, :] = got[rows, :]

    @pl.when(jnp.logical_not(final))
    def _():
        for g in range(steps):
            copy(g).wait_send()


CHAIN_STEPS = 8


def carry_chain(decay, local, direction):
    return comm_call(
        functools.partial(chain_kernel, direction, CHAIN_STEPS),
        1 if direction > 0 else 2,
        (decay, local),
        ((local.shape, bf16),),
        (
            pltpu.VMEM(local.shape, bf16),
            pltpu.VMEM(local.shape, bf16),
            pltpu.SemaphoreType.DMA((CHAIN_STEPS,)),
            pltpu.SemaphoreType.DMA((CHAIN_STEPS,)),
        ),
        (pltpu.SMEM, pltpu.VMEM),
        (pltpu.VMEM,),
        local.size * 2,
    )[0]


def bits_of(size):
    return [1 << b for b in range(size.bit_length() - 1)]


def total_kernel(in_ref, out_ref, work, got, send, recv):
    dp = lax.axis_index("dp")
    me = lax.axis_index("fsdp")
    half = in_ref.shape[0] // 2
    core = me % MB
    partners = [("f", b) for b in bits_of(lax.axis_size("fsdp")) if b > 1]
    partners += [("d", b) for b in bits_of(lax.axis_size("dp"))]

    def across(kind, bit):
        ids, other = (me, lambda v: (dp, v)) if kind == "f" else (dp, lambda v: (v, me))
        return other(jnp.where((ids // bit) % 2 == 1, ids - bit, ids + bit))

    mate = across("f", 1)
    barrier = pltpu.get_barrier_semaphore()
    for target in [mate] + [across(*p) for p in partners]:
        pl.semaphore_signal(barrier, inc=1, device_id=target, device_id_type=MESH)
    pl.semaphore_wait(barrier, 1 + len(partners))

    mine = pl.ds(pl.multiple_of(core * half, 8), half)
    theirs = pl.ds(pl.multiple_of((1 - core) * half, 8), half)
    copy = remote(in_ref.at[theirs], got.at[0], send.at[0], recv.at[0], *mate)
    copy.start()
    copy.wait()
    work[0] = in_ref[mine, :] + got[0]
    for i, p in enumerate(partners):
        copy = remote(work.at[i], got.at[i + 1], send.at[i + 1], recv.at[i + 1], *across(*p))
        copy.start()
        copy.wait()
        work[i + 1] = work[i] + got[i + 1]
    n = len(partners)
    copy = remote(work.at[n], got.at[n + 1], send.at[n + 1], recv.at[n + 1], *mate)
    copy.start()
    copy.wait()
    out_ref[mine, :] = work[n]
    out_ref[theirs, :] = got[n + 1]


def total_of(array):
    rows = array.shape[0]
    steps = len(bits_of(lax.axis_size("fsdp"))) - 1 + len(bits_of(lax.axis_size("dp")))
    return comm_call(
        total_kernel,
        3,
        (array,),
        ((array.shape, f32),),
        (
            pltpu.VMEM((steps + 1, rows // 2, LANES), f32),
            pltpu.VMEM((steps + 2, rows // 2, LANES), f32),
            pltpu.SemaphoreType.DMA((steps + 2,)),
            pltpu.SemaphoreType.DMA((steps + 2,)),
        ),
        (pltpu.VMEM,),
        (pltpu.VMEM,),
        array.size * 4 * 3,
    )[0]


def snake(place, size):
    return jnp.where(place < size // 2, place, size // 2 + size - 1 - place)


def wrap(value, size):
    return lax.rem(value + size, size)


def gather_kernel(*refs):
    arrays = 2 * LAYERS
    own = refs[:arrays]
    full = refs[arrays : 2 * arrays]
    local_sem, z_send, z_recv, ring_send, ring_recv, mate_send, mate_recv = refs[2 * arrays :]
    dp = lax.axis_index("dp")
    me = lax.axis_index("fsdp")
    size = lax.axis_size("dp")
    count = lax.axis_size("fsdp") // MB
    core = me % MB
    k = me // MB
    ring = snake(dp, size)
    reach = size // 2
    right = snake(wrap(ring + 1, size), size)
    left = snake(wrap(ring - 1, size), size)
    mate = k * MB + 1 - core
    up, down = me + MB, me - MB
    has_up, has_down = k < count - 1, k > 0
    barrier = pltpu.get_barrier_semaphore()
    for target in ((right, me), (left, me), (dp, mate)):
        pl.semaphore_signal(barrier, inc=1, device_id=target, device_id_type=MESH)

    @pl.when(has_up)
    def _():
        pl.semaphore_signal(barrier, inc=1, device_id=(dp, up), device_id_type=MESH)

    @pl.when(has_down)
    def _():
        pl.semaphore_signal(barrier, inc=1, device_id=(dp, down), device_id_type=MESH)

    pl.semaphore_wait(barrier, 3 + jnp.where(has_up, 1, 0) + jnp.where(has_down, 1, 0))

    def spot(a, d, z, c):
        return full[a].at[d, z, c]

    def chain(a, src, z, side):
        return remote(
            src, spot(a, dp, z, core), z_send.at[a, z], z_recv.at[a, z], dp, up if side == 0 else down
        )

    def chain_own(a, side):
        return remote(
            own[a],
            spot(a, dp, k, core),
            z_send.at[a, count + side],
            z_recv.at[a, k],
            dp,
            up if side == 0 else down,
        )

    def round_ring(a, src, d, z, side):
        return remote(
            src,
            spot(a, d, z, core),
            ring_send.at[a, side],
            ring_recv.at[a, d, z],
            right if side == 0 else left,
            me,
        )

    def to_mate(a, src, d, z):
        return remote(src, spot(a, d, z, core), mate_send.at[a], mate_recv.at[a], dp, mate)

    def carried(a, side):
        return (a < arrays // 2) == (side == 0)

    for a in range(arrays):

        @pl.when(has_up)
        def _(a=a):
            chain_own(a, 0).start()

        @pl.when(has_down)
        def _(a=a):
            chain_own(a, 1).start()

    for a in range(arrays):
        for side in (0, 1):
            round_ring(a, own[a], dp, k, side).start()
    for a in range(arrays):
        to_mate(a, own[a], dp, k).start()
        pltpu.make_async_copy(own[a], spot(a, dp, k, core), local_sem.at[a]).start()

    def ring_step(z, s):
        for side in (0, 1):
            origin = snake(wrap(ring - s if side == 0 else ring + s, size), size)
            for a in range(arrays):
                if s == reach and not carried(a, side):
                    continue
                piece = spot(a, origin, z, core)
                round_ring(a, piece, origin, z, side).wait_recv()
                if s + 1 < reach or (s + 1 == reach and carried(a, side)):
                    round_ring(a, piece, origin, z, side).start()
                to_mate(a, piece, origin, z).start()

    def arrive(z, side):
        for a in range(arrays):
            piece = spot(a, dp, z, core)
            chain(a, piece, z, side).wait_recv()

            @pl.when(has_up if side == 0 else has_down)
            def _(a=a, piece=piece):
                chain(a, piece, z, side).start()

            for way in (0, 1):
                round_ring(a, piece, dp, z, way).start()
            to_mate(a, piece, dp, z).start()

    def both_ways(far, act):
        if far == 0:
            act(k, 0)
            return

        @pl.when(k >= far)
        def _():
            act(k - far, 0)

        @pl.when(k + far < count)
        def _():
            act(k + far, 1)

    for turn in range(1, count + reach):
        if turn < count:
            both_ways(turn, arrive)
        for s in range(1, reach + 1):
            if 0 <= turn - s < count:
                both_ways(turn - s, lambda z, side, s=s: ring_step(z, s))

    for a in range(arrays):
        pltpu.make_async_copy(own[a], spot(a, dp, k, core), local_sem.at[a]).wait()
        for side in (0, 1):
            sent = full[a].at[pl.ds(0, reach if carried(a, side) else reach - 1), :, core]
            remote(sent, sent, ring_send.at[a, side], ring_recv.at[a, 0, 0], dp, mate).wait_send()
        whole = full[a].at[:, :, core]
        remote(whole, whole, mate_send.at[a], mate_recv.at[a], dp, mate).wait_send()
        whole = full[a].at[:, :, 1 - core]
        remote(whole, whole, mate_send.at[a], mate_recv.at[a], dp, mate).wait_recv()

        @pl.when(has_up)
        def _(a=a):
            chain_own(a, 0).wait_send()

        @pl.when(has_down)
        def _(a=a):
            chain_own(a, 1).wait_send()

        for far in range(1, count):

            @pl.when(jnp.logical_and(k >= far, has_up))
            def _(a=a, far=far):
                chain(a, spot(a, dp, k - far, core), k - far, 0).wait_send()

            @pl.when(jnp.logical_and(k + far < count, has_down))
            def _(a=a, far=far):
                chain(a, spot(a, dp, k + far, core), k + far, 1).wait_send()


def gather_layers(shards):
    size, count = lax.axis_size("dp"), lax.axis_size("fsdp") // MB
    arrays = len(shards)
    outs = comm_call(
        gather_kernel,
        4,
        shards,
        tuple(((size, count, MB) + s.shape, bf16) for s in shards),
        (
            pltpu.SemaphoreType.DMA((arrays,)),
            pltpu.SemaphoreType.DMA((arrays, count + 2)),
            pltpu.SemaphoreType.DMA((arrays, count)),
            pltpu.SemaphoreType.DMA((arrays, 2)),
            pltpu.SemaphoreType.DMA((arrays, size, count)),
            pltpu.SemaphoreType.DMA((arrays,)),
            pltpu.SemaphoreType.DMA((arrays,)),
        ),
        (pltpu.VMEM,) * arrays,
        (pl.ANY,) * arrays,
        sum(s.size * 2 for s in shards) * 24,
    )
    return [o.reshape(size * count * MB * s.shape[0], s.shape[1]) for o, s in zip(outs, shards)]


def add_rows(dst, first, *others):
    rows = dst.shape[0]
    step = min(rows, 16)

    def one(i, _):
        at = pl.ds(pl.multiple_of(i * step, step), step)
        total = first[at, :].astype(f32)
        for other in others:
            total = total + other[at, :].astype(f32)
        dst[at, :] = total.astype(dst.dtype)
        return 0

    lax.fori_loop(0, rows // step, one, 0)


def reduce_kernel(*refs):
    arrays = 2 * LAYERS
    grads = refs[:arrays]
    outs = refs[arrays : 2 * arrays]
    held, given, come, chained = (
        refs[(2 + i) * arrays : (3 + i) * arrays] for i in range(4)
    )
    load_sem, mate_send, mate_recv, ring_send, ring_recv, z_send, z_recv = refs[6 * arrays :]
    dp = lax.axis_index("dp")
    me = lax.axis_index("fsdp")
    size = lax.axis_size("dp")
    count = lax.axis_size("fsdp") // MB
    core = me % MB
    k = me // MB
    ring = snake(dp, size)
    reach = size // 2
    right = snake(wrap(ring + 1, size), size)
    left = snake(wrap(ring - 1, size), size)
    mate = k * MB + 1 - core
    up, down = me + MB, me - MB
    has_up, has_down = k < count - 1, k > 0

    def load(a):
        return pltpu.make_async_copy(grads[a].at[:, :, core], held[a], load_sem.at[a])

    for a in range(arrays):
        load(a).start()
    barrier = pltpu.get_barrier_semaphore()
    for target in ((right, me), (left, me), (dp, mate)):
        pl.semaphore_signal(barrier, inc=1, device_id=target, device_id_type=MESH)

    @pl.when(has_up)
    def _():
        pl.semaphore_signal(barrier, inc=1, device_id=(dp, up), device_id_type=MESH)

    @pl.when(has_down)
    def _():
        pl.semaphore_signal(barrier, inc=1, device_id=(dp, down), device_id_type=MESH)

    pl.semaphore_wait(barrier, 3 + jnp.where(has_up, 1, 0) + jnp.where(has_down, 1, 0))

    def away(j, side):
        return snake(wrap(ring + j if side == 0 else ring - j, size), size)

    def to_mate(a, d):
        return remote(
            grads[a].at[d, :, 1 - core], given[a].at[d], mate_send.at[a], mate_recv.at[a, d], dp, mate
        )

    def carried(a, side):
        return (a < arrays // 2) == (side == 0)

    def targets(j):
        if j == 0:
            return [dp]
        if j == reach:
            return [away(j, 0)]
        return [away(j, 0), away(j, 1)]

    for j in range(reach, -1, -1):
        for d in targets(j):
            for a in range(arrays):
                to_mate(a, d).start()

    for a in range(arrays):
        load(a).wait()

    def add_mate(d):
        for a in range(arrays):
            to_mate(a, d).wait_recv()

            def one(z, _, a=a):
                add_rows(held[a].at[d, z], held[a].at[d, z], given[a].at[d, z])
                return 0

            lax.fori_loop(0, count, one, 0)

    def first_step(a, side):
        d = away(reach, 0)
        return remote(
            held[a].at[d], come[a].at[side, 0], ring_send.at[a, side], ring_recv.at[a, side, 0, 0],
            right if side == 0 else left, me,
        )

    def next_step(a, side, s, z):
        d = away(reach - s, side)
        return remote(
            held[a].at[d, z], come[a].at[side, s, z], ring_send.at[a, side],
            ring_recv.at[a, side, s, z], right if side == 0 else left, me,
        )

    far_most = jnp.maximum(k, count - 1 - k)
    near_most = jnp.minimum(k, count - 1 - k)
    uneven = far_most - near_most
    long_side = jnp.where(count - 1 - k > k, 1, -1)

    def chunk_at(i):
        j = jnp.maximum(i - uneven, 0)
        paired = k + (1 - 2 * (j % 2)) * (near_most - j // 2)
        return jnp.where(i < uneven, k + long_side * (far_most - i), paired)

    add_mate(away(reach, 0))
    for a in range(arrays):
        first_step(a, 0 if carried(a, 0) else 1).start()
    for s in range(1, reach):
        for side in (0, 1):
            add_mate(away(reach - s, side))
        if s == 1:
            for a in range(arrays):
                first_step(a, 0 if carried(a, 0) else 1).wait_recv()

        def pass_on(i, _, s=s):
            z = chunk_at(i)
            for side in (0, 1):
                d = away(reach - s, side)
                for a in range(arrays):
                    if s > 1:
                        next_step(a, side, s - 1, z).wait_recv()
                    if s > 1 or carried(a, side):
                        add_rows(held[a].at[d, z], held[a].at[d, z], come[a].at[side, s - 1, z])
                    next_step(a, side, s, z).start()
            return 0

        lax.fori_loop(0, count, pass_on, 0)
    add_mate(dp)

    def along(a, side, z):
        return remote(
            held[a].at[dp, z], chained[a].at[side, z], z_send.at[a, z], z_recv.at[a, side, z],
            dp, up if side == 0 else down,
        )

    def finish(i, _):
        z = chunk_at(i)
        for a in range(arrays):
            for side in (0, 1):
                next_step(a, side, reach - 1, z).wait_recv()
            add_rows(
                held[a].at[dp, z],
                held[a].at[dp, z],
                come[a].at[0, reach - 1, z],
                come[a].at[1, reach - 1, z],
            )
            for side in (0, 1):
                beyond = z > k if side == 0 else z < k
                fed = has_down if side == 0 else has_up

                @pl.when(jnp.logical_and(fed, jnp.logical_or(beyond, z == k)))
                def _(a=a, side=side):
                    along(a, side, z).wait_recv()
                    add_rows(held[a].at[dp, z], held[a].at[dp, z], chained[a].at[side, z])

                @pl.when(beyond)
                def _(a=a, side=side):
                    along(a, side, z).start()

        return 0

    lax.fori_loop(0, count, finish, 0)
    for a in range(arrays):
        add_rows(outs[a], held[a].at[dp, k])
        for side in (0, 1):
            sent = held[a].at[pl.ds(0, reach if carried(a, side) else reach - 1)]
            remote(
                sent, sent, ring_send.at[a, side], ring_recv.at[a, side, 0, 0], dp, mate
            ).wait_send()
        remote(
            given[a], given[a], mate_send.at[a], mate_recv.at[a, 0], dp, mate
        ).wait_send()

    def sent_along(z, _):
        for a in range(arrays):

            @pl.when(z != k)
            def _(a=a):
                along(a, 0, z).wait_send()

        return 0

    lax.fori_loop(0, count, sent_along, 0)


def reduce_layers(grads):
    size, count = lax.axis_size("dp"), lax.axis_size("fsdp") // MB
    arrays = len(grads)
    reach = size // 2
    shards = [(g.shape[0] // (size * count * MB), g.shape[1]) for g in grads]
    blocks = [g.reshape((size, count, MB) + s) for g, s in zip(grads, shards)]
    return comm_call(
        reduce_kernel,
        5,
        blocks,
        tuple((s, f32) for s in shards),
        tuple(pltpu.VMEM((size, count) + s, bf16) for s in shards) * 2
        + tuple(pltpu.VMEM((2, reach, count) + s, bf16) for s in shards)
        + tuple(pltpu.VMEM((2, count) + s, bf16) for s in shards)
        + (
            pltpu.SemaphoreType.DMA((arrays,)),
            pltpu.SemaphoreType.DMA((arrays,)),
            pltpu.SemaphoreType.DMA((arrays, size)),
            pltpu.SemaphoreType.DMA((arrays, 2)),
            pltpu.SemaphoreType.DMA((arrays, 2, reach, count)),
            pltpu.SemaphoreType.DMA((arrays, count)),
            pltpu.SemaphoreType.DMA((arrays, 2, count)),
        ),
        (pl.ANY,) * arrays,
        (pltpu.VMEM,) * arrays,
        sum(g.size * 2 for g in grads),
    )


def pair_lanes(p):
    return pl.ds(pl.multiple_of(p * LANES, LANES), LANES)


def first_half(rows):
    return lax.broadcasted_iota(jnp.int32, (rows, LANES), 1) < HDIM


def spread_columns(values, column, per_pair, rows):
    half = first_half(rows)
    for p in range(PAIRS):
        left = jnp.broadcast_to(values[:, 2 * p : 2 * p + 1], (rows, LANES))
        right = jnp.broadcast_to(values[:, 2 * p + 1 : 2 * p + 2], (rows, LANES))
        if column is not None:
            column[2 * p] = left
            column[2 * p + 1] = right
        if per_pair is not None:
            per_pair[p] = jnp.where(half, left, right)


def front_kernel(
    proj_ref, halo_ref, cw_ref, cb_ref, dtb_ref, al_ref, sk_ref,
    pre_ref, y_ref, st_ref, dt_ref, cum_ref,
    pad, col, tcol, lcol, lrow,
):
    rows = proj_ref.shape[0]
    pad[0:8, :] = halo_ref[...]
    pad[8:, :] = proj_ref[:, DI : DI + XBC]

    def conv(i, _):
        xs = pair_lanes(i)
        out = jnp.broadcast_to(cb_ref[0:1, xs], (rows, LANES))
        for k in range(CONV):
            out = out + cw_ref[k : k + 1, xs] * pad[5 + k : 5 + k + rows, xs]
        pre_ref[:, xs] = out
        return 0

    lax.fori_loop(0, XBC // LANES, conv, 0)

    dt_ref[...] = jnp.zeros((rows, LANES), f32)
    dt_ref[:, 0:HEADS] = proj_ref[:, DI + XBC :]
    drive = dt_ref[...] + dtb_ref[...]
    dt = jnp.maximum(drive, 0.0) + jnp.log1p(jnp.exp(-jnp.abs(drive)))
    dt_ref[...] = dt
    rate = dt * (-jnp.exp(al_ref[...]))
    ri = lax.broadcasted_iota(jnp.int32, (rows, rows), 0)
    ci = lax.broadcasted_iota(jnp.int32, (rows, rows), 1)
    causal = ri >= ci
    cum = dot_nn(jnp.where(causal, 1.0, 0.0), rate, highest)
    cum_ref[...] = cum
    lrow[...] = cum.T
    spread_columns(cum, col, lcol, rows)
    spread_columns(dt, None, tcol, rows)
    bm = silu(pre_ref[:, DI : DI + NSTATE]).astype(bf16)
    cm = silu(pre_ref[:, DI + NSTATE :]).astype(bf16)
    cb = dot_nt(cm, bm)
    half = first_half(rows)

    def pair(p, _):
        xs = pair_lanes(p)
        x = silu(pre_ref[:, xs])
        xt = tcol[p] * x
        xtb = xt.astype(bf16)
        parts = []
        for j in range(2):
            h = 2 * p + j
            c = col[h]
            d = jnp.concatenate([c] * (rows // LANES), axis=1) - lrow[pl.ds(h, 1), :]
            m = (jnp.exp(jnp.where(causal, d, OFF)) * cb).astype(bf16)
            parts.append(dot_nn(m, xtb))
        y_ref[:, xs] = jnp.where(half, parts[0], parts[1]) + sk_ref[0:1, xs] * x
        lp = lcol[p]
        tail = jnp.exp(lp[rows - 1 : rows, :] - lp)
        st_ref[xs, :] = dot_tn((tail * xt).astype(bf16), bm)
        return 0

    lax.fori_loop(0, PAIRS, pair, 0)


def gate_kernel(
    y0_ref, proj_ref, pre_ref, cum_ref, sin_ref, gg_ref, y_ref, yn_ref, lcol
):
    rows = y0_ref.shape[0]
    spread_columns(cum_ref[...], None, lcol, rows)
    cm = silu(pre_ref[:, DI + NSTATE :]).astype(bf16)

    def pair(p, total):
        xs = pair_lanes(p)
        y = y0_ref[:, xs] + jnp.exp(lcol[p]) * dot_nt(cm, sin_ref[xs, :])
        y_ref[:, xs] = y
        g = y * silu(proj_ref[:, xs])
        return total + g * g

    total = lax.fori_loop(0, PAIRS, pair, jnp.zeros((rows, LANES), f32))
    scale = lax.rsqrt(jnp.sum(total, axis=1, keepdims=True) / DI + epsilon)

    def put(p, _):
        xs = pair_lanes(p)
        g = y_ref[:, xs] * silu(proj_ref[:, xs])
        yn_ref[:, xs] = (g * scale * gg_ref[0:1, xs]).astype(bf16)
        return 0

    lax.fori_loop(0, PAIRS, put, 0)


def ungate_kernel(
    dyn_ref, y_ref, proj_ref, pre_ref, cum_ref, gg_ref,
    dy_ref, dz_ref, dgg_ref, gst_ref, lcol,
):
    rows = y_ref.shape[0]
    spread_columns(cum_ref[...], None, lcol, rows)
    cm = silu(pre_ref[:, DI + NSTATE :]).astype(bf16)
    zero = jnp.zeros((rows, LANES), f32)

    def sums(p, carry):
        xs = pair_lanes(p)
        g = y_ref[:, xs] * silu(proj_ref[:, xs])
        return carry[0] + g * g, carry[1] + g * (dyn_ref[:, xs] * gg_ref[0:1, xs])

    square, cross = lax.fori_loop(0, PAIRS, sums, (zero, zero))
    scale = lax.rsqrt(jnp.sum(square, axis=1, keepdims=True) / DI + epsilon)
    mean = jnp.sum(cross, axis=1, keepdims=True) * scale / DI

    def pair(p, _):
        xs = pair_lanes(p)
        z = proj_ref[:, xs]
        y = y_ref[:, xs]
        sz = silu(z)
        ghat = y * sz * scale
        dyn = dyn_ref[:, xs]
        dgg_ref[0:1, xs] = jnp.sum(dyn * ghat, axis=0, keepdims=True)
        dg = scale * (dyn * gg_ref[0:1, xs] - ghat * mean)
        dy = dg * sz
        dy_ref[:, xs] = dy
        dz_ref[:, xs] = (dg * y * silu_grad(z)).astype(bf16)
        gst_ref[xs, :] = dot_tn((jnp.exp(lcol[p]) * dy).astype(bf16), cm)
        return 0

    lax.fori_loop(0, PAIRS, pair, 0)


def back_kernel(
    dy_ref, y_ref, proj_ref, halo_ref, pre_ref, dt_ref, cum_ref, sin_ref, gin_ref,
    cw_ref, dtb_ref, al_ref, sk_ref,
    dx_ref, dhalo_ref, ddr_ref, dcw_ref, dsm_ref,
    pad, grad, col, tcol, lcol, lrow, dcb, dbm, dcm, dlog, dtx, ends,
):
    rows = y_ref.shape[0]
    pad[0:8, :] = halo_ref[...]
    pad[8:, :] = proj_ref[:, DI : DI + XBC]
    grad[0:8, :] = jnp.zeros((8, XBC), f32)
    grad[rows + 8 :, :] = jnp.zeros((8, XBC), f32)
    cum = cum_ref[...]
    dt = dt_ref[...]
    lrow[...] = cum.T
    spread_columns(cum, col, lcol, rows)
    spread_columns(dt, None, tcol, rows)
    bm = silu(pre_ref[:, DI : DI + NSTATE]).astype(bf16)
    cm = silu(pre_ref[:, DI + NSTATE :]).astype(bf16)
    cbt = dot_nt(bm, cm)
    ri = lax.broadcasted_iota(jnp.int32, (rows, rows), 0)
    ci = lax.broadcasted_iota(jnp.int32, (rows, rows), 1)
    causal = ri <= ci
    half = first_half(rows)
    dcb[...] = jnp.zeros((rows, rows), f32)
    zero = jnp.zeros((rows, LANES), f32)
    dbm[...] = zero
    dcm[...] = zero
    dlog[...] = zero
    dtx[...] = zero
    ends[...] = jnp.zeros((16, LANES), f32)
    lane_row = lax.broadcasted_iota(jnp.int32, (LANES, LANES), 0)
    lane_col = lax.broadcasted_iota(jnp.int32, (LANES, LANES), 1)
    ones = jnp.ones((8, NSTATE), f32)

    def pair(p, _):
        xs = pair_lanes(p)
        pre = pre_ref[:, xs]
        x = silu(pre)
        tp = tcol[p]
        xt = tp * x
        dy = dy_ref[:, xs]
        dyb = dy.astype(bf16)
        parts = []
        for j in range(2):
            h = 2 * p + j
            c = col[h]
            d = lrow[pl.ds(h, 1), :] - jnp.concatenate([c] * (rows // LANES), axis=1)
            w = jnp.exp(jnp.where(causal, d, OFF))
            parts.append(dot_nn((w * cbt).astype(bf16), dyb))
            own = half if j == 0 else jnp.logical_not(half)
            q = dot_nt(jnp.where(own, xt, 0.0).astype(bf16), dyb)
            dcb[...] += w * q
        lp = lcol[p]
        last = lp[rows - 1 : rows, :]
        tail = jnp.exp(last - lp)
        gin = gin_ref[xs, :]
        sin = sin_ref[xs, :]
        dst = tail * dot_nt(bm, gin)
        dxt = jnp.where(half, parts[0], parts[1]) + dst
        dbm[...] += dot_nn((tail * xt).astype(bf16), gin)
        dcm[...] += dot_nn((jnp.exp(lp) * dy).astype(bf16), sin)
        sk = sk_ref[0:1, xs]
        pick = jnp.where(lane_col == 2 * p + jnp.where(lane_row >= HDIM, 1, 0), 1.0, 0.0)
        dlog[...] += dot_nn(dy * (y_ref[:, xs] - sk * x) - xt * dxt, pick, highest)
        dtx[...] += dot_nn(x * dxt, pick, highest)
        held = dot_nt(ones, gin.astype(f32) * sin.astype(f32), highest)
        end = jnp.sum(xt * dst, axis=0, keepdims=True) + jnp.exp(last) * held[0:1, :]
        skip = jnp.sum(dy * x, axis=0, keepdims=True)
        stacked = jnp.concatenate(
            [jnp.broadcast_to(end, (8, LANES)), jnp.broadcast_to(skip, (8, LANES))], axis=0
        )
        ends[...] += dot_nn(stacked, pick, highest)
        grad[pl.ds(8, rows), xs] = (tp * dxt + sk * dy) * silu_grad(pre)
        return 0

    lax.fori_loop(0, PAIRS, pair, 0)
    dcbb = dcb[...].astype(bf16)
    dc = dcm[...] + dot_tn(dcbb, bm)
    db = dbm[...] + dot_nn(dcbb, cm)
    grad[8 : 8 + rows, DI : DI + NSTATE] = db * silu_grad(pre_ref[:, DI : DI + NSTATE])
    grad[8 : 8 + rows, DI + NSTATE :] = dc * silu_grad(pre_ref[:, DI + NSTATE :])

    last_row = lax.broadcasted_iota(jnp.int32, (rows, LANES), 0) == rows - 1
    dl = dlog[...] + jnp.where(last_row, ends[0:1, :], 0.0)
    da = dot_nn(jnp.where(causal, 1.0, 0.0), dl, highest)
    decay = -jnp.exp(al_ref[...])
    ddt = dtx[...] + da * decay
    ddr_ref[...] = jnp.zeros((rows, LANES), f32)
    ddr_ref[:, 0:HEADS] = proj_ref[:, DI + XBC :]
    ddr = ddt * lax.logistic(ddr_ref[...] + dtb_ref[...])
    ddr_ref[...] = ddr
    dsm_ref[...] = jnp.zeros((8, LANES), f32)
    dsm_ref[0:1, :] = jnp.sum(ddr, axis=0, keepdims=True)
    dsm_ref[1:2, :] = jnp.sum(da * dt, axis=0, keepdims=True) * decay
    dsm_ref[2:3, :] = ends[8:9, :]

    def conv(i, _):
        xs = pair_lanes(i)
        own = grad[pl.ds(8, rows), xs]
        out = jnp.zeros((rows, LANES), f32)
        edge = jnp.zeros((8, LANES), f32)
        for k in range(CONV):
            wk = cw_ref[k : k + 1, xs]
            out = out + wk * grad[11 - k : 11 - k + rows, xs]
            edge = edge + wk * grad[3 - k : 11 - k, xs]
            dcw_ref[k : k + 1, xs] = jnp.sum(
                own * pad[5 + k : 5 + k + rows, xs], axis=0, keepdims=True
            )
        dcw_ref[4:5, xs] = jnp.sum(own, axis=0, keepdims=True)
        dx_ref[:, xs] = out
        dhalo_ref[:, xs] = edge
        return 0

    lax.fori_loop(0, XBC // LANES, conv, 0)


VTILE = 640
NTILE = 512


def head_specs(width, tokens):
    return dict(
        table=pl.BlockSpec((VTILE, width), lambda i: (i, 0)),
        kept=pl.BlockSpec((VTILE, tokens), lambda i: (i, 0)),
        row=pl.BlockSpec((1, tokens), lambda i: (0, 0)),
        tile_row=pl.BlockSpec((1, 1, tokens), lambda i: (i, 0, 0)),
    )


def head_params():
    return pltpu.CompilerParams(
        dimension_semantics=("arbitrary",), vmem_limit_bytes=VMEM_LIMIT
    )


def head_stats_kernel(vocab_rows, e_ref, ht_ref, lab_ref, q_ref, st_ref):
    first = pl.program_id(0) * VTILE
    tokens = ht_ref.shape[1]
    e = e_ref[...]

    def chunk(j, _):
        ns = pl.ds(pl.multiple_of(j * NTILE, NTILE), NTILE)
        logits = dot_nn(e, ht_ref[:, ns])
        rid = lax.broadcasted_iota(jnp.int32, (VTILE, NTILE), 0) + first
        real = rid < vocab_rows
        shown = jnp.where(real, logits, OFF)
        top = jnp.max(shown, axis=0, keepdims=True)
        p = jnp.exp(shown - top)
        q_ref[:, ns] = p.astype(bf16)
        st_ref[0, 0:1, ns] = top
        st_ref[0, 1:2, ns] = jnp.sum(p, axis=0, keepdims=True)
        hit = jnp.where(jnp.logical_and(real, rid == lab_ref[0:1, ns]), logits, 0.0)
        st_ref[0, 2:3, ns] = jnp.sum(hit, axis=0, keepdims=True)
        st_ref[0, 3:4, ns] = jnp.sum(jnp.where(real, logits, 0.0), axis=0, keepdims=True)
        return 0

    lax.fori_loop(0, tokens // NTILE, chunk, 0)


def head_stats(table, hidden_t, labels):
    vocab_rows, width = table.shape
    tokens = hidden_t.shape[1]
    tiles = pl.cdiv(vocab_rows, VTILE)
    sp = head_specs(width, tokens)
    return pl.pallas_call(
        functools.partial(head_stats_kernel, vocab_rows),
        name="head_stats",
        grid=(tiles,),
        in_specs=[
            sp["table"],
            pl.BlockSpec((width, tokens), lambda i: (0, 0)),
            sp["row"],
        ],
        out_specs=[sp["kept"], pl.BlockSpec((1, 8, tokens), lambda i: (i, 0, 0))],
        out_shape=[
            jax.ShapeDtypeStruct((tiles * VTILE, tokens), bf16),
            jax.ShapeDtypeStruct((tiles, 8, tokens), f32),
        ],
        compiler_params=head_params(),
        cost_estimate=pl.CostEstimate(
            flops=2 * vocab_rows * width * tokens,
            transcendentals=vocab_rows * tokens,
            bytes_accessed=2 * vocab_rows * (width + tokens),
        ),
    )(table, hidden_t, labels)


def logit_grads(q, fac, weight, rid, label):
    hit = jnp.where(rid == label, 0.9 + 0.1 / VOCAB, 0.1 / VOCAB)
    return (q.astype(f32) * fac - weight * hit).astype(bf16)


def head_rows_kernel(vocab_rows, e_ref, q_ref, fac_ref, w_ref, lab_ref, out_ref, et):
    first = pl.program_id(0) * VTILE
    tokens = q_ref.shape[1]

    @pl.when(pl.program_id(0) == 0)
    def _():
        out_ref[...] = jnp.zeros(out_ref.shape, f32)

    eid = lax.broadcasted_iota(jnp.int32, (VTILE, e_ref.shape[1]), 0) + first
    et[...] = jnp.where(eid < vocab_rows, e_ref[...].astype(f32), 0.0).T.astype(bf16)

    def chunk(j, _):
        ns = pl.ds(pl.multiple_of(j * NTILE, NTILE), NTILE)
        rid = lax.broadcasted_iota(jnp.int32, (VTILE, NTILE), 0) + first
        dl = logit_grads(
            q_ref[:, ns], fac_ref[0, 0:1, ns], w_ref[0:1, ns], rid, lab_ref[0:1, ns]
        )
        out_ref[:, ns] += dot_nn(et[...], dl)
        return 0

    lax.fori_loop(0, tokens // NTILE, chunk, 0)


def head_rows(table, kept, fac, weight, labels):
    vocab_rows, width = table.shape
    tokens = kept.shape[1]
    tiles = pl.cdiv(vocab_rows, VTILE)
    sp = head_specs(width, tokens)
    return pl.pallas_call(
        functools.partial(head_rows_kernel, vocab_rows),
        name="head_rows",
        grid=(tiles,),
        in_specs=[sp["table"], sp["kept"], sp["tile_row"], sp["row"], sp["row"]],
        out_specs=pl.BlockSpec((width, tokens), lambda i: (0, 0)),
        out_shape=jax.ShapeDtypeStruct((width, tokens), f32),
        scratch_shapes=[pltpu.VMEM((width, VTILE), bf16)],
        compiler_params=head_params(),
        cost_estimate=pl.CostEstimate(
            flops=2 * vocab_rows * width * tokens,
            transcendentals=0,
            bytes_accessed=2 * vocab_rows * (width + tokens),
        ),
    )(table, kept, fac, weight, labels)


def head_table_kernel(h_ref, q_ref, fac_ref, w_ref, lab_ref, out_ref, dl_ref):
    first = pl.program_id(0) * VTILE
    tokens = q_ref.shape[1]

    def chunk(j, _):
        ns = pl.ds(pl.multiple_of(j * NTILE, NTILE), NTILE)
        rid = lax.broadcasted_iota(jnp.int32, (VTILE, NTILE), 0) + first
        dl_ref[:, ns] = logit_grads(
            q_ref[:, ns], fac_ref[0, 0:1, ns], w_ref[0:1, ns], rid, lab_ref[0:1, ns]
        )
        return 0

    lax.fori_loop(0, tokens // NTILE, chunk, 0)

    def cols(j, _):
        ds = pl.ds(pl.multiple_of(j * 256, 256), 256)
        out_ref[:, ds] = dot_nn(dl_ref[...], h_ref[:, ds]).astype(bf16)
        return 0

    lax.fori_loop(0, h_ref.shape[1] // 256, cols, 0)


def head_table(hidden, kept, fac, weight, labels, vocab_rows):
    tokens, width = hidden.shape
    tiles = pl.cdiv(vocab_rows, VTILE)
    sp = head_specs(width, tokens)
    return pl.pallas_call(
        head_table_kernel,
        name="head_table",
        grid=(tiles,),
        in_specs=[
            pl.BlockSpec((tokens, width), lambda i: (0, 0)),
            sp["kept"],
            sp["tile_row"],
            sp["row"],
            sp["row"],
        ],
        out_specs=sp["table"],
        out_shape=jax.ShapeDtypeStruct((vocab_rows, width), bf16),
        scratch_shapes=[pltpu.VMEM((VTILE, tokens), bf16)],
        compiler_params=head_params(),
        cost_estimate=pl.CostEstimate(
            flops=2 * vocab_rows * width * tokens,
            transcendentals=0,
            bytes_accessed=2 * vocab_rows * (width + tokens),
        ),
    )(hidden, kept, fac, weight, labels)


def shift_chunks(block, distance):
    size = lax.axis_size("fsdp")
    route = [(i - 2 * distance, i) for i in range(size) if 0 <= i - 2 * distance < size]
    return lax.ppermute(block, "fsdp", route)


def after(value, earlier):
    return lax.optimization_barrier((value, earlier))[0]


def norm_scale(values):
    return lax.rsqrt(jnp.mean(values * values, axis=-1, keepdims=True) + epsilon)


def norm_back(grad, values, gain):
    scale = norm_scale(values)
    unit = values * scale
    inner = grad * gain
    back = scale * (inner - unit * jnp.mean(inner * unit, axis=-1, keepdims=True))
    return back, jnp.sum(grad * unit, axis=0)


def wide(row):
    return jnp.pad(row, (0, LANES - row.shape[0]))[None]


def layer_vectors(vector_params, layer_index):
    offset = layer_index * PER
    pieces = []
    for size in (CONV * XBC, XBC, HEADS, HEADS, HEADS, D, DI):
        pieces.append(vector_params[offset : offset + size])
        offset += size
    conv_w, conv_b, dt_bias, decay_log, skip, pre_gain, gate_gain = pieces
    return dict(
        conv_w=conv_w.reshape(CONV, XBC),
        conv_b=conv_b[None],
        dt_bias=wide(dt_bias),
        decay_log=wide(decay_log),
        skip=jnp.repeat(skip, HDIM)[None],
        pre_gain=pre_gain,
        gate_gain=gate_gain[None],
    )


def layer_forward(hidden, w_in, w_out, vec):
    rows = hidden.shape[0]
    normed = (hidden * norm_scale(hidden) * vec["pre_gain"]).astype(bf16)
    proj = jnp.dot(normed, w_in, preferred_element_type=f32)
    halo = shift_chunks(proj[rows - 8 :, DI : DI + XBC], 1)
    pre, y0, local, dt, cum = local_call(
        front_kernel,
        (proj, halo, vec["conv_w"], vec["conv_b"], vec["dt_bias"], vec["decay_log"], vec["skip"]),
        (
            ((rows, XBC), f32),
            ((rows, DI), f32),
            ((DI, NSTATE), f32),
            ((rows, LANES), f32),
            ((rows, LANES), f32),
        ),
        scratch=(
            pltpu.VMEM((rows + 8, XBC), f32),
            pltpu.VMEM((HEADS, rows, LANES), f32),
            pltpu.VMEM((PAIRS, rows, LANES), f32),
            pltpu.VMEM((PAIRS, rows, LANES), f32),
            pltpu.VMEM((LANES, rows), f32),
        ),
    )
    decay = jnp.exp(cum[rows - 1, :HEADS])
    entering = carry_chain(decay, local, 1)
    y, mixed = local_call(
        gate_kernel,
        (y0, proj, pre, cum, entering, vec["gate_gain"]),
        (((rows, DI), f32), ((rows, DI), bf16)),
        scratch=(pltpu.VMEM((PAIRS, rows, LANES), f32),),
    )
    branch = jnp.dot(mixed, w_out, preferred_element_type=f32)
    record = (hidden, normed, proj, halo, pre, dt, cum, decay, entering, y, mixed)
    return hidden + branch, record


def layer_backward(grad_hidden, w_in, w_out, vec, record):
    hidden, normed, proj, halo, pre, dt, cum, decay, entering, y, mixed = record
    rows = hidden.shape[0]
    grad_branch = grad_hidden.astype(bf16)
    grad_mixed = dot_nt(grad_branch, w_out)
    dy, dz, dgate, gstate = local_call(
        ungate_kernel,
        (grad_mixed, y, proj, pre, cum, vec["gate_gain"]),
        (
            ((rows, DI), f32),
            ((rows, DI), bf16),
            ((1, DI), f32),
            ((DI, NSTATE), f32),
        ),
        scratch=(pltpu.VMEM((PAIRS, rows, LANES), f32),),
    )
    later = carry_chain(decay, gstate, -1)
    grad_out = dot_tn(mixed, grad_branch).astype(bf16)
    dx, dhalo, ddr, dconv, dsmall = local_call(
        back_kernel,
        (
            dy, y, proj, halo, pre, dt, cum, entering, later,
            vec["conv_w"], vec["dt_bias"], vec["decay_log"], vec["skip"],
        ),
        (
            ((rows, XBC), f32),
            ((8, XBC), f32),
            ((rows, LANES), f32),
            ((8, XBC), f32),
            ((8, LANES), f32),
        ),
        scratch=(
            pltpu.VMEM((rows + 8, XBC), f32),
            pltpu.VMEM((rows + 16, XBC), f32),
            pltpu.VMEM((HEADS, rows, LANES), f32),
            pltpu.VMEM((PAIRS, rows, LANES), f32),
            pltpu.VMEM((PAIRS, rows, LANES), f32),
            pltpu.VMEM((LANES, rows), f32),
            pltpu.VMEM((rows, rows), f32),
            pltpu.VMEM((rows, LANES), f32),
            pltpu.VMEM((rows, LANES), f32),
            pltpu.VMEM((rows, LANES), f32),
            pltpu.VMEM((rows, LANES), f32),
            pltpu.VMEM((16, LANES), f32),
        ),
    )
    from_next = shift_chunks(dhalo, -1)
    dx = jnp.concatenate([dx[: rows - 8], dx[rows - 8 :] + from_next], axis=0)
    grad_proj = jnp.concatenate(
        [dz, dx.astype(bf16), ddr[:, :HEADS].astype(bf16)], axis=1
    )
    grad_normed = dot_nt(grad_proj, w_in)
    grad_in = dot_tn(normed, grad_proj).astype(bf16)
    grad_prev, dpre_gain = norm_back(grad_normed, hidden, vec["pre_gain"])
    grad_vec = jnp.concatenate(
        [
            dconv[:CONV].reshape(-1),
            dconv[CONV],
            dsmall[0, :HEADS],
            dsmall[1, :HEADS],
            jnp.sum(dsmall[2:3, :HEADS], axis=0),
            dpre_gain,
            dgate[0],
        ]
    )
    return grad_hidden + grad_prev, grad_in, grad_out, grad_vec


def advance(weight, moment, average, grad, factor):
    scaled = grad * factor
    moment_new = 0.5 * moment + scaled
    weight_new = weight - step_rate * (scaled + 0.5 * moment_new)
    average_new = 0.5 * average + 0.5 * weight_new
    return (weight_new, moment_new, average_new, weight_new.astype(bf16))


def whole_step(
    token_ids,
    target_ids,
    seq_lengths,
    embedding,
    embedding_mom,
    embedding_avg,
    in_proj,
    in_proj_mom,
    in_proj_avg,
    out_proj,
    out_proj_mom,
    out_proj_avg,
    vector_params,
    vector_mom,
    vector_avg,
):
    groups = lax.axis_size("dp")
    shards = lax.axis_size("fsdp")
    group_index = lax.axis_index("dp")
    shard_index = lax.axis_index("fsdp")
    chunks = shards // MB
    seq_rows = token_ids.shape[2]
    rows = seq_rows // chunks
    vocab_rows, own_cols = embedding.shape
    tokens = MB * seq_rows
    total_count = jnp.sum(seq_lengths).astype(f32)
    embed_low = embedding.astype(bf16)
    in_low = in_proj.astype(bf16)
    out_low = out_proj.astype(bf16)

    ids_all = lax.all_gather(token_ids[:, 0, :], "dp", axis=0)
    ids_all = ids_all.reshape(groups, MB, chunks, rows).transpose(2, 1, 0, 3).reshape(-1)
    every = ids_all.shape[0]
    local_ids = ids_all - shard_index * vocab_rows
    inside = (local_ids >= 0) & (local_ids < vocab_rows)
    sorted_ids, sorted_tok = lax.sort(
        (jnp.where(inside, local_ids, vocab_rows), jnp.arange(every, dtype=jnp.int32)),
        num_keys=1,
    )
    held_here = sorted_ids < vocab_rows
    count = jnp.sum(held_here.astype(jnp.int32)).reshape(1)
    row_list = jnp.where(held_here, sorted_ids, 0)
    tok_list = jnp.where(held_here, sorted_tok, every)
    (looked,) = local_call(
        lookup_kernel,
        (count, row_list, tok_list, embedding),
        (((every, own_cols), bf16),),
        scratch=(pltpu.VMEM((every + 8, own_cols), f32),),
        in_smem=(0, 1, 2),
    )
    mine = lax.psum_scatter(
        looked.reshape(shards * groups * rows, own_cols), "fsdp", scatter_dimension=0, tiled=True
    )
    mine = lax.all_to_all(mine.reshape(groups, rows, own_cols), "dp", 0, 0)
    hidden = mine.transpose(1, 0, 2).reshape(rows, D).astype(f32)

    shards = []
    for l in range(LAYERS):
        shards += [in_low[l], out_low[l]]
    shards = after(shards, looked)
    gathered = gather_layers(shards)
    w_in, w_out = gathered[0::2], gathered[1::2]
    embed_low = after(embed_low, gathered)
    table = lax.all_gather(embed_low, "dp", axis=1, tiled=True)

    vecs = [layer_vectors(vector_params, l) for l in range(LAYERS)]
    final_gain = vector_params[LAYERS * PER :]
    records = []
    for l in range(LAYERS):
        hidden, record = layer_forward(hidden, w_in[l], w_out[l], vecs[l])
        records.append(record)

    final_low = (hidden * norm_scale(hidden) * final_gain).astype(bf16)
    group_hidden = lax.all_gather(final_low, "fsdp", axis=0, tiled=True)

    def in_order(per_seq):
        return per_seq.reshape(MB, chunks, rows).transpose(1, 0, 2).reshape(1, tokens)

    labels = in_order(target_ids[:, 0, :])
    lengths = lax.dynamic_index_in_dim(seq_lengths, group_index, 1, keepdims=True)
    valid = in_order((jnp.arange(seq_rows)[None, :] < lengths).astype(f32))
    local_labels = labels - shard_index * vocab_rows
    kept, tile_stats = head_stats(table, group_hidden.T, local_labels)
    top = jnp.max(tile_stats[:, 0], axis=0)
    summed = jnp.sum(tile_stats[:, 1] * jnp.exp(tile_stats[:, 0] - top), axis=0)
    stats = jnp.stack(
        [top, summed, jnp.sum(tile_stats[:, 2], axis=0), jnp.sum(tile_stats[:, 3], axis=0)]
    )
    stats = lax.all_gather(stats, "fsdp", axis=0)
    row_top = jnp.max(stats[:, 0], axis=0)
    expsum = jnp.sum(stats[:, 1] * jnp.exp(stats[:, 0] - row_top), axis=0)
    target = jnp.sum(stats[:, 2], axis=0)
    logit_sum = jnp.sum(stats[:, 3], axis=0)
    log_total = row_top + jnp.log(expsum)
    per_row = log_total - 0.9 * target - 0.1 * logit_sum / VOCAB + z_weight * log_total * log_total
    own_mask = jnp.arange(tokens) // rows == shard_index
    loss_sum = jnp.sum(jnp.where(own_mask, per_row * valid[0], 0.0))
    weight = valid / total_count
    scale = weight[0] * (1.0 + 2.0 * z_weight * log_total)
    fac = (scale * jnp.exp(tile_stats[:, 0] - log_total))[:, None, :]

    rows_grad = head_rows(table, kept, fac, weight, local_labels)
    own_grad = lax.psum_scatter(
        rows_grad.T.astype(bf16), "fsdp", scatter_dimension=0, tiled=True
    ).astype(f32)
    table_grad = head_table(group_hidden, kept, fac, weight, local_labels, vocab_rows)
    table_part = lax.psum_scatter(table_grad, "dp", scatter_dimension=1, tiled=True)

    grad_hidden, dfinal = norm_back(after(own_grad, table_grad), hidden, final_gain)
    in_parts = [None] * LAYERS
    out_parts = [None] * LAYERS
    vec_parts = [None] * LAYERS
    for l in reversed(range(LAYERS)):
        grad_hidden, grad_in, grad_out, vec_parts[l] = layer_backward(
            grad_hidden, w_in[l], w_out[l], vecs[l], records[l]
        )
        if l == 0:
            sent = grad_hidden.astype(bf16).reshape(rows, groups, own_cols).transpose(1, 0, 2)
            sent = lax.all_to_all(sent, "dp", 0, 0)
            spread = lax.all_gather(sent, "fsdp", axis=0).reshape(every, own_cols)
        in_parts[l], out_parts[l] = grad_in, grad_out
    whole = []
    for l in range(LAYERS):
        whole += [in_parts[l], out_parts[l]]
    summed_parts = reduce_layers(whole)
    spread = after(spread, summed_parts)
    (table_total,) = local_call(
        spread_kernel,
        (count, row_list, tok_list, spread, table_part),
        (((vocab_rows, own_cols), f32),),
        scratch=(pltpu.VMEM((every + 8, own_cols), f32),),
        in_smem=(0, 1, 2),
    )
    grad_in_all = jnp.stack(summed_parts[0::2])
    grad_out_all = jnp.stack(summed_parts[1::2])
    owner_squares = (
        jnp.sum(grad_in_all * grad_in_all)
        + jnp.sum(grad_out_all * grad_out_all)
        + jnp.sum(table_total * table_total)
    )
    small = vector_params.shape[0]
    padded = pl.cdiv(small + 2, 16 * LANES) * 16 * LANES
    packed = jnp.concatenate(
        vec_parts
        + [
            dfinal,
            owner_squares.reshape(1),
            loss_sum.reshape(1),
            jnp.zeros((padded - small - 2,), f32),
        ]
    )
    packed = total_of(packed.reshape(-1, LANES)).reshape(-1)
    vector_total = packed[:small]
    squares_total, loss_total = packed[small], packed[small + 1]
    grad_norm = jnp.sqrt(squares_total + jnp.sum(vector_total * vector_total))
    factor = jnp.minimum(1.0, clip_limit / grad_norm)
    loss_value = loss_total / total_count
    return (
        loss_value,
        grad_norm,
        *advance(embedding, embedding_mom, embedding_avg, table_total, factor),
        *advance(in_proj, in_proj_mom, in_proj_avg, grad_in_all, factor),
        *advance(out_proj, out_proj_mom, out_proj_avg, grad_out_all, factor),
        *advance(vector_params, vector_mom, vector_avg, vector_total, factor),
    )


def solution(mesh):
    table_spec = P("fsdp", "dp")
    weight_spec = P(None, ("dp", "fsdp"), None)
    return jax.shard_map(
        whole_step,
        mesh=mesh,
        in_specs=(
            P(None, "dp", None),
            P(None, "dp", None),
            P(),
            *(table_spec,) * 3,
            *(weight_spec,) * 6,
            *(P(),) * 3,
        ),
        out_specs=(
            P(),
            P(),
            *(table_spec,) * 4,
            *(weight_spec,) * 8,
            *(P(),) * 4,
        ),
        check_vma=False,
    )
```

time: 2800 us -> 1250 us (0.45)
  waiting for transfers between devices: 1440 us -> 210 us
  Pallas kernels: 0 us -> 754 us
  matrix products: 493 us -> 62.6 us
  other arithmetic: 422 us -> 57.7 us
  blocking collectives: 195 us -> 32.3 us
  local copies, waits for them, and re-layouts: 169 us -> 71.7 us
    reduce_scatter x10 -> x3, waiting for transfers between devices: 922 us -> 44 us  [the longest x1 44 us: whole_step(): lax.psum_scatter(looked.reshape(shards * groups * rows, own_cols), 'fsdp'...]
    pallas_call x0 -> x20, Pallas kernels: none -> 754 us  [the longest x7 428 us: comm_call(): pl.pallas_call(kernel, out_shape=[jax.ShapeDtypeStruct(shape, kind) for s...]
    dot_general x88 -> x12, matrix products: 493 us -> 62.6 us  [the longest x4 22.3 us: dot_tn(): lax.dot_general(a, b, (((0,), (0,)), ((), ())), precision=precision, pref...]
    all_gather x17 -> x3, waiting for transfers between devices: 512 us -> 163 us  [the longest x1 121 us: whole_step(): table = lax.all_gather(embed_low, 'dp', axis=1, tiled=True)]
    all_gather x12 -> x2, blocking collectives: 150 us -> 22.6 us  [the longest x1 14.4 us: whole_step(): stats = lax.all_gather(stats, 'fsdp', axis=0)]
    reduce_sum x45 -> x10, other arithmetic: 124 us -> 12.6 us  [the longest x1 5.11 us: whole_step(): jnp.sum(table_total * table_total)]
    select_n x35 -> x2, other arithmetic: 65.3 us -> 1.27 us  [the longest x1 1.27 us: whole_step(): tok_list = jnp.where(held_here, sorted_tok, every)]
    scatter-add x2 -> x0, other arithmetic: 53.8 us -> none  [body(): table_grad.at[jnp.where(inside, local_ids, vocab_rows)]]
  transfers between devices with their start and end apart: 36 -> 11, of which waited for: 25 -> 5; matrix products, arithmetic and copies ran while one was open for 22% -> 6% of each run, Pallas kernels for 0% -> 31%
where the time goes in v1:
time: 1250 us; the launch traced here: 1230 us
  Pallas kernels  754 us (60%)
  waiting for transfers between devices  210 us (17%)
  local copies, waits for them, and re-layouts  71.7 us (6%)
  matrix products  62.6 us (5%)
  other arithmetic  57.7 us (5%)
  blocking collectives  32.3 us (3%)
  starting transfers between devices  24.6 us (2%)
  between operations  22.1 us (2%)
    pallas_call x7, Pallas kernels, comm_call(): pl.pallas_call(kernel, out_shape=[jax.ShapeDtypeStruct(shape, kind) for s...  428 us
    pallas_call x10, Pallas kernels, local_call(): pl.pallas_call(kernel, out_shape=[jax.ShapeDtypeStruct(shape, kind) for s...  160 us
    all_gather x1, waiting for transfers between devices, whole_step(): table = lax.all_gather(embed_low, 'dp', axis=1, tiled=True)  121 us
    pallas_call x1, Pallas kernels, head_stats(): pl.pallas_call(functools.partial(head_stats_kernel, vocab_rows), name='he...  61.4 us
    pallas_call x1, Pallas kernels, head_rows(): pl.pallas_call(functools.partial(head_rows_kernel, vocab_rows), name='hea...  53.9 us
    pallas_call x1, Pallas kernels, head_table(): pl.pallas_call(head_table_kernel, name='head_table', grid=(tiles,), in_sp...  51.5 us
    reduce_scatter x1, waiting for transfers between devices, whole_step(): lax.psum_scatter(looked.reshape(shards * groups * rows, own_cols), 'fsdp'...  44 us
    all_gather x1, waiting for transfers between devices, whole_step(): group_hidden = lax.all_gather(final_low, 'fsdp', axis=0, tiled=True)  41.8 us
  transfers between devices with their start and end apart: 11, of which 5 were waited for; matrix products, arithmetic and copies ran while one was open for 6% of the time, Pallas kernels for 31%

profile of v1, /device:TPU:12, one launch (start us, length us, event | category | flops | bytes accessed | tf_op | source)
XLA Modules:
  0.0 1234.9 jit_solution(17845454264339302520)
XLA Ops:
  7.2 8.2 all-gather
  23.0 10.7 shard_map.286
  38.2 44.0 %reduce-scatter.4.cloned.1.call-done = bf16[1024,256]{1,0:T(8,128)(2,1)} async-done(((bf16[8192,256]{1,0:T(8,128)(2,1)}), bf16[1024,256]{1,0:T(8,128)(2,1)}) %reduce-scatter.4.cloned.1.call-update) | async-done | bytes 524304 | tf_op jit(solution)/shard_map/reduce_scatter | solution.py:1358
  89.2 116.6 %shard_map.287 = (bf16[4,4,2,32,4384]{4,3,2,1,0:T(8,128)(2,1)}, bf16[4,4,2,64,1024]{4,3,2,1,0:T(8,128)(2,1)}, bf16[4,4,2,32,4384]{4,3,2,1,0:T(8,128)(2,1)}, bf16[4,4,2,64,1024]{4,3,2,1,0:T(8,128)(2,1)}) custom-call(bf16[32,4384]{1,0:T(8,128)(2,1)} %get-tuple-element.71.refs_0_, bf16[64,1024]{1,0:T(8,128)(2,1)} %get-tuple-element.72.refs_1_, ...), custom_call_target="tpu_custom_call" | custom-call | flops 19759104 | bytes 39518208 | tf_op jit(solution)/shard_map/pallas_call | solution.py:159
  222.6 13.5 %shard_map.288 = (f32[256,2304]{1,0:T(8,128)}, f32[256,2048]{1,0:T(8,128)}, f32[2048,128]{1,0:T(8,128)}, f32[256,128]{1,0:T(8,128)}, f32[256,128]{1,0:T(8,128)}) custom-call(f32[256,4384]{1,0:T(8,128)} %copy-done, f32[8,2304]{1,0:T(8,128)} %copy-done.35, f32[4,2304]{1,0:T(4,128)} %reshape.285.cw_ref, f32[1,2304]{1,0:T(1,128)} %broadcast_in_dim.31.cb_ref, ...), custom_call_target="tpu_custom_call" | custom-call | flops 4618240 | bytes 9236480 | tf_op jit(solution)/shard_map/pallas_call | solution.py:65
  237.3 17.5 %shard_map.289.sin_ref = bf16[2048,128]{1,0:T(8,128)(2,1)} custom-call(f32[32]{0:T(128)} %exponential_bitcast_fusion.1.decay_ref, f32[2048,128]{1,0:T(8,128)} %get-tuple-element.79.local_ref), custom_call_target="tpu_custom_call" | custom-call | flops 524288 | bytes 1048576 | tf_op jit(solution)/shard_map/pallas_call | solution.py:159
  254.8 10.4 shard_map.290
  286.8 13.4 %shard_map.291 = (f32[256,2304]{1,0:T(8,128)}, f32[256,2048]{1,0:T(8,128)}, f32[2048,128]{1,0:T(8,128)}, f32[256,128]{1,0:T(8,128)}, f32[256,128]{1,0:T(8,128)}) custom-call(f32[256,4384]{1,0:T(8,128)} %copy-done.1, f32[8,2304]{1,0:T(8,128)} %copy-done.36, f32[4,2304]{1,0:T(4,128)} %reshape.288.cw_ref, f32[1,2304]{1,0:T(1,128)} %broadcast_in_dim.68.cb_ref, ...), custom_call_target="tpu_custom_call" | custom-call | flops 4618240 | bytes 9236480 | tf_op jit(solution)/shard_map/pallas_call | solution.py:65
  301.5 15.3 %shard_map.292.sin_ref = bf16[2048,128]{1,0:T(8,128)(2,1)} custom-call(f32[32]{0:T(128)} %exponential_bitcast_fusion.decay_ref, f32[2048,128]{1,0:T(8,128)} %get-tuple-element.86.local_ref), custom_call_target="tpu_custom_call" | custom-call | flops 524288 | bytes 1048576 | tf_op jit(solution)/shard_map/pallas_call | solution.py:159
  316.8 10.4 shard_map.293
  340.4 41.8 %all-gather.10.cloned.1.call-done.h_ref = bf16[2048,1024]{1,0:T(8,128)(2,1)} async-done(((bf16[256,1024]{1,0:T(8,128)(2,1)}), bf16[2048,1024]{1,0:T(8,128)(2,1)}) %all-gather.10.cloned.1.call-update) | async-done | bytes 4194320 | tf_op jit(solution)/shard_map/all_gather | solution.py:1381
  388.6 120.8 %all-gather.8.cloned.1.call-done.e_ref = bf16[6286,1024]{1,0:T(8,128)(2,1)} async-done(((bf16[6286,256]{1,0:T(8,128)(2,1)}), bf16[6286,1024]{1,0:T(8,128)(2,1)}) %all-gather.8.cloned.1.call-update) | async-done | bytes 12873744 | tf_op jit(solution)/shard_map/all_gather | solution.py:1371
  509.4 61.4 %head_stats.1 = (bf16[6400,2048]{1,0:T(8,128)(2,1)}, f32[10,8,2048]{2,1,0:T(8,128)}) custom-call(bf16[6286,1024]{1,0:T(8,128)(2,1)} %all-gather.8.cloned.1.call-done.e_ref, bf16[1024,2048]{1,0:T(8,128)(2,1)} %copy.102.ht_ref, s32[1,2048]{1,0:T(1,128)} %sub.102.lab_ref), custom_call_target="tpu_custom_call" | custom-call | flops 26365394944 | bytes 38621184 | tf_op jit(solution)/shard_map/head_stats/pallas_call | solution.py:1029
  574.5 14.4 %all-gather.3 = f32[8,4,2048]{2,1,0:T(4,128)S(1)} all-gather(f32[1,4,2048]{2,1,0:T(4,128)S(1)} %maximum_bitcast_fusion), channel_id=3, replica_groups=mesh['dp'=4,'fsdp'=8] {'fsdp'}, dimensions={0}, use_global_device_ids=true | all-gather | bytes 294912 | tf_op jit(solution)/shard_map/all_gather | solution.py:1396
  591.7 53.9 %head_rows.1 = f32[1024,2048]{1,0:T(8,128)} custom-call(bf16[6286,1024]{1,0:T(8,128)(2,1)} %all-gather.8.cloned.1.call-done.e_ref, bf16[6400,2048]{1,0:T(8,128)(2,1)} %get-tuple-element.90.q_ref, f32[10,1,2048]{2,1,0:T(1,128)} %exponential_multiply_fusion.fac_ref, f32[1,2048]{1,0:T(1,128)} %div.64.w_ref, s32[1,2048]{1,0:T(1,128)} %sub.102.lab_ref), custom_call_target="tpu_custom_call" | custom-call | flops 26365394944 | bytes 38621184 | tf_op jit(solution)/shard_map/head_rows/pallas_call | solution.py:1085
  645.7 7.3 copy.105
  653.0 51.5 %head_table.1 = bf16[6286,1024]{1,0:T(8,128)(2,1)} custom-call(bf16[2048,1024]{1,0:T(8,128)(2,1)} %all-gather.10.cloned.1.call-done.h_ref, bf16[6400,2048]{1,0:T(8,128)(2,1)} %get-tuple-element.90.q_ref, f32[10,1,2048]{2,1,0:T(1,128)} %exponential_multiply_fusion.fac_ref, f32[1,2048]{1,0:T(1,128)} %div.64.w_ref, s32[1,2048]{1,0:T(1,128)} %sub.102.lab_ref), custom_call_target="tpu_custom_call" | custom-call | flops 26365394944 | bytes 38621184 | tf_op jit(solution)/shard_map/head_table/pallas_call | solution.py:1128
  710.4 13.5 %shard_map.294 = (f32[256,2048]{1,0:T(8,128)}, bf16[256,2048]{1,0:T(8,128)(2,1)}, f32[1,2048]{1,0:T(1,128)}, f32[2048,128]{1,0:T(8,128)}) custom-call(f32[256,2048]{1,0:T(8,128)} %fusion.8.dyn_ref, f32[256,2048]{1,0:T(8,128)} %get-tuple-element.93.y_ref, f32[256,4384]{1,0:T(8,128)} %copy-done.1, f32[256,2304]{1,0:T(8,128)} %get-tuple-element.84.pre_ref, ...), custom_call_target="tpu_custom_call" | custom-call | flops 11182080 | bytes 22364160 | tf_op jit(solution)/shard_map/pallas_call | solution.py:65
  723.9 22.3 %shard_map.295.gin_ref = bf16[2048,128]{1,0:T(8,128)(2,1)} custom-call(f32[32]{0:T(128)} %exponential_bitcast_fusion.decay_ref, f32[2048,128]{1,0:T(8,128)} %get-tuple-element.97.local_ref), custom_call_target="tpu_custom_call" | custom-call | flops 524288 | bytes 1048576 | tf_op jit(solution)/shard_map/pallas_call | solution.py:159
  746.3 30.5 %shard_map.296 = (f32[256,2304]{1,0:T(8,128)}, f32[8,2304]{1,0:T(8,128)}, f32[256,128]{1,0:T(8,128)}, f32[8,2304]{1,0:T(8,128)}, f32[8,128]{1,0:T(8,128)}) custom-call(f32[256,2048]{1,0:T(8,128)} %get-tuple-element.95.dy_ref, f32[256,2048]{1,0:T(8,128)} %get-tuple-element.93.y_ref, f32[256,4384]{1,0:T(8,128)} %copy-done.1, f32[8,2304]{1,0:T(8,128)} %copy-done.36, ...), custom_call_target="tpu_custom_call" | custom-call | flops 12473344 | bytes 24946688 | tf_op jit(solution)/shard_map/pallas_call | solution.py:65
  797.3 13.5 %shard_map.297 = (f32[256,2048]{1,0:T(8,128)}, bf16[256,2048]{1,0:T(8,128)(2,1)}, f32[1,2048]{1,0:T(1,128)}, f32[2048,128]{1,0:T(8,128)}) custom-call(f32[256,2048]{1,0:T(8,128)} %fusion.5.dyn_ref, f32[256,2048]{1,0:T(8,128)} %get-tuple-element.101.y_ref, f32[256,4384]{1,0:T(8,128)} %copy-done, f32[256,2304]{1,0:T(8,128)} %get-tuple-element.77.pre_ref, ...), custom_call_target="tpu_custom_call" | custom-call | flops 11182080 | bytes 22364160 | tf_op jit(solution)/shard_map/pallas_call | solution.py:65
  810.9 18.5 %shard_map.298.gin_ref = bf16[2048,128]{1,0:T(8,128)(2,1)} custom-call(f32[32]{0:T(128)} %exponential_bitcast_fusion.1.decay_ref, f32[2048,128]{1,0:T(8,128)} %get-tuple-element.104.local_ref), custom_call_target="tpu_custom_call" | custom-call | flops 524288 | bytes 1048576 | tf_op jit(solution)/shard_map/pallas_call | solution.py:159
  829.4 30.5 %shard_map.299 = (f32[256,2304]{1,0:T(8,128)}, f32[8,2304]{1,0:T(8,128)}, f32[256,128]{1,0:T(8,128)}, f32[8,2304]{1,0:T(8,128)}, f32[8,128]{1,0:T(8,128)}) custom-call(f32[256,2048]{1,0:T(8,128)} %get-tuple-element.102.dy_ref, f32[256,2048]{1,0:T(8,128)} %get-tuple-element.101.y_ref, f32[256,4384]{1,0:T(8,128)} %copy-done, f32[8,2304]{1,0:T(8,128)} %copy-done.35, ...), custom_call_target="tpu_custom_call" | custom-call | flops 12473344 | bytes 24946688 | tf_op jit(solution)/shard_map/pallas_call | solution.py:65
  868.3 7.1 multiply_reduce_fusion.2
  875.9 9.6 all_to_all.10
  891.9 8.3 convolution_convert_fusion
  900.2 12.1 copy.111
  922.6 11.9 copy.110
  934.5 216.8 %shard_map.300 = (f32[32,4384]{1,0:T(8,128)}, f32[64,1024]{1,0:T(8,128)}, f32[32,4384]{1,0:T(8,128)}, f32[64,1024]{1,0:T(8,128)}) custom-call(bf16[4,4,2,32,4384]{4,3,2,1,0:T(8,128)(2,1)} %bitcast.127, bf16[4,4,2,64,1024]{4,3,2,1,0:T(8,128)(2,1)} %bitcast.129, bf16[4,4,2,32,4384]{4,3,2,1,0:T(8,128)(2,1)} %bitcast.126, bf16[4,4,2,64,1024]{4,3,2,1,0:T(8,128)(2,1)} %bitcast.128), custom_call_target="tpu_custom_call" | custom-call | flops 26345472 | bytes 52690944 | tf_op jit(solution)/shard_map/pallas_call | solution.py:159
  1156.6 13.2 %shard_map.301 = f32[6286,256]{1,0:T(8,128)} custom-call(s32[1]{0:T(128)} %bitcast.1.count_ref, s32[8192]{0:T(1024)} %get-tuple-element.176.row_ref, s32[8192]{0:T(1024)} %get-tuple-element.175.tok_ref, bf16[8192,256]{1,0:T(8,128)(2,1)} %bitcast.137, bf16[6286,256]{1,0:T(8,128)(2,1)} %reduce-scatter.8.cloned.1.call-done.base_ref), custom_call_target="tpu_custom_call" | custom-call | flops 7478276 | bytes 14956552 | tf_op jit(solution)/shard_map/pallas_call | solution.py:65
  1177.0 20.8 %shard_map.302 = f32[240,128]{1,0:T(8,128)} custom-call(f32[240,128]{1,0:T(8,128)} %bitcast.159), custom_call_target="tpu_custom_call" | custom-call | flops 368640 | bytes 737280 | tf_op jit(solution)/shard_map/pallas_call | solution.py:159
  1202.7 11.8 fusion.32
  (231 shorter events, 161.1 us)
Async XLA Ops:
  7.2 75.0 %reduce-scatter.4.cloned.1.call-start = ((), (), s32[]{:S(2)}) async-start(), calls=%async_computation.5 | async-start | bytes 4718592 | tf_op jit(solution)/shard_map/reduce_scatter | solution.py:1358
  82.2 124.3 %all-to-all-start = ((bf16[4,256,256]{2,1,0:T(8,128)(2,1)}), bf16[4,256,256]{2,1,0:T(8,128)(2,1)S(1)}, u32[]{:S(2)}, u32[]{:S(2)}) async-start(bf16[4,256,256]{2,1,0:T(8,128)(2,1)} %bitcast.158), calls=%async_computation.1 | async-start | bytes 1048576 | tf_op jit(solution)/shard_map/all_to_all | solution.py:1361
  86.4 295.8 %all-gather.10.cloned.1.call-start = ((), (), s32[]{:S(2)}) async-start(), calls=%async_computation.7 | async-start | bytes 4718592 | tf_op jit(solution)/shard_map/all_gather | solution.py:1381
  215.6 6.4 collective-permute-start
  220.7 44.6 %copy-start.13 = (f32[256,1024]{1,0:T(8,128)}, f32[256,1024]{1,0:T(8,128)S(1)}, u32[]{:S(2)}) copy-start(f32[256,1024]{1,0:T(8,128)S(1)} %copy.115) | copy-start | bytes 3145732
  269.1 6.7 copy-start.6
  277.9 8.2 collective-permute-start.1
  331.4 374.5 %copy-start.5 = (f32[256,1024]{1,0:T(8,128)}, f32[256,1024]{1,0:T(8,128)S(1)}, u32[]{:S(2)}) copy-start(f32[256,1024]{1,0:T(8,128)S(1)} %get-tuple-element.187) | copy-start | bytes 3145732
  332.5 5.0 copy-start.43
  332.5 5.6 copy-start.44
  332.5 176.8 %all-gather.8.cloned.1.call-start = ((), (), s32[]{:S(2)}) async-start(), calls=%async_computation.6 | async-start | bytes 16097280 | tf_op jit(solution)/shard_map/all_gather | solution.py:1371
  337.4 367.1 %reduce-scatter.6.cloned.1.call-start = ((), (), s32[]{:S(2)}) async-start(), calls=%async_computation.8 | async-start | bytes 4718592 | tf_op jit(solution)/shard_map/reduce_scatter | solution.py:1410
  653.0 503.6 %all-gather.12.cloned.1.call-start = ((), (), s32[]{:S(2)}) async-start(), calls=%async_computation.10 | async-start | bytes 4718592 | tf_op jit(solution)/shard_map/all_gather | solution.py:1427
  776.7 7.3 collective-permute-start.2
  785.1 7.1 copy-start.7
  859.8 7.5 collective-permute-start.3
  867.3 8.1 copy-start.25
  868.3 7.1 copy-start.4
  868.3 7.1 copy-start.14
  885.5 271.1 %reduce-scatter.8.cloned.1.call-start = ((), (), s32[]{:S(2)}) async-start(), calls=%async_computation.9 | async-start | bytes 16097280 | tf_op jit(solution)/shard_map/reduce_scatter | solution.py:1414
  900.2 12.9 %copy-start.16 = (bf16[256,2048]{1,0:T(8,128)(2,1)S(1)}, bf16[256,2048]{1,0:T(8,128)(2,1)}, u32[]{:S(2)}) copy-start(bf16[256,2048]{1,0:T(8,128)(2,1)} %get-tuple-element.80) | copy-start | bytes 3145732
  1169.8 5.8 copy-start.41
  1169.8 5.8 copy-start.42
  1202.7 16.6 %slice-start = ((s8[6438912]{0:T(1024)(128)(4,1)}), s8[2244608]{0:T(1024)(128)(4,1)S(1)}, s32[]{:S(2)}) async-start(s8[6438912]{0:T(1024)(128)(4,1)} %bitcast.135), calls=%async_computation.11 | async-start | bytes 4489216
  1202.7 11.9 copy-start.9
  1202.7 11.9 copy-start.17
  1202.7 11.8 copy-start.18
  1202.7 11.8 copy-start.22
  1202.7 16.5 %slice-start.1 = ((s8[6438912]{0:T(1024)(128)(4,1)}), s8[4194304]{0:T(1024)(128)(4,1)S(1)}, s32[]{:S(2)}) async-start(s8[6438912]{0:T(1024)(128)(4,1)} %bitcast.135), calls=%async_computation.12 | async-start | bytes 8388608
  1217.2 5.7 copy-start.10
  1218.4 5.6 copy-start.19
  1219.3 5.6 copy-start.34
  (27 other events, 68.8 us)
Sparse Core Ops, SparseCore 0:
  33.9 48.2 reduce-scatter.3
  332.6 49.5 all-gather.9
  384.6 124.7 all-gather.7
  653.1 46.8 reduce-scatter.5
  885.6 44.0 all-gather.11
  932.7 221.5 reduce-scatter.7

commit v2 on v1

--- a/solution.py
+++ b/solution.py
@@ -18,6 +18,7 @@
 MB = 2
 DI = 2048
 XBC = 2304
+ZW = 4384
 PER = 14688
 LANES = 128
 PAIRS = DI // LANES
@@ -107,7 +108,7 @@
     lax.fori_loop(0, tokens // step, put, 0)
 
 
-def spread_kernel(count_ref, row_ref, tok_ref, grad_ref, base_ref, out_ref, held):
+def spread_kernel(count_ref, row_ref, tok_ref, grad_ref, base_ref, out_ref, square_ref, held):
     tokens = grad_ref.shape[0]
     step = 512
     rows_all = out_ref.shape[0]
@@ -139,6 +140,16 @@
         return 0
 
     lax.fori_loop(0, (count_ref[0] + 7) // 8, move, 0)
+
+    def square(i, total):
+        part = out_ref[pl.ds(pl.multiple_of(i * step, step), step), :]
+        return total + jnp.sum((part * part).reshape(step // 8, 8, -1), axis=0)
+
+    total = lax.fori_loop(0, whole, square, jnp.zeros(square_ref.shape, f32))
+    square_ref[...] = total
+    if rows_all > whole * step:
+        part = out_ref[whole * step :, :]
+        square_ref[0:1, :] += jnp.sum(part * part, axis=0, keepdims=True)
 
 
 MESH = pl.DeviceIdType.MESH
@@ -978,125 +989,145 @@
     lax.fori_loop(0, XBC // LANES, conv, 0)
 
 
-VTILE = 640
-NTILE = 512
+VTILE = 1280
+NTILE = 256
 
 
 def head_specs(width, tokens):
     return dict(
         table=pl.BlockSpec((VTILE, width), lambda i: (i, 0)),
+        hidden=pl.BlockSpec((tokens, width), lambda i: (0, 0)),
         kept=pl.BlockSpec((VTILE, tokens), lambda i: (i, 0)),
         row=pl.BlockSpec((1, tokens), lambda i: (0, 0)),
         tile_row=pl.BlockSpec((1, 1, tokens), lambda i: (i, 0, 0)),
     )
 
 
-def head_params():
-    return pltpu.CompilerParams(
-        dimension_semantics=("arbitrary",), vmem_limit_bytes=VMEM_LIMIT
-    )
-
-
-def head_stats_kernel(vocab_rows, e_ref, ht_ref, lab_ref, q_ref, st_ref):
+def head_call(kernel, grid, in_specs, out_specs, outs, scratch, ins, cells):
+    return pl.pallas_call(
+        kernel,
+        grid=(grid,),
+        in_specs=in_specs,
+        out_specs=out_specs,
+        out_shape=[jax.ShapeDtypeStruct(shape, kind) for shape, kind in outs],
+        scratch_shapes=list(scratch),
+        compiler_params=pltpu.CompilerParams(
+            dimension_semantics=("arbitrary",), vmem_limit_bytes=VMEM_LIMIT
+        ),
+        cost_estimate=pl.CostEstimate(
+            flops=2 * cells * D, transcendentals=cells, bytes_accessed=4 * cells
+        ),
+    )(*ins)
+
+
+def head_stats_kernel(vocab_rows, e_ref, h_ref, lab_ref, q_ref, st_ref):
     first = pl.program_id(0) * VTILE
-    tokens = ht_ref.shape[1]
-    e = e_ref[...]
-
-    def chunk(j, _):
+    tokens = h_ref.shape[0]
+
+    def chunk(j, ragged):
         ns = pl.ds(pl.multiple_of(j * NTILE, NTILE), NTILE)
-        logits = dot_nn(e, ht_ref[:, ns])
-        rid = lax.broadcasted_iota(jnp.int32, (VTILE, NTILE), 0) + first
-        real = rid < vocab_rows
-        shown = jnp.where(real, logits, OFF)
-        top = jnp.max(shown, axis=0, keepdims=True)
-        p = jnp.exp(shown - top)
+        logits = dot_nt(e_ref[...], h_ref[ns, :])
+        rid = lax.broadcasted_iota(jnp.int32, (VTILE, NTILE), 0)
+        if ragged:
+            logits = jnp.where(rid < vocab_rows - first, logits, OFF)
+        top = jnp.max(logits, axis=0, keepdims=True)
+        p = jnp.exp(logits - top)
         q_ref[:, ns] = p.astype(bf16)
         st_ref[0, 0:1, ns] = top
         st_ref[0, 1:2, ns] = jnp.sum(p, axis=0, keepdims=True)
-        hit = jnp.where(jnp.logical_and(real, rid == lab_ref[0:1, ns]), logits, 0.0)
-        st_ref[0, 2:3, ns] = jnp.sum(hit, axis=0, keepdims=True)
-        st_ref[0, 3:4, ns] = jnp.sum(jnp.where(real, logits, 0.0), axis=0, keepdims=True)
-        return 0
-
-    lax.fori_loop(0, tokens // NTILE, chunk, 0)
-
-
-def head_stats(table, hidden_t, labels):
+        label = lab_ref[0:1, ns]
+        hit = jnp.where(rid == label - first, logits, 0.0)
+        inside = jnp.logical_and(label >= 0, label < vocab_rows)
+        st_ref[0, 2:3, ns] = jnp.where(inside, jnp.sum(hit, axis=0, keepdims=True), 0.0)
+
+    def run(ragged):
+        lax.fori_loop(
+            0, tokens // NTILE, lambda j, _: (chunk(j, ragged), 0)[1], 0, unroll=UNROLL
+        )
+
+    end = pl.program_id(0) == pl.num_programs(0) - 1
+
+    @pl.when(end)
+    def _():
+        run(True)
+
+    @pl.when(jnp.logical_not(end))
+    def _():
+        run(False)
+
+
+UNROLL = 8
+
+
+def head_stats(table, hidden, labels):
     vocab_rows, width = table.shape
-    tokens = hidden_t.shape[1]
+    tokens = hidden.shape[0]
     tiles = pl.cdiv(vocab_rows, VTILE)
     sp = head_specs(width, tokens)
-    return pl.pallas_call(
+    return head_call(
         functools.partial(head_stats_kernel, vocab_rows),
-        name="head_stats",
-        grid=(tiles,),
-        in_specs=[
-            sp["table"],
-            pl.BlockSpec((width, tokens), lambda i: (0, 0)),
-            sp["row"],
-        ],
-        out_specs=[sp["kept"], pl.BlockSpec((1, 8, tokens), lambda i: (i, 0, 0))],
-        out_shape=[
-            jax.ShapeDtypeStruct((tiles * VTILE, tokens), bf16),
-            jax.ShapeDtypeStruct((tiles, 8, tokens), f32),
-        ],
-        compiler_params=head_params(),
-        cost_estimate=pl.CostEstimate(
-            flops=2 * vocab_rows * width * tokens,
-            transcendentals=vocab_rows * tokens,
-            bytes_accessed=2 * vocab_rows * (width + tokens),
-        ),
-    )(table, hidden_t, labels)
+        tiles,
+        [sp["table"], sp["hidden"], sp["row"]],
+        [sp["kept"], pl.BlockSpec((1, 8, tokens), lambda i: (i, 0, 0))],
+        [((tiles * VTILE, tokens), bf16), ((tiles, 8, tokens), f32)],
+        (),
+        (table, hidden, labels),
+        vocab_rows * tokens,
+    )
 
 
 def logit_grads(q, fac, weight, rid, label):
-    hit = jnp.where(rid == label, 0.9 + 0.1 / VOCAB, 0.1 / VOCAB)
-    return (q.astype(f32) * fac - weight * hit).astype(bf16)
-
-
-def head_rows_kernel(vocab_rows, e_ref, q_ref, fac_ref, w_ref, lab_ref, out_ref, et):
-    first = pl.program_id(0) * VTILE
+    other = weight * (0.1 / VOCAB)
+    return (q.astype(f32) * fac - jnp.where(rid == label, other + 0.9 * weight, other)).astype(bf16)
+
+
+def head_rows_kernel(vocab_rows, e_ref, q_ref, fac_ref, w_ref, lab_ref, out_ref, acc, et):
+    step = pl.program_id(0)
+    first = step * VTILE
     tokens = q_ref.shape[1]
 
-    @pl.when(pl.program_id(0) == 0)
+    @pl.when(step == 0)
     def _():
-        out_ref[...] = jnp.zeros(out_ref.shape, f32)
-
-    eid = lax.broadcasted_iota(jnp.int32, (VTILE, e_ref.shape[1]), 0) + first
-    et[...] = jnp.where(eid < vocab_rows, e_ref[...].astype(f32), 0.0).T.astype(bf16)
+        acc[...] = jnp.zeros(acc.shape, f32)
+
+    eid = lax.broadcasted_iota(jnp.int32, (VTILE, e_ref.shape[1]), 0)
+    et[...] = jnp.where(eid < vocab_rows - first, e_ref[...].astype(f32), 0.0).T.astype(bf16)
 
     def chunk(j, _):
         ns = pl.ds(pl.multiple_of(j * NTILE, NTILE), NTILE)
-        rid = lax.broadcasted_iota(jnp.int32, (VTILE, NTILE), 0) + first
+        rid = lax.broadcasted_iota(jnp.int32, (VTILE, NTILE), 0)
         dl = logit_grads(
-            q_ref[:, ns], fac_ref[0, 0:1, ns], w_ref[0:1, ns], rid, lab_ref[0:1, ns]
+            q_ref[:, ns], fac_ref[0, 0:1, ns], w_ref[0:1, ns], rid, lab_ref[0:1, ns] - first
         )
-        out_ref[:, ns] += dot_nn(et[...], dl)
-        return 0
-
-    lax.fori_loop(0, tokens // NTILE, chunk, 0)
+        acc[:, ns] += dot_nn(et[...], dl)
+        return 0
+
+    lax.fori_loop(0, tokens // NTILE, chunk, 0, unroll=UNROLL)
+
+    @pl.when(step == pl.num_programs(0) - 1)
+    def _():
+        def put(j, _):
+            ns = pl.ds(pl.multiple_of(j * NTILE, NTILE), NTILE)
+            out_ref[ns, :] = acc[:, ns].T.astype(bf16)
+            return 0
+
+        lax.fori_loop(0, tokens // NTILE, put, 0)
 
 
 def head_rows(table, kept, fac, weight, labels):
     vocab_rows, width = table.shape
     tokens = kept.shape[1]
-    tiles = pl.cdiv(vocab_rows, VTILE)
     sp = head_specs(width, tokens)
-    return pl.pallas_call(
+    return head_call(
         functools.partial(head_rows_kernel, vocab_rows),
-        name="head_rows",
-        grid=(tiles,),
-        in_specs=[sp["table"], sp["kept"], sp["tile_row"], sp["row"], sp["row"]],
-        out_specs=pl.BlockSpec((width, tokens), lambda i: (0, 0)),
-        out_shape=jax.ShapeDtypeStruct((width, tokens), f32),
-        scratch_shapes=[pltpu.VMEM((width, VTILE), bf16)],
-        compiler_params=head_params(),
-        cost_estimate=pl.CostEstimate(
-            flops=2 * vocab_rows * width * tokens,
-            transcendentals=0,
-            bytes_accessed=2 * vocab_rows * (width + tokens),
-        ),
-    )(table, kept, fac, weight, labels)
+        pl.cdiv(vocab_rows, VTILE),
+        [sp["table"], sp["kept"], sp["tile_row"], sp["row"], sp["row"]],
+        [sp["hidden"]],
+        [((tokens, width), bf16)],
+        (pltpu.VMEM((width, tokens), f32), pltpu.VMEM((width, VTILE), bf16)),
+        (table, kept, fac, weight, labels),
+        vocab_rows * tokens,
+    )[0]
 
 
 def head_table_kernel(h_ref, q_ref, fac_ref, w_ref, lab_ref, out_ref, dl_ref):
@@ -1105,47 +1136,64 @@
 
     def chunk(j, _):
         ns = pl.ds(pl.multiple_of(j * NTILE, NTILE), NTILE)
-        rid = lax.broadcasted_iota(jnp.int32, (VTILE, NTILE), 0) + first
+        rid = lax.broadcasted_iota(jnp.int32, (VTILE, NTILE), 0)
         dl_ref[:, ns] = logit_grads(
-            q_ref[:, ns], fac_ref[0, 0:1, ns], w_ref[0:1, ns], rid, lab_ref[0:1, ns]
+            q_ref[:, ns], fac_ref[0, 0:1, ns], w_ref[0:1, ns], rid, lab_ref[0:1, ns] - first
         )
         return 0
 
-    lax.fori_loop(0, tokens // NTILE, chunk, 0)
+    lax.fori_loop(0, tokens // NTILE, chunk, 0, unroll=UNROLL)
 
     def cols(j, _):
         ds = pl.ds(pl.multiple_of(j * 256, 256), 256)
         out_ref[:, ds] = dot_nn(dl_ref[...], h_ref[:, ds]).astype(bf16)
         return 0
 
-    lax.fori_loop(0, h_ref.shape[1] // 256, cols, 0)
+    lax.fori_loop(0, h_ref.shape[1] // 256, cols, 0, unroll=True)
 
 
 def head_table(hidden, kept, fac, weight, labels, vocab_rows):
     tokens, width = hidden.shape
-    tiles = pl.cdiv(vocab_rows, VTILE)
     sp = head_specs(width, tokens)
-    return pl.pallas_call(
+    return head_call(
         head_table_kernel,
-        name="head_table",
-        grid=(tiles,),
-        in_specs=[
-            pl.BlockSpec((tokens, width), lambda i: (0, 0)),
-            sp["kept"],
-            sp["tile_row"],
-            sp["row"],
-            sp["row"],
+        pl.cdiv(vocab_rows, VTILE),
+        [sp["hidden"], sp["kept"], sp["tile_row"], sp["row"], sp["row"]],
+        [sp["table"]],
+        [((vocab_rows, width), bf16)],
+        (pltpu.VMEM((VTILE, tokens), bf16),),
+        (hidden, kept, fac, weight, labels),
+        vocab_rows * tokens,
+    )[0]
+
+
+def weight_grads_kernel(u_ref, dp_ref, yn_ref, db_ref, in_ref, out_ref):
+    wide_cols = dp_ref.shape[1]
+    for c in range(0, wide_cols, 1024):
+        cs = pl.ds(c, min(1024, wide_cols - c))
+        in_ref[:, cs] = dot_tn(u_ref[...], dp_ref[:, cs]).astype(bf16)
+    out_ref[...] = dot_tn(yn_ref[...], db_ref[...]).astype(bf16)
+
+
+def weight_grads(normed, grad_proj, mixed, grad_branch):
+    rows = normed.shape[0]
+    steps = D // LANES
+    part = DI // steps
+    return head_call(
+        weight_grads_kernel,
+        steps,
+        [
+            pl.BlockSpec((rows, LANES), lambda i: (0, i)),
+            pl.BlockSpec((rows, ZW), lambda i: (0, 0)),
+            pl.BlockSpec((rows, part), lambda i: (0, i)),
+            pl.BlockSpec((rows, D), lambda i: (0, 0)),
         ],
-        out_specs=sp["table"],
-        out_shape=jax.ShapeDtypeStruct((vocab_rows, width), bf16),
-        scratch_shapes=[pltpu.VMEM((VTILE, tokens), bf16)],
-        compiler_params=head_params(),
-        cost_estimate=pl.CostEstimate(
-            flops=2 * vocab_rows * width * tokens,
-            transcendentals=0,
-            bytes_accessed=2 * vocab_rows * (width + tokens),
-        ),
-    )(hidden, kept, fac, weight, labels)
+        [pl.BlockSpec((LANES, ZW), lambda i: (i, 0)), pl.BlockSpec((part, D), lambda i: (i, 0))],
+        [((D, ZW), bf16), ((DI, D), bf16)],
+        (),
+        (normed, grad_proj, mixed, grad_branch),
+        rows * (ZW + DI),
+    )
 
 
 def shift_chunks(block, distance):
@@ -1245,7 +1293,6 @@
         scratch=(pltpu.VMEM((PAIRS, rows, LANES), f32),),
     )
     later = carry_chain(decay, gstate, -1)
-    grad_out = dot_tn(mixed, grad_branch).astype(bf16)
     dx, dhalo, ddr, dconv, dsmall = local_call(
         back_kernel,
         (
@@ -1280,7 +1327,7 @@
         [dz, dx.astype(bf16), ddr[:, :HEADS].astype(bf16)], axis=1
     )
     grad_normed = dot_nt(grad_proj, w_in)
-    grad_in = dot_tn(normed, grad_proj).astype(bf16)
+    grad_in, grad_out = weight_grads(normed, grad_proj, mixed, grad_branch)
     grad_prev, dpre_gain = norm_back(grad_normed, hidden, vec["pre_gain"])
     grad_vec = jnp.concatenate(
         [
@@ -1387,28 +1434,29 @@
     lengths = lax.dynamic_index_in_dim(seq_lengths, group_index, 1, keepdims=True)
     valid = in_order((jnp.arange(seq_rows)[None, :] < lengths).astype(f32))
     local_labels = labels - shard_index * vocab_rows
-    kept, tile_stats = head_stats(table, group_hidden.T, local_labels)
+    kept, tile_stats = head_stats(table, group_hidden, local_labels)
     top = jnp.max(tile_stats[:, 0], axis=0)
     summed = jnp.sum(tile_stats[:, 1] * jnp.exp(tile_stats[:, 0] - top), axis=0)
-    stats = jnp.stack(
-        [top, summed, jnp.sum(tile_stats[:, 2], axis=0), jnp.sum(tile_stats[:, 3], axis=0)]
-    )
-    stats = lax.all_gather(stats, "fsdp", axis=0)
+    stats = lax.all_gather(jnp.stack([top, summed]), "fsdp", axis=0)
     row_top = jnp.max(stats[:, 0], axis=0)
     expsum = jnp.sum(stats[:, 1] * jnp.exp(stats[:, 0] - row_top), axis=0)
-    target = jnp.sum(stats[:, 2], axis=0)
-    logit_sum = jnp.sum(stats[:, 3], axis=0)
     log_total = row_top + jnp.log(expsum)
-    per_row = log_total - 0.9 * target - 0.1 * logit_sum / VOCAB + z_weight * log_total * log_total
     own_mask = jnp.arange(tokens) // rows == shard_index
-    loss_sum = jnp.sum(jnp.where(own_mask, per_row * valid[0], 0.0))
+    per_row = jnp.where(own_mask, log_total + z_weight * log_total * log_total, 0.0)
+    loss_sum = jnp.sum((per_row - 0.9 * jnp.sum(tile_stats[:, 2], axis=0)) * valid[0])
     weight = valid / total_count
     scale = weight[0] * (1.0 + 2.0 * z_weight * log_total)
     fac = (scale * jnp.exp(tile_stats[:, 0] - log_total))[:, None, :]
+    own_valid = lax.dynamic_slice_in_dim(valid[0], shard_index * rows, rows)
+    hidden_sum = jnp.sum(final_low.astype(f32) * own_valid[:, None], axis=0)
+    column_sum = jnp.zeros((groups, own_cols), f32)
+    column_sum = jnp.where(
+        jnp.arange(groups)[:, None] == group_index, jnp.sum(embed_low.astype(f32), axis=0), column_sum
+    ).reshape(D)
 
     rows_grad = head_rows(table, kept, fac, weight, local_labels)
     own_grad = lax.psum_scatter(
-        rows_grad.T.astype(bf16), "fsdp", scatter_dimension=0, tiled=True
+        rows_grad, "fsdp", scatter_dimension=0, tiled=True
     ).astype(f32)
     table_grad = head_table(group_hidden, kept, fac, weight, local_labels, vocab_rows)
     table_part = lax.psum_scatter(table_grad, "dp", scatter_dimension=1, tiled=True)
@@ -1431,10 +1479,10 @@
         whole += [in_parts[l], out_parts[l]]
     summed_parts = reduce_layers(whole)
     spread = after(spread, summed_parts)
-    (table_total,) = local_call(
+    table_total, table_squares = local_call(
         spread_kernel,
         (count, row_list, tok_list, spread, table_part),
-        (((vocab_rows, own_cols), f32),),
+        (((vocab_rows, own_cols), f32), ((8, own_cols), f32)),
         scratch=(pltpu.VMEM((every + 8, own_cols), f32),),
         in_smem=(0, 1, 2),
     )
@@ -1443,22 +1491,29 @@
     owner_squares = (
         jnp.sum(grad_in_all * grad_in_all)
         + jnp.sum(grad_out_all * grad_out_all)
-        + jnp.sum(table_total * table_total)
+        + jnp.sum(table_squares)
     )
     small = vector_params.shape[0]
-    padded = pl.cdiv(small + 2, 16 * LANES) * 16 * LANES
+    used = small + 2 * D + 2
+    padded = pl.cdiv(used, 16 * LANES) * 16 * LANES
     packed = jnp.concatenate(
         vec_parts
         + [
             dfinal,
+            hidden_sum,
+            column_sum,
             owner_squares.reshape(1),
             loss_sum.reshape(1),
-            jnp.zeros((padded - small - 2,), f32),
+            jnp.zeros((padded - used,), f32),
         ]
     )
     packed = total_of(packed.reshape(-1, LANES)).reshape(-1)
     vector_total = packed[:small]
-    squares_total, loss_total = packed[small], packed[small + 1]
+    hidden_total = packed[small : small + D]
+    column_total = packed[small + D : small + 2 * D]
+    squares_total = packed[used - 2]
+    mean_part = jnp.sum(hidden_total * column_total) * (0.1 / VOCAB)
+    loss_total = packed[used - 1] - mean_part
     grad_norm = jnp.sqrt(squares_total + jnp.sum(vector_total * vector_total))
     factor = jnp.minimum(1.0, clip_limit / grad_norm)
     loss_value = loss_total / total_count

time: 1250 us -> 1200 us (0.960)
  local copies, waits for them, and re-layouts: 71.7 us -> 37.6 us
  waiting for transfers between devices: 210 us -> 243 us
  Pallas kernels: 754 us -> 722 us
  matrix products: 62.6 us -> 39.3 us
  other arithmetic: 57.7 us -> 71.2 us
    pallas_call x3 -> x5, Pallas kernels: 167 us -> 141 us  [head_call(): pl.pallas_call(kernel, grid=(grid,), in_specs=in_specs, out_specs=out_spe...]
    convert_element_type x2 -> x0, local copies, waits for them, and re-layouts: 24 us -> none  [layer_backward(): grad_in = dot_tn(normed, grad_proj).astype(bf16)]
    dot_general x4 -> x0, matrix products: 22.3 us -> none  [dot_tn(): lax.dot_general(a, b, (((0,), (0,)), ((), ())), precision=precision, pref...]
    reduce_scatter x1, waiting for transfers between devices: 0.01 us -> 13.2 us  [whole_step(): lax.psum_scatter(rows_grad, 'fsdp', scatter_dimension=0, tiled=True)]
  transfers between devices with their start and end apart: 11 -> 11, of which waited for: 5 -> 7; matrix products, arithmetic and copies ran while one was open for 6% -> 3% of each run, Pallas kernels for 31% -> 32%
where the time goes in v2:
time: 1200 us; the launch traced here: 1190 us
  Pallas kernels  722 us (60%)
  waiting for transfers between devices  243 us (20%)
  other arithmetic  71.2 us (6%)
  matrix products  39.3 us (3%)
  local copies, waits for them, and re-layouts  37.6 us (3%)
  blocking collectives  32.3 us (3%)
  between operations  22.8 us (2%)
  starting transfers between devices  22.7 us (2%)
    pallas_call x7, Pallas kernels, comm_call(): pl.pallas_call(kernel, out_shape=[jax.ShapeDtypeStruct(shape, kind) for s...  421 us
    pallas_call x10, Pallas kernels, local_call(): pl.pallas_call(kernel, out_shape=[jax.ShapeDtypeStruct(shape, kind) for s...  161 us
    pallas_call x5, Pallas kernels, head_call(): pl.pallas_call(kernel, grid=(grid,), in_specs=in_specs, out_specs=out_spe...  141 us
    all_gather x1, waiting for transfers between devices, whole_step(): table = lax.all_gather(embed_low, 'dp', axis=1, tiled=True)  127 us
    all_gather x1, waiting for transfers between devices, whole_step(): group_hidden = lax.all_gather(final_low, 'fsdp', axis=0, tiled=True)  44.7 us
    reduce_scatter x1, waiting for transfers between devices, whole_step(): lax.psum_scatter(looked.reshape(shards * groups * rows, own_cols), 'fsdp'...  44.3 us
  transfers between devices with their start and end apart: 11, of which 7 were waited for; matrix products, arithmetic and copies ran while one was open for 3% of the time, Pallas kernels for 32%

profile of v2, /device:TPU:12, one launch (start us, length us, event | category | flops | bytes accessed | tf_op | source)
XLA Modules:
  0.0 1191.1 jit_solution(4056452357122996984)
XLA Ops:
  7.2 8.2 all-gather
  23.0 10.7 shard_map.286
  37.9 44.3 %reduce-scatter.4.cloned.1.call-done = bf16[1024,256]{1,0:T(8,128)(2,1)} async-done(((bf16[8192,256]{1,0:T(8,128)(2,1)}), bf16[1024,256]{1,0:T(8,128)(2,1)}) %reduce-scatter.4.cloned.1.call-update) | async-done | bytes 524304 | tf_op jit(solution)/shard_map/reduce_scatter | solution.py:1405
  90.5 116.2 %shard_map.287 = (bf16[4,4,2,32,4384]{4,3,2,1,0:T(8,128)(2,1)}, bf16[4,4,2,64,1024]{4,3,2,1,0:T(8,128)(2,1)}, bf16[4,4,2,32,4384]{4,3,2,1,0:T(8,128)(2,1)}, bf16[4,4,2,64,1024]{4,3,2,1,0:T(8,128)(2,1)}) custom-call(bf16[32,4384]{1,0:T(8,128)(2,1)} %get-tuple-element.77.refs_0_, bf16[64,1024]{1,0:T(8,128)(2,1)} %get-tuple-element.78.refs_1_, ...), custom_call_target="tpu_custom_call" | custom-call | flops 19759104 | bytes 39518208 | tf_op jit(solution)/shard_map/pallas_call | solution.py:170
  224.2 13.5 %shard_map.288 = (f32[256,2304]{1,0:T(8,128)}, f32[256,2048]{1,0:T(8,128)}, f32[2048,128]{1,0:T(8,128)}, f32[256,128]{1,0:T(8,128)}, f32[256,128]{1,0:T(8,128)}) custom-call(f32[256,4384]{1,0:T(8,128)} %copy-done, f32[8,2304]{1,0:T(8,128)} %copy-done.31, f32[4,2304]{1,0:T(4,128)} %reshape.296.cw_ref, f32[1,2304]{1,0:T(1,128)} %broadcast_in_dim.45.cb_ref, ...), custom_call_target="tpu_custom_call" | custom-call | flops 4618240 | bytes 9236480 | tf_op jit(solution)/shard_map/pallas_call | solution.py:66
  238.9 18.2 %shard_map.289.sin_ref = bf16[2048,128]{1,0:T(8,128)(2,1)} custom-call(f32[32]{0:T(128)} %exponential_bitcast_fusion.1.decay_ref, f32[2048,128]{1,0:T(8,128)} %get-tuple-element.85.local_ref), custom_call_target="tpu_custom_call" | custom-call | flops 524288 | bytes 1048576 | tf_op jit(solution)/shard_map/pallas_call | solution.py:170
  257.0 10.4 shard_map.290
  289.6 13.4 %shard_map.291 = (f32[256,2304]{1,0:T(8,128)}, f32[256,2048]{1,0:T(8,128)}, f32[2048,128]{1,0:T(8,128)}, f32[256,128]{1,0:T(8,128)}, f32[256,128]{1,0:T(8,128)}) custom-call(f32[256,4384]{1,0:T(8,128)} %copy-done.1, f32[8,2304]{1,0:T(8,128)} %copy-done.32, f32[4,2304]{1,0:T(4,128)} %reshape.299.cw_ref, f32[1,2304]{1,0:T(1,128)} %broadcast_in_dim.85.cb_ref, ...), custom_call_target="tpu_custom_call" | custom-call | flops 4618240 | bytes 9236480 | tf_op jit(solution)/shard_map/pallas_call | solution.py:66
  304.2 15.4 %shard_map.292.sin_ref = bf16[2048,128]{1,0:T(8,128)(2,1)} custom-call(f32[32]{0:T(128)} %exponential_bitcast_fusion.decay_ref, f32[2048,128]{1,0:T(8,128)} %get-tuple-element.92.local_ref), custom_call_target="tpu_custom_call" | custom-call | flops 524288 | bytes 1048576 | tf_op jit(solution)/shard_map/pallas_call | solution.py:170
  319.6 10.5 shard_map.293
  342.3 44.7 %all-gather.10.cloned.1.call-done.h_ref = bf16[2048,1024]{1,0:T(8,128)(2,1)} async-done(((bf16[256,1024]{1,0:T(8,128)(2,1)}), bf16[2048,1024]{1,0:T(8,128)(2,1)}) %all-gather.10.cloned.1.call-update) | async-done | bytes 4194320 | tf_op jit(solution)/shard_map/all_gather | solution.py:1428
  387.0 127.2 %all-gather.8.cloned.1.call-done.e_ref = bf16[6286,1024]{1,0:T(8,128)(2,1)} async-done(((bf16[6286,256]{1,0:T(8,128)(2,1)}), bf16[6286,1024]{1,0:T(8,128)(2,1)}) %all-gather.8.cloned.1.call-update) | async-done | bytes 12873744 | tf_op jit(solution)/shard_map/all_gather | solution.py:1418
  514.2 50.1 %shard_map.294 = (bf16[6400,2048]{1,0:T(8,128)(2,1)}, f32[5,8,2048]{2,1,0:T(8,128)}) custom-call(bf16[6286,1024]{1,0:T(8,128)(2,1)} %all-gather.8.cloned.1.call-done.e_ref, bf16[2048,1024]{1,0:T(8,128)(2,1)} %all-gather.10.cloned.1.call-done.h_ref, s32[1,2048]{1,0:T(1,128)} %sub.98.lab_ref), custom_call_target="tpu_custom_call" | custom-call | flops 26365394944 | bytes 51494912 | tf_op jit(solution)/shard_map/pallas_call | solution.py:1007
  566.8 14.0 %all-gather.3 = f32[8,2,2048]{2,1,0:T(2,128)S(1)} all-gather(f32[1,2,2048]{2,1,0:T(2,128)S(1)} %maximum_bitcast_fusion), channel_id=3, replica_groups=mesh['dp'=4,'fsdp'=8] {'fsdp'}, dimensions={0}, use_global_device_ids=true | all-gather | bytes 147456 | tf_op jit(solution)/shard_map/all_gather | solution.py:1440
  583.3 36.5 %shard_map.295 = bf16[2048,1024]{1,0:T(8,128)(2,1)} custom-call(bf16[6286,1024]{1,0:T(8,128)(2,1)} %all-gather.8.cloned.1.call-done.e_ref, bf16[6400,2048]{1,0:T(8,128)(2,1)} %get-tuple-element.96.q_ref, f32[5,1,2048]{2,1,0:T(1,128)} %exponential_multiply_fusion.fac_ref, f32[1,2048]{1,0:T(1,128)} %div.58.w_ref, s32[1,2048]{1,0:T(1,128)} %sub.98.lab_ref), custom_call_target="tpu_custom_call" | custom-call | flops 26365394944 | bytes 51494912 | tf_op jit(solution)/shard_map/pallas_call | solution.py:1007
  619.9 33.7 %shard_map.296 = bf16[6286,1024]{1,0:T(8,128)(2,1)} custom-call(bf16[2048,1024]{1,0:T(8,128)(2,1)} %all-gather.10.cloned.1.call-done.h_ref, bf16[6400,2048]{1,0:T(8,128)(2,1)} %get-tuple-element.96.q_ref, f32[5,1,2048]{2,1,0:T(1,128)} %exponential_multiply_fusion.fac_ref, f32[1,2048]{1,0:T(1,128)} %div.58.w_ref, s32[1,2048]{1,0:T(1,128)} %sub.98.lab_ref), custom_call_target="tpu_custom_call" | custom-call | flops 26365394944 | bytes 51494912 | tf_op jit(solution)/shard_map/pallas_call | solution.py:1007
  653.6 13.2 %reduce-scatter.6.cloned.1.call-done = bf16[256,1024]{1,0:T(8,128)(2,1)} async-done(((bf16[2048,1024]{1,0:T(8,128)(2,1)}), bf16[256,1024]{1,0:T(8,128)(2,1)}) %reduce-scatter.6.cloned.1.call-update) | async-done | bytes 524304 | tf_op jit(solution)/shard_map/reduce_scatter | solution.py:1458
  673.5 13.5 %shard_map.297 = (f32[256,2048]{1,0:T(8,128)}, bf16[256,2048]{1,0:T(8,128)(2,1)}, f32[1,2048]{1,0:T(1,128)}, f32[2048,128]{1,0:T(8,128)}) custom-call(f32[256,2048]{1,0:T(8,128)} %fusion.31.dyn_ref, f32[256,2048]{1,0:T(8,128)} %get-tuple-element.99.y_ref, f32[256,4384]{1,0:T(8,128)} %copy-done.1, f32[256,2304]{1,0:T(8,128)} %get-tuple-element.90.pre_ref, ...), custom_call_target="tpu_custom_call" | custom-call | flops 11182080 | bytes 22364160 | tf_op jit(solution)/shard_map/pallas_call | solution.py:66
  687.0 23.6 %shard_map.298.gin_ref = bf16[2048,128]{1,0:T(8,128)(2,1)} custom-call(f32[32]{0:T(128)} %exponential_bitcast_fusion.decay_ref, f32[2048,128]{1,0:T(8,128)} %get-tuple-element.103.local_ref), custom_call_target="tpu_custom_call" | custom-call | flops 524288 | bytes 1048576 | tf_op jit(solution)/shard_map/pallas_call | solution.py:170
  710.6 30.8 %shard_map.299 = (f32[256,2304]{1,0:T(8,128)}, f32[8,2304]{1,0:T(8,128)}, f32[256,128]{1,0:T(8,128)}, f32[8,2304]{1,0:T(8,128)}, f32[8,128]{1,0:T(8,128)}) custom-call(f32[256,2048]{1,0:T(8,128)} %get-tuple-element.101.dy_ref, f32[256,2048]{1,0:T(8,128)} %get-tuple-element.99.y_ref, f32[256,4384]{1,0:T(8,128)} %copy-done.1, f32[8,2304]{1,0:T(8,128)} %copy-done.32, ...), custom_call_target="tpu_custom_call" | custom-call | flops 12473344 | bytes 24946688 | tf_op jit(solution)/shard_map/pallas_call | solution.py:66
  749.6 7.1 multiply_reduce_fusion.4
  762.1 13.5 %shard_map.300 = (f32[256,2048]{1,0:T(8,128)}, bf16[256,2048]{1,0:T(8,128)(2,1)}, f32[1,2048]{1,0:T(1,128)}, f32[2048,128]{1,0:T(8,128)}) custom-call(f32[256,2048]{1,0:T(8,128)} %fusion.32.dyn_ref, f32[256,2048]{1,0:T(8,128)} %get-tuple-element.107.y_ref, f32[256,4384]{1,0:T(8,128)} %copy-done, f32[256,2304]{1,0:T(8,128)} %get-tuple-element.83.pre_ref, ...), custom_call_target="tpu_custom_call" | custom-call | flops 11182080 | bytes 22364160 | tf_op jit(solution)/shard_map/pallas_call | solution.py:66
  775.6 19.5 %shard_map.301.gin_ref = bf16[2048,128]{1,0:T(8,128)(2,1)} custom-call(f32[32]{0:T(128)} %exponential_bitcast_fusion.1.decay_ref, f32[2048,128]{1,0:T(8,128)} %get-tuple-element.110.local_ref), custom_call_target="tpu_custom_call" | custom-call | flops 524288 | bytes 1048576 | tf_op jit(solution)/shard_map/pallas_call | solution.py:170
  795.1 30.5 %shard_map.302 = (f32[256,2304]{1,0:T(8,128)}, f32[8,2304]{1,0:T(8,128)}, f32[256,128]{1,0:T(8,128)}, f32[8,2304]{1,0:T(8,128)}, f32[8,128]{1,0:T(8,128)}) custom-call(f32[256,2048]{1,0:T(8,128)} %get-tuple-element.108.dy_ref, f32[256,2048]{1,0:T(8,128)} %get-tuple-element.107.y_ref, f32[256,4384]{1,0:T(8,128)} %copy-done, f32[8,2304]{1,0:T(8,128)} %copy-done.31, ...), custom_call_target="tpu_custom_call" | custom-call | flops 12473344 | bytes 24946688 | tf_op jit(solution)/shard_map/pallas_call | solution.py:66
  841.9 10.1 all_to_all.10
  861.9 10.2 shard_map.304
  874.8 10.2 shard_map.303
  885.0 205.9 %shard_map.305 = (f32[32,4384]{1,0:T(8,128)}, f32[64,1024]{1,0:T(8,128)}, f32[32,4384]{1,0:T(8,128)}, f32[64,1024]{1,0:T(8,128)}) custom-call(bf16[4,4,2,32,4384]{4,3,2,1,0:T(8,128)(2,1)} %bitcast.131, bf16[4,4,2,64,1024]{4,3,2,1,0:T(8,128)(2,1)} %bitcast.133, bf16[4,4,2,32,4384]{4,3,2,1,0:T(8,128)(2,1)} %bitcast.130, bf16[4,4,2,64,1024]{4,3,2,1,0:T(8,128)(2,1)} %bitcast.132), custom_call_target="tpu_custom_call" | custom-call | flops 26345472 | bytes 52690944 | tf_op jit(solution)/shard_map/pallas_call | solution.py:170
  1096.2 11.0 reduce-scatter.8.cloned.1.call-done.base_ref
  1107.2 13.8 %shard_map.306 = (f32[6286,256]{1,0:T(8,128)}, f32[8,256]{1,0:T(8,128)}) custom-call(s32[1]{0:T(128)} %bitcast.1.count_ref, s32[8192]{0:T(1024)} %get-tuple-element.188.row_ref, s32[8192]{0:T(1024)} %get-tuple-element.187.tok_ref, bf16[8192,256]{1,0:T(8,128)(2,1)} %bitcast.134, bf16[6286,256]{1,0:T(8,128)(2,1)} %reduce-scatter.8.cloned.1.call-done.base_ref), custom_call_target="tpu_custom_call" | custom-call | flops 7478276 | bytes 14956552 | tf_op jit(solution)/shard_map/pallas_call | solution.py:66
  1124.4 21.8 %shard_map.307 = f32[256,128]{1,0:T(8,128)} custom-call(f32[256,128]{1,0:T(8,128)} %bitcast.152), custom_call_target="tpu_custom_call" | custom-call | flops 393216 | bytes 786432 | tf_op jit(solution)/shard_map/pallas_call | solution.py:170
  1172.7 9.1 add_multiply_fusion
  (224 shorter events, 157.3 us)
Async XLA Ops:
  7.2 75.0 %reduce-scatter.4.cloned.1.call-start = ((), (), s32[]{:S(2)}) async-start(), calls=%async_computation.5 | async-start | bytes 4718592 | tf_op jit(solution)/shard_map/reduce_scatter | solution.py:1405
  82.2 125.7 %all-to-all-start = ((bf16[4,256,256]{2,1,0:T(8,128)(2,1)}), bf16[4,256,256]{2,1,0:T(8,128)(2,1)S(1)}, u32[]{:S(2)}, u32[]{:S(2)}) async-start(bf16[4,256,256]{2,1,0:T(8,128)(2,1)} %bitcast.151), calls=%async_computation.1 | async-start | bytes 1048576 | tf_op jit(solution)/shard_map/all_to_all | solution.py:1408
  86.4 300.6 %all-gather.10.cloned.1.call-start = ((), (), s32[]{:S(2)}) async-start(), calls=%async_computation.7 | async-start | bytes 4718592 | tf_op jit(solution)/shard_map/all_gather | solution.py:1428
  216.9 6.4 collective-permute-start
  223.2 44.3 %copy-start.15 = (f32[256,1024]{1,0:T(8,128)}, f32[256,1024]{1,0:T(8,128)S(1)}, u32[]{:S(2)}) copy-start(f32[256,1024]{1,0:T(8,128)S(1)} %copy.99) | copy-start | bytes 3145732
  280.7 8.3 collective-permute-start.1
  319.6 10.5 copy-start.18
  336.1 178.2 %all-gather.8.cloned.1.call-start = ((), (), s32[]{:S(2)}) async-start(), calls=%async_computation.6 | async-start | bytes 16097280 | tf_op jit(solution)/shard_map/all_gather | solution.py:1418
  341.0 325.8 %reduce-scatter.6.cloned.1.call-start = ((), (), s32[]{:S(2)}) async-start(), calls=%async_computation.8 | async-start | bytes 4718592 | tf_op jit(solution)/shard_map/reduce_scatter | solution.py:1458
  619.8 476.3 %all-gather.12.cloned.1.call-start = ((), (), s32[]{:S(2)}) async-start(), calls=%async_computation.10 | async-start | bytes 4718592 | tf_op jit(solution)/shard_map/all_gather | solution.py:1475
  653.6 16.2 %copy-start.5 = (f32[256,1024]{1,0:T(8,128)S(1)}, f32[256,1024]{1,0:T(8,128)}, u32[]{:S(2)}) copy-start(f32[256,1024]{1,0:T(8,128)} %copy-done.4) | copy-start | bytes 3145732
  741.5 7.1 collective-permute-start.2
  748.6 8.1 copy-start.11
  749.6 7.1 copy-start.6
  749.6 7.1 copy-start.19
  795.1 38.8 %copy-start.16 = (f32[256,1024]{1,0:T(8,128)S(1)}, f32[256,1024]{1,0:T(8,128)}, u32[]{:S(2)}) copy-start(f32[256,1024]{1,0:T(8,128)} %copy-done.15) | copy-start | bytes 3145732
  825.6 7.3 collective-permute-start.3
  832.9 7.9 copy-start.12
  852.1 255.1 %reduce-scatter.8.cloned.1.call-start = ((), (), s32[]{:S(2)}) async-start(), calls=%async_computation.9 | async-start | bytes 16097280 | tf_op jit(solution)/shard_map/reduce_scatter | solution.py:1462
  861.9 10.2 copy-start.13
  1092.7 30.4 %copy-start.35 = (f32[1,2048]{1,0:T(1,128)S(1)}, f32[1,2048]{1,0:T(1,128)}, u32[]{:S(2)}) copy-start(f32[1,2048]{1,0:T(1,128)} %get-tuple-element.120) | copy-start | bytes 24580
  1092.7 30.4 %copy-start.36 = (f32[1,2048]{1,0:T(1,128)S(1)}, f32[1,2048]{1,0:T(1,128)}, u32[]{:S(2)}) copy-start(f32[1,2048]{1,0:T(1,128)} %get-tuple-element.117) | copy-start | bytes 24580
  1094.8 58.5 %copy-start.29 = (f32[30400]{0:T(1024)S(1)}, f32[30400]{0:T(1024)}, u32[]{:S(2)}) copy-start(f32[30400]{0:T(1024)} %param.27) | copy-start | bytes 364804
  1094.8 58.5 %copy-start.33 = (f32[30400]{0:T(1024)S(1)}, f32[30400]{0:T(1024)}, u32[]{:S(2)}) copy-start(f32[30400]{0:T(1024)} %param.28) | copy-start | bytes 364804
  1096.2 58.9 %copy-start.25 = (f32[64,1024]{1,0:T(8,128)S(1)}, f32[64,1024]{1,0:T(8,128)}, u32[]{:S(2)}) copy-start(f32[64,1024]{1,0:T(8,128)} %get-tuple-element.127) | copy-start | bytes 786436
  1096.2 61.3 %copy-start.9 = (f32[2,32,4384]{2,1,0:T(8,128)S(1)}, f32[2,32,4384]{2,1,0:T(8,128)}, u32[]{:S(2)}) copy-start(f32[2,32,4384]{2,1,0:T(8,128)} %param.21) | copy-start | bytes 3366916
  1155.1 10.0 copy-start.24
  1155.1 11.2 slice-start
  1157.5 8.7 copy-start.21
  1157.6 8.7 slice-start.1
  1157.6 8.6 copy-start.7
  1172.6 9.1 copy-start.3
  (22 other events, 63.0 us)
Sparse Core Ops, SparseCore 0:
  33.9 48.2 reduce-scatter.3
  336.2 50.8 all-gather.9
  389.4 124.7 all-gather.7
  620.0 46.7 reduce-scatter.5
  852.2 44.0 all-gather.11
  899.3 207.8 reduce-scatter.7

commit v3 on v2

--- a/solution.py
+++ b/solution.py
@@ -1020,60 +1020,198 @@
     )(*ins)
 
 
-def head_stats_kernel(vocab_rows, e_ref, h_ref, lab_ref, q_ref, st_ref):
-    first = pl.program_id(0) * VTILE
-    tokens = h_ref.shape[0]
-
-    def chunk(j, ragged):
-        ns = pl.ds(pl.multiple_of(j * NTILE, NTILE), NTILE)
-        logits = dot_nt(e_ref[...], h_ref[ns, :])
-        rid = lax.broadcasted_iota(jnp.int32, (VTILE, NTILE), 0)
-        if ragged:
-            logits = jnp.where(rid < vocab_rows - first, logits, OFF)
-        top = jnp.max(logits, axis=0, keepdims=True)
-        p = jnp.exp(logits - top)
-        q_ref[:, ns] = p.astype(bf16)
-        st_ref[0, 0:1, ns] = top
-        st_ref[0, 1:2, ns] = jnp.sum(p, axis=0, keepdims=True)
+UNROLL = 8
+
+
+def head_stats_kernel(
+    table_ref, own_ref, lab_ref, w_ref,
+    q_ref, all_ref, lse_ref, fac_ref, hit_ref,
+    kept, tops, sums, hits, shown, own_sem, put_sem, z_send, z_recv, m_send, m_recv, s_send, s_recv,
+):
+    dp = lax.axis_index("dp")
+    me = lax.axis_index("fsdp")
+    shards = lax.axis_size("fsdp")
+    count = shards // MB
+    core = me % MB
+    k = me // MB
+    mate = k * MB + 1 - core
+    vocab_rows = table_ref.shape[0]
+    rows = own_ref.shape[0]
+    tiles = tops.shape[0]
+    barrier = pltpu.get_barrier_semaphore()
+    for other in range(1, shards):
+        pl.semaphore_signal(
+            barrier, inc=1, device_id=(dp, lax.rem(me + other, shards)), device_id_type=MESH
+        )
+    pl.semaphore_wait(barrier, shards - 1)
+
+    near = jnp.minimum(k, count - 1 - k)
+    long_side = jnp.where(count - 1 - k > k, 1, -1)
+
+    def chunk_at(i):
+        paired = k + (2 * (i % 2) - 1) * ((i + 1) // 2)
+        return jnp.where(i <= 2 * near, paired, k + long_side * (i - near))
+
+    def along(z):
+        return remote(
+            own_ref, all_ref.at[me], z_send.at[z], z_recv.at[k], dp, z * MB + core
+        )
+
+    def landed(z):
+        return remote(
+            own_ref, all_ref.at[z * MB + core], z_send.at[z], z_recv.at[z], dp, me
+        )
+
+    def to_mate(z):
+        at = all_ref.at[z * MB + core]
+        return remote(at, at, m_send.at[z], m_recv.at[z], dp, mate)
+
+    def from_mate(z):
+        at = all_ref.at[z * MB + 1 - core]
+        return remote(at, at, m_send.at[z], m_recv.at[z], dp, mate)
+
+    keep = pltpu.make_async_copy(own_ref, all_ref.at[me], own_sem)
+    keep.start()
+    for i in range(1, count):
+        along(chunk_at(i)).start()
+    keep.wait()
+    to_mate(k).start()
+    whole = vocab_rows - vocab_rows % 16
+    for slot in range(2):
+        kept[slot, whole:, :] = jnp.zeros((kept.shape[1] - whole, rows), bf16)
+
+    def put(step, b):
+        return pltpu.make_async_copy(
+            kept.at[step % 2],
+            q_ref.at[:, pl.ds(pl.multiple_of(b * rows, rows), rows)],
+            put_sem.at[step % 2],
+        )
+
+    def block(step, b):
+        @pl.when(step >= 2)
+        def _():
+            put(step, b).wait()
+
+        slot = step % 2
+        ns = pl.ds(pl.multiple_of(b * rows, rows), rows)
+        h = all_ref[b]
         label = lab_ref[0:1, ns]
-        hit = jnp.where(rid == label - first, logits, 0.0)
-        inside = jnp.logical_and(label >= 0, label < vocab_rows)
-        st_ref[0, 2:3, ns] = jnp.where(inside, jnp.sum(hit, axis=0, keepdims=True), 0.0)
-
-    def run(ragged):
-        lax.fori_loop(
-            0, tokens // NTILE, lambda j, _: (chunk(j, ragged), 0)[1], 0, unroll=UNROLL
-        )
-
-    end = pl.program_id(0) == pl.num_programs(0) - 1
-
-    @pl.when(end)
-    def _():
-        run(True)
-
-    @pl.when(jnp.logical_not(end))
-    def _():
-        run(False)
-
-
-UNROLL = 8
-
-
-def head_stats(table, hidden, labels):
+        for t in range(tiles):
+            first = t * VTILE
+            size = min(VTILE, vocab_rows - first)
+            logits = dot_nt(table_ref[first : first + size, :], h)
+            top = jnp.max(logits, axis=0, keepdims=True)
+            p = jnp.exp(logits - top)
+            kept[slot, first : first + size, :] = p.astype(bf16)
+            tops[t, 0:1, ns] = top
+            sums[t, 0:1, ns] = jnp.sum(p, axis=0, keepdims=True)
+            rid = lax.broadcasted_iota(jnp.int32, (size, rows), 0)
+            hits[t, 0:1, ns] = jnp.sum(
+                jnp.where(rid == label - first, logits, 0.0), axis=0, keepdims=True
+            )
+        put(step, b).start()
+
+    def chunk(i, _):
+        z = chunk_at(i)
+
+        @pl.when(i > 0)
+        def _():
+            landed(z).wait_recv()
+            to_mate(z).start()
+
+        block(2 * i, z * MB + core)
+        from_mate(z).wait_recv()
+        block(2 * i + 1, z * MB + 1 - core)
+        return 0
+
+    lax.fori_loop(0, count, chunk, 0)
+    top = tops[0, 0:1, :]
+    for t in range(1, tiles):
+        top = jnp.maximum(top, tops[t, 0:1, :])
+    total = jnp.zeros_like(top)
+    hit = jnp.zeros_like(top)
+    for t in range(tiles):
+        total = total + sums[t, 0:1, :] * jnp.exp(tops[t, 0:1, :] - top)
+        hit = hit + hits[t, 0:1, :]
+    hit_ref[...] = hit
+    shown[me, 0:1, :] = top
+    shown[me, 1:2, :] = total
+
+    def tell(other):
+        at = shown.at[me]
+        return remote(
+            at, at, s_send.at[other], s_recv.at[me], dp, lax.rem(me + other, shards)
+        )
+
+    def told(other):
+        at = shown.at[lax.rem(me + other, shards)]
+        return remote(
+            at, at, s_send.at[other], s_recv.at[lax.rem(me + other, shards)], dp, mate
+        )
+
+    for other in range(1, shards):
+        tell(other).start()
+    for other in range(1, shards):
+        told(other).wait_recv()
+    top = shown[0, 0:1, :]
+    for f in range(1, shards):
+        top = jnp.maximum(top, shown[f, 0:1, :])
+    total = jnp.zeros_like(top)
+    for f in range(shards):
+        total = total + shown[f, 1:2, :] * jnp.exp(shown[f, 0:1, :] - top)
+    lse = top + jnp.log(total)
+    lse_ref[...] = lse
+    scale = w_ref[...] * (1.0 + 2.0 * z_weight * lse)
+    for t in range(tiles):
+        fac_ref[t, 0:1, :] = scale * jnp.exp(tops[t, 0:1, :] - lse)
+    for other in range(1, shards):
+        tell(other).wait_send()
+    for i in range(1, count):
+        along(chunk_at(i)).wait_send()
+    for z in range(count):
+        to_mate(z).wait_send()
+    put(0, 0).wait()
+    put(1, 0).wait()
+
+
+def head_stats(table, own, labels, weight):
     vocab_rows, width = table.shape
-    tokens = hidden.shape[0]
+    rows = own.shape[0]
+    shards = lax.axis_size("fsdp")
+    count = shards // MB
+    tokens = shards * rows
     tiles = pl.cdiv(vocab_rows, VTILE)
-    sp = head_specs(width, tokens)
-    return head_call(
-        functools.partial(head_stats_kernel, vocab_rows),
-        tiles,
-        [sp["table"], sp["hidden"], sp["row"]],
-        [sp["kept"], pl.BlockSpec((1, 8, tokens), lambda i: (i, 0, 0))],
-        [((tiles * VTILE, tokens), bf16), ((tiles, 8, tokens), f32)],
-        (),
-        (table, hidden, labels),
-        vocab_rows * tokens,
-    )
+    kept, everyone, lse, fac, hit = comm_call(
+        head_stats_kernel,
+        6,
+        (table, own, labels, weight),
+        (
+            ((tiles * VTILE, tokens), bf16),
+            ((shards, rows, width), bf16),
+            ((1, tokens), f32),
+            ((tiles, 1, tokens), f32),
+            ((1, tokens), f32),
+        ),
+        (
+            pltpu.VMEM((2, tiles * VTILE, rows), bf16),
+            pltpu.VMEM((tiles, 1, tokens), f32),
+            pltpu.VMEM((tiles, 1, tokens), f32),
+            pltpu.VMEM((tiles, 1, tokens), f32),
+            pltpu.VMEM((shards, 2, tokens), f32),
+            pltpu.SemaphoreType.DMA,
+            pltpu.SemaphoreType.DMA((2,)),
+            pltpu.SemaphoreType.DMA((count,)),
+            pltpu.SemaphoreType.DMA((count,)),
+            pltpu.SemaphoreType.DMA((count,)),
+            pltpu.SemaphoreType.DMA((count,)),
+            pltpu.SemaphoreType.DMA((shards,)),
+            pltpu.SemaphoreType.DMA((shards,)),
+        ),
+        (pltpu.VMEM,) * 4,
+        (pl.ANY, pltpu.VMEM, pltpu.VMEM, pltpu.VMEM, pltpu.VMEM),
+        own.size * 2 * 7,
+    )
+    return kept, everyone.reshape(tokens, width), lse, fac, hit
 
 
 def logit_grads(q, fac, weight, rid, label):
@@ -1425,7 +1563,6 @@
         records.append(record)
 
     final_low = (hidden * norm_scale(hidden) * final_gain).astype(bf16)
-    group_hidden = lax.all_gather(final_low, "fsdp", axis=0, tiled=True)
 
     def in_order(per_seq):
         return per_seq.reshape(MB, chunks, rows).transpose(1, 0, 2).reshape(1, tokens)
@@ -1434,19 +1571,11 @@
     lengths = lax.dynamic_index_in_dim(seq_lengths, group_index, 1, keepdims=True)
     valid = in_order((jnp.arange(seq_rows)[None, :] < lengths).astype(f32))
     local_labels = labels - shard_index * vocab_rows
-    kept, tile_stats = head_stats(table, group_hidden, local_labels)
-    top = jnp.max(tile_stats[:, 0], axis=0)
-    summed = jnp.sum(tile_stats[:, 1] * jnp.exp(tile_stats[:, 0] - top), axis=0)
-    stats = lax.all_gather(jnp.stack([top, summed]), "fsdp", axis=0)
-    row_top = jnp.max(stats[:, 0], axis=0)
-    expsum = jnp.sum(stats[:, 1] * jnp.exp(stats[:, 0] - row_top), axis=0)
-    log_total = row_top + jnp.log(expsum)
+    weight = valid / total_count
+    kept, group_hidden, lse, fac, target = head_stats(table, final_low, local_labels, weight)
     own_mask = jnp.arange(tokens) // rows == shard_index
-    per_row = jnp.where(own_mask, log_total + z_weight * log_total * log_total, 0.0)
-    loss_sum = jnp.sum((per_row - 0.9 * jnp.sum(tile_stats[:, 2], axis=0)) * valid[0])
-    weight = valid / total_count
-    scale = weight[0] * (1.0 + 2.0 * z_weight * log_total)
-    fac = (scale * jnp.exp(tile_stats[:, 0] - log_total))[:, None, :]
+    per_row = jnp.where(own_mask, lse[0] + z_weight * lse[0] * lse[0], 0.0)
+    loss_sum = jnp.sum((per_row - 0.9 * target[0]) * valid[0])
     own_valid = lax.dynamic_slice_in_dim(valid[0], shard_index * rows, rows)
     hidden_sum = jnp.sum(final_low.astype(f32) * own_valid[:, None], axis=0)
     column_sum = jnp.zeros((groups, own_cols), f32)

time: 1200 us -> 1010 us (0.84)
  waiting for transfers between devices: 243 us -> 37.6 us
  Pallas kernels: 722 us -> 742 us
  blocking collectives: 32.3 us -> 18.3 us
    all_gather x1, waiting for transfers between devices: 127 us -> 0.01 us  [whole_step(): table = lax.all_gather(embed_low, 'dp', axis=1, tiled=True)]
    pallas_call x7 -> x8, Pallas kernels: 421 us -> 489 us  [comm_call(): pl.pallas_call(kernel, out_shape=[jax.ShapeDtypeStruct(shape, kind) for s...]
    pallas_call x5 -> x4, Pallas kernels: 141 us -> 91.5 us  [head_call(): pl.pallas_call(kernel, grid=(grid,), in_specs=in_specs, out_specs=out_spe...]
    all_gather x1 -> x0, waiting for transfers between devices: 44.7 us -> none  [whole_step(): group_hidden = lax.all_gather(final_low, 'fsdp', axis=0, tiled=True)]
    reduce_scatter x1, waiting for transfers between devices: 44.3 us -> 0.01 us  [whole_step(): lax.psum_scatter(looked.reshape(shards * groups * rows, own_cols), 'fsdp'...]
    ppermute x4, waiting for transfers between devices: 2.07 us -> 16.2 us  [shift_chunks(): return lax.ppermute(block, 'fsdp', route)]
    all_gather x1 -> x0, blocking collectives: 14 us -> none  [whole_step(): stats = lax.all_gather(jnp.stack([top, summed]), 'fsdp', axis=0)]
  transfers between devices with their start and end apart: 11 -> 10, of which waited for: 7 -> 4; matrix products, arithmetic and copies ran while one was open for 3% -> 7% of each run, Pallas kernels for 32% -> 44%
where the time goes in v3:
time: 1010 us; the launch traced here: 998 us
  Pallas kernels  742 us (73%)
  other arithmetic  71.1 us (7%)
  matrix products  41.8 us (4%)
  local copies, waits for them, and re-layouts  39.4 us (4%)
  waiting for transfers between devices  37.6 us (4%)
  starting transfers between devices  23.9 us (2%)
  between operations  23.9 us (2%)
  blocking collectives  18.3 us (2%)
    pallas_call x8, Pallas kernels, comm_call(): pl.pallas_call(kernel, out_shape=[jax.ShapeDtypeStruct(shape, kind) for s...  489 us
    pallas_call x10, Pallas kernels, local_call(): pl.pallas_call(kernel, out_shape=[jax.ShapeDtypeStruct(shape, kind) for s...  161 us
    pallas_call x4, Pallas kernels, head_call(): pl.pallas_call(kernel, grid=(grid,), in_specs=in_specs, out_specs=out_spe...  91.5 us
    dot_general x4, matrix products, dot_nt(): lax.dot_general(a, b, (((1,), (1,)), ((), ())), precision=precision, pref...  20.4 us
  transfers between devices with their start and end apart: 10, of which 4 were waited for; matrix products, arithmetic and copies ran while one was open for 7% of the time, Pallas kernels for 44%

profile of v3, /device:TPU:12, one launch (start us, length us, event | category | flops | bytes accessed | tf_op | source)
XLA Modules:
  0.0 997.6 jit_solution(735534396774051738)
XLA Ops:
  8.1 8.2 all-gather
  23.9 10.7 %shard_map.286 = bf16[8192,256]{1,0:T(8,128)(2,1)} custom-call(s32[1]{0:T(128)} %bitcast.1.count_ref, s32[8192]{0:T(1024)} %get-tuple-element.186.row_ref, s32[8192]{0:T(1024)} %get-tuple-element.185.tok_ref, f32[6286,256]{1,0:T(8,128)} %table_ref.1), custom_call_target="tpu_custom_call" | custom-call | flops 6502404 | bytes 13004808 | tf_op jit(solution)/shard_map/pallas_call | solution.py:66
  41.3 118.4 %shard_map.287 = (bf16[4,4,2,32,4384]{4,3,2,1,0:T(8,128)(2,1)}, bf16[4,4,2,64,1024]{4,3,2,1,0:T(8,128)(2,1)}, bf16[4,4,2,32,4384]{4,3,2,1,0:T(8,128)(2,1)}, bf16[4,4,2,64,1024]{4,3,2,1,0:T(8,128)(2,1)}) custom-call(bf16[32,4384]{1,0:T(8,128)(2,1)} %get-tuple-element.80.refs_0_, bf16[64,1024]{1,0:T(8,128)(2,1)} %get-tuple-element.81.refs_1_, ...), custom_call_target="tpu_custom_call" | custom-call | flops 19759104 | bytes 39518208 | tf_op jit(solution)/shard_map/pallas_call | solution.py:170
  172.5 7.7 all-to-all-done
  180.8 7.4 fusion.16.proj_ref
  197.6 14.8 %collective-permute-done.halo_ref = f32[8,2304]{1,0:T(8,128)S(1)} collective-permute-done((f32[8,2304]{1,0:T(8,128)S(1)}, f32[8,2304]{1,0:T(8,128)S(1)}, u32[]{:S(2)}, u32[]{:S(2)}) %collective-permute-start) | collective-permute-done | bytes 73760 | tf_op jit(solution)/shard_map/ppermute | solution.py:1340
  213.1 13.5 %shard_map.288 = (f32[256,2304]{1,0:T(8,128)}, f32[256,2048]{1,0:T(8,128)}, f32[2048,128]{1,0:T(8,128)}, f32[256,128]{1,0:T(8,128)}, f32[256,128]{1,0:T(8,128)}) custom-call(f32[256,4384]{1,0:T(8,128)} %copy-done, f32[8,2304]{1,0:T(8,128)} %copy-done.30, f32[4,2304]{1,0:T(4,128)} %reshape.322.cw_ref, f32[1,2304]{1,0:T(1,128)} %broadcast_in_dim.75.cb_ref, ...), custom_call_target="tpu_custom_call" | custom-call | flops 4618240 | bytes 9236480 | tf_op jit(solution)/shard_map/pallas_call | solution.py:66
  227.7 17.5 %shard_map.289.sin_ref = bf16[2048,128]{1,0:T(8,128)(2,1)} custom-call(f32[32]{0:T(128)} %exponential_bitcast_fusion.1.decay_ref, f32[2048,128]{1,0:T(8,128)} %get-tuple-element.88.local_ref), custom_call_target="tpu_custom_call" | custom-call | flops 524288 | bytes 1048576 | tf_op jit(solution)/shard_map/pallas_call | solution.py:170
  245.2 10.8 %shard_map.290 = (f32[256,2048]{1,0:T(8,128)}, bf16[256,2048]{1,0:T(8,128)(2,1)}) custom-call(f32[256,2048]{1,0:T(8,128)} %get-tuple-element.85.y0_ref, f32[256,4384]{1,0:T(8,128)} %copy-done, f32[256,2304]{1,0:T(8,128)} %get-tuple-element.86.pre_ref, f32[256,128]{1,0:T(8,128)} %get-tuple-element.87.cum_ref, bf16[2048,128]{1,0:T(8,128)(2,1)} %shard_map.289.sin_ref, ...), custom_call_target="tpu_custom_call" | custom-call | flops 9609216 | bytes 19218432 | tf_op jit(solution)/shard_map/pallas_call | solution.py:66
  278.0 13.4 %shard_map.291 = (f32[256,2304]{1,0:T(8,128)}, f32[256,2048]{1,0:T(8,128)}, f32[2048,128]{1,0:T(8,128)}, f32[256,128]{1,0:T(8,128)}, f32[256,128]{1,0:T(8,128)}) custom-call(f32[256,4384]{1,0:T(8,128)} %copy-done.1, f32[8,2304]{1,0:T(8,128)} %copy-done.31, f32[4,2304]{1,0:T(4,128)} %reshape.325.cw_ref, f32[1,2304]{1,0:T(1,128)} %broadcast_in_dim.80.cb_ref, ...), custom_call_target="tpu_custom_call" | custom-call | flops 4618240 | bytes 9236480 | tf_op jit(solution)/shard_map/pallas_call | solution.py:66
  292.7 15.5 %shard_map.292.sin_ref = bf16[2048,128]{1,0:T(8,128)(2,1)} custom-call(f32[32]{0:T(128)} %exponential_bitcast_fusion.decay_ref, f32[2048,128]{1,0:T(8,128)} %get-tuple-element.95.local_ref), custom_call_target="tpu_custom_call" | custom-call | flops 524288 | bytes 1048576 | tf_op jit(solution)/shard_map/pallas_call | solution.py:170
  308.2 10.6 %shard_map.293 = (f32[256,2048]{1,0:T(8,128)}, bf16[256,2048]{1,0:T(8,128)(2,1)}) custom-call(f32[256,2048]{1,0:T(8,128)} %get-tuple-element.92.y0_ref, f32[256,4384]{1,0:T(8,128)} %copy-done.1, f32[256,2304]{1,0:T(8,128)} %get-tuple-element.93.pre_ref, f32[256,128]{1,0:T(8,128)} %get-tuple-element.94.cum_ref, bf16[2048,128]{1,0:T(8,128)(2,1)} %shard_map.292.sin_ref, ...), custom_call_target="tpu_custom_call" | custom-call | flops 9609216 | bytes 19218432 | tf_op jit(solution)/shard_map/pallas_call | solution.py:66
  325.3 87.6 %shard_map.294 = (bf16[6400,2048]{1,0:T(8,128)(2,1)}, bf16[8,256,1024]{2,1,0:T(8,128)(2,1)}, f32[1,2048]{1,0:T(1,128)}, f32[5,1,2048]{2,1,0:T(1,128)}, f32[1,2048]{1,0:T(1,128)}) custom-call(bf16[6286,1024]{1,0:T(8,128)(2,1)} %all-gather.5.cloned.1.call-done.table_ref.e_ref, bf16[256,1024]{1,0:T(8,128)(2,1)} %get-tuple-element.157.own_ref, ...), custom_call_target="tpu_custom_call" | custom-call | flops 3670016 | bytes 7340032 | tf_op jit(solution)/shard_map/pallas_call | solution.py:170
  412.8 36.9 %shard_map.295 = bf16[2048,1024]{1,0:T(8,128)(2,1)} custom-call(bf16[6286,1024]{1,0:T(8,128)(2,1)} %all-gather.5.cloned.1.call-done.table_ref.e_ref, bf16[6400,2048]{1,0:T(8,128)(2,1)} %get-tuple-element.99.q_ref, f32[5,1,2048]{2,1,0:T(1,128)} %get-tuple-element.100.fac_ref, f32[1,2048]{1,0:T(1,128)} %broadcast_select_fusion.2.w_ref, s32[1,2048]{1,0:T(1,128)} %sub.71.lab_ref), custom_call_target="tpu_custom_call" | custom-call | flops 26365394944 | bytes 51494912 | tf_op jit(solution)/shard_map/pallas_call | solution.py:1007
  449.8 33.7 %shard_map.296 = bf16[6286,1024]{1,0:T(8,128)(2,1)} custom-call(bf16[2048,1024]{1,0:T(8,128)(2,1)} %bitcast.141, bf16[6400,2048]{1,0:T(8,128)(2,1)} %get-tuple-element.99.q_ref, f32[5,1,2048]{2,1,0:T(1,128)} %get-tuple-element.100.fac_ref, f32[1,2048]{1,0:T(1,128)} %broadcast_select_fusion.2.w_ref, s32[1,2048]{1,0:T(1,128)} %sub.71.lab_ref), custom_call_target="tpu_custom_call" | custom-call | flops 26365394944 | bytes 51494912 | tf_op jit(solution)/shard_map/pallas_call | solution.py:1007
  483.5 13.1 %reduce-scatter.6.cloned.1.call-done = bf16[256,1024]{1,0:T(8,128)(2,1)} async-done(((bf16[2048,1024]{1,0:T(8,128)(2,1)}), bf16[256,1024]{1,0:T(8,128)(2,1)}) %reduce-scatter.6.cloned.1.call-update) | async-done | bytes 524304 | tf_op jit(solution)/shard_map/reduce_scatter | solution.py:1587
  503.9 13.5 %shard_map.297 = (f32[256,2048]{1,0:T(8,128)}, bf16[256,2048]{1,0:T(8,128)(2,1)}, f32[1,2048]{1,0:T(1,128)}, f32[2048,128]{1,0:T(8,128)}) custom-call(f32[256,2048]{1,0:T(8,128)} %fusion.18.dyn_ref, f32[256,2048]{1,0:T(8,128)} %get-tuple-element.103.y_ref, f32[256,4384]{1,0:T(8,128)} %copy-done.1, f32[256,2304]{1,0:T(8,128)} %get-tuple-element.93.pre_ref, ...), custom_call_target="tpu_custom_call" | custom-call | flops 11182080 | bytes 22364160 | tf_op jit(solution)/shard_map/pallas_call | solution.py:66
  517.4 23.6 %shard_map.298.gin_ref = bf16[2048,128]{1,0:T(8,128)(2,1)} custom-call(f32[32]{0:T(128)} %exponential_bitcast_fusion.decay_ref, f32[2048,128]{1,0:T(8,128)} %get-tuple-element.107.local_ref), custom_call_target="tpu_custom_call" | custom-call | flops 524288 | bytes 1048576 | tf_op jit(solution)/shard_map/pallas_call | solution.py:170
  541.0 30.6 %shard_map.299 = (f32[256,2304]{1,0:T(8,128)}, f32[8,2304]{1,0:T(8,128)}, f32[256,128]{1,0:T(8,128)}, f32[8,2304]{1,0:T(8,128)}, f32[8,128]{1,0:T(8,128)}) custom-call(f32[256,2048]{1,0:T(8,128)} %get-tuple-element.105.dy_ref, f32[256,2048]{1,0:T(8,128)} %get-tuple-element.103.y_ref, f32[256,4384]{1,0:T(8,128)} %copy-done.1, f32[8,2304]{1,0:T(8,128)} %copy-done.31, ...), custom_call_target="tpu_custom_call" | custom-call | flops 12473344 | bytes 24946688 | tf_op jit(solution)/shard_map/pallas_call | solution.py:66
  579.8 7.7 multiply_reduce_fusion.4
  592.9 13.5 %shard_map.300 = (f32[256,2048]{1,0:T(8,128)}, bf16[256,2048]{1,0:T(8,128)(2,1)}, f32[1,2048]{1,0:T(1,128)}, f32[2048,128]{1,0:T(8,128)}) custom-call(f32[256,2048]{1,0:T(8,128)} %fusion.19.dyn_ref, f32[256,2048]{1,0:T(8,128)} %get-tuple-element.111.y_ref, f32[256,4384]{1,0:T(8,128)} %copy-done, f32[256,2304]{1,0:T(8,128)} %get-tuple-element.86.pre_ref, ...), custom_call_target="tpu_custom_call" | custom-call | flops 11182080 | bytes 22364160 | tf_op jit(solution)/shard_map/pallas_call | solution.py:66
  606.4 19.4 %shard_map.301.gin_ref = bf16[2048,128]{1,0:T(8,128)(2,1)} custom-call(f32[32]{0:T(128)} %exponential_bitcast_fusion.1.decay_ref, f32[2048,128]{1,0:T(8,128)} %get-tuple-element.114.local_ref), custom_call_target="tpu_custom_call" | custom-call | flops 524288 | bytes 1048576 | tf_op jit(solution)/shard_map/pallas_call | solution.py:170
  625.9 30.5 %shard_map.302 = (f32[256,2304]{1,0:T(8,128)}, f32[8,2304]{1,0:T(8,128)}, f32[256,128]{1,0:T(8,128)}, f32[8,2304]{1,0:T(8,128)}, f32[8,128]{1,0:T(8,128)}) custom-call(f32[256,2048]{1,0:T(8,128)} %get-tuple-element.112.dy_ref, f32[256,2048]{1,0:T(8,128)} %get-tuple-element.111.y_ref, f32[256,4384]{1,0:T(8,128)} %copy-done, f32[8,2304]{1,0:T(8,128)} %copy-done.30, ...), custom_call_target="tpu_custom_call" | custom-call | flops 12473344 | bytes 24946688 | tf_op jit(solution)/shard_map/pallas_call | solution.py:66
  664.7 7.4 multiply_reduce_fusion.1
  673.3 10.1 %all_to_all.10 = bf16[4,256,256]{2,1,0:T(8,128)(2,1)} all-to-all(bf16[4,256,256]{2,1,0:T(8,128)(2,1)S(1)} %bitcast.115), channel_id=1, replica_groups=mesh['dp'=4,'fsdp'=8] {'dp'}, dimensions={0} | all-to-all | bytes 1048576 | tf_op jit(solution)/shard_map/all_to_all | solution.py:1603
  699.0 10.2 %shard_map.304 = (bf16[1024,4384]{1,0:T(8,128)(2,1)}, bf16[2048,1024]{1,0:T(8,128)(2,1)}) custom-call(bf16[256,1024]{1,0:T(8,128)(2,1)} %copy-done.20, bf16[256,4384]{1,0:T(8,128)(2,1)} %pad_maximum_fusion.dp_ref, bf16[256,2048]{1,0:T(8,128)(2,1)} %get-tuple-element.96.yn_ref, bf16[256,1024]{1,0:T(8,128)(2,1)} %copy-done.27), custom_call_target="tpu_custom_call" | custom-call | flops 3372220416 | bytes 6586368 | tf_op jit(solution)/shard_map/pallas_call | solution.py:1007
  712.1 10.7 %shard_map.303 = (bf16[1024,4384]{1,0:T(8,128)(2,1)}, bf16[2048,1024]{1,0:T(8,128)(2,1)}) custom-call(bf16[256,1024]{1,0:T(8,128)(2,1)} %get-tuple-element.163.u_ref, bf16[256,4384]{1,0:T(8,128)(2,1)} %pad_maximum_fusion.1.dp_ref, bf16[256,2048]{1,0:T(8,128)(2,1)} %get-tuple-element.89.yn_ref, bf16[256,1024]{1,0:T(8,128)(2,1)} %copy-done.26), custom_call_target="tpu_custom_call" | custom-call | flops 3372220416 | bytes 6586368 | tf_op jit(solution)/shard_map/pallas_call | solution.py:1007
  722.8 186.5 %shard_map.305 = (f32[32,4384]{1,0:T(8,128)}, f32[64,1024]{1,0:T(8,128)}, f32[32,4384]{1,0:T(8,128)}, f32[64,1024]{1,0:T(8,128)}) custom-call(bf16[4,4,2,32,4384]{4,3,2,1,0:T(8,128)(2,1)} %bitcast.104, bf16[4,4,2,64,1024]{4,3,2,1,0:T(8,128)(2,1)} %bitcast.106, bf16[4,4,2,32,4384]{4,3,2,1,0:T(8,128)(2,1)} %bitcast.103, bf16[4,4,2,64,1024]{4,3,2,1,0:T(8,128)(2,1)} %bitcast.105), custom_call_target="tpu_custom_call" | custom-call | flops 26345472 | bytes 52690944 | tf_op jit(solution)/shard_map/pallas_call | solution.py:170
  914.8 13.9 %shard_map.306 = (f32[6286,256]{1,0:T(8,128)}, f32[8,256]{1,0:T(8,128)}) custom-call(s32[1]{0:T(128)} %bitcast.1.count_ref, s32[8192]{0:T(1024)} %get-tuple-element.186.row_ref, s32[8192]{0:T(1024)} %get-tuple-element.185.tok_ref, bf16[8192,256]{1,0:T(8,128)(2,1)} %bitcast.107, bf16[6286,256]{1,0:T(8,128)(2,1)} %reduce-scatter.8.cloned.1.call-done.base_ref), custom_call_target="tpu_custom_call" | custom-call | flops 7478276 | bytes 14956552 | tf_op jit(solution)/shard_map/pallas_call | solution.py:66
  932.2 20.3 %shard_map.307 = f32[256,128]{1,0:T(8,128)} custom-call(f32[256,128]{1,0:T(8,128)} %bitcast.125), custom_call_target="tpu_custom_call" | custom-call | flops 393216 | bytes 786432 | tf_op jit(solution)/shard_map/pallas_call | solution.py:170
  972.4 6.4 fusion.8
  978.9 9.1 add_multiply_fusion
  (229 shorter events, 140.3 us)
Async XLA Ops:
  8.0 159.1 %reduce-scatter.4.cloned.1.call-start = ((), (), s32[]{:S(2)}) async-start(), calls=%async_computation.5 | async-start | bytes 4718592 | tf_op jit(solution)/shard_map/reduce_scatter | solution.py:1543
  34.6 290.7 %all-gather.5.cloned.1.call-start = ((), (), s32[]{:S(2)}) async-start(), calls=%async_computation.6 | async-start | bytes 16097280 | tf_op jit(solution)/shard_map/all_gather | solution.py:1556
  39.6 120.2 %copy-start.42 = (s32[2,4]{1,0:T(2,128)S(1)}, s32[2,4]{1,0:T(2,128)}, u32[]{:S(2)}) copy-start(s32[2,4]{1,0:T(2,128)} %param.17) | copy-start | bytes 100
  39.6 121.8 %copy-start.39 = (s32[2,1,1024]{2,1,0:T(1,128)S(1)}, s32[2,1,1024]{2,1,0:T(1,128)}, u32[]{:S(2)}) copy-start(s32[2,1,1024]{2,1,0:T(1,128)} %param.16) | copy-start | bytes 24580
  39.6 122.4 %copy-start.28 = (f32[30400]{0:T(1024)S(1)}, f32[30400]{0:T(1024)}, u32[]{:S(2)}) copy-start(f32[30400]{0:T(1024)} %param.27) | copy-start | bytes 364804
  167.1 13.1 %all-to-all-start = ((bf16[4,256,256]{2,1,0:T(8,128)(2,1)}), bf16[4,256,256]{2,1,0:T(8,128)(2,1)S(1)}, u32[]{:S(2)}, u32[]{:S(2)}) async-start(bf16[4,256,256]{2,1,0:T(8,128)(2,1)} %bitcast.124), calls=%async_computation.1 | async-start | bytes 1048576 | tf_op jit(solution)/shard_map/all_to_all | solution.py:1546
  171.9 324.7 %reduce-scatter.6.cloned.1.call-start = ((), (), s32[]{:S(2)}) async-start(), calls=%async_computation.7 | async-start | bytes 4718592 | tf_op jit(solution)/shard_map/reduce_scatter | solution.py:1587
  190.3 22.1 %collective-permute-start = (f32[8,2304]{1,0:T(8,128)S(1)}, f32[8,2304]{1,0:T(8,128)S(1)}, u32[]{:S(2)}, u32[]{:S(2)}) collective-permute-start(f32[8,2304]{1,0:T(8,128)S(1)} %slice.184), channel_id=1, source_target_pairs={{0,2},{1,3},{2,4},{3,5},{4,6},{5,7},{8,10},{9,11},{10,12},{11,13},... | collective-permute-start | bytes 221192 | tf_op jit(solution)/shard_map/ppermute | solution.py:1340
  197.6 58.4 %copy-start.15 = (f32[256,1024]{1,0:T(8,128)}, f32[256,1024]{1,0:T(8,128)S(1)}, u32[]{:S(2)}) copy-start(f32[256,1024]{1,0:T(8,128)S(1)} %copy.91) | copy-start | bytes 3145732
  269.5 7.9 collective-permute-start.1
  449.8 464.9 %all-gather.7.cloned.1.call-start = ((), (), s32[]{:S(2)}) async-start(), calls=%async_computation.9 | async-start | bytes 4718592 | tf_op jit(solution)/shard_map/all_gather | solution.py:1604
  483.5 16.7 %copy-start.5 = (f32[256,1024]{1,0:T(8,128)S(1)}, f32[256,1024]{1,0:T(8,128)}, u32[]{:S(2)}) copy-start(f32[256,1024]{1,0:T(8,128)} %copy-done.4) | copy-start | bytes 3145732
  571.7 7.1 collective-permute-start.2
  625.9 38.8 %copy-start.16 = (f32[256,1024]{1,0:T(8,128)S(1)}, f32[256,1024]{1,0:T(8,128)}, u32[]{:S(2)}) copy-start(f32[256,1024]{1,0:T(8,128)} %copy-done.15) | copy-start | bytes 3145732
  656.4 7.3 collective-permute-start.3
  683.5 231.3 %reduce-scatter.8.cloned.1.call-start = ((), (), s32[]{:S(2)}) async-start(), calls=%async_computation.8 | async-start | bytes 16097280 | tf_op jit(solution)/shard_map/reduce_scatter | solution.py:1591
  911.1 19.6 %copy-start.33 = (f32[2304]{0:T(1024)S(1)}, f32[2304]{0:T(1024)}, u32[]{:S(2)}) copy-start(f32[2304]{0:T(1024)} %slice_reduce_fusion.1) | copy-start | bytes 27652
  911.1 19.6 %copy-start.34 = (f32[1024]{0:T(1024)S(1)}, f32[1024]{0:T(1024)}, u32[]{:S(2)}) copy-start(f32[1024]{0:T(1024)} %get-tuple-element.156) | copy-start | bytes 12292
  911.1 19.6 %copy-start.35 = (f32[1024]{0:T(1024)S(1)}, f32[1024]{0:T(1024)}, u32[]{:S(2)}) copy-start(f32[1024]{0:T(1024)} %get-tuple-element.140) | copy-start | bytes 12292
  911.1 19.6 %copy-start.36 = (f32[1,2,4,128]{3,1,2,0:T(2,128)S(1)}, f32[1,2,4,128]{3,1,2,0:T(2,128)}, u32[]{:S(2)}) copy-start(f32[1,2,4,128]{3,1,2,0:T(2,128)} %copy.95) | copy-start | bytes 12292
  911.1 19.6 %copy-start.37 = (f32[1,2048]{1,0:T(1,128)S(1)}, f32[1,2048]{1,0:T(1,128)}, u32[]{:S(2)}) copy-start(f32[1,2048]{1,0:T(1,128)} %get-tuple-element.124) | copy-start | bytes 24580
  911.1 19.6 %copy-start.38 = (f32[1,2048]{1,0:T(1,128)S(1)}, f32[1,2048]{1,0:T(1,128)}, u32[]{:S(2)}) copy-start(f32[1,2048]{1,0:T(1,128)} %get-tuple-element.121) | copy-start | bytes 24580
  911.1 19.6 %copy-start.40 = (f32[1024]{0:T(1024)S(1)}, f32[1024]{0:T(1024)}, u32[]{:S(2)}) copy-start(f32[1024]{0:T(1024)} %get-tuple-element.142) | copy-start | bytes 12292
  911.1 19.6 %copy-start.41 = (f32[1024]{0:T(1024)S(1)}, f32[1024]{0:T(1024)}, u32[]{:S(2)}) copy-start(f32[1024]{0:T(1024)} %get-tuple-element.139) | copy-start | bytes 12292
  911.1 19.6 %copy-start.43 = (f32[32]{0:T(128)S(1)}, f32[32]{0:T(128)}, u32[]{:S(2)}) copy-start(f32[32]{0:T(128)} %get-tuple-element.190) | copy-start | bytes 388
  911.1 19.6 %copy-start.44 = (f32[32]{0:T(128)S(1)}, f32[32]{0:T(128)}, u32[]{:S(2)}) copy-start(f32[32]{0:T(128)} %get-tuple-element.191) | copy-start | bytes 388
  911.1 19.6 %copy-start.45 = (f32[32]{0:T(128)S(1)}, f32[32]{0:T(128)}, u32[]{:S(2)}) copy-start(f32[32]{0:T(128)} %get-tuple-element.192) | copy-start | bytes 388
  911.1 19.6 %copy-start.46 = (f32[32]{0:T(128)S(1)}, f32[32]{0:T(128)}, u32[]{:S(2)}) copy-start(f32[32]{0:T(128)} %get-tuple-element.193) | copy-start | bytes 388
  913.3 46.2 %copy-start.32 = (f32[30400]{0:T(1024)S(1)}, f32[30400]{0:T(1024)}, u32[]{:S(2)}) copy-start(f32[30400]{0:T(1024)} %param.28) | copy-start | bytes 364804
  914.7 46.6 %copy-start.25 = (f32[64,1024]{1,0:T(8,128)S(1)}, f32[64,1024]{1,0:T(8,128)}, u32[]{:S(2)}) copy-start(f32[64,1024]{1,0:T(8,128)} %get-tuple-element.131) | copy-start | bytes 786436
  914.7 49.0 %copy-start.9 = (f32[2,32,4384]{2,1,0:T(8,128)S(1)}, f32[2,32,4384]{2,1,0:T(8,128)}, u32[]{:S(2)}) copy-start(f32[2,32,4384]{2,1,0:T(8,128)} %param.21) | copy-start | bytes 3366916
  961.3 11.2 %slice-start = ((s8[6438912]{0:T(1024)(128)(4,1)}), s8[4194304]{0:T(1024)(128)(4,1)S(1)}, s32[]{:S(2)}) async-start(s8[6438912]{0:T(1024)(128)(4,1)} %bitcast.97), calls=%async_computation.10 | async-start | bytes 8388608
  (29 other events, 156.9 us)
Sparse Core Ops, SparseCore 0:
  34.7 84.8 reduce-scatter.3
  449.9 46.6 reduce-scatter.5
  683.6 44.0 all-gather.6
Sparse Core Ops, SparseCore 1:
  159.8 142.5 all-gather.4
  687.1 191.7 reduce-scatter.7

commit v4 on v3

--- a/solution.py
+++ b/solution.py
@@ -180,15 +180,21 @@
     )(*ins)
 
 
-def chain_kernel(direction, steps, decay_ref, local_ref, out_ref, got, give, send, recv):
-    dp = lax.axis_index("dp")
-    me = lax.axis_index("fsdp")
-    place = me // MB
+CHAIN_STEPS = 8
+PART = DI // CHAIN_STEPS
+
+
+def chunk_place(direction):
+    place = lax.axis_index("fsdp") // MB
     count = lax.axis_size("fsdp") // MB
     first = place == (0 if direction > 0 else count - 1)
     final = place == (count - 1 if direction > 0 else 0)
-    part = DI // steps
-    heads = part // HDIM
+    return first, final
+
+
+def chain_barrier(direction, first, final):
+    dp = lax.axis_index("dp")
+    me = lax.axis_index("fsdp")
     barrier = pltpu.get_barrier_semaphore()
 
     @pl.when(jnp.logical_not(first))
@@ -201,59 +207,36 @@
     def _():
         pl.semaphore_wait(barrier, 1)
 
-    @pl.when(first)
-    def _():
-        got[...] = jnp.zeros(got.shape, bf16)
-
-    def copy(g):
-        rows = pl.ds(g * part, part)
-        return remote(
-            give.at[rows], got.at[rows], send.at[g], recv.at[g], dp, me + MB * direction
-        )
-
-    for g in range(steps):
-        rows = pl.ds(g * part, part)
-
-        @pl.when(jnp.logical_not(first))
-        def _():
-            copy(g).wait_recv()
-
-        @pl.when(jnp.logical_not(final))
-        def _():
-            for i in range(heads):
-                h = pl.ds(g * part + i * HDIM, HDIM)
-                give[h, :] = (
-                    decay_ref[g * heads + i] * got[h, :].astype(f32) + local_ref[h, :]
-                ).astype(bf16)
-            copy(g).start()
-
-        out_ref[rows, :] = got[rows, :]
+
+def to_next(src, dst, send, recv, direction):
+    dp = lax.axis_index("dp")
+    return remote(src, dst, send, recv, dp, lax.axis_index("fsdp") + MB * direction)
+
+
+def chain_step(g, direction, first, final, got, give, local, col, rows, send, recv):
+    def copy():
+        at = pl.ds(pl.multiple_of(g * PART, PART), PART)
+        return to_next(give.at[at], got.at[at], send.at[g], recv.at[g], direction)
+
+    @pl.when(jnp.logical_not(first))
+    def _():
+        copy().wait_recv()
 
     @pl.when(jnp.logical_not(final))
     def _():
-        for g in range(steps):
-            copy(g).wait_send()
-
-
-CHAIN_STEPS = 8
-
-
-def carry_chain(decay, local, direction):
-    return comm_call(
-        functools.partial(chain_kernel, direction, CHAIN_STEPS),
-        1 if direction > 0 else 2,
-        (decay, local),
-        ((local.shape, bf16),),
-        (
-            pltpu.VMEM(local.shape, bf16),
-            pltpu.VMEM(local.shape, bf16),
-            pltpu.SemaphoreType.DMA((CHAIN_STEPS,)),
-            pltpu.SemaphoreType.DMA((CHAIN_STEPS,)),
-        ),
-        (pltpu.SMEM, pltpu.VMEM),
-        (pltpu.VMEM,),
-        local.size * 2,
-    )[0]
+        for i in range(PART // HDIM):
+            h = pl.ds(pl.multiple_of(g * PART + i * HDIM, HDIM), HDIM)
+            decay = jnp.exp(col[g * (PART // HDIM) + i, rows - 1 : rows, :])
+            give[h, :] = (decay * got[h, :].astype(f32) + local[h, :]).astype(bf16)
+        copy().start()
+
+
+def chain_end(direction, final, got, give, send, recv):
+    @pl.when(jnp.logical_not(final))
+    def _():
+        for g in range(CHAIN_STEPS):
+            at = pl.ds(g * PART, PART)
+            to_next(give.at[at], got.at[at], send.at[g], recv.at[g], direction).wait_send()
 
 
 def bits_of(size):
@@ -752,25 +735,28 @@
             per_pair[p] = jnp.where(half, left, right)
 
 
-def front_kernel(
-    proj_ref, halo_ref, cw_ref, cb_ref, dtb_ref, al_ref, sk_ref,
-    pre_ref, y_ref, st_ref, dt_ref, cum_ref,
-    pad, col, tcol, lcol, lrow,
+def scan_kernel(
+    proj_ref, cw_ref, cb_ref, dtb_ref, al_ref, sk_ref, gg_ref,
+    pre_ref, y_ref, yn_ref, dt_ref, cum_ref, got, halo_ref,
+    pad, col, tcol, lcol, lrow, st, give, square, edge_send, edge_recv, send, recv,
 ):
     rows = proj_ref.shape[0]
-    pad[0:8, :] = halo_ref[...]
+    first, final = chunk_place(1)
+    chain_barrier(1, first, final)
+    edge = to_next(
+        proj_ref.at[pl.ds(rows - 8, 8), pl.ds(DI, XBC)], halo_ref, edge_send, edge_recv, 1
+    )
+
+    @pl.when(jnp.logical_not(final))
+    def _():
+        edge.start()
+
+    @pl.when(first)
+    def _():
+        halo_ref[...] = jnp.zeros(halo_ref.shape, f32)
+        got[...] = jnp.zeros(got.shape, bf16)
+
     pad[8:, :] = proj_ref[:, DI : DI + XBC]
-
-    def conv(i, _):
-        xs = pair_lanes(i)
-        out = jnp.broadcast_to(cb_ref[0:1, xs], (rows, LANES))
-        for k in range(CONV):
-            out = out + cw_ref[k : k + 1, xs] * pad[5 + k : 5 + k + rows, xs]
-        pre_ref[:, xs] = out
-        return 0
-
-    lax.fori_loop(0, XBC // LANES, conv, 0)
-
     dt_ref[...] = jnp.zeros((rows, LANES), f32)
     dt_ref[:, 0:HEADS] = proj_ref[:, DI + XBC :]
     drive = dt_ref[...] + dtb_ref[...]
@@ -785,16 +771,41 @@
     lrow[...] = cum.T
     spread_columns(cum, col, lcol, rows)
     spread_columns(dt, None, tcol, rows)
+
+    @pl.when(jnp.logical_not(first))
+    def _():
+        edge.wait_recv()
+
+    pad[0:8, :] = halo_ref[...]
+
+    def conv(i, _):
+        xs = pair_lanes(i)
+        out = jnp.broadcast_to(cb_ref[0:1, xs], (rows, LANES))
+        for k in range(CONV):
+            out = out + cw_ref[k : k + 1, xs] * pad[5 + k : 5 + k + rows, xs]
+        pre_ref[:, xs] = out
+        return 0
+
+    lax.fori_loop(0, XBC // LANES, conv, 0)
     bm = silu(pre_ref[:, DI : DI + NSTATE]).astype(bf16)
     cm = silu(pre_ref[:, DI + NSTATE :]).astype(bf16)
     cb = dot_nt(cm, bm)
     half = first_half(rows)
 
-    def pair(p, _):
+    def states(p, _):
+        xs = pair_lanes(p)
+        lp = lcol[p]
+        tail = jnp.exp(lp[rows - 1 : rows, :] - lp) * tcol[p]
+        st[xs, :] = dot_tn((tail * silu(pre_ref[:, xs])).astype(bf16), bm)
+        return 0
+
+    lax.fori_loop(0, PAIRS, states, 0, unroll=2)
+    square[...] = jnp.zeros(square.shape, f32)
+
+    def pair(p):
         xs = pair_lanes(p)
         x = silu(pre_ref[:, xs])
-        xt = tcol[p] * x
-        xtb = xt.astype(bf16)
+        xtb = (tcol[p] * x).astype(bf16)
         parts = []
         for j in range(2):
             h = 2 * p + j
@@ -802,31 +813,22 @@
             d = jnp.concatenate([c] * (rows // LANES), axis=1) - lrow[pl.ds(h, 1), :]
             m = (jnp.exp(jnp.where(causal, d, OFF)) * cb).astype(bf16)
             parts.append(dot_nn(m, xtb))
-        y_ref[:, xs] = jnp.where(half, parts[0], parts[1]) + sk_ref[0:1, xs] * x
-        lp = lcol[p]
-        tail = jnp.exp(lp[rows - 1 : rows, :] - lp)
-        st_ref[xs, :] = dot_tn((tail * xt).astype(bf16), bm)
-        return 0
-
-    lax.fori_loop(0, PAIRS, pair, 0)
-
-
-def gate_kernel(
-    y0_ref, proj_ref, pre_ref, cum_ref, sin_ref, gg_ref, y_ref, yn_ref, lcol
-):
-    rows = y0_ref.shape[0]
-    spread_columns(cum_ref[...], None, lcol, rows)
-    cm = silu(pre_ref[:, DI + NSTATE :]).astype(bf16)
-
-    def pair(p, total):
-        xs = pair_lanes(p)
-        y = y0_ref[:, xs] + jnp.exp(lcol[p]) * dot_nt(cm, sin_ref[xs, :])
+        y = jnp.where(half, parts[0], parts[1]) + sk_ref[0:1, xs] * x
+        y = y + jnp.exp(lcol[p]) * dot_nt(cm, got[xs, :])
         y_ref[:, xs] = y
         g = y * silu(proj_ref[:, xs])
-        return total + g * g
-
-    total = lax.fori_loop(0, PAIRS, pair, jnp.zeros((rows, LANES), f32))
-    scale = lax.rsqrt(jnp.sum(total, axis=1, keepdims=True) / DI + epsilon)
+        return g * g
+
+    def step(g, _):
+        chain_step(g, 1, first, final, got, give, st, col, rows, send, recv)
+        total = square[...]
+        for i in range(PART // LANES):
+            total = total + pair(g * (PART // LANES) + i)
+        square[...] = total
+        return 0
+
+    lax.fori_loop(0, CHAIN_STEPS, step, 0)
+    scale = lax.rsqrt(jnp.sum(square[...], axis=1, keepdims=True) / DI + epsilon)
 
     def put(p, _):
         xs = pair_lanes(p)
@@ -834,56 +836,31 @@
         yn_ref[:, xs] = (g * scale * gg_ref[0:1, xs]).astype(bf16)
         return 0
 
-    lax.fori_loop(0, PAIRS, put, 0)
-
-
-def ungate_kernel(
-    dyn_ref, y_ref, proj_ref, pre_ref, cum_ref, gg_ref,
-    dy_ref, dz_ref, dgg_ref, gst_ref, lcol,
+    lax.fori_loop(0, PAIRS, put, 0, unroll=2)
+
+    @pl.when(jnp.logical_not(final))
+    def _():
+        edge.wait_send()
+
+    chain_end(1, final, got, give, send, recv)
+
+
+def back_kernel(
+    dyn_ref, y_ref, proj_ref, halo_ref, pre_ref, dt_ref, cum_ref, sin_ref,
+    cw_ref, dtb_ref, al_ref, sk_ref, gg_ref,
+    dp_ref, dcw_ref, dsm_ref, dgg_ref,
+    pad, grad, col, tcol, lcol, lrow, dcb, dbm, dcm, dlog, dtx, ends, dy_ref, drive_ref,
+    got, give, gst, dx_ref, edge_ref, from_ref, edge_send, edge_recv, send, recv,
 ):
     rows = y_ref.shape[0]
-    spread_columns(cum_ref[...], None, lcol, rows)
-    cm = silu(pre_ref[:, DI + NSTATE :]).astype(bf16)
-    zero = jnp.zeros((rows, LANES), f32)
-
-    def sums(p, carry):
-        xs = pair_lanes(p)
-        g = y_ref[:, xs] * silu(proj_ref[:, xs])
-        return carry[0] + g * g, carry[1] + g * (dyn_ref[:, xs] * gg_ref[0:1, xs])
-
-    square, cross = lax.fori_loop(0, PAIRS, sums, (zero, zero))
-    scale = lax.rsqrt(jnp.sum(square, axis=1, keepdims=True) / DI + epsilon)
-    mean = jnp.sum(cross, axis=1, keepdims=True) * scale / DI
-
-    def pair(p, _):
-        xs = pair_lanes(p)
-        z = proj_ref[:, xs]
-        y = y_ref[:, xs]
-        sz = silu(z)
-        ghat = y * sz * scale
-        dyn = dyn_ref[:, xs]
-        dgg_ref[0:1, xs] = jnp.sum(dyn * ghat, axis=0, keepdims=True)
-        dg = scale * (dyn * gg_ref[0:1, xs] - ghat * mean)
-        dy = dg * sz
-        dy_ref[:, xs] = dy
-        dz_ref[:, xs] = (dg * y * silu_grad(z)).astype(bf16)
-        gst_ref[xs, :] = dot_tn((jnp.exp(lcol[p]) * dy).astype(bf16), cm)
-        return 0
-
-    lax.fori_loop(0, PAIRS, pair, 0)
-
-
-def back_kernel(
-    dy_ref, y_ref, proj_ref, halo_ref, pre_ref, dt_ref, cum_ref, sin_ref, gin_ref,
-    cw_ref, dtb_ref, al_ref, sk_ref,
-    dx_ref, dhalo_ref, ddr_ref, dcw_ref, dsm_ref,
-    pad, grad, col, tcol, lcol, lrow, dcb, dbm, dcm, dlog, dtx, ends,
-):
-    rows = y_ref.shape[0]
-    pad[0:8, :] = halo_ref[...]
-    pad[8:, :] = proj_ref[:, DI : DI + XBC]
-    grad[0:8, :] = jnp.zeros((8, XBC), f32)
-    grad[rows + 8 :, :] = jnp.zeros((8, XBC), f32)
+    first, final = chunk_place(-1)
+    chain_barrier(-1, first, final)
+
+    @pl.when(first)
+    def _():
+        from_ref[...] = jnp.zeros(from_ref.shape, f32)
+        got[...] = jnp.zeros(got.shape, bf16)
+
     cum = cum_ref[...]
     dt = dt_ref[...]
     lrow[...] = cum.T
@@ -891,13 +868,44 @@
     spread_columns(dt, None, tcol, rows)
     bm = silu(pre_ref[:, DI : DI + NSTATE]).astype(bf16)
     cm = silu(pre_ref[:, DI + NSTATE :]).astype(bf16)
+    zero = jnp.zeros((rows, LANES), f32)
+
+    def sums(p, carry):
+        xs = pair_lanes(p)
+        g = y_ref[:, xs] * silu(proj_ref[:, xs])
+        return carry[0] + g * g, carry[1] + g * (dyn_ref[:, xs] * gg_ref[0:1, xs])
+
+    square, cross = lax.fori_loop(0, PAIRS, sums, (zero, zero))
+    scale = lax.rsqrt(jnp.sum(square, axis=1, keepdims=True) / DI + epsilon)
+    mean = jnp.sum(cross, axis=1, keepdims=True) * scale / DI
+
+    def ungate(p, _):
+        xs = pair_lanes(p)
+        z = proj_ref[:, xs]
+        y = y_ref[:, xs]
+        sg = lax.logistic(z)
+        sz = z * sg
+        ghat = y * sz * scale
+        dyn = dyn_ref[:, xs]
+        dgg_ref[0:1, xs] = jnp.sum(dyn * ghat, axis=0, keepdims=True)
+        dg = scale * (dyn * gg_ref[0:1, xs] - ghat * mean)
+        dy = dg * sz
+        dy_ref[:, xs] = dy
+        dp_ref[:, xs] = (dg * y * (sg * (1.0 + z * (1.0 - sg)))).astype(bf16)
+        gst[xs, :] = dot_tn((jnp.exp(lcol[p]) * dy).astype(bf16), cm)
+        return 0
+
+    lax.fori_loop(0, PAIRS, ungate, 0, unroll=2)
+    pad[0:8, :] = halo_ref[...]
+    pad[8:, :] = proj_ref[:, DI : DI + XBC]
+    grad[0:8, :] = jnp.zeros((8, XBC), f32)
+    grad[rows + 8 :, :] = jnp.zeros((8, XBC), f32)
     cbt = dot_nt(bm, cm)
     ri = lax.broadcasted_iota(jnp.int32, (rows, rows), 0)
     ci = lax.broadcasted_iota(jnp.int32, (rows, rows), 1)
     causal = ri <= ci
     half = first_half(rows)
     dcb[...] = jnp.zeros((rows, rows), f32)
-    zero = jnp.zeros((rows, LANES), f32)
     dbm[...] = zero
     dcm[...] = zero
     dlog[...] = zero
@@ -907,10 +915,11 @@
     lane_col = lax.broadcasted_iota(jnp.int32, (LANES, LANES), 1)
     ones = jnp.ones((8, NSTATE), f32)
 
-    def pair(p, _):
+    def pair(p):
         xs = pair_lanes(p)
         pre = pre_ref[:, xs]
-        x = silu(pre)
+        sg = lax.logistic(pre)
+        x = pre * sg
         tp = tcol[p]
         xt = tp * x
         dy = dy_ref[:, xs]
@@ -928,7 +937,7 @@
         lp = lcol[p]
         last = lp[rows - 1 : rows, :]
         tail = jnp.exp(last - lp)
-        gin = gin_ref[xs, :]
+        gin = got[xs, :]
         sin = sin_ref[xs, :]
         dst = tail * dot_nt(bm, gin)
         dxt = jnp.where(half, parts[0], parts[1]) + dst
@@ -945,25 +954,45 @@
             [jnp.broadcast_to(end, (8, LANES)), jnp.broadcast_to(skip, (8, LANES))], axis=0
         )
         ends[...] += dot_nn(stacked, pick, highest)
-        grad[pl.ds(8, rows), xs] = (tp * dxt + sk * dy) * silu_grad(pre)
-        return 0
-
-    lax.fori_loop(0, PAIRS, pair, 0)
+        grad[pl.ds(8, rows), xs] = (tp * dxt + sk * dy) * (sg * (1.0 + pre * (1.0 - sg)))
+
+    def step(g, _):
+        chain_step(g, -1, first, final, got, give, gst, col, rows, send, recv)
+        for i in range(PART // LANES):
+            pair(g * (PART // LANES) + i)
+        return 0
+
+    lax.fori_loop(0, CHAIN_STEPS, step, 0)
     dcbb = dcb[...].astype(bf16)
     dc = dcm[...] + dot_tn(dcbb, bm)
     db = dbm[...] + dot_nn(dcbb, cm)
     grad[8 : 8 + rows, DI : DI + NSTATE] = db * silu_grad(pre_ref[:, DI : DI + NSTATE])
     grad[8 : 8 + rows, DI + NSTATE :] = dc * silu_grad(pre_ref[:, DI + NSTATE :])
 
+    def edges(i, _):
+        xs = pair_lanes(i)
+        edge = jnp.zeros((8, LANES), f32)
+        for k in range(CONV):
+            edge = edge + cw_ref[k : k + 1, xs] * grad[3 - k : 11 - k, xs]
+        edge_ref[:, xs] = edge
+        return 0
+
+    lax.fori_loop(0, XBC // LANES, edges, 0)
+    edge = to_next(edge_ref, from_ref, edge_send, edge_recv, -1)
+
+    @pl.when(jnp.logical_not(final))
+    def _():
+        edge.start()
+
     last_row = lax.broadcasted_iota(jnp.int32, (rows, LANES), 0) == rows - 1
     dl = dlog[...] + jnp.where(last_row, ends[0:1, :], 0.0)
     da = dot_nn(jnp.where(causal, 1.0, 0.0), dl, highest)
     decay = -jnp.exp(al_ref[...])
     ddt = dtx[...] + da * decay
-    ddr_ref[...] = jnp.zeros((rows, LANES), f32)
-    ddr_ref[:, 0:HEADS] = proj_ref[:, DI + XBC :]
-    ddr = ddt * lax.logistic(ddr_ref[...] + dtb_ref[...])
-    ddr_ref[...] = ddr
+    drive_ref[...] = jnp.zeros((rows, LANES), f32)
+    drive_ref[:, 0:HEADS] = proj_ref[:, DI + XBC :]
+    ddr = ddt * lax.logistic(drive_ref[...] + dtb_ref[...])
+    dp_ref[:, DI + XBC :] = ddr[:, 0:HEADS].astype(bf16)
     dsm_ref[...] = jnp.zeros((8, LANES), f32)
     dsm_ref[0:1, :] = jnp.sum(ddr, axis=0, keepdims=True)
     dsm_ref[1:2, :] = jnp.sum(da * dt, axis=0, keepdims=True) * decay
@@ -973,20 +1002,29 @@
         xs = pair_lanes(i)
         own = grad[pl.ds(8, rows), xs]
         out = jnp.zeros((rows, LANES), f32)
-        edge = jnp.zeros((8, LANES), f32)
         for k in range(CONV):
-            wk = cw_ref[k : k + 1, xs]
-            out = out + wk * grad[11 - k : 11 - k + rows, xs]
-            edge = edge + wk * grad[3 - k : 11 - k, xs]
+            out = out + cw_ref[k : k + 1, xs] * grad[11 - k : 11 - k + rows, xs]
             dcw_ref[k : k + 1, xs] = jnp.sum(
                 own * pad[5 + k : 5 + k + rows, xs], axis=0, keepdims=True
             )
         dcw_ref[4:5, xs] = jnp.sum(own, axis=0, keepdims=True)
         dx_ref[:, xs] = out
-        dhalo_ref[:, xs] = edge
         return 0
 
     lax.fori_loop(0, XBC // LANES, conv, 0)
+
+    @pl.when(jnp.logical_not(first))
+    def _():
+        edge.wait_recv()
+
+    dx_ref[rows - 8 :, :] += from_ref[...]
+    dp_ref[:, DI : DI + XBC] = dx_ref[...].astype(bf16)
+
+    @pl.when(jnp.logical_not(final))
+    def _():
+        edge.wait_send()
+
+    chain_end(-1, final, got, give, send, recv)
 
 
 VTILE = 1280
@@ -1052,14 +1090,10 @@
         paired = k + (2 * (i % 2) - 1) * ((i + 1) // 2)
         return jnp.where(i <= 2 * near, paired, k + long_side * (i - near))
 
-    def along(z):
+    def along(z, side):
+        at = all_ref.at[z * MB + core]
         return remote(
-            own_ref, all_ref.at[me], z_send.at[z], z_recv.at[k], dp, z * MB + core
-        )
-
-    def landed(z):
-        return remote(
-            own_ref, all_ref.at[z * MB + core], z_send.at[z], z_recv.at[z], dp, me
+            at, at, z_send.at[side, z], z_recv.at[z], dp, me + MB if side == 0 else me - MB
         )
 
     def to_mate(z):
@@ -1072,9 +1106,16 @@
 
     keep = pltpu.make_async_copy(own_ref, all_ref.at[me], own_sem)
     keep.start()
-    for i in range(1, count):
-        along(chunk_at(i)).start()
     keep.wait()
+
+    @pl.when(k < count - 1)
+    def _():
+        along(k, 0).start()
+
+    @pl.when(k > 0)
+    def _():
+        along(k, 1).start()
+
     to_mate(k).start()
     whole = vocab_rows - vocab_rows % 16
     for slot in range(2):
@@ -1114,10 +1155,25 @@
     def chunk(i, _):
         z = chunk_at(i)
 
-        @pl.when(i > 0)
+        @pl.when(jnp.logical_and(i > 0, k >= i))
         def _():
-            landed(z).wait_recv()
-            to_mate(z).start()
+            along(k - i, 0).wait_recv()
+
+            @pl.when(k < count - 1)
+            def _():
+                along(k - i, 0).start()
+
+            to_mate(k - i).start()
+
+        @pl.when(jnp.logical_and(i > 0, k + i < count))
+        def _():
+            along(k + i, 1).wait_recv()
+
+            @pl.when(k > 0)
+            def _():
+                along(k + i, 1).start()
+
+            to_mate(k + i).start()
 
         block(2 * i, z * MB + core)
         from_mate(z).wait_recv()
@@ -1166,9 +1222,16 @@
         fac_ref[t, 0:1, :] = scale * jnp.exp(tops[t, 0:1, :] - lse)
     for other in range(1, shards):
         tell(other).wait_send()
-    for i in range(1, count):
-        along(chunk_at(i)).wait_send()
     for z in range(count):
+
+        @pl.when(jnp.logical_and(k >= z, k < count - 1))
+        def _(z=z):
+            along(z, 0).wait_send()
+
+        @pl.when(jnp.logical_and(k <= z, k > 0))
+        def _(z=z):
+            along(z, 1).wait_send()
+
         to_mate(z).wait_send()
     put(0, 0).wait()
     put(1, 0).wait()
@@ -1200,7 +1263,7 @@
             pltpu.VMEM((shards, 2, tokens), f32),
             pltpu.SemaphoreType.DMA,
             pltpu.SemaphoreType.DMA((2,)),
-            pltpu.SemaphoreType.DMA((count,)),
+            pltpu.SemaphoreType.DMA((2, count)),
             pltpu.SemaphoreType.DMA((count,)),
             pltpu.SemaphoreType.DMA((count,)),
             pltpu.SemaphoreType.DMA((count,)),
@@ -1334,12 +1397,6 @@
     )
 
 
-def shift_chunks(block, distance):
-    size = lax.axis_size("fsdp")
-    route = [(i - 2 * distance, i) for i in range(size) if 0 <= i - 2 * distance < size]
-    return lax.ppermute(block, "fsdp", route)
-
-
 def after(value, earlier):
     return lax.optimization_barrier((value, earlier))[0]
 
@@ -1382,69 +1439,64 @@
     rows = hidden.shape[0]
     normed = (hidden * norm_scale(hidden) * vec["pre_gain"]).astype(bf16)
     proj = jnp.dot(normed, w_in, preferred_element_type=f32)
-    halo = shift_chunks(proj[rows - 8 :, DI : DI + XBC], 1)
-    pre, y0, local, dt, cum = local_call(
-        front_kernel,
-        (proj, halo, vec["conv_w"], vec["conv_b"], vec["dt_bias"], vec["decay_log"], vec["skip"]),
+    pre, y, mixed, dt, cum, entering, halo = comm_call(
+        scan_kernel,
+        1,
+        (
+            proj, vec["conv_w"], vec["conv_b"], vec["dt_bias"], vec["decay_log"], vec["skip"],
+            vec["gate_gain"],
+        ),
         (
             ((rows, XBC), f32),
             ((rows, DI), f32),
-            ((DI, NSTATE), f32),
+            ((rows, DI), bf16),
             ((rows, LANES), f32),
             ((rows, LANES), f32),
+            ((DI, NSTATE), bf16),
+            ((8, XBC), f32),
         ),
-        scratch=(
+        (
             pltpu.VMEM((rows + 8, XBC), f32),
             pltpu.VMEM((HEADS, rows, LANES), f32),
             pltpu.VMEM((PAIRS, rows, LANES), f32),
             pltpu.VMEM((PAIRS, rows, LANES), f32),
             pltpu.VMEM((LANES, rows), f32),
+            pltpu.VMEM((DI, NSTATE), f32),
+            pltpu.VMEM((DI, NSTATE), bf16),
+            pltpu.VMEM((rows, LANES), f32),
+            pltpu.SemaphoreType.DMA,
+            pltpu.SemaphoreType.DMA,
+            pltpu.SemaphoreType.DMA((CHAIN_STEPS,)),
+            pltpu.SemaphoreType.DMA((CHAIN_STEPS,)),
         ),
-    )
-    decay = jnp.exp(cum[rows - 1, :HEADS])
-    entering = carry_chain(decay, local, 1)
-    y, mixed = local_call(
-        gate_kernel,
-        (y0, proj, pre, cum, entering, vec["gate_gain"]),
-        (((rows, DI), f32), ((rows, DI), bf16)),
-        scratch=(pltpu.VMEM((PAIRS, rows, LANES), f32),),
+        (pltpu.VMEM,) * 7,
+        (pltpu.VMEM,) * 7,
+        DI * NSTATE * 2,
     )
     branch = jnp.dot(mixed, w_out, preferred_element_type=f32)
-    record = (hidden, normed, proj, halo, pre, dt, cum, decay, entering, y, mixed)
+    record = (hidden, normed, proj, halo, pre, dt, cum, entering, y, mixed)
     return hidden + branch, record
 
 
 def layer_backward(grad_hidden, w_in, w_out, vec, record):
-    hidden, normed, proj, halo, pre, dt, cum, decay, entering, y, mixed = record
+    hidden, normed, proj, halo, pre, dt, cum, entering, y, mixed = record
     rows = hidden.shape[0]
     grad_branch = grad_hidden.astype(bf16)
     grad_mixed = dot_nt(grad_branch, w_out)
-    dy, dz, dgate, gstate = local_call(
-        ungate_kernel,
-        (grad_mixed, y, proj, pre, cum, vec["gate_gain"]),
+    grad_proj, dconv, dsmall, dgate = comm_call(
+        back_kernel,
+        2,
         (
-            ((rows, DI), f32),
-            ((rows, DI), bf16),
-            ((1, DI), f32),
-            ((DI, NSTATE), f32),
-        ),
-        scratch=(pltpu.VMEM((PAIRS, rows, LANES), f32),),
-    )
-    later = carry_chain(decay, gstate, -1)
-    dx, dhalo, ddr, dconv, dsmall = local_call(
-        back_kernel,
-        (
-            dy, y, proj, halo, pre, dt, cum, entering, later,
-            vec["conv_w"], vec["dt_bias"], vec["decay_log"], vec["skip"],
+            grad_mixed, y, proj, halo, pre, dt, cum, entering,
+            vec["conv_w"], vec["dt_bias"], vec["decay_log"], vec["skip"], vec["gate_gain"],
         ),
         (
-            ((rows, XBC), f32),
-            ((8, XBC), f32),
-            ((rows, LANES), f32),
+            ((rows, ZW), bf16),
             ((8, XBC), f32),
             ((8, LANES), f32),
+            ((1, DI), f32),
         ),
-        scratch=(
+        (
             pltpu.VMEM((rows + 8, XBC), f32),
             pltpu.VMEM((rows + 16, XBC), f32),
             pltpu.VMEM((HEADS, rows, LANES), f32),
@@ -1457,12 +1509,22 @@
             pltpu.VMEM((rows, LANES), f32),
             pltpu.VMEM((rows, LANES), f32),
             pltpu.VMEM((16, LANES), f32),
+            pltpu.VMEM((rows, DI), f32),
+            pltpu.VMEM((rows, LANES), f32),
+            pltpu.VMEM((DI, NSTATE), bf16),
+            pltpu.VMEM((DI, NSTATE), bf16),
+            pltpu.VMEM((DI, NSTATE), f32),
+            pltpu.VMEM((rows, XBC), f32),
+            pltpu.VMEM((8, XBC), f32),
+            pltpu.VMEM((8, XBC), f32),
+            pltpu.SemaphoreType.DMA,
+            pltpu.SemaphoreType.DMA,
+            pltpu.SemaphoreType.DMA((CHAIN_STEPS,)),
+            pltpu.SemaphoreType.DMA((CHAIN_STEPS,)),
         ),
-    )
-    from_next = shift_chunks(dhalo, -1)
-    dx = jnp.concatenate([dx[: rows - 8], dx[rows - 8 :] + from_next], axis=0)
-    grad_proj = jnp.concatenate(
-        [dz, dx.astype(bf16), ddr[:, :HEADS].astype(bf16)], axis=1
+        (pltpu.VMEM,) * 13,
+        (pltpu.VMEM,) * 4,
+        DI * NSTATE * 2,
     )
     grad_normed = dot_nt(grad_proj, w_in)
     grad_in, grad_out = weight_grads(normed, grad_proj, mixed, grad_branch)
@@ -1473,7 +1535,7 @@
             dconv[CONV],
             dsmall[0, :HEADS],
             dsmall[1, :HEADS],
-            jnp.sum(dsmall[2:3, :HEADS], axis=0),
+            dsmall[2, :HEADS],
             dpre_gain,
             dgate[0],
         ]

time: 1010 us -> 897 us (0.89)
  Pallas kernels: 742 us -> 677 us
  local copies, waits for them, and re-layouts: 39.4 us -> 20.3 us
  starting transfers between devices: 23.9 us -> 4.97 us
  other arithmetic: 71.1 us -> 60.6 us
    pallas_call x10 -> x2, Pallas kernels: 161 us -> 24.8 us  [local_call(): pl.pallas_call(kernel, out_shape=[jax.ShapeDtypeStruct(shape, kind) for s...]
    pallas_call x8, Pallas kernels: 489 us -> 561 us  [comm_call(): pl.pallas_call(kernel, out_shape=[jax.ShapeDtypeStruct(shape, kind) for s...]
    ppermute x4 -> x0, starting transfers between devices: 19 us -> none  [shift_chunks(): return lax.ppermute(block, 'fsdp', route)]
    all_gather x1, waiting for transfers between devices: 0.01 us -> 16.5 us  [whole_step(): table = lax.all_gather(embed_low, 'dp', axis=1, tiled=True)]
    ppermute x4 -> x0, waiting for transfers between devices: 16.2 us -> none  [shift_chunks(): return lax.ppermute(block, 'fsdp', route)]
  transfers between devices with their start and end apart: 10 -> 6, of which waited for: 4 -> 3; matrix products, arithmetic and copies ran while one was open for 7% -> 6% of each run, Pallas kernels for 44% -> 51%
where the time goes in v4:
time: 897 us; the launch traced here: 885 us
  Pallas kernels  677 us (75%)
  other arithmetic  60.6 us (7%)
  matrix products  43.4 us (5%)
  waiting for transfers between devices  37.4 us (4%)
  between operations  23.7 us (3%)
  local copies, waits for them, and re-layouts  20.3 us (2%)
  blocking collectives  18.3 us (2%)
    pallas_call x8, Pallas kernels, comm_call(): pl.pallas_call(kernel, out_shape=[jax.ShapeDtypeStruct(shape, kind) for s...  561 us
    pallas_call x4, Pallas kernels, head_call(): pl.pallas_call(kernel, grid=(grid,), in_specs=in_specs, out_specs=out_spe...  90.6 us
    pallas_call x2, Pallas kernels, local_call(): pl.pallas_call(kernel, out_shape=[jax.ShapeDtypeStruct(shape, kind) for s...  24.8 us
    dot_general x4, matrix products, dot_nt(): lax.dot_general(a, b, (((1,), (1,)), ((), ())), precision=precision, pref...  18.8 us
  transfers between devices with their start and end apart: 6, of which 3 were waited for; matrix products, arithmetic and copies ran while one was open for 6% of the time, Pallas kernels for 51%

profile of v4, /device:TPU:12, one launch (start us, length us, event | category | flops | bytes accessed | tf_op | source)
XLA Modules:
  0.0 885.3 jit_solution(43732772531786089)
XLA Ops:
  8.1 8.2 all-gather
  16.4 6.2 sort.15
  23.9 10.7 %shard_map.286 = bf16[8192,256]{1,0:T(8,128)(2,1)} custom-call(s32[1]{0:T(128)} %bitcast.1.count_ref, s32[8192]{0:T(1024)} %get-tuple-element.166.row_ref, s32[8192]{0:T(1024)} %get-tuple-element.165.tok_ref, f32[6286,256]{1,0:T(8,128)} %table_ref.1), custom_call_target="tpu_custom_call" | custom-call | flops 6502404 | bytes 13004808 | tf_op jit(solution)/shard_map/pallas_call | solution.py:66
  34.7 4.9 convert_element_type.96
  41.3 118.4 %shard_map.287 = (bf16[4,4,2,32,4384]{4,3,2,1,0:T(8,128)(2,1)}, bf16[4,4,2,64,1024]{4,3,2,1,0:T(8,128)(2,1)}, bf16[4,4,2,32,4384]{4,3,2,1,0:T(8,128)(2,1)}, bf16[4,4,2,64,1024]{4,3,2,1,0:T(8,128)(2,1)}) custom-call(bf16[32,4384]{1,0:T(8,128)(2,1)} %get-tuple-element.70.refs_0_, bf16[64,1024]{1,0:T(8,128)(2,1)} %get-tuple-element.71.refs_1_, ...), custom_call_target="tpu_custom_call" | custom-call | flops 19759104 | bytes 39518208 | tf_op jit(solution)/shard_map/pallas_call | solution.py:170
  168.2 4.8 all-to-all-start
  173.6 7.7 all-to-all-done
  184.7 8.3 fusion.14.proj_ref
  192.9 45.6 %shard_map.288 = (f32[256,2304]{1,0:T(8,128)}, f32[256,2048]{1,0:T(8,128)}, bf16[256,2048]{1,0:T(8,128)(2,1)}, f32[256,128]{1,0:T(8,128)}, f32[256,128]{1,0:T(8,...) custom-call(f32[256,4384]{1,0:T(8,128)} %fusion.14.proj_ref, f32[4,2304]{1,0:T(4,128)} %reshape.318.cw_ref, ...), custom_call_target="tpu_custom_call" | custom-call | flops 524288 | bytes 1048576 | tf_op jit(solution)/shard_map/pallas_call | solution.py:170
  238.5 4.1 multiply_reduce_fusion.9
  243.7 8.4 fusion.15.proj_ref
  252.1 27.9 %shard_map.289 = (f32[256,2304]{1,0:T(8,128)}, f32[256,2048]{1,0:T(8,128)}, bf16[256,2048]{1,0:T(8,128)(2,1)}, f32[256,128]{1,0:T(8,128)}, f32[256,128]{1,0:T(8,...) custom-call(f32[256,4384]{1,0:T(8,128)} %fusion.15.proj_ref, f32[4,2304]{1,0:T(4,128)} %reshape.321.cw_ref, ...), custom_call_target="tpu_custom_call" | custom-call | flops 524288 | bytes 1048576 | tf_op jit(solution)/shard_map/pallas_call | solution.py:170
  280.0 3.9 multiply_reduce_fusion.8
  285.9 16.5 %all-gather.5.cloned.1.call-done.table_ref.e_ref = bf16[6286,1024]{1,0:T(8,128)(2,1)} async-done(((bf16[6286,256]{1,0:T(8,128)(2,1)}), bf16[6286,1024]{1,0:T(8,128)(2,1)}) %all-gather.5.cloned.1.call-update) | async-done | bytes 12873744 | tf_op jit(solution)/shard_map/all_gather | solution.py:1618
  302.4 63.3 %shard_map.290 = (bf16[6400,2048]{1,0:T(8,128)(2,1)}, bf16[8,256,1024]{2,1,0:T(8,128)(2,1)}, f32[1,2048]{1,0:T(1,128)}, f32[5,1,2048]{2,1,0:T(1,128)}, f32[1,2048]{1,0:T(1,128)}) custom-call(bf16[6286,1024]{1,0:T(8,128)(2,1)} %all-gather.5.cloned.1.call-done.table_ref.e_ref, bf16[256,1024]{1,0:T(8,128)(2,1)} %get-tuple-element.137.own_ref, ...), custom_call_target="tpu_custom_call" | custom-call | flops 3670016 | bytes 7340032 | tf_op jit(solution)/shard_map/pallas_call | solution.py:170
  365.7 36.5 %shard_map.291 = bf16[2048,1024]{1,0:T(8,128)(2,1)} custom-call(bf16[6286,1024]{1,0:T(8,128)(2,1)} %all-gather.5.cloned.1.call-done.table_ref.e_ref, bf16[6400,2048]{1,0:T(8,128)(2,1)} %get-tuple-element.81.q_ref, f32[5,1,2048]{2,1,0:T(1,128)} %get-tuple-element.82.fac_ref, f32[1,2048]{1,0:T(1,128)} %broadcast_select_fusion.2.w_ref, s32[1,2048]{1,0:T(1,128)} %sub.71.lab_ref), custom_call_target="tpu_custom_call" | custom-call | flops 26365394944 | bytes 51494912 | tf_op jit(solution)/shard_map/pallas_call | solution.py:1045
  402.3 33.7 %shard_map.292 = bf16[6286,1024]{1,0:T(8,128)(2,1)} custom-call(bf16[2048,1024]{1,0:T(8,128)(2,1)} %bitcast.139, bf16[6400,2048]{1,0:T(8,128)(2,1)} %get-tuple-element.81.q_ref, f32[5,1,2048]{2,1,0:T(1,128)} %get-tuple-element.82.fac_ref, f32[1,2048]{1,0:T(1,128)} %broadcast_select_fusion.2.w_ref, s32[1,2048]{1,0:T(1,128)} %sub.71.lab_ref), custom_call_target="tpu_custom_call" | custom-call | flops 26365394944 | bytes 51494912 | tf_op jit(solution)/shard_map/pallas_call | solution.py:1045
  436.0 12.6 %reduce-scatter.6.cloned.1.call-done = bf16[256,1024]{1,0:T(8,128)(2,1)} async-done(((bf16[2048,1024]{1,0:T(8,128)(2,1)}), bf16[256,1024]{1,0:T(8,128)(2,1)}) %reduce-scatter.6.cloned.1.call-update) | async-done | bytes 524304 | tf_op jit(solution)/shard_map/reduce_scatter | solution.py:1649
  455.3 42.8 %shard_map.293 = (bf16[256,4384]{1,0:T(8,128)(2,1)}, f32[8,2304]{1,0:T(8,128)}, f32[8,128]{1,0:T(8,128)}, f32[1,2048]{1,0:T(1,128)}) custom-call(f32[256,2048]{1,0:T(8,128)} %fusion.16.dyn_ref, f32[256,2048]{1,0:T(8,128)} %get-tuple-element.85.y_ref, f32[256,4384]{1,0:T(8,128)} %fusion.15.proj_ref, f32[8,2304]{1,0:T(8,128)} %get-tuple-element.86.halo_ref, ...), custom_call_target="tpu_custom_call" | custom-call | flops 524288 | bytes 1048576 | tf_op jit(solution)/shard_map/pallas_call | solution.py:170
  498.1 7.4 multiply_reduce_fusion.4
  510.9 38.7 %shard_map.294 = (bf16[256,4384]{1,0:T(8,128)(2,1)}, f32[8,2304]{1,0:T(8,128)}, f32[8,128]{1,0:T(8,128)}, f32[1,2048]{1,0:T(1,128)}) custom-call(f32[256,2048]{1,0:T(8,128)} %fusion.17.dyn_ref, f32[256,2048]{1,0:T(8,128)} %get-tuple-element.92.y_ref, f32[256,4384]{1,0:T(8,128)} %fusion.14.proj_ref, f32[8,2304]{1,0:T(8,128)} %get-tuple-element.93.halo_ref, ...), custom_call_target="tpu_custom_call" | custom-call | flops 524288 | bytes 1048576 | tf_op jit(solution)/shard_map/pallas_call | solution.py:170
  549.6 6.2 multiply_reduce_fusion.1
  557.1 10.1 %all_to_all.10 = bf16[4,256,256]{2,1,0:T(8,128)(2,1)} all-to-all(bf16[4,256,256]{2,1,0:T(8,128)(2,1)S(1)} %bitcast.113), channel_id=1, replica_groups=mesh['dp'=4,'fsdp'=8] {'dp'}, dimensions={0} | all-to-all | bytes 1048576 | tf_op jit(solution)/shard_map/all_to_all | solution.py:1665
  570.8 10.1 %shard_map.296 = (bf16[1024,4384]{1,0:T(8,128)(2,1)}, bf16[2048,1024]{1,0:T(8,128)(2,1)}) custom-call(bf16[256,1024]{1,0:T(8,128)(2,1)} %copy-done.15, bf16[256,4384]{1,0:T(8,128)(2,1)} %get-tuple-element.91.dp_ref, bf16[256,2048]{1,0:T(8,128)(2,1)} %get-tuple-element.78.yn_ref, bf16[256,1024]{1,0:T(8,128)(2,1)} %copy-done.22), custom_call_target="tpu_custom_call" | custom-call | flops 3372220416 | bytes 6586368 | tf_op jit(solution)/shard_map/pallas_call | solution.py:1045
  580.9 10.2 %shard_map.295 = (bf16[1024,4384]{1,0:T(8,128)(2,1)}, bf16[2048,1024]{1,0:T(8,128)(2,1)}) custom-call(bf16[256,1024]{1,0:T(8,128)(2,1)} %get-tuple-element.143.u_ref, bf16[256,4384]{1,0:T(8,128)(2,1)} %get-tuple-element.100.dp_ref, bf16[256,2048]{1,0:T(8,128)(2,1)} %get-tuple-element.75.yn_ref, bf16[256,1024]{1,0:T(8,128)(2,1)} %copy-done.21), custom_call_target="tpu_custom_call" | custom-call | flops 3372220416 | bytes 6586368 | tf_op jit(solution)/shard_map/pallas_call | solution.py:1045
  591.1 202.5 %shard_map.297 = (f32[32,4384]{1,0:T(8,128)}, f32[64,1024]{1,0:T(8,128)}, f32[32,4384]{1,0:T(8,128)}, f32[64,1024]{1,0:T(8,128)}) custom-call(bf16[4,4,2,32,4384]{4,3,2,1,0:T(8,128)(2,1)} %bitcast.102, bf16[4,4,2,64,1024]{4,3,2,1,0:T(8,128)(2,1)} %bitcast.104, bf16[4,4,2,32,4384]{4,3,2,1,0:T(8,128)(2,1)} %bitcast.101, bf16[4,4,2,64,1024]{4,3,2,1,0:T(8,128)(2,1)} %bitcast.103), custom_call_target="tpu_custom_call" | custom-call | flops 26345472 | bytes 52690944 | tf_op jit(solution)/shard_map/pallas_call | solution.py:170
  800.5 14.1 %shard_map.298 = (f32[6286,256]{1,0:T(8,128)}, f32[8,256]{1,0:T(8,128)}) custom-call(s32[1]{0:T(128)} %bitcast.1.count_ref, s32[8192]{0:T(1024)} %get-tuple-element.166.row_ref, s32[8192]{0:T(1024)} %get-tuple-element.165.tok_ref, bf16[8192,256]{1,0:T(8,128)(2,1)} %bitcast.105, bf16[6286,256]{1,0:T(8,128)(2,1)} %reduce-scatter.8.cloned.1.call-done.base_ref), custom_call_target="tpu_custom_call" | custom-call | flops 7478276 | bytes 14956552 | tf_op jit(solution)/shard_map/pallas_call | solution.py:66
  818.0 22.2 %shard_map.299 = f32[256,128]{1,0:T(8,128)} custom-call(f32[256,128]{1,0:T(8,128)} %bitcast.123), custom_call_target="tpu_custom_call" | custom-call | flops 393216 | bytes 786432 | tf_op jit(solution)/shard_map/pallas_call | solution.py:170
  851.5 3.0 fusion.5
  854.5 2.6 add_multiply_fusion.3
  860.2 6.4 fusion.6
  866.6 9.1 %add_multiply_fusion = f32[6286,256]{1,0:T(8,128)} fusion(f32[6286,256]{1,0:T(8,128)} %param.20, f32[6286,256]{1,0:T(8,128)S(1)} %get-tuple-element.134), kind=kLoop, calls=%fused_computation | loop fusion | flops 3218432 | bytes 19310592 | tf_op jit(solution)/shard_map/add | solution.py:1550
  (175 shorter events, 54.7 us)
Async XLA Ops:
  8.0 160.2 %reduce-scatter.4.cloned.1.call-start = ((), (), s32[]{:S(2)}) async-start(), calls=%async_computation.5 | async-start | bytes 4718592 | tf_op jit(solution)/shard_map/reduce_scatter | solution.py:1605
  34.6 5.0 copy-start.17
  34.6 5.1 copy-start.6
  34.6 267.8 %all-gather.5.cloned.1.call-start = ((), (), s32[]{:S(2)}) async-start(), calls=%async_computation.6 | async-start | bytes 16097280 | tf_op jit(solution)/shard_map/all_gather | solution.py:1618
  39.6 120.2 %copy-start.33 = (s32[2,4]{1,0:T(2,128)S(1)}, s32[2,4]{1,0:T(2,128)}, u32[]{:S(2)}) copy-start(s32[2,4]{1,0:T(2,128)} %param.17) | copy-start | bytes 100
  39.6 121.8 %copy-start.30 = (s32[2,1,1024]{2,1,0:T(1,128)S(1)}, s32[2,1,1024]{2,1,0:T(1,128)}, u32[]{:S(2)}) copy-start(s32[2,1,1024]{2,1,0:T(1,128)} %param.16) | copy-start | bytes 24580
  39.6 122.4 %copy-start.23 = (f32[30400]{0:T(1024)S(1)}, f32[30400]{0:T(1024)}, u32[]{:S(2)}) copy-start(f32[30400]{0:T(1024)} %param.27) | copy-start | bytes 364804
  168.2 13.1 %all-to-all-start = ((bf16[4,256,256]{2,1,0:T(8,128)(2,1)}), bf16[4,256,256]{2,1,0:T(8,128)(2,1)S(1)}, u32[]{:S(2)}, u32[]{:S(2)}) async-start(bf16[4,256,256]{2,1,0:T(8,128)(2,1)} %bitcast.122), calls=%async_computation.1 | async-start | bytes 1048576 | tf_op jit(solution)/shard_map/all_to_all | solution.py:1608
  173.0 275.7 %reduce-scatter.6.cloned.1.call-start = ((), (), s32[]{:S(2)}) async-start(), calls=%async_computation.7 | async-start | bytes 4718592 | tf_op jit(solution)/shard_map/reduce_scatter | solution.py:1649
  184.3 54.2 %copy-start.10 = (f32[256,1024]{1,0:T(8,128)}, f32[256,1024]{1,0:T(8,128)S(1)}, u32[]{:S(2)}) copy-start(f32[256,1024]{1,0:T(8,128)S(1)} %copy.67) | copy-start | bytes 3145732
  243.7 8.4 copy-start.15
  252.1 27.9 %copy-start.13 = (f32[256,1024]{1,0:T(8,128)S(1)}, f32[256,1024]{1,0:T(8,128)}, u32[]{:S(2)}) copy-start(f32[256,1024]{1,0:T(8,128)} %copy-done.12) | copy-start | bytes 3145732
  402.3 398.2 %all-gather.7.cloned.1.call-start = ((), (), s32[]{:S(2)}) async-start(), calls=%async_computation.9 | async-start | bytes 4718592 | tf_op jit(solution)/shard_map/all_gather | solution.py:1666
  436.0 15.6 %copy-start.3 = (f32[256,1024]{1,0:T(8,128)S(1)}, f32[256,1024]{1,0:T(8,128)}, u32[]{:S(2)}) copy-start(f32[256,1024]{1,0:T(8,128)} %copy-done.2) | copy-start | bytes 3145732
  498.1 7.5 copy-start.4
  498.1 7.5 copy-start.14
  510.9 38.7 %copy-start.11 = (f32[256,1024]{1,0:T(8,128)S(1)}, f32[256,1024]{1,0:T(8,128)}, u32[]{:S(2)}) copy-start(f32[256,1024]{1,0:T(8,128)} %copy-done.10) | copy-start | bytes 3145732
  549.6 6.2 copy-start.9
  567.2 233.3 %reduce-scatter.8.cloned.1.call-start = ((), (), s32[]{:S(2)}) async-start(), calls=%async_computation.8 | async-start | bytes 16097280 | tf_op jit(solution)/shard_map/reduce_scatter | solution.py:1653
  795.3 21.3 %copy-start.28 = (f32[1,2048]{1,0:T(1,128)S(1)}, f32[1,2048]{1,0:T(1,128)}, u32[]{:S(2)}) copy-start(f32[1,2048]{1,0:T(1,128)} %get-tuple-element.104) | copy-start | bytes 24580
  795.3 21.3 %copy-start.29 = (f32[1,2048]{1,0:T(1,128)S(1)}, f32[1,2048]{1,0:T(1,128)}, u32[]{:S(2)}) copy-start(f32[1,2048]{1,0:T(1,128)} %get-tuple-element.101) | copy-start | bytes 24580
  797.5 49.8 %copy-start.25 = (f32[30400]{0:T(1024)S(1)}, f32[30400]{0:T(1024)}, u32[]{:S(2)}) copy-start(f32[30400]{0:T(1024)} %param.28) | copy-start | bytes 364804
  800.5 48.5 %copy-start.20 = (f32[64,1024]{1,0:T(8,128)S(1)}, f32[64,1024]{1,0:T(8,128)}, u32[]{:S(2)}) copy-start(f32[64,1024]{1,0:T(8,128)} %get-tuple-element.111) | copy-start | bytes 786436
  800.5 51.0 %copy-start.7 = (f32[2,32,4384]{2,1,0:T(8,128)S(1)}, f32[2,32,4384]{2,1,0:T(8,128)}, u32[]{:S(2)}) copy-start(f32[2,32,4384]{2,1,0:T(8,128)} %param.21) | copy-start | bytes 3366916
  849.0 5.5 copy-start.24
  849.0 10.0 %copy-start.19 = (f32[2,32,4384]{2,1,0:T(8,128)S(1)}, f32[2,32,4384]{2,1,0:T(8,128)}, u32[]{:S(2)}) copy-start(f32[2,32,4384]{2,1,0:T(8,128)} %param.23) | copy-start | bytes 3366916
  849.0 11.2 %slice-start = ((s8[6438912]{0:T(1024)(128)(4,1)}), s8[4194304]{0:T(1024)(128)(4,1)S(1)}, s32[]{:S(2)}) async-start(s8[6438912]{0:T(1024)(128)(4,1)} %bitcast.95), calls=%async_computation.10 | async-start | bytes 8388608
  851.5 8.7 copy-start.16
  851.5 8.7 slice-start.1
  851.5 8.6 copy-start.5
  854.5 5.7 copy-start.8
  866.6 9.1 %copy-start.1 = (f32[6286,256]{1,0:T(8,128)}, f32[6286,256]{1,0:T(8,128)S(1)}, u32[]{:S(2)}) copy-start(f32[6286,256]{1,0:T(8,128)S(1)} %get-tuple-element.134) | copy-start | bytes 19310596
  (12 other events, 32.2 us)
Sparse Core Ops, SparseCore 0:
  34.7 84.8 reduce-scatter.3
  402.4 46.2 reduce-scatter.5
  567.3 47.3 all-gather.6
Sparse Core Ops, SparseCore 1:
  159.8 142.5 all-gather.4
  570.9 213.7 reduce-scatter.7

commit v5 on v4

--- a/solution.py
+++ b/solution.py
@@ -79,7 +79,7 @@
     )(*ins)
 
 
-def lookup_kernel(count_ref, row_ref, tok_ref, table_ref, out_ref, held):
+def lookup_kernel(count_ref, row_ref, tok_ref, table_ref, out_ref, low_ref, sum_ref, held):
     tokens = out_ref.shape[0]
     step = 512
 
@@ -106,6 +106,20 @@
         return 0
 
     lax.fori_loop(0, tokens // step, put, 0)
+    rows_all = table_ref.shape[0]
+    whole = rows_all // step
+
+    def cast(i, total):
+        rows = pl.ds(pl.multiple_of(i * step, step), step)
+        low = table_ref[rows, :].astype(bf16)
+        low_ref[rows, :] = low
+        return total + jnp.sum(low.astype(f32).reshape(step // 8, 8, -1), axis=0)
+
+    sum_ref[...] = lax.fori_loop(0, whole, cast, jnp.zeros(sum_ref.shape, f32))
+    if rows_all > whole * step:
+        low = table_ref[whole * step :, :].astype(bf16)
+        low_ref[whole * step :, :] = low
+        sum_ref[0:1, :] += jnp.sum(low.astype(f32), axis=0, keepdims=True)
 
 
 def spread_kernel(count_ref, row_ref, tok_ref, grad_ref, base_ref, out_ref, square_ref, held):
@@ -178,6 +192,72 @@
         ),
         cost_estimate=pl.CostEstimate(flops=sent, transcendentals=0, bytes_accessed=2 * sent),
     )(*ins)
+
+
+def greet_groups():
+    dp = lax.axis_index("dp")
+    me = lax.axis_index("fsdp")
+    groups = lax.axis_size("dp")
+    barrier = pltpu.get_barrier_semaphore()
+    others = [lax.rem(dp + other, groups) for other in range(1, groups)]
+    for other in others:
+        pl.semaphore_signal(barrier, inc=1, device_id=(other, me), device_id_type=MESH)
+    pl.semaphore_wait(barrier, groups - 1)
+    return dp, me, others
+
+
+def share_kernel(in_ref, out_ref, send, recv):
+    dp, me, others = greet_groups()
+    for other in others:
+        remote(in_ref, out_ref.at[dp], send.at[other], recv.at[dp], other, me).start()
+    out_ref[dp] = in_ref[...]
+    for other in others:
+        copy = remote(in_ref, out_ref.at[other], send.at[other], recv.at[other], other, me)
+        copy.wait_recv()
+        copy.wait_send()
+
+
+def to_rows_kernel(in_ref, out_ref, landed, send, recv):
+    dp, me, others = greet_groups()
+    for other in others:
+        remote(in_ref.at[other], landed.at[dp], send.at[other], recv.at[dp], other, me).start()
+    landed[dp] = in_ref[dp]
+    for other in others:
+        remote(in_ref.at[other], landed.at[other], send.at[other], recv.at[other], other, me).wait_recv()
+    cols = in_ref.shape[2]
+    for g in range(in_ref.shape[0]):
+        out_ref[:, g * cols : (g + 1) * cols] = landed[g].astype(f32)
+    for other in others:
+        remote(in_ref.at[other], landed.at[other], send.at[other], recv.at[other], other, me).wait_send()
+
+
+def to_columns_kernel(in_ref, out_ref, parts, send, recv):
+    dp, me, others = greet_groups()
+    cols = out_ref.shape[2]
+    for g in range(out_ref.shape[0]):
+        parts[g] = in_ref[:, g * cols : (g + 1) * cols].astype(bf16)
+    for other in others:
+        remote(parts.at[other], out_ref.at[dp], send.at[other], recv.at[dp], other, me).start()
+    out_ref[dp] = parts[dp]
+    for other in others:
+        copy = remote(parts.at[other], out_ref.at[other], send.at[other], recv.at[other], other, me)
+        copy.wait_recv()
+        copy.wait_send()
+
+
+def group_call(kernel, number, array, out, scratch=()):
+    groups = lax.axis_size("dp")
+    return comm_call(
+        kernel,
+        number,
+        (array,),
+        (out,),
+        tuple(scratch)
+        + (pltpu.SemaphoreType.DMA((groups,)), pltpu.SemaphoreType.DMA((groups,))),
+        (pltpu.VMEM,),
+        (pltpu.VMEM,),
+        array.size * 2,
+    )[0]
 
 
 CHAIN_STEPS = 8
@@ -1062,7 +1142,7 @@
 
 
 def head_stats_kernel(
-    table_ref, own_ref, lab_ref, w_ref,
+    lead_ref, table_ref, own_ref, lab_ref, w_ref,
     q_ref, all_ref, lse_ref, fac_ref, hit_ref,
     kept, tops, sums, hits, shown, own_sem, put_sem, z_send, z_recv, m_send, m_recv, s_send, s_recv,
 ):
@@ -1073,7 +1153,7 @@
     core = me % MB
     k = me // MB
     mate = k * MB + 1 - core
-    vocab_rows = table_ref.shape[0]
+    vocab_rows = lead_ref.shape[0] + table_ref.shape[0]
     rows = own_ref.shape[0]
     tiles = tops.shape[0]
     barrier = pltpu.get_barrier_semaphore()
@@ -1140,7 +1220,8 @@
         for t in range(tiles):
             first = t * VTILE
             size = min(VTILE, vocab_rows - first)
-            logits = dot_nt(table_ref[first : first + size, :], h)
+            part = lead_ref[...] if t == 0 else table_ref[first - VTILE : first - VTILE + size, :]
+            logits = dot_nt(part, h)
             top = jnp.max(logits, axis=0, keepdims=True)
             p = jnp.exp(logits - top)
             kept[slot, first : first + size, :] = p.astype(bf16)
@@ -1237,8 +1318,8 @@
     put(1, 0).wait()
 
 
-def head_stats(table, own, labels, weight):
-    vocab_rows, width = table.shape
+def head_stats(lead, table, own, labels, weight):
+    vocab_rows, width = lead.shape[0] + table.shape[0], table.shape[1]
     rows = own.shape[0]
     shards = lax.axis_size("fsdp")
     count = shards // MB
@@ -1247,7 +1328,7 @@
     kept, everyone, lse, fac, hit = comm_call(
         head_stats_kernel,
         6,
-        (table, own, labels, weight),
+        (lead, table, own, labels, weight),
         (
             ((tiles * VTILE, tokens), bf16),
             ((shards, rows, width), bf16),
@@ -1270,7 +1351,7 @@
             pltpu.SemaphoreType.DMA((shards,)),
             pltpu.SemaphoreType.DMA((shards,)),
         ),
-        (pltpu.VMEM,) * 4,
+        (pltpu.VMEM,) * 5,
         (pl.ANY, pltpu.VMEM, pltpu.VMEM, pltpu.VMEM, pltpu.VMEM),
         own.size * 2 * 7,
     )
@@ -1282,7 +1363,7 @@
     return (q.astype(f32) * fac - jnp.where(rid == label, other + 0.9 * weight, other)).astype(bf16)
 
 
-def head_rows_kernel(vocab_rows, e_ref, q_ref, fac_ref, w_ref, lab_ref, out_ref, acc, et):
+def head_rows_kernel(vocab_rows, lead_ref, e_ref, q_ref, fac_ref, w_ref, lab_ref, out_ref, acc, et):
     step = pl.program_id(0)
     first = step * VTILE
     tokens = q_ref.shape[1]
@@ -1291,8 +1372,15 @@
     def _():
         acc[...] = jnp.zeros(acc.shape, f32)
 
-    eid = lax.broadcasted_iota(jnp.int32, (VTILE, e_ref.shape[1]), 0)
-    et[...] = jnp.where(eid < vocab_rows - first, e_ref[...].astype(f32), 0.0).T.astype(bf16)
+    @pl.when(step == 0)
+    def _():
+        et[...] = lead_ref[...].astype(f32).T.astype(bf16)
+
+    @pl.when(step > 0)
+    def _():
+        eid = lax.broadcasted_iota(jnp.int32, (VTILE, e_ref.shape[1]), 0)
+        et[...] = jnp.where(eid < vocab_rows - first, e_ref[...].astype(f32), 0.0).T.astype(bf16)
+
 
     def chunk(j, _):
         ns = pl.ds(pl.multiple_of(j * NTILE, NTILE), NTILE)
@@ -1315,18 +1403,25 @@
         lax.fori_loop(0, tokens // NTILE, put, 0)
 
 
-def head_rows(table, kept, fac, weight, labels):
-    vocab_rows, width = table.shape
+def head_rows(lead, table, kept, fac, weight, labels):
+    vocab_rows, width = lead.shape[0] + table.shape[0], table.shape[1]
     tokens = kept.shape[1]
     sp = head_specs(width, tokens)
     return head_call(
         functools.partial(head_rows_kernel, vocab_rows),
         pl.cdiv(vocab_rows, VTILE),
-        [sp["table"], sp["kept"], sp["tile_row"], sp["row"], sp["row"]],
+        [
+            pl.BlockSpec((VTILE, width), lambda i: (0, 0)),
+            pl.BlockSpec((VTILE, width), lambda i: (jnp.maximum(i - 1, 0), 0)),
+            sp["kept"],
+            sp["tile_row"],
+            sp["row"],
+            sp["row"],
+        ],
         [sp["hidden"]],
         [((tokens, width), bf16)],
         (pltpu.VMEM((width, tokens), f32), pltpu.VMEM((width, VTILE), bf16)),
-        (table, kept, fac, weight, labels),
+        (lead, table, kept, fac, weight, labels),
         vocab_rows * tokens,
     )[0]
 
@@ -1578,11 +1673,11 @@
     vocab_rows, own_cols = embedding.shape
     tokens = MB * seq_rows
     total_count = jnp.sum(seq_lengths).astype(f32)
-    embed_low = embedding.astype(bf16)
     in_low = in_proj.astype(bf16)
     out_low = out_proj.astype(bf16)
 
-    ids_all = lax.all_gather(token_ids[:, 0, :], "dp", axis=0)
+    lead = lax.all_gather(embedding[:VTILE].astype(bf16), "dp", axis=1, tiled=True)
+    ids_all = group_call(share_kernel, 7, token_ids[:, 0, :], ((groups, MB, seq_rows), jnp.int32))
     ids_all = ids_all.reshape(groups, MB, chunks, rows).transpose(2, 1, 0, 3).reshape(-1)
     every = ids_all.shape[0]
     local_ids = ids_all - shard_index * vocab_rows
@@ -1595,18 +1690,23 @@
     count = jnp.sum(held_here.astype(jnp.int32)).reshape(1)
     row_list = jnp.where(held_here, sorted_ids, 0)
     tok_list = jnp.where(held_here, sorted_tok, every)
-    (looked,) = local_call(
+    looked, embed_low, own_sums = local_call(
         lookup_kernel,
         (count, row_list, tok_list, embedding),
-        (((every, own_cols), bf16),),
+        (((every, own_cols), bf16), ((vocab_rows, own_cols), bf16), ((8, own_cols), f32)),
         scratch=(pltpu.VMEM((every + 8, own_cols), f32),),
         in_smem=(0, 1, 2),
     )
     mine = lax.psum_scatter(
         looked.reshape(shards * groups * rows, own_cols), "fsdp", scatter_dimension=0, tiled=True
     )
-    mine = lax.all_to_all(mine.reshape(groups, rows, own_cols), "dp", 0, 0)
-    hidden = mine.transpose(1, 0, 2).reshape(rows, D).astype(f32)
+    hidden = group_call(
+        to_rows_kernel,
+        8,
+        mine.reshape(groups, rows, own_cols),
+        ((rows, D), f32),
+        (pltpu.VMEM((groups, rows, own_cols), bf16),),
+    )
 
     shards = []
     for l in range(LAYERS):
@@ -1615,7 +1715,7 @@
     gathered = gather_layers(shards)
     w_in, w_out = gathered[0::2], gathered[1::2]
     embed_low = after(embed_low, gathered)
-    table = lax.all_gather(embed_low, "dp", axis=1, tiled=True)
+    table = lax.all_gather(embed_low[VTILE:], "dp", axis=1, tiled=True)
 
     vecs = [layer_vectors(vector_params, l) for l in range(LAYERS)]
     final_gain = vector_params[LAYERS * PER :]
@@ -1634,7 +1734,7 @@
     valid = in_order((jnp.arange(seq_rows)[None, :] < lengths).astype(f32))
     local_labels = labels - shard_index * vocab_rows
     weight = valid / total_count
-    kept, group_hidden, lse, fac, target = head_stats(table, final_low, local_labels, weight)
+    kept, group_hidden, lse, fac, target = head_stats(lead, table, final_low, local_labels, weight)
     own_mask = jnp.arange(tokens) // rows == shard_index
     per_row = jnp.where(own_mask, lse[0] + z_weight * lse[0] * lse[0], 0.0)
     loss_sum = jnp.sum((per_row - 0.9 * target[0]) * valid[0])
@@ -1642,10 +1742,10 @@
     hidden_sum = jnp.sum(final_low.astype(f32) * own_valid[:, None], axis=0)
     column_sum = jnp.zeros((groups, own_cols), f32)
     column_sum = jnp.where(
-        jnp.arange(groups)[:, None] == group_index, jnp.sum(embed_low.astype(f32), axis=0), column_sum
+        jnp.arange(groups)[:, None] == group_index, jnp.sum(own_sums, axis=0), column_sum
     ).reshape(D)
 
-    rows_grad = head_rows(table, kept, fac, weight, local_labels)
+    rows_grad = head_rows(lead, table, kept, fac, weight, local_labels)
     own_grad = lax.psum_scatter(
         rows_grad, "fsdp", scatter_dimension=0, tiled=True
     ).astype(f32)
@@ -1661,8 +1761,13 @@
             grad_hidden, w_in[l], w_out[l], vecs[l], records[l]
         )
         if l == 0:
-            sent = grad_hidden.astype(bf16).reshape(rows, groups, own_cols).transpose(1, 0, 2)
-            sent = lax.all_to_all(sent, "dp", 0, 0)
+            sent = group_call(
+                to_columns_kernel,
+                9,
+                grad_hidden,
+                ((groups, rows, own_cols), bf16),
+                (pltpu.VMEM((groups, rows, own_cols), bf16),),
+            )
             spread = lax.all_gather(sent, "fsdp", axis=0).reshape(every, own_cols)
         in_parts[l], out_parts[l] = grad_in, grad_out
     whole = []

time: 897 us -> 899 us (level)
  Pallas kernels: 677 us -> 722 us
  waiting for transfers between devices: 37.4 us -> 13 us
  blocking collectives: 18.3 us -> 0 us
    pallas_call x8 -> x11, Pallas kernels: 561 us -> 600 us  [comm_call(): pl.pallas_call(kernel, out_shape=[jax.ShapeDtypeStruct(shape, kind) for s...]
    all_gather x1 -> x2, waiting for transfers between devices: 16.5 us -> 0.01 us  [the longest x1 0.01 us: whole_step(): lax.all_gather(embedding[:VTILE].astype(bf16), 'dp', axis=1, tiled=True)]
    all_to_all x1 -> x0, blocking collectives: 10.1 us -> none  [whole_step(): sent = lax.all_to_all(sent, 'dp', 0, 0)]
  transfers between devices with their start and end apart: 6 -> 6, of which waited for: 3 -> 1; matrix products, arithmetic and copies ran while one was open for 6% -> 6% of each run, Pallas kernels for 51% -> 53%
where the time goes in v5:
time: 899 us; the launch traced here: 887 us
  Pallas kernels  722 us (80%)
  other arithmetic  55.7 us (6%)
  matrix products  44.2 us (5%)
  local copies, waits for them, and re-layouts  28 us (3%)
  between operations  24 us (3%)
  waiting for transfers between devices  13 us (1%)
    pallas_call x11, Pallas kernels, comm_call(): pl.pallas_call(kernel, out_shape=[jax.ShapeDtypeStruct(shape, kind) for s...  600 us
    pallas_call x4, Pallas kernels, head_call(): pl.pallas_call(kernel, grid=(grid,), in_specs=in_specs, out_specs=out_spe...  95.6 us
    pallas_call x2, Pallas kernels, local_call(): pl.pallas_call(kernel, out_shape=[jax.ShapeDtypeStruct(shape, kind) for s...  26.6 us
    dot_general x4, matrix products, dot_nt(): lax.dot_general(a, b, (((1,), (1,)), ((), ())), precision=precision, pref...  20.1 us
  transfers between devices with their start and end apart: 6, of which 1 were waited for; matrix products, arithmetic and copies ran while one was open for 6% of the time, Pallas kernels for 53%

profile of v5, /device:TPU:12, one launch (start us, length us, event | category | flops | bytes accessed | tf_op | source)
XLA Modules:
  0.0 887.4 jit_solution(9591996825872960109)
XLA Ops:
  9.4 6.0 shard_map.286
  16.3 6.2 sort.15
  23.7 12.6 %shard_map.287 = (bf16[8192,256]{1,0:T(8,128)(2,1)}, bf16[6286,256]{1,0:T(8,128)(2,1)}, f32[8,256]{1,0:T(8,128)}) custom-call(s32[1]{0:T(128)} %bitcast.1.count_ref, s32[8192]{0:T(1024)} %get-tuple-element.170.row_ref, s32[8192]{0:T(1024)} %get-tuple-element.169.tok_ref, f32[6286,256]{1,0:T(8,128)} %table_ref.1), custom_call_target="tpu_custom_call" | custom-call | flops 6502404 | bytes 13004808 | tf_op jit(solution)/shard_map/pallas_call | solution.py:66
  40.5 136.0 %shard_map.289 = (bf16[4,4,2,32,4384]{4,3,2,1,0:T(8,128)(2,1)}, bf16[4,4,2,64,1024]{4,3,2,1,0:T(8,128)(2,1)}, bf16[4,4,2,32,4384]{4,3,2,1,0:T(8,128)(2,1)}, bf16[4,4,2,64,1024]{4,3,2,1,0:T(8,128)(2,1)}) custom-call(bf16[32,4384]{1,0:T(8,128)(2,1)} %get-tuple-element.74.refs_0_, bf16[64,1024]{1,0:T(8,128)(2,1)} %get-tuple-element.75.refs_1_, ...), custom_call_target="tpu_custom_call" | custom-call | flops 19759104 | bytes 39518208 | tf_op jit(solution)/shard_map/pallas_call | solution.py:184
  176.5 3.4 slice.128
  189.0 16.8 %shard_map.288 = f32[256,1024]{1,0:T(8,128)} custom-call(bf16[4,256,256]{2,1,0:T(8,128)(2,1)} %bitcast.108), custom_call_target="tpu_custom_call" | custom-call | flops 524288 | bytes 1048576 | tf_op jit(solution)/shard_map/pallas_call | solution.py:184
  208.6 8.0 fusion.14.proj_ref
  216.7 28.3 %shard_map.290 = (f32[256,2304]{1,0:T(8,128)}, f32[256,2048]{1,0:T(8,128)}, bf16[256,2048]{1,0:T(8,128)(2,1)}, f32[256,128]{1,0:T(8,128)}, f32[256,128]{1,0:T(8,...) custom-call(f32[256,4384]{1,0:T(8,128)} %fusion.14.proj_ref, f32[4,2304]{1,0:T(4,128)} %reshape.301.cw_ref, ...), custom_call_target="tpu_custom_call" | custom-call | flops 524288 | bytes 1048576 | tf_op jit(solution)/shard_map/pallas_call | solution.py:184
  245.0 3.9 multiply_reduce_fusion.9
  250.1 8.0 fusion.15.proj_ref
  258.1 27.3 %shard_map.291 = (f32[256,2304]{1,0:T(8,128)}, f32[256,2048]{1,0:T(8,128)}, bf16[256,2048]{1,0:T(8,128)(2,1)}, f32[256,128]{1,0:T(8,128)}, f32[256,128]{1,0:T(8,...) custom-call(f32[256,4384]{1,0:T(8,128)} %fusion.15.proj_ref, f32[4,2304]{1,0:T(4,128)} %reshape.304.cw_ref, ...), custom_call_target="tpu_custom_call" | custom-call | flops 524288 | bytes 1048576 | tf_op jit(solution)/shard_map/pallas_call | solution.py:184
  285.4 4.1 multiply_reduce_fusion.8
  292.1 68.6 %shard_map.292 = (bf16[6400,2048]{1,0:T(8,128)(2,1)}, bf16[8,256,1024]{2,1,0:T(8,128)(2,1)}, f32[1,2048]{1,0:T(1,128)}, f32[5,1,2048]{2,1,0:T(1,128)}, f32[1,2048]{1,0:T(1,128)}) custom-call(bf16[1280,1024]{1,0:T(8,128)(2,1)} %all-gather.5.cloned.1.call-done.lead_ref, bf16[5006,1024]{1,0:T(8,128)(2,1)} %all-gather.7.cloned.1.call-done.table_ref.e_ref, ...), custom_call_target="tpu_custom_call" | custom-call | flops 3670016 | bytes 7340032 | tf_op jit(solution)/shard_map/pallas_call | solution.py:184
  360.7 41.0 %shard_map.293 = bf16[2048,1024]{1,0:T(8,128)(2,1)} custom-call(bf16[1280,1024]{1,0:T(8,128)(2,1)} %all-gather.5.cloned.1.call-done.lead_ref, bf16[5006,1024]{1,0:T(8,128)(2,1)} %all-gather.7.cloned.1.call-done.table_ref.e_ref, bf16[6400,2048]{1,0:T(8,128)(2,1)} %get-tuple-element.86.q_ref, f32[5,1,2048]{2,1,0:T(1,128)} %get-tuple-element.87.fac_ref, ...), custom_call_target="tpu_custom_call" | custom-call | flops 26365394944 | bytes 51494912 | tf_op jit(solution)/shard_map/pallas_call | solution.py:1125
  401.7 33.9 %shard_map.294 = bf16[6286,1024]{1,0:T(8,128)(2,1)} custom-call(bf16[2048,1024]{1,0:T(8,128)(2,1)} %bitcast.128, bf16[6400,2048]{1,0:T(8,128)(2,1)} %get-tuple-element.86.q_ref, f32[5,1,2048]{2,1,0:T(1,128)} %get-tuple-element.87.fac_ref, f32[1,2048]{1,0:T(1,128)} %broadcast_select_fusion.2.w_ref, s32[1,2048]{1,0:T(1,128)} %sub.71.lab_ref), custom_call_target="tpu_custom_call" | custom-call | flops 26365394944 | bytes 51494912 | tf_op jit(solution)/shard_map/pallas_call | solution.py:1125
  435.6 12.4 %reduce-scatter.6.cloned.1.call-done = bf16[256,1024]{1,0:T(8,128)(2,1)} async-done(((bf16[2048,1024]{1,0:T(8,128)(2,1)}), bf16[256,1024]{1,0:T(8,128)(2,1)}) %reduce-scatter.6.cloned.1.call-update) | async-done | bytes 524304 | tf_op jit(solution)/shard_map/reduce_scatter | solution.py:1749
  449.4 2.7 multiply_reduce_fusion.3
  453.1 2.6 fusion.16.dyn_ref
  455.7 42.8 %shard_map.295 = (bf16[256,4384]{1,0:T(8,128)(2,1)}, f32[8,2304]{1,0:T(8,128)}, f32[8,128]{1,0:T(8,128)}, f32[1,2048]{1,0:T(1,128)}) custom-call(f32[256,2048]{1,0:T(8,128)} %fusion.16.dyn_ref, f32[256,2048]{1,0:T(8,128)} %get-tuple-element.90.y_ref, f32[256,4384]{1,0:T(8,128)} %fusion.15.proj_ref, f32[8,2304]{1,0:T(8,128)} %get-tuple-element.91.halo_ref, ...), custom_call_target="tpu_custom_call" | custom-call | flops 524288 | bytes 1048576 | tf_op jit(solution)/shard_map/pallas_call | solution.py:184
  498.5 8.0 multiply_reduce_fusion.4
  509.3 2.7 fusion.17.dyn_ref
  512.0 38.7 %shard_map.296 = (bf16[256,4384]{1,0:T(8,128)(2,1)}, f32[8,2304]{1,0:T(8,128)}, f32[8,128]{1,0:T(8,128)}, f32[1,2048]{1,0:T(1,128)}) custom-call(f32[256,2048]{1,0:T(8,128)} %fusion.17.dyn_ref, f32[256,2048]{1,0:T(8,128)} %get-tuple-element.97.y_ref, f32[256,4384]{1,0:T(8,128)} %fusion.14.proj_ref, f32[8,2304]{1,0:T(8,128)} %get-tuple-element.98.halo_ref, ...), custom_call_target="tpu_custom_call" | custom-call | flops 524288 | bytes 1048576 | tf_op jit(solution)/shard_map/pallas_call | solution.py:184
  550.7 6.8 multiply_reduce_fusion.1
  558.7 9.5 %shard_map.300 = bf16[4,256,256]{2,1,0:T(8,128)(2,1)} custom-call(f32[256,1024]{1,0:T(8,128)} %multiply_add_fusion.2.in_ref), custom_call_target="tpu_custom_call" | custom-call | flops 524288 | bytes 1048576 | tf_op jit(solution)/shard_map/pallas_call | solution.py:184
  571.1 10.1 %shard_map.297 = (bf16[1024,4384]{1,0:T(8,128)(2,1)}, bf16[2048,1024]{1,0:T(8,128)(2,1)}) custom-call(bf16[256,1024]{1,0:T(8,128)(2,1)} %copy-done.15, bf16[256,4384]{1,0:T(8,128)(2,1)} %get-tuple-element.105.dp_ref, bf16[256,2048]{1,0:T(8,128)(2,1)} %get-tuple-element.79.yn_ref, bf16[256,1024]{1,0:T(8,128)(2,1)} %copy-done.25), custom_call_target="tpu_custom_call" | custom-call | flops 3372220416 | bytes 6586368 | tf_op jit(solution)/shard_map/pallas_call | solution.py:1125
  581.2 10.6 %shard_map.298 = (bf16[1024,4384]{1,0:T(8,128)(2,1)}, bf16[2048,1024]{1,0:T(8,128)(2,1)}) custom-call(bf16[256,1024]{1,0:T(8,128)(2,1)} %copy-done.16, bf16[256,4384]{1,0:T(8,128)(2,1)} %get-tuple-element.96.dp_ref, bf16[256,2048]{1,0:T(8,128)(2,1)} %get-tuple-element.82.yn_ref, bf16[256,1024]{1,0:T(8,128)(2,1)} %copy-done.26), custom_call_target="tpu_custom_call" | custom-call | flops 3372220416 | bytes 6586368 | tf_op jit(solution)/shard_map/pallas_call | solution.py:1125
  591.8 204.0 %shard_map.299 = (f32[32,4384]{1,0:T(8,128)}, f32[64,1024]{1,0:T(8,128)}, f32[32,4384]{1,0:T(8,128)}, f32[64,1024]{1,0:T(8,128)}) custom-call(bf16[4,4,2,32,4384]{4,3,2,1,0:T(8,128)(2,1)} %bitcast.91, bf16[4,4,2,64,1024]{4,3,2,1,0:T(8,128)(2,1)} %bitcast.93, bf16[4,4,2,32,4384]{4,3,2,1,0:T(8,128)(2,1)} %bitcast.92, bf16[4,4,2,64,1024]{4,3,2,1,0:T(8,128)(2,1)} %bitcast.94), custom_call_target="tpu_custom_call" | custom-call | flops 26345472 | bytes 52690944 | tf_op jit(solution)/shard_map/pallas_call | solution.py:184
  804.5 14.0 %shard_map.301 = (f32[6286,256]{1,0:T(8,128)}, f32[8,256]{1,0:T(8,128)}) custom-call(s32[1]{0:T(128)} %bitcast.1.count_ref, s32[8192]{0:T(1024)} %get-tuple-element.170.row_ref, s32[8192]{0:T(1024)} %get-tuple-element.169.tok_ref, bf16[8192,256]{1,0:T(8,128)(2,1)} %bitcast.95, bf16[6286,256]{1,0:T(8,128)(2,1)} %reduce-scatter.8.cloned.1.call-done.base_ref), custom_call_target="tpu_custom_call" | custom-call | flops 7478276 | bytes 14956552 | tf_op jit(solution)/shard_map/pallas_call | solution.py:66
  822.7 22.1 %shard_map.302 = f32[256,128]{1,0:T(8,128)} custom-call(f32[256,128]{1,0:T(8,128)} %bitcast.109), custom_call_target="tpu_custom_call" | custom-call | flops 393216 | bytes 786432 | tf_op jit(solution)/shard_map/pallas_call | solution.py:184
  851.9 3.1 fusion.5
  858.4 7.8 fusion.6
  866.1 8.8 add_multiply_fusion
  (179 shorter events, 52.7 us)
Async XLA Ops:
  8.0 181.0 %reduce-scatter.4.cloned.1.call-start = ((), (), s32[]{:S(2)}) async-start(), calls=%async_computation.3 | async-start | bytes 4718592 | tf_op jit(solution)/shard_map/reduce_scatter | solution.py:1700
  36.3 255.8 %all-gather.5.cloned.1.call-start = ((), (), s32[]{:S(2)}) async-start(), calls=%async_computation.4 | async-start | bytes 3276800 | tf_op jit(solution)/shard_map/all_gather | solution.py:1679
  38.8 253.4 %all-gather.7.cloned.1.call-start = ((), (), s32[]{:S(2)}) async-start(), calls=%async_computation.5 | async-start | bytes 12820480 | tf_op jit(solution)/shard_map/all_gather | solution.py:1718
  40.5 139.5 %copy-start.27 = (f32[30400]{0:T(1024)S(1)}, f32[30400]{0:T(1024)}, u32[]{:S(2)}) copy-start(f32[30400]{0:T(1024)} %param.27) | copy-start | bytes 364804
  176.5 5.7 copy-start.38
  176.5 8.6 copy-start.35
  179.9 268.1 %reduce-scatter.6.cloned.1.call-start = ((), (), s32[]{:S(2)}) async-start(), calls=%async_computation.6 | async-start | bytes 4718592 | tf_op jit(solution)/shard_map/reduce_scatter | solution.py:1749
  208.6 8.0 copy-start.15
  216.7 28.3 %copy-start.1 = (f32[256,1024]{1,0:T(8,128)S(1)}, f32[256,1024]{1,0:T(8,128)}, u32[]{:S(2)}) copy-start(f32[256,1024]{1,0:T(8,128)} %shard_map.288) | copy-start | bytes 3145732
  250.1 8.0 copy-start.16
  401.7 402.8 %all-gather.9.cloned.1.call-start = ((), (), s32[]{:S(2)}) async-start(), calls=%async_computation.8 | async-start | bytes 4718592 | tf_op jit(solution)/shard_map/all_gather | solution.py:1771
  435.6 16.4 %copy-start.5 = (f32[256,1024]{1,0:T(8,128)S(1)}, f32[256,1024]{1,0:T(8,128)}, u32[]{:S(2)}) copy-start(f32[256,1024]{1,0:T(8,128)} %copy-done.4) | copy-start | bytes 3145732
  498.5 8.0 copy-start.3
  498.5 8.0 copy-start.6
  498.5 8.0 copy-start.13
  508.0 42.6 %copy-start.25 = (bf16[256,1024]{1,0:T(8,128)(2,1)}, bf16[256,1024]{1,0:T(8,128)(2,1)S(1)}, u32[]{:S(2)}) copy-start(bf16[256,1024]{1,0:T(8,128)(2,1)S(1)} %get-tuple-element.146.db_ref) | copy-start | bytes 1572868
  550.7 6.8 copy-start.11
  568.3 236.2 %reduce-scatter.8.cloned.1.call-start = ((), (), s32[]{:S(2)}) async-start(), calls=%async_computation.7 | async-start | bytes 16097280 | tf_op jit(solution)/shard_map/reduce_scatter | solution.py:1753
  799.7 52.1 %copy-start.9 = (f32[2,32,4384]{2,1,0:T(8,128)S(1)}, f32[2,32,4384]{2,1,0:T(8,128)}, u32[]{:S(2)}) copy-start(f32[2,32,4384]{2,1,0:T(8,128)} %param.21) | copy-start | bytes 3366916
  799.7 52.2 %copy-start.14 = (f32[32,4384]{1,0:T(8,128)S(1)}, f32[32,4384]{1,0:T(8,128)}, u32[]{:S(2)}) copy-start(f32[32,4384]{1,0:T(8,128)} %get-tuple-element.115) | copy-start | bytes 1683460
  818.5 36.5 %copy-start.22 = (f32[64,1024]{1,0:T(8,128)S(1)}, f32[64,1024]{1,0:T(8,128)}, u32[]{:S(2)}) copy-start(f32[64,1024]{1,0:T(8,128)} %get-tuple-element.117) | copy-start | bytes 786436
  844.8 10.2 %copy-start.19 = (f32[2,64,1024]{2,1,0:T(8,128)S(1)}, f32[2,64,1024]{2,1,0:T(8,128)}, u32[]{:S(2)}) copy-start(f32[2,64,1024]{2,1,0:T(8,128)} %param.24) | copy-start | bytes 1572868
  844.8 10.2 %copy-start.23 = (f32[64,1024]{1,0:T(8,128)S(1)}, f32[64,1024]{1,0:T(8,128)}, u32[]{:S(2)}) copy-start(f32[64,1024]{1,0:T(8,128)} %get-tuple-element.118) | copy-start | bytes 786436
  851.9 5.7 copy-start.21
  851.9 5.6 copy-start.28
  851.9 6.4 copy-start.7
  855.0 19.9 %copy-start.10 = (f32[2,32,4384]{2,1,0:T(8,128)}, f32[2,32,4384]{2,1,0:T(8,128)S(1)}, u32[]{:S(2)}) copy-start(f32[2,32,4384]{2,1,0:T(8,128)S(1)} %get-tuple-element.137) | copy-start | bytes 3366916
  857.6 18.5 %copy-start.17 = (f32[2,64,1024]{2,1,0:T(8,128)}, f32[2,64,1024]{2,1,0:T(8,128)S(1)}, u32[]{:S(2)}) copy-start(f32[2,64,1024]{2,1,0:T(8,128)S(1)} %get-tuple-element.134) | copy-start | bytes 1572868
  858.4 18.6 %copy-start.29 = (f32[30400]{0:T(1024)}, f32[30400]{0:T(1024)S(1)}, u32[]{:S(2)}) copy-start(f32[30400]{0:T(1024)S(1)} %get-tuple-element.131) | copy-start | bytes 364804
  866.1 8.8 copy-start
  866.1 8.8 copy-start.20
  866.1 9.9 %copy-start.24 = (f32[2,64,1024]{2,1,0:T(8,128)S(1)}, f32[2,64,1024]{2,1,0:T(8,128)}, u32[]{:S(2)}) copy-start(f32[2,64,1024]{2,1,0:T(8,128)} %param.26) | copy-start | bytes 1572868
  (15 other events, 33.7 us)
Sparse Core Ops, SparseCore 0:
  36.5 83.5 reduce-scatter.3
  401.8 46.1 reduce-scatter.5
  568.4 48.2 all-gather.8
Sparse Core Ops, SparseCore 1:
  39.2 62.9 all-gather.4
  180.0 109.4 all-gather.6
  571.9 214.2 reduce-scatter.7

commit v6 on v5

--- a/solution.py
+++ b/solution.py
@@ -107,18 +107,27 @@
 
     lax.fori_loop(0, tokens // step, put, 0)
     rows_all = table_ref.shape[0]
-    whole = rows_all // step
+    part = VTILE // 5
+    whole = rows_all // part
+
+    def low_rows(i):
+        return table_ref[pl.ds(pl.multiple_of(i * part, part), part), :].astype(bf16)
+
+    def add(low, total):
+        return total + jnp.sum(low.astype(f32).reshape(part // 8, 8, -1), axis=0)
 
     def cast(i, total):
-        rows = pl.ds(pl.multiple_of(i * step, step), step)
-        low = table_ref[rows, :].astype(bf16)
-        low_ref[rows, :] = low
-        return total + jnp.sum(low.astype(f32).reshape(step // 8, 8, -1), axis=0)
-
-    sum_ref[...] = lax.fori_loop(0, whole, cast, jnp.zeros(sum_ref.shape, f32))
-    if rows_all > whole * step:
-        low = table_ref[whole * step :, :].astype(bf16)
-        low_ref[whole * step :, :] = low
+        low = low_rows(i)
+        low_ref[pl.ds(pl.multiple_of(i * part - VTILE, part), part), :] = low
+        return add(low, total)
+
+    total = lax.fori_loop(
+        0, VTILE // part, lambda i, t: add(low_rows(i), t), jnp.zeros(sum_ref.shape, f32)
+    )
+    sum_ref[...] = lax.fori_loop(VTILE // part, whole, cast, total)
+    if rows_all > whole * part:
+        low = table_ref[whole * part :, :].astype(bf16)
+        low_ref[whole * part - VTILE :, :] = low
         sum_ref[0:1, :] += jnp.sum(low.astype(f32), axis=0, keepdims=True)
 
 
@@ -323,10 +332,20 @@
     return [1 << b for b in range(size.bit_length() - 1)]
 
 
-def total_kernel(in_ref, out_ref, work, got, send, recv):
+TCHUNK = 512
+
+
+def stepped(weight, moment, average, grad, factor):
+    scaled = grad * factor
+    moment_new = 0.5 * moment + scaled
+    weight_new = weight - step_rate * (scaled + 0.5 * moment_new)
+    return weight_new, moment_new, 0.5 * average + 0.5 * weight_new
+
+
+def total_kernel(small, squares_at, packed_ref, total_ref, norm_ref, work, got, send, recv):
     dp = lax.axis_index("dp")
     me = lax.axis_index("fsdp")
-    half = in_ref.shape[0] // 2
+    half = packed_ref.shape[0] // 2
     core = me % MB
     partners = [("f", b) for b in bits_of(lax.axis_size("fsdp")) if b > 1]
     partners += [("d", b) for b in bits_of(lax.axis_size("dp"))]
@@ -343,10 +362,10 @@
 
     mine = pl.ds(pl.multiple_of(core * half, 8), half)
     theirs = pl.ds(pl.multiple_of((1 - core) * half, 8), half)
-    copy = remote(in_ref.at[theirs], got.at[0], send.at[0], recv.at[0], *mate)
+    copy = remote(packed_ref.at[theirs], got.at[0], send.at[0], recv.at[0], *mate)
     copy.start()
     copy.wait()
-    work[0] = in_ref[mine, :] + got[0]
+    work[0] = packed_ref[mine, :] + got[0]
     for i, p in enumerate(partners):
         copy = remote(work.at[i], got.at[i + 1], send.at[i + 1], recv.at[i + 1], *across(*p))
         copy.start()
@@ -356,18 +375,29 @@
     copy = remote(work.at[n], got.at[n + 1], send.at[n + 1], recv.at[n + 1], *mate)
     copy.start()
     copy.wait()
-    out_ref[mine, :] = work[n]
-    out_ref[theirs, :] = got[n + 1]
-
-
-def total_of(array):
-    rows = array.shape[0]
+    total_ref[mine, :] = work[n]
+    total_ref[theirs, :] = got[n + 1]
+
+    total = total_ref[...]
+    index = lax.broadcasted_iota(jnp.int32, total.shape, 0) * LANES
+    index = index + lax.broadcasted_iota(jnp.int32, total.shape, 1)
+    parts = jnp.where(index < small, total * total, jnp.where(index == squares_at, total, 0.0))
+    square = jnp.sum(jnp.sum(parts, axis=0, keepdims=True), axis=1, keepdims=True)
+    norm = jnp.sqrt(square)
+    factor = jnp.minimum(1.0, clip_limit / norm)
+    norm_ref[0:1, :] = jnp.broadcast_to(norm, (1, LANES))
+    norm_ref[1:2, :] = jnp.broadcast_to(factor, (1, LANES))
+    norm_ref[2:8, :] = jnp.zeros((6, LANES), f32)
+
+
+def total_of(packed, small, squares_at):
     steps = len(bits_of(lax.axis_size("fsdp"))) - 1 + len(bits_of(lax.axis_size("dp")))
+    rows = packed.shape[0]
     return comm_call(
-        total_kernel,
+        functools.partial(total_kernel, small, squares_at),
         3,
-        (array,),
-        ((array.shape, f32),),
+        (packed,),
+        ((packed.shape, f32), ((8, LANES), f32)),
         (
             pltpu.VMEM((steps + 1, rows // 2, LANES), f32),
             pltpu.VMEM((steps + 2, rows // 2, LANES), f32),
@@ -375,9 +405,60 @@
             pltpu.SemaphoreType.DMA((steps + 2,)),
         ),
         (pltpu.VMEM,),
-        (pltpu.VMEM,),
-        array.size * 4 * 3,
-    )[0]
+        (pltpu.VMEM, pltpu.VMEM),
+        packed.size * 4 * 3,
+    )
+
+
+def update_table_kernel(norm_ref, w_ref, m_ref, a_ref, g_ref, *outs):
+    new = stepped(w_ref[...], m_ref[...], a_ref[...], g_ref[...], norm_ref[1:2, 0:1])
+    for out, value in zip(outs, new + (new[0].astype(bf16),)):
+        out[...] = value
+
+
+def update_table(norms, weight, moment, average, grad):
+    rows, cols = weight.shape
+    block = pl.BlockSpec((TCHUNK, cols), lambda i: (i, 0))
+    return pl.pallas_call(
+        update_table_kernel,
+        name="update_table",
+        grid=(pl.cdiv(rows, TCHUNK),),
+        in_specs=[pl.BlockSpec((8, LANES), lambda i: (0, 0))] + [block] * 4,
+        out_specs=[block] * 4,
+        out_shape=[jax.ShapeDtypeStruct((rows, cols), kind) for kind in (f32, f32, f32, bf16)],
+        compiler_params=pltpu.CompilerParams(vmem_limit_bytes=VMEM_LIMIT),
+        cost_estimate=pl.CostEstimate(
+            flops=8 * weight.size, transcendentals=0, bytes_accessed=30 * weight.size
+        ),
+    )(norms, weight, moment, average, grad)
+
+
+def update_projections_kernel(norm_ref, *refs):
+    factor = norm_ref[1:2, 0:1]
+    sources = (refs[0:3], refs[3:6])
+    grads = refs[6 : 6 + 2 * LAYERS]
+    outs = refs[6 + 2 * LAYERS :]
+    for group in (0, 1):
+        for l in range(LAYERS):
+            grad = grads[2 * l + group]
+            step = min(grad.shape[0], 16)
+
+            def some(r, _, l=l, group=group, grad=grad, step=step):
+                rows = pl.ds(pl.multiple_of(r * step, step), step)
+                new = stepped(*(ref[l, rows, :] for ref in sources[group]), grad[rows, :], factor)
+                for i in range(3):
+                    outs[4 * group + i][l, rows, :] = new[i]
+                outs[4 * group + 3][l, rows, :] = new[0].astype(bf16)
+                return 0
+
+            lax.fori_loop(0, grad.shape[0] // step, some, 0)
+
+
+def update_projections(norms, projections, grads):
+    outs = []
+    for i in (0, 3):
+        outs += [(projections[i].shape, f32)] * 3 + [(projections[i].shape, bf16)]
+    return local_call(update_projections_kernel, (norms, *projections, *grads), tuple(outs))
 
 
 def snake(place, size):
@@ -815,12 +896,36 @@
             per_pair[p] = jnp.where(half, left, right)
 
 
+def take_vectors(layer_ref, conv_ref, head_ref, gate_ref, cw_ref, dtb_ref, al_ref, sk_ref, gg_ref):
+    layer = layer_ref[0]
+    cw_ref[0 : CONV + 1, :] = conv_ref[layer]
+    heads = head_ref[layer]
+    dtb_ref[...] = heads[0:1, :]
+    al_ref[...] = heads[1:2, :]
+    half = first_half(1)
+    for p in range(PAIRS):
+        left = jnp.broadcast_to(heads[2:3, 2 * p : 2 * p + 1], (1, LANES))
+        right = jnp.broadcast_to(heads[2:3, 2 * p + 1 : 2 * p + 2], (1, LANES))
+        sk_ref[p : p + 1, :] = jnp.where(half, left, right)
+    gg_ref[...] = gate_ref[layer]
+
+
+VECTOR_SCRATCH = (
+    pltpu.VMEM((8, XBC), f32),
+    pltpu.VMEM((1, LANES), f32),
+    pltpu.VMEM((1, LANES), f32),
+    pltpu.VMEM((PAIRS, LANES), f32),
+    pltpu.VMEM((1, DI), f32),
+)
+
+
 def scan_kernel(
-    proj_ref, cw_ref, cb_ref, dtb_ref, al_ref, sk_ref, gg_ref,
+    layer_ref, proj_ref, conv_ref, head_ref, gate_ref,
     pre_ref, y_ref, yn_ref, dt_ref, cum_ref, got, halo_ref,
-    pad, col, tcol, lcol, lrow, st, give, square, edge_send, edge_recv, send, recv,
+    cw_ref, dtb_ref, al_ref, sk_ref, gg_ref, pad, col, tcol, lcol, lrow, st, give, square, edge_send, edge_recv, send, recv,
 ):
     rows = proj_ref.shape[0]
+    take_vectors(layer_ref, conv_ref, head_ref, gate_ref, cw_ref, dtb_ref, al_ref, sk_ref, gg_ref)
     first, final = chunk_place(1)
     chain_barrier(1, first, final)
     edge = to_next(
@@ -860,7 +965,7 @@
 
     def conv(i, _):
         xs = pair_lanes(i)
-        out = jnp.broadcast_to(cb_ref[0:1, xs], (rows, LANES))
+        out = jnp.broadcast_to(cw_ref[CONV : CONV + 1, xs], (rows, LANES))
         for k in range(CONV):
             out = out + cw_ref[k : k + 1, xs] * pad[5 + k : 5 + k + rows, xs]
         pre_ref[:, xs] = out
@@ -893,7 +998,7 @@
             d = jnp.concatenate([c] * (rows // LANES), axis=1) - lrow[pl.ds(h, 1), :]
             m = (jnp.exp(jnp.where(causal, d, OFF)) * cb).astype(bf16)
             parts.append(dot_nn(m, xtb))
-        y = jnp.where(half, parts[0], parts[1]) + sk_ref[0:1, xs] * x
+        y = jnp.where(half, parts[0], parts[1]) + sk_ref[pl.ds(p, 1), :] * x
         y = y + jnp.exp(lcol[p]) * dot_nt(cm, got[xs, :])
         y_ref[:, xs] = y
         g = y * silu(proj_ref[:, xs])
@@ -926,13 +1031,14 @@
 
 
 def back_kernel(
-    dyn_ref, y_ref, proj_ref, halo_ref, pre_ref, dt_ref, cum_ref, sin_ref,
-    cw_ref, dtb_ref, al_ref, sk_ref, gg_ref,
+    layer_ref, dyn_ref, y_ref, proj_ref, halo_ref, pre_ref, dt_ref, cum_ref, sin_ref,
+    conv_ref, head_ref, gate_ref,
     dp_ref, dcw_ref, dsm_ref, dgg_ref,
-    pad, grad, col, tcol, lcol, lrow, dcb, dbm, dcm, dlog, dtx, ends, dy_ref, drive_ref,
+    cw_ref, dtb_ref, al_ref, sk_ref, gg_ref, pad, grad, col, tcol, lcol, lrow, dcb, dbm, dcm, dlog, dtx, ends, dy_ref, drive_ref,
     got, give, gst, dx_ref, edge_ref, from_ref, edge_send, edge_recv, send, recv,
 ):
     rows = y_ref.shape[0]
+    take_vectors(layer_ref, conv_ref, head_ref, gate_ref, cw_ref, dtb_ref, al_ref, sk_ref, gg_ref)
     first, final = chunk_place(-1)
     chain_barrier(-1, first, final)
 
@@ -1023,7 +1129,7 @@
         dxt = jnp.where(half, parts[0], parts[1]) + dst
         dbm[...] += dot_nn((tail * xt).astype(bf16), gin)
         dcm[...] += dot_nn((jnp.exp(lp) * dy).astype(bf16), sin)
-        sk = sk_ref[0:1, xs]
+        sk = sk_ref[pl.ds(p, 1), :]
         pick = jnp.where(lane_col == 2 * p + jnp.where(lane_row >= HDIM, 1, 0), 1.0, 0.0)
         dlog[...] += dot_nn(dy * (y_ref[:, xs] - sk * x) - xt * dxt, pick, highest)
         dtx[...] += dot_nn(x * dxt, pick, highest)
@@ -1372,15 +1478,9 @@
     def _():
         acc[...] = jnp.zeros(acc.shape, f32)
 
-    @pl.when(step == 0)
-    def _():
-        et[...] = lead_ref[...].astype(f32).T.astype(bf16)
-
-    @pl.when(step > 0)
-    def _():
-        eid = lax.broadcasted_iota(jnp.int32, (VTILE, e_ref.shape[1]), 0)
-        et[...] = jnp.where(eid < vocab_rows - first, e_ref[...].astype(f32), 0.0).T.astype(bf16)
-
+    eid = lax.broadcasted_iota(jnp.int32, (VTILE, e_ref.shape[1]), 0)
+    part = jnp.where(step == 0, lead_ref[...].astype(f32), e_ref[...].astype(f32))
+    et[...] = jnp.where(eid < vocab_rows - first, part, 0.0).T.astype(bf16)
 
     def chunk(j, _):
         ns = pl.ds(pl.multiple_of(j * NTILE, NTILE), NTILE)
@@ -1508,39 +1608,27 @@
     return back, jnp.sum(grad * unit, axis=0)
 
 
-def wide(row):
-    return jnp.pad(row, (0, LANES - row.shape[0]))[None]
-
-
-def layer_vectors(vector_params, layer_index):
-    offset = layer_index * PER
-    pieces = []
-    for size in (CONV * XBC, XBC, HEADS, HEADS, HEADS, D, DI):
-        pieces.append(vector_params[offset : offset + size])
-        offset += size
-    conv_w, conv_b, dt_bias, decay_log, skip, pre_gain, gate_gain = pieces
+def all_vectors(vector_params):
+    rows = vector_params[: LAYERS * PER].reshape(LAYERS, PER)
+    at = (CONV + 1) * XBC
+    heads = rows[:, at : at + 3 * HEADS].reshape(LAYERS, 3, HEADS)
+    after_heads = at + 3 * HEADS
     return dict(
-        conv_w=conv_w.reshape(CONV, XBC),
-        conv_b=conv_b[None],
-        dt_bias=wide(dt_bias),
-        decay_log=wide(decay_log),
-        skip=jnp.repeat(skip, HDIM)[None],
-        pre_gain=pre_gain,
-        gate_gain=gate_gain[None],
-    )
-
-
-def layer_forward(hidden, w_in, w_out, vec):
+        conv=rows[:, :at].reshape(LAYERS, CONV + 1, XBC),
+        heads=jnp.pad(heads, ((0, 0), (0, 5), (0, LANES - HEADS))),
+        gate=rows[:, after_heads + D :].reshape(LAYERS, 1, DI),
+        pre=rows[:, after_heads : after_heads + D],
+    )
+
+
+def layer_forward(hidden, w_in, w_out, vec, layer):
     rows = hidden.shape[0]
-    normed = (hidden * norm_scale(hidden) * vec["pre_gain"]).astype(bf16)
+    normed = (hidden * norm_scale(hidden) * vec["pre"][layer]).astype(bf16)
     proj = jnp.dot(normed, w_in, preferred_element_type=f32)
     pre, y, mixed, dt, cum, entering, halo = comm_call(
         scan_kernel,
         1,
-        (
-            proj, vec["conv_w"], vec["conv_b"], vec["dt_bias"], vec["decay_log"], vec["skip"],
-            vec["gate_gain"],
-        ),
+        (jnp.full((1,), layer, jnp.int32), proj, vec["conv"], vec["heads"], vec["gate"]),
         (
             ((rows, XBC), f32),
             ((rows, DI), f32),
@@ -1550,7 +1638,8 @@
             ((DI, NSTATE), bf16),
             ((8, XBC), f32),
         ),
-        (
+        VECTOR_SCRATCH
+        + (
             pltpu.VMEM((rows + 8, XBC), f32),
             pltpu.VMEM((HEADS, rows, LANES), f32),
             pltpu.VMEM((PAIRS, rows, LANES), f32),
@@ -1564,7 +1653,7 @@
             pltpu.SemaphoreType.DMA((CHAIN_STEPS,)),
             pltpu.SemaphoreType.DMA((CHAIN_STEPS,)),
         ),
-        (pltpu.VMEM,) * 7,
+        (pltpu.SMEM,) + (pltpu.VMEM,) * 4,
         (pltpu.VMEM,) * 7,
         DI * NSTATE * 2,
     )
@@ -1573,7 +1662,7 @@
     return hidden + branch, record
 
 
-def layer_backward(grad_hidden, w_in, w_out, vec, record):
+def layer_backward(grad_hidden, w_in, w_out, vec, layer, record):
     hidden, normed, proj, halo, pre, dt, cum, entering, y, mixed = record
     rows = hidden.shape[0]
     grad_branch = grad_hidden.astype(bf16)
@@ -1582,8 +1671,8 @@
         back_kernel,
         2,
         (
-            grad_mixed, y, proj, halo, pre, dt, cum, entering,
-            vec["conv_w"], vec["dt_bias"], vec["decay_log"], vec["skip"], vec["gate_gain"],
+            jnp.full((1,), layer, jnp.int32), grad_mixed, y, proj, halo, pre, dt, cum, entering,
+            vec["conv"], vec["heads"], vec["gate"],
         ),
         (
             ((rows, ZW), bf16),
@@ -1591,7 +1680,8 @@
             ((8, LANES), f32),
             ((1, DI), f32),
         ),
-        (
+        VECTOR_SCRATCH
+        + (
             pltpu.VMEM((rows + 8, XBC), f32),
             pltpu.VMEM((rows + 16, XBC), f32),
             pltpu.VMEM((HEADS, rows, LANES), f32),
@@ -1617,17 +1707,16 @@
             pltpu.SemaphoreType.DMA((CHAIN_STEPS,)),
             pltpu.SemaphoreType.DMA((CHAIN_STEPS,)),
         ),
-        (pltpu.VMEM,) * 13,
+        (pltpu.SMEM,) + (pltpu.VMEM,) * 11,
         (pltpu.VMEM,) * 4,
         DI * NSTATE * 2,
     )
     grad_normed = dot_nt(grad_proj, w_in)
     grad_in, grad_out = weight_grads(normed, grad_proj, mixed, grad_branch)
-    grad_prev, dpre_gain = norm_back(grad_normed, hidden, vec["pre_gain"])
+    grad_prev, dpre_gain = norm_back(grad_normed, hidden, vec["pre"][layer])
     grad_vec = jnp.concatenate(
         [
-            dconv[:CONV].reshape(-1),
-            dconv[CONV],
+            dconv[: CONV + 1].reshape(-1),
             dsmall[0, :HEADS],
             dsmall[1, :HEADS],
             dsmall[2, :HEADS],
@@ -1636,14 +1725,6 @@
         ]
     )
     return grad_hidden + grad_prev, grad_in, grad_out, grad_vec
-
-
-def advance(weight, moment, average, grad, factor):
-    scaled = grad * factor
-    moment_new = 0.5 * moment + scaled
-    weight_new = weight - step_rate * (scaled + 0.5 * moment_new)
-    average_new = 0.5 * average + 0.5 * weight_new
-    return (weight_new, moment_new, average_new, weight_new.astype(bf16))
 
 
 def whole_step(
@@ -1693,7 +1774,7 @@
     looked, embed_low, own_sums = local_call(
         lookup_kernel,
         (count, row_list, tok_list, embedding),
-        (((every, own_cols), bf16), ((vocab_rows, own_cols), bf16), ((8, own_cols), f32)),
+        (((every, own_cols), bf16), ((vocab_rows - VTILE, own_cols), bf16), ((8, own_cols), f32)),
         scratch=(pltpu.VMEM((every + 8, own_cols), f32),),
         in_smem=(0, 1, 2),
     )
@@ -1715,13 +1796,13 @@
     gathered = gather_layers(shards)
     w_in, w_out = gathered[0::2], gathered[1::2]
     embed_low = after(embed_low, gathered)
-    table = lax.all_gather(embed_low[VTILE:], "dp", axis=1, tiled=True)
-
-    vecs = [layer_vectors(vector_params, l) for l in range(LAYERS)]
+    table = lax.all_gather(embed_low, "dp", axis=1, tiled=True)
+
+    vecs = all_vectors(vector_params)
     final_gain = vector_params[LAYERS * PER :]
     records = []
     for l in range(LAYERS):
-        hidden, record = layer_forward(hidden, w_in[l], w_out[l], vecs[l])
+        hidden, record = layer_forward(hidden, w_in[l], w_out[l], vecs, l)
         records.append(record)
 
     final_low = (hidden * norm_scale(hidden) * final_gain).astype(bf16)
@@ -1758,7 +1839,7 @@
     vec_parts = [None] * LAYERS
     for l in reversed(range(LAYERS)):
         grad_hidden, grad_in, grad_out, vec_parts[l] = layer_backward(
-            grad_hidden, w_in[l], w_out[l], vecs[l], records[l]
+            grad_hidden, w_in[l], w_out[l], vecs, l, records[l]
         )
         if l == 0:
             sent = group_call(
@@ -1782,13 +1863,9 @@
         scratch=(pltpu.VMEM((every + 8, own_cols), f32),),
         in_smem=(0, 1, 2),
     )
-    grad_in_all = jnp.stack(summed_parts[0::2])
-    grad_out_all = jnp.stack(summed_parts[1::2])
-    owner_squares = (
-        jnp.sum(grad_in_all * grad_in_all)
-        + jnp.sum(grad_out_all * grad_out_all)
-        + jnp.sum(table_squares)
-    )
+    owner_squares = jnp.sum(table_squares)
+    for part in summed_parts:
+        owner_squares = owner_squares + jnp.sum(part * part)
     small = vector_params.shape[0]
     used = small + 2 * D + 2
     padded = pl.cdiv(used, 16 * LANES) * 16 * LANES
@@ -1803,23 +1880,30 @@
             jnp.zeros((padded - used,), f32),
         ]
     )
-    packed = total_of(packed.reshape(-1, LANES)).reshape(-1)
+    packed, norms = total_of(packed.reshape(-1, LANES), small, used - 2)
+    updated = list(update_table(norms, embedding, embedding_mom, embedding_avg, table_total))
+    updated += update_projections(
+        norms,
+        (in_proj, in_proj_mom, in_proj_avg, out_proj, out_proj_mom, out_proj_avg),
+        summed_parts,
+    )
+    packed = packed.reshape(-1)
     vector_total = packed[:small]
     hidden_total = packed[small : small + D]
     column_total = packed[small + D : small + 2 * D]
-    squares_total = packed[used - 2]
     mean_part = jnp.sum(hidden_total * column_total) * (0.1 / VOCAB)
-    loss_total = packed[used - 1] - mean_part
-    grad_norm = jnp.sqrt(squares_total + jnp.sum(vector_total * vector_total))
-    factor = jnp.minimum(1.0, clip_limit / grad_norm)
-    loss_value = loss_total / total_count
+    loss_value = (packed[used - 1] - mean_part) / total_count
+    vector_new, vector_mom_new, vector_avg_new = stepped(
+        vector_params, vector_mom, vector_avg, vector_total, norms[1, 0]
+    )
     return (
         loss_value,
-        grad_norm,
-        *advance(embedding, embedding_mom, embedding_avg, table_total, factor),
-        *advance(in_proj, in_proj_mom, in_proj_avg, grad_in_all, factor),
-        *advance(out_proj, out_proj_mom, out_proj_avg, grad_out_all, factor),
-        *advance(vector_params, vector_mom, vector_avg, vector_total, factor),
+        norms[0, 0],
+        *updated,
+        vector_new,
+        vector_mom_new,
+        vector_avg_new,
+        vector_new.astype(bf16),
     )
 
 

time: 899 us -> 884 us (0.983)
  other arithmetic: 55.7 us -> 30.2 us
  Pallas kernels: 722 us -> 740 us
  local copies, waits for them, and re-layouts: 28 us -> 17.5 us
    pallas_call x0 -> x1, Pallas kernels: none -> 21.1 us  [update_table(): pl.pallas_call(update_table_kernel, name='update_table', grid=(pl.cdiv(ro...]
    convert_element_type x6 -> x3, other arithmetic: 15.7 us -> 3.79 us  [the longest x1 2.25 us: whole_step(): vector_new.astype(bf16)]
    add x4 -> x1, other arithmetic: 11.4 us -> 0.68 us  [stepped(): return (weight_new, moment_new, 0.5 * average + 0.5 * weight_new)]
    pallas_call x2 -> x3, Pallas kernels: 26.6 us -> 32.5 us  [local_call(): pl.pallas_call(kernel, out_shape=[jax.ShapeDtypeStruct(shape, kind) for s...]
  transfers between devices with their start and end apart: 6 -> 6, of which waited for: 1 -> 2; matrix products, arithmetic and copies ran while one was open for 6% -> 5% of each run, Pallas kernels for 53% -> 53%
where the time goes in v6:
time: 884 us; the launch traced here: 872 us
  Pallas kernels  740 us (84%)
  matrix products  43.1 us (5%)
  other arithmetic  30.2 us (3%)
  between operations  22.7 us (3%)
  waiting for transfers between devices  18.4 us (2%)
  local copies, waits for them, and re-layouts  17.5 us (2%)
    pallas_call x11, Pallas kernels, comm_call(): pl.pallas_call(kernel, out_shape=[jax.ShapeDtypeStruct(shape, kind) for s...  591 us
    pallas_call x4, Pallas kernels, head_call(): pl.pallas_call(kernel, grid=(grid,), in_specs=in_specs, out_specs=out_spe...  94.5 us
    pallas_call x3, Pallas kernels, local_call(): pl.pallas_call(kernel, out_shape=[jax.ShapeDtypeStruct(shape, kind) for s...  32.5 us
    pallas_call x1, Pallas kernels, update_table(): pl.pallas_call(update_table_kernel, name='update_table', grid=(pl.cdiv(ro...  21.1 us
    dot_general x4, matrix products, dot_nt(): lax.dot_general(a, b, (((1,), (1,)), ((), ())), precision=precision, pref...  18.8 us
  transfers between devices with their start and end apart: 6, of which 2 were waited for; matrix products, arithmetic and copies ran while one was open for 5% of the time, Pallas kernels for 53%

profile of v6, /device:TPU:12, one launch (start us, length us, event | category | flops | bytes accessed | tf_op | source)
XLA Modules:
  0.0 871.7 jit_solution(16991431906335121891)
XLA Ops:
  9.4 6.0 shard_map.286
  16.3 6.2 sort.15
  23.7 12.5 %shard_map.287 = (bf16[8192,256]{1,0:T(8,128)(2,1)}, bf16[5006,256]{1,0:T(8,128)(2,1)}, f32[8,256]{1,0:T(8,128)}) custom-call(s32[1]{0:T(128)} %bitcast.1.count_ref, s32[8192]{0:T(1024)} %get-tuple-element.174.row_ref, s32[8192]{0:T(1024)} %get-tuple-element.173.tok_ref, f32[6286,256]{1,0:T(8,128)} %w_ref.1), custom_call_target="tpu_custom_call" | custom-call | flops 6502404 | bytes 13004808 | tf_op jit(solution)/shard_map/pallas_call | solution.py:66
  36.3 2.3 slice.144
  40.4 135.9 %shard_map.289 = (bf16[4,4,2,32,4384]{4,3,2,1,0:T(8,128)(2,1)}, bf16[4,4,2,64,1024]{4,3,2,1,0:T(8,128)(2,1)}, bf16[4,4,2,32,4384]{4,3,2,1,0:T(8,128)(2,1)}, bf16[4,4,2,64,1024]{4,3,2,1,0:T(8,128)(2,1)}) custom-call(bf16[32,4384]{1,0:T(8,128)(2,1)} %get-tuple-element.88.refs_0_, bf16[64,1024]{1,0:T(8,128)(2,1)} %get-tuple-element.89.refs_1_, ...), custom_call_target="tpu_custom_call" | custom-call | flops 19759104 | bytes 39518208 | tf_op jit(solution)/shard_map/pallas_call | solution.py:193
  181.9 13.7 %shard_map.288 = f32[256,1024]{1,0:T(8,128)} custom-call(bf16[4,256,256]{2,1,0:T(8,128)(2,1)} %bitcast.87), custom_call_target="tpu_custom_call" | custom-call | flops 524288 | bytes 1048576 | tf_op jit(solution)/shard_map/pallas_call | solution.py:193
  198.4 8.0 fusion.7.proj_ref
  206.4 27.5 %shard_map.290 = (f32[256,2304]{1,0:T(8,128)}, f32[256,2048]{1,0:T(8,128)}, bf16[256,2048]{1,0:T(8,128)(2,1)}, f32[256,128]{1,0:T(8,128)}, f32[256,128]{1,0:T(8,...) custom-call(s32[1]{0:T(128)} %constant.64.clone.1.layer_ref, f32[256,4384]{1,0:T(8,128)} %fusion.7.proj_ref, ...), custom_call_target="tpu_custom_call" | custom-call | flops 524288 | bytes 1048576 | tf_op jit(solution)/shard_map/pallas_call | solution.py:193
  233.9 4.1 multiply_reduce_fusion.8
  239.1 8.1 fusion.8.proj_ref
  247.2 26.4 %shard_map.291 = (f32[256,2304]{1,0:T(8,128)}, f32[256,2048]{1,0:T(8,128)}, bf16[256,2048]{1,0:T(8,128)(2,1)}, f32[256,128]{1,0:T(8,128)}, f32[256,128]{1,0:T(8,...) custom-call(s32[1]{0:T(128)} %constant.72.clone.1.layer_ref, f32[256,4384]{1,0:T(8,128)} %fusion.8.proj_ref, ...), custom_call_target="tpu_custom_call" | custom-call | flops 524288 | bytes 1048576 | tf_op jit(solution)/shard_map/pallas_call | solution.py:193
  273.7 4.1 multiply_reduce_fusion.7
  279.8 3.8 all-gather.7.cloned.1.call-done.table_ref.e_ref
  283.6 64.7 %shard_map.292 = (bf16[6400,2048]{1,0:T(8,128)(2,1)}, bf16[8,256,1024]{2,1,0:T(8,128)(2,1)}, f32[1,2048]{1,0:T(1,128)}, f32[5,1,2048]{2,1,0:T(1,128)}, f32[1,2048]{1,0:T(1,128)}) custom-call(bf16[1280,1024]{1,0:T(8,128)(2,1)} %all-gather.5.cloned.1.call-done.lead_ref, bf16[5006,1024]{1,0:T(8,128)(2,1)} %all-gather.7.cloned.1.call-done.table_ref.e_ref, ...), custom_call_target="tpu_custom_call" | custom-call | flops 3670016 | bytes 7340032 | tf_op jit(solution)/shard_map/pallas_call | solution.py:193
  348.3 39.6 %shard_map.293 = bf16[2048,1024]{1,0:T(8,128)(2,1)} custom-call(bf16[1280,1024]{1,0:T(8,128)(2,1)} %all-gather.5.cloned.1.call-done.lead_ref, bf16[5006,1024]{1,0:T(8,128)(2,1)} %all-gather.7.cloned.1.call-done.table_ref.e_ref, bf16[6400,2048]{1,0:T(8,128)(2,1)} %get-tuple-element.100.q_ref, f32[5,1,2048]{2,1,0:T(1,128)} %get-tuple-element.101.fac_ref, ...), custom_call_target="tpu_custom_call" | custom-call | flops 26365394944 | bytes 51494912 | tf_op jit(solution)/shard_map/pallas_call | solution.py:1231
  387.9 34.2 %shard_map.294 = bf16[6286,1024]{1,0:T(8,128)(2,1)} custom-call(bf16[2048,1024]{1,0:T(8,128)(2,1)} %bitcast.114, bf16[6400,2048]{1,0:T(8,128)(2,1)} %get-tuple-element.100.q_ref, f32[5,1,2048]{2,1,0:T(1,128)} %get-tuple-element.101.fac_ref, f32[1,2048]{1,0:T(1,128)} %broadcast_select_fusion.2.w_ref, s32[1,2048]{1,0:T(1,128)} %sub.62.lab_ref), custom_call_target="tpu_custom_call" | custom-call | flops 26365394944 | bytes 51494912 | tf_op jit(solution)/shard_map/pallas_call | solution.py:1231
  422.1 14.0 %reduce-scatter.6.cloned.1.call-done = bf16[256,1024]{1,0:T(8,128)(2,1)} async-done(((bf16[2048,1024]{1,0:T(8,128)(2,1)}), bf16[256,1024]{1,0:T(8,128)(2,1)}) %reduce-scatter.6.cloned.1.call-update) | async-done | bytes 524304 | tf_op jit(solution)/shard_map/reduce_scatter | solution.py:1830
  440.6 2.6 fusion.9.dyn_ref
  443.2 42.3 %shard_map.295 = (bf16[256,4384]{1,0:T(8,128)(2,1)}, f32[8,2304]{1,0:T(8,128)}, f32[8,128]{1,0:T(8,128)}, f32[1,2048]{1,0:T(1,128)}) custom-call(s32[1]{0:T(128)} %constant.72.clone.1.layer_ref, f32[256,2048]{1,0:T(8,128)} %fusion.9.dyn_ref, f32[256,2048]{1,0:T(8,128)} %get-tuple-element.104.y_ref, f32[256,4384]{1,0:T(8,128)} %fusion.8.proj_ref, ...), custom_call_target="tpu_custom_call" | custom-call | flops 524288 | bytes 1048576 | tf_op jit(solution)/shard_map/pallas_call | solution.py:193
  485.5 7.4 multiply_reduce_fusion.3
  495.7 2.6 fusion.10.dyn_ref
  498.3 38.0 %shard_map.296 = (bf16[256,4384]{1,0:T(8,128)(2,1)}, f32[8,2304]{1,0:T(8,128)}, f32[8,128]{1,0:T(8,128)}, f32[1,2048]{1,0:T(1,128)}) custom-call(s32[1]{0:T(128)} %constant.64.clone.1.layer_ref, f32[256,2048]{1,0:T(8,128)} %fusion.10.dyn_ref, f32[256,2048]{1,0:T(8,128)} %get-tuple-element.111.y_ref, f32[256,4384]{1,0:T(8,128)} %fusion.7.proj_ref, ...), custom_call_target="tpu_custom_call" | custom-call | flops 524288 | bytes 1048576 | tf_op jit(solution)/shard_map/pallas_call | solution.py:193
  536.4 6.2 multiply_reduce_fusion
  543.8 9.5 %shard_map.297 = bf16[4,256,256]{2,1,0:T(8,128)(2,1)} custom-call(f32[256,1024]{1,0:T(8,128)} %multiply_add_fusion.in_ref), custom_call_target="tpu_custom_call" | custom-call | flops 524288 | bytes 1048576 | tf_op jit(solution)/shard_map/pallas_call | solution.py:193
  554.9 10.1 %shard_map.298 = (bf16[1024,4384]{1,0:T(8,128)(2,1)}, bf16[2048,1024]{1,0:T(8,128)(2,1)}) custom-call(bf16[256,1024]{1,0:T(8,128)(2,1)} %copy-done.10, bf16[256,4384]{1,0:T(8,128)(2,1)} %get-tuple-element.119.dp_ref, bf16[256,2048]{1,0:T(8,128)(2,1)} %get-tuple-element.93.yn_ref, bf16[256,1024]{1,0:T(8,128)(2,1)} %copy-done.13), custom_call_target="tpu_custom_call" | custom-call | flops 3372220416 | bytes 6586368 | tf_op jit(solution)/shard_map/pallas_call | solution.py:1231
  565.1 10.6 %shard_map.299 = (bf16[1024,4384]{1,0:T(8,128)(2,1)}, bf16[2048,1024]{1,0:T(8,128)(2,1)}) custom-call(bf16[256,1024]{1,0:T(8,128)(2,1)} %copy-done.11, bf16[256,4384]{1,0:T(8,128)(2,1)} %get-tuple-element.110.dp_ref, bf16[256,2048]{1,0:T(8,128)(2,1)} %get-tuple-element.96.yn_ref, bf16[256,1024]{1,0:T(8,128)(2,1)} %copy-done.14), custom_call_target="tpu_custom_call" | custom-call | flops 3372220416 | bytes 6586368 | tf_op jit(solution)/shard_map/pallas_call | solution.py:1231
  575.7 205.3 %shard_map.300 = (f32[32,4384]{1,0:T(8,128)}, f32[64,1024]{1,0:T(8,128)}, f32[32,4384]{1,0:T(8,128)}, f32[64,1024]{1,0:T(8,128)}) custom-call(bf16[4,4,2,32,4384]{4,3,2,1,0:T(8,128)(2,1)} %bitcast.82, bf16[4,4,2,64,1024]{4,3,2,1,0:T(8,128)(2,1)} %bitcast.84, bf16[4,4,2,32,4384]{4,3,2,1,0:T(8,128)(2,1)} %bitcast.83, bf16[4,4,2,64,1024]{4,3,2,1,0:T(8,128)(2,1)} %bitcast.85), custom_call_target="tpu_custom_call" | custom-call | flops 26345472 | bytes 52690944 | tf_op jit(solution)/shard_map/pallas_call | solution.py:193
  785.6 13.8 %shard_map.301 = (f32[6286,256]{1,0:T(8,128)}, f32[8,256]{1,0:T(8,128)}) custom-call(s32[1]{0:T(128)} %bitcast.1.count_ref, s32[8192]{0:T(1024)} %get-tuple-element.174.row_ref, s32[8192]{0:T(1024)} %get-tuple-element.173.tok_ref, bf16[8192,256]{1,0:T(8,128)(2,1)} %bitcast.86, bf16[6286,256]{1,0:T(8,128)(2,1)} %reduce-scatter.8.cloned.1.call-done.base_ref), custom_call_target="tpu_custom_call" | custom-call | flops 7478276 | bytes 14956552 | tf_op jit(solution)/shard_map/pallas_call | solution.py:66
  805.4 22.0 %shard_map.302 = (f32[256,128]{1,0:T(8,128)}, f32[8,128]{1,0:T(8,128)}) custom-call(f32[256,128]{1,0:T(8,128)} %bitcast.88), custom_call_target="tpu_custom_call" | custom-call | flops 393216 | bytes 786432 | tf_op jit(solution)/shard_map/pallas_call | solution.py:193
  832.8 2.2 fusion.3
  835.7 21.1 %update_table.1 = (f32[6286,256]{1,0:T(8,128)}, f32[6286,256]{1,0:T(8,128)}, f32[6286,256]{1,0:T(8,128)}, bf16[6286,256]{1,0:T(8,128)(2,1)}) custom-call(f32[8,128]{1,0:T(8,128)} %get-tuple-element.138.norm_ref, f32[6286,256]{1,0:T(8,128)} %w_ref.1, f32[6286,256]{1,0:T(8,128)} %m_ref.1, f32[6286,256]{1,0:T(8,128)} %a_ref.1, f32[6286,256]{1,0:T(8,128)} %get-tuple-element.139.g_ref), custom_call_target="tpu_custom_call" | custom-call | flops 12873728 | bytes 48276480 | tf_op jit(solution)/shard_map/update_table/pallas_call | solution.py:422
  856.8 6.2 shard_map.303
  (144 shorter events, 37.8 us)
Async XLA Ops:
  8.0 173.8 %reduce-scatter.4.cloned.1.call-start = ((), (), s32[]{:S(2)}) async-start(), calls=%async_computation.3 | async-start | bytes 4718592 | tf_op jit(solution)/shard_map/reduce_scatter | solution.py:1781
  36.2 2.5 copy-start.6
  36.2 2.6 copy-start.12
  36.2 243.6 %all-gather.5.cloned.1.call-start = ((), (), s32[]{:S(2)}) async-start(), calls=%async_computation.4 | async-start | bytes 3276800 | tf_op jit(solution)/shard_map/all_gather | solution.py:1760
  38.6 137.8 %slice-start = ((f32[30400]{0:T(1024)}), f32[29376]{0:T(1024)S(1)}, s32[]{:S(2)}) async-start(f32[30400]{0:T(1024)} %param.27), calls=%async_computation.9 | async-start | bytes 237568 | tf_op jit(solution)/shard_map/slice | solution.py:1612
  38.6 138.1 %copy-start.15 = (f32[30400]{0:T(1024)S(1)}, f32[30400]{0:T(1024)}, u32[]{:S(2)}) copy-start(f32[30400]{0:T(1024)} %param.27) | copy-start | bytes 364804
  38.6 139.6 %copy-start.27 = (s32[2,4]{1,0:T(2,128)S(1)}, s32[2,4]{1,0:T(2,128)}, u32[]{:S(2)}) copy-start(s32[2,4]{1,0:T(2,128)} %param.17) | copy-start | bytes 100
  38.6 140.5 %copy-start.24 = (s32[2,1,1024]{2,1,0:T(1,128)S(1)}, s32[2,1,1024]{2,1,0:T(1,128)}, u32[]{:S(2)}) copy-start(s32[2,1,1024]{2,1,0:T(1,128)} %param.16) | copy-start | bytes 24580
  38.7 244.9 %all-gather.7.cloned.1.call-start = ((), (), s32[]{:S(2)}) async-start(), calls=%async_computation.5 | async-start | bytes 12820480 | tf_op jit(solution)/shard_map/all_gather | solution.py:1799
  176.4 259.7 %reduce-scatter.6.cloned.1.call-start = ((), (), s32[]{:S(2)}) async-start(), calls=%async_computation.6 | async-start | bytes 4718592 | tf_op jit(solution)/shard_map/reduce_scatter | solution.py:1830
  198.4 8.0 copy-start.10
  206.4 27.5 %copy-start = (f32[256,1024]{1,0:T(8,128)S(1)}, f32[256,1024]{1,0:T(8,128)}, u32[]{:S(2)}) copy-start(f32[256,1024]{1,0:T(8,128)} %shard_map.288) | copy-start | bytes 3145732
  238.0 1.0 copy-start.8
  239.1 8.1 copy-start.11
  387.9 397.7 %all-gather.9.cloned.1.call-start = ((), (), s32[]{:S(2)}) async-start(), calls=%async_computation.8 | async-start | bytes 4718592 | tf_op jit(solution)/shard_map/all_gather | solution.py:1852
  422.1 17.4 %copy-start.4 = (f32[256,1024]{1,0:T(8,128)S(1)}, f32[256,1024]{1,0:T(8,128)}, u32[]{:S(2)}) copy-start(f32[256,1024]{1,0:T(8,128)} %copy-done.3) | copy-start | bytes 3145732
  436.1 4.5 copy-start.29
  437.4 2.1 copy-start.1
  485.5 7.5 copy-start.2
  485.5 7.5 copy-start.5
  485.5 7.5 copy-start.9
  493.0 2.8 copy-start.28
  494.5 41.9 %copy-start.13 = (bf16[256,1024]{1,0:T(8,128)(2,1)}, bf16[256,1024]{1,0:T(8,128)(2,1)S(1)}, u32[]{:S(2)}) copy-start(bf16[256,1024]{1,0:T(8,128)(2,1)S(1)} %get-tuple-element.165.db_ref) | copy-start | bytes 1572868
  536.3 6.2 copy-start.7
  553.4 1.5 copy-start.20
  553.4 1.5 copy-start.19
  553.4 232.2 %reduce-scatter.8.cloned.1.call-start = ((), (), s32[]{:S(2)}) async-start(), calls=%async_computation.7 | async-start | bytes 16097280 | tf_op jit(solution)/shard_map/reduce_scatter | solution.py:1834
  782.7 21.3 %copy-start.21 = (f32[1,2048]{1,0:T(1,128)S(1)}, f32[1,2048]{1,0:T(1,128)}, u32[]{:S(2)}) copy-start(f32[1,2048]{1,0:T(1,128)} %get-tuple-element.123) | copy-start | bytes 24580
  782.7 21.3 %copy-start.22 = (f32[1,2048]{1,0:T(1,128)S(1)}, f32[1,2048]{1,0:T(1,128)}, u32[]{:S(2)}) copy-start(f32[1,2048]{1,0:T(1,128)} %get-tuple-element.120) | copy-start | bytes 24580
  784.8 48.0 %copy-start.17 = (f32[30400]{0:T(1024)S(1)}, f32[30400]{0:T(1024)}, u32[]{:S(2)}) copy-start(f32[30400]{0:T(1024)} %param.28) | copy-start | bytes 364804
  785.6 49.5 %copy-start.18 = (f32[30400]{0:T(1024)S(1)}, f32[30400]{0:T(1024)}, u32[]{:S(2)}) copy-start(f32[30400]{0:T(1024)} %param.29) | copy-start | bytes 364804
  835.0 21.8 %copy-start.16 = (f32[30400]{0:T(1024)}, f32[30400]{0:T(1024)S(1)}, u32[]{:S(2)}) copy-start(f32[30400]{0:T(1024)S(1)} %get-tuple-element.159) | copy-start | bytes 364804
  (5 other events, 4.1 us)
Sparse Core Ops, SparseCore 0:
  36.3 83.5 reduce-scatter.3
  388.0 48.0 reduce-scatter.5
  553.5 48.2 all-gather.8
Sparse Core Ops, SparseCore 1:
  39.1 62.9 all-gather.4
  176.5 107.1 all-gather.6
  557.0 215.4 reduce-scatter.7

commit v7 on v6

--- a/solution.py
+++ b/solution.py
@@ -330,9 +330,6 @@
 
 def bits_of(size):
     return [1 << b for b in range(size.bit_length() - 1)]
-
-
-TCHUNK = 512
 
 
 def stepped(weight, moment, average, grad, factor):
@@ -408,29 +405,6 @@
         (pltpu.VMEM, pltpu.VMEM),
         packed.size * 4 * 3,
     )
-
-
-def update_table_kernel(norm_ref, w_ref, m_ref, a_ref, g_ref, *outs):
-    new = stepped(w_ref[...], m_ref[...], a_ref[...], g_ref[...], norm_ref[1:2, 0:1])
-    for out, value in zip(outs, new + (new[0].astype(bf16),)):
-        out[...] = value
-
-
-def update_table(norms, weight, moment, average, grad):
-    rows, cols = weight.shape
-    block = pl.BlockSpec((TCHUNK, cols), lambda i: (i, 0))
-    return pl.pallas_call(
-        update_table_kernel,
-        name="update_table",
-        grid=(pl.cdiv(rows, TCHUNK),),
-        in_specs=[pl.BlockSpec((8, LANES), lambda i: (0, 0))] + [block] * 4,
-        out_specs=[block] * 4,
-        out_shape=[jax.ShapeDtypeStruct((rows, cols), kind) for kind in (f32, f32, f32, bf16)],
-        compiler_params=pltpu.CompilerParams(vmem_limit_bytes=VMEM_LIMIT),
-        cost_estimate=pl.CostEstimate(
-            flops=8 * weight.size, transcendentals=0, bytes_accessed=30 * weight.size
-        ),
-    )(norms, weight, moment, average, grad)
 
 
 def update_projections_kernel(norm_ref, *refs):
@@ -687,11 +661,15 @@
     up, down = me + MB, me - MB
     has_up, has_down = k < count - 1, k > 0
 
-    def load(a):
-        return pltpu.make_async_copy(grads[a].at[:, :, core], held[a], load_sem.at[a])
-
-    for a in range(arrays):
-        load(a).start()
+    def load(a, d):
+        return pltpu.make_async_copy(grads[a].at[d, :, core], held[a].at[d], load_sem.at[a, d])
+
+    for j in range(reach, -1, -1):
+        for d in {reach: [(0, j)], 0: [(0, 0)]}.get(j, [(0, j), (1, j)]):
+            side, step = d
+            d = snake(wrap(ring + step if side == 0 else ring - step, size), size)
+            for a in range(arrays):
+                load(a, d).start()
     barrier = pltpu.get_barrier_semaphore()
     for target in ((right, me), (left, me), (dp, mate)):
         pl.semaphore_signal(barrier, inc=1, device_id=target, device_id_type=MESH)
@@ -724,16 +702,14 @@
             return [away(j, 0)]
         return [away(j, 0), away(j, 1)]
 
-    for j in range(reach, -1, -1):
+    def send_mate(j):
         for d in targets(j):
             for a in range(arrays):
                 to_mate(a, d).start()
 
-    for a in range(arrays):
-        load(a).wait()
-
     def add_mate(d):
         for a in range(arrays):
+            load(a, d).wait()
             to_mate(a, d).wait_recv()
 
             def one(z, _, a=a):
@@ -766,9 +742,12 @@
         paired = k + (1 - 2 * (j % 2)) * (near_most - j // 2)
         return jnp.where(i < uneven, k + long_side * (far_most - i), paired)
 
+    send_mate(reach)
     add_mate(away(reach, 0))
     for a in range(arrays):
         first_step(a, 0 if carried(a, 0) else 1).start()
+    for j in range(reach - 1, -1, -1):
+        send_mate(j)
     for s in range(1, reach):
         for side in (0, 1):
             add_mate(away(reach - s, side))
@@ -862,7 +841,7 @@
         + tuple(pltpu.VMEM((2, reach, count) + s, bf16) for s in shards)
         + tuple(pltpu.VMEM((2, count) + s, bf16) for s in shards)
         + (
-            pltpu.SemaphoreType.DMA((arrays,)),
+            pltpu.SemaphoreType.DMA((arrays, size)),
             pltpu.SemaphoreType.DMA((arrays,)),
             pltpu.SemaphoreType.DMA((arrays, size)),
             pltpu.SemaphoreType.DMA((arrays, 2)),
@@ -1250,7 +1229,7 @@
 def head_stats_kernel(
     lead_ref, table_ref, own_ref, lab_ref, w_ref,
     q_ref, all_ref, lse_ref, fac_ref, hit_ref,
-    kept, tops, sums, hits, shown, own_sem, put_sem, z_send, z_recv, m_send, m_recv, s_send, s_recv,
+    lead_v, table_v, kept, tops, sums, hits, shown, load_sem, own_sem, put_sem, z_send, z_recv, m_send, m_recv, s_send, s_recv,
 ):
     dp = lax.axis_index("dp")
     me = lax.axis_index("fsdp")
@@ -1262,6 +1241,16 @@
     vocab_rows = lead_ref.shape[0] + table_ref.shape[0]
     rows = own_ref.shape[0]
     tiles = tops.shape[0]
+
+    def load(t):
+        if t == 0:
+            return pltpu.make_async_copy(lead_ref, lead_v, load_sem.at[0])
+        first = (t - 1) * VTILE
+        at = pl.ds(first, min(VTILE, table_ref.shape[0] - first))
+        return pltpu.make_async_copy(table_ref.at[at], table_v.at[at], load_sem.at[t])
+
+    for t in range(tiles):
+        load(t).start()
     barrier = pltpu.get_barrier_semaphore()
     for other in range(1, shards):
         pl.semaphore_signal(
@@ -1326,7 +1315,12 @@
         for t in range(tiles):
             first = t * VTILE
             size = min(VTILE, vocab_rows - first)
-            part = lead_ref[...] if t == 0 else table_ref[first - VTILE : first - VTILE + size, :]
+
+            @pl.when(step == 0)
+            def _(t=t):
+                load(t).wait()
+
+            part = lead_v[...] if t == 0 else table_v[first - VTILE : first - VTILE + size, :]
             logits = dot_nt(part, h)
             top = jnp.max(logits, axis=0, keepdims=True)
             p = jnp.exp(logits - top)
@@ -1443,11 +1437,14 @@
             ((1, tokens), f32),
         ),
         (
+            pltpu.VMEM(lead.shape, bf16),
+            pltpu.VMEM(table.shape, bf16),
             pltpu.VMEM((2, tiles * VTILE, rows), bf16),
             pltpu.VMEM((tiles, 1, tokens), f32),
             pltpu.VMEM((tiles, 1, tokens), f32),
             pltpu.VMEM((tiles, 1, tokens), f32),
             pltpu.VMEM((shards, 2, tokens), f32),
+            pltpu.SemaphoreType.DMA((tiles,)),
             pltpu.SemaphoreType.DMA,
             pltpu.SemaphoreType.DMA((2,)),
             pltpu.SemaphoreType.DMA((2, count)),
@@ -1457,7 +1454,7 @@
             pltpu.SemaphoreType.DMA((shards,)),
             pltpu.SemaphoreType.DMA((shards,)),
         ),
-        (pltpu.VMEM,) * 5,
+        (pl.ANY, pl.ANY) + (pltpu.VMEM,) * 3,
         (pl.ANY, pltpu.VMEM, pltpu.VMEM, pltpu.VMEM, pltpu.VMEM),
         own.size * 2 * 7,
     )
@@ -1503,16 +1500,19 @@
         lax.fori_loop(0, tokens // NTILE, put, 0)
 
 
-def head_rows(lead, table, kept, fac, weight, labels):
-    vocab_rows, width = lead.shape[0] + table.shape[0], table.shape[1]
+ROW_PARTS = 2
+
+
+def head_rows(lead, table, kept, fac, weight, labels, part):
+    vocab_rows, width = lead.shape[0] + table.shape[0], table.shape[1] // ROW_PARTS
     tokens = kept.shape[1]
     sp = head_specs(width, tokens)
     return head_call(
         functools.partial(head_rows_kernel, vocab_rows),
         pl.cdiv(vocab_rows, VTILE),
         [
-            pl.BlockSpec((VTILE, width), lambda i: (0, 0)),
-            pl.BlockSpec((VTILE, width), lambda i: (jnp.maximum(i - 1, 0), 0)),
+            pl.BlockSpec((VTILE, width), lambda i: (0, part)),
+            pl.BlockSpec((VTILE, width), lambda i: (jnp.maximum(i - 1, 0), part)),
             sp["kept"],
             sp["tile_row"],
             sp["row"],
@@ -1573,18 +1573,18 @@
 
 def weight_grads(normed, grad_proj, mixed, grad_branch):
     rows = normed.shape[0]
-    steps = D // LANES
+    steps = D // 256
     part = DI // steps
     return head_call(
         weight_grads_kernel,
         steps,
         [
-            pl.BlockSpec((rows, LANES), lambda i: (0, i)),
+            pl.BlockSpec((rows, 256), lambda i: (0, i)),
             pl.BlockSpec((rows, ZW), lambda i: (0, 0)),
             pl.BlockSpec((rows, part), lambda i: (0, i)),
             pl.BlockSpec((rows, D), lambda i: (0, 0)),
         ],
-        [pl.BlockSpec((LANES, ZW), lambda i: (i, 0)), pl.BlockSpec((part, D), lambda i: (i, 0))],
+        [pl.BlockSpec((256, ZW), lambda i: (i, 0)), pl.BlockSpec((part, D), lambda i: (i, 0))],
         [((D, ZW), bf16), ((DI, D), bf16)],
         (),
         (normed, grad_proj, mixed, grad_branch),
@@ -1826,11 +1826,16 @@
         jnp.arange(groups)[:, None] == group_index, jnp.sum(own_sums, axis=0), column_sum
     ).reshape(D)
 
-    rows_grad = head_rows(lead, table, kept, fac, weight, local_labels)
-    own_grad = lax.psum_scatter(
-        rows_grad, "fsdp", scatter_dimension=0, tiled=True
-    ).astype(f32)
-    table_grad = head_table(group_hidden, kept, fac, weight, local_labels, vocab_rows)
+    own_grad = []
+    ready = kept
+    for part in range(ROW_PARTS):
+        part_grad = head_rows(lead, table, ready, fac, weight, local_labels, part)
+        ready = after(kept, part_grad)
+        own_grad.append(
+            lax.psum_scatter(part_grad, "fsdp", scatter_dimension=0, tiled=True)
+        )
+    own_grad = jnp.concatenate(own_grad, axis=1).astype(f32)
+    table_grad = head_table(group_hidden, ready, fac, weight, local_labels, vocab_rows)
     table_part = lax.psum_scatter(table_grad, "dp", scatter_dimension=1, tiled=True)
 
     grad_hidden, dfinal = norm_back(after(own_grad, table_grad), hidden, final_gain)
@@ -1841,19 +1846,19 @@
         grad_hidden, grad_in, grad_out, vec_parts[l] = layer_backward(
             grad_hidden, w_in[l], w_out[l], vecs, l, records[l]
         )
-        if l == 0:
-            sent = group_call(
-                to_columns_kernel,
-                9,
-                grad_hidden,
-                ((groups, rows, own_cols), bf16),
-                (pltpu.VMEM((groups, rows, own_cols), bf16),),
-            )
-            spread = lax.all_gather(sent, "fsdp", axis=0).reshape(every, own_cols)
         in_parts[l], out_parts[l] = grad_in, grad_out
     whole = []
     for l in range(LAYERS):
         whole += [in_parts[l], out_parts[l]]
+    sent = group_call(
+        to_columns_kernel,
+        9,
+        after(grad_hidden, whole),
+        ((groups, rows, own_cols), bf16),
+        (pltpu.VMEM((groups, rows, own_cols), bf16),),
+    )
+    whole = after(whole, sent)
+    spread = lax.all_gather(sent, "fsdp", axis=0).reshape(every, own_cols)
     summed_parts = reduce_layers(whole)
     spread = after(spread, summed_parts)
     table_total, table_squares = local_call(
@@ -1881,7 +1886,11 @@
         ]
     )
     packed, norms = total_of(packed.reshape(-1, LANES), small, used - 2)
-    updated = list(update_table(norms, embedding, embedding_mom, embedding_avg, table_total))
+    factor = norms[1, 0]
+    table_new, table_mom, table_avg = stepped(
+        embedding, embedding_mom, embedding_avg, table_total, factor
+    )
+    updated = [table_new, table_mom, table_avg, table_new.astype(bf16)]
     updated += update_projections(
         norms,
         (in_proj, in_proj_mom, in_proj_avg, out_proj, out_proj_mom, out_proj_avg),
@@ -1894,7 +1903,7 @@
     mean_part = jnp.sum(hidden_total * column_total) * (0.1 / VOCAB)
     loss_value = (packed[used - 1] - mean_part) / total_count
     vector_new, vector_mom_new, vector_avg_new = stepped(
-        vector_params, vector_mom, vector_avg, vector_total, norms[1, 0]
+        vector_params, vector_mom, vector_avg, vector_total, factor
     )
     return (
         loss_value,

time: 884 us -> 952 us (1.077)
  waiting for transfers between devices: 18.4 us -> 42.6 us
  other arithmetic: 30.2 us -> 51.4 us
  Pallas kernels: 740 us -> 759 us
    pallas_call x11, Pallas kernels: 591 us -> 628 us  [comm_call(): pl.pallas_call(kernel, out_shape=[jax.ShapeDtypeStruct(shape, kind) for s...]
    reduce_scatter x1 -> x2, waiting for transfers between devices: 14 us -> 37.4 us  [whole_step(): lax.psum_scatter(part_grad, 'fsdp', scatter_dimension=0, tiled=True)]
    pallas_call x1 -> x0, Pallas kernels: 21.1 us -> none  [update_table(): pl.pallas_call(update_table_kernel, name='update_table', grid=(pl.cdiv(ro...]
    convert_element_type x1 -> x2, other arithmetic: 1.3 us -> 13.3 us  [the longest x1 12 us: whole_step(): updated = [table_new, table_mom, table_avg, table_new.astype(bf16)]]
    pallas_call x4 -> x5, Pallas kernels: 94.5 us -> 98.4 us  [head_call(): pl.pallas_call(kernel, grid=(grid,), in_specs=in_specs, out_specs=out_spe...]
  transfers between devices with their start and end apart: 6 -> 7, of which waited for: 2 -> 2; matrix products, arithmetic and copies ran while one was open for 5% -> 4% of each run, Pallas kernels for 53% -> 49%
where the time goes in v7:
time: 952 us; the launch traced here: 942 us
  Pallas kernels  759 us (80%)
  other arithmetic  51.4 us (5%)
  matrix products  44.9 us (5%)
  waiting for transfers between devices  42.6 us (4%)
  between operations  22.8 us (2%)
  local copies, waits for them, and re-layouts  20.2 us (2%)
    pallas_call x11, Pallas kernels, comm_call(): pl.pallas_call(kernel, out_shape=[jax.ShapeDtypeStruct(shape, kind) for s...  628 us
    pallas_call x5, Pallas kernels, head_call(): pl.pallas_call(kernel, grid=(grid,), in_specs=in_specs, out_specs=out_spe...  98.4 us
    reduce_scatter x2, waiting for transfers between devices, whole_step(): lax.psum_scatter(part_grad, 'fsdp', scatter_dimension=0, tiled=True)  37.4 us
    pallas_call x3, Pallas kernels, local_call(): pl.pallas_call(kernel, out_shape=[jax.ShapeDtypeStruct(shape, kind) for s...  32.8 us
    dot_general x4, matrix products, dot_nt(): lax.dot_general(a, b, (((1,), (1,)), ((), ())), precision=precision, pref...  20.7 us
  transfers between devices with their start and end apart: 7, of which 2 were waited for; matrix products, arithmetic and copies ran while one was open for 4% of the time, Pallas kernels for 49%

profile of v7, /device:TPU:12, one launch (start us, length us, event | category | flops | bytes accessed | tf_op | source)
XLA Modules:
  0.0 941.5 jit_solution(7044439417236388983)
XLA Ops:
  9.4 6.0 shard_map.286
  16.3 6.2 sort.15
  23.7 12.5 %shard_map.287 = (bf16[8192,256]{1,0:T(8,128)(2,1)}, bf16[5006,256]{1,0:T(8,128)(2,1)}, f32[8,256]{1,0:T(8,128)}) custom-call(s32[1]{0:T(128)} %bitcast.1.count_ref, s32[8192]{0:T(1024)} %get-tuple-element.183.row_ref, s32[8192]{0:T(1024)} %get-tuple-element.182.tok_ref, f32[6286,256]{1,0:T(8,128)} %table_ref.1), custom_call_target="tpu_custom_call" | custom-call | flops 6502404 | bytes 13004808 | tf_op jit(solution)/shard_map/pallas_call | solution.py:66
  40.4 135.9 %shard_map.289 = (bf16[4,4,2,32,4384]{4,3,2,1,0:T(8,128)(2,1)}, bf16[4,4,2,64,1024]{4,3,2,1,0:T(8,128)(2,1)}, bf16[4,4,2,32,4384]{4,3,2,1,0:T(8,128)(2,1)}, bf16[4,4,2,64,1024]{4,3,2,1,0:T(8,128)(2,1)}) custom-call(bf16[32,4384]{1,0:T(8,128)(2,1)} %get-tuple-element.91.refs_0_, bf16[64,1024]{1,0:T(8,128)(2,1)} %get-tuple-element.92.refs_1_, ...), custom_call_target="tpu_custom_call" | custom-call | flops 19759104 | bytes 39518208 | tf_op jit(solution)/shard_map/pallas_call | solution.py:193
  181.9 13.7 %shard_map.288 = f32[256,1024]{1,0:T(8,128)} custom-call(bf16[4,256,256]{2,1,0:T(8,128)(2,1)} %bitcast.87), custom_call_target="tpu_custom_call" | custom-call | flops 524288 | bytes 1048576 | tf_op jit(solution)/shard_map/pallas_call | solution.py:193
  198.4 8.0 fusion.8.proj_ref
  206.4 27.6 %shard_map.290 = (f32[256,2304]{1,0:T(8,128)}, f32[256,2048]{1,0:T(8,128)}, bf16[256,2048]{1,0:T(8,128)(2,1)}, f32[256,128]{1,0:T(8,128)}, f32[256,128]{1,0:T(8,...) custom-call(s32[1]{0:T(128)} %constant.66.clone.1.layer_ref, f32[256,4384]{1,0:T(8,128)} %fusion.8.proj_ref, ...), custom_call_target="tpu_custom_call" | custom-call | flops 524288 | bytes 1048576 | tf_op jit(solution)/shard_map/pallas_call | solution.py:193
  234.0 4.1 multiply_reduce_fusion.8
  239.2 8.1 fusion.9.proj_ref
  247.3 26.3 %shard_map.291 = (f32[256,2304]{1,0:T(8,128)}, f32[256,2048]{1,0:T(8,128)}, bf16[256,2048]{1,0:T(8,128)(2,1)}, f32[256,128]{1,0:T(8,128)}, f32[256,128]{1,0:T(8,...) custom-call(s32[1]{0:T(128)} %constant.74.clone.1.layer_ref, f32[256,4384]{1,0:T(8,128)} %fusion.9.proj_ref, ...), custom_call_target="tpu_custom_call" | custom-call | flops 524288 | bytes 1048576 | tf_op jit(solution)/shard_map/pallas_call | solution.py:193
  273.6 4.1 multiply_reduce_fusion.7
  279.7 3.9 all-gather.7.cloned.1.call-done.table_ref.e_ref
  283.6 86.3 %shard_map.292 = (bf16[6400,2048]{1,0:T(8,128)(2,1)}, bf16[8,256,1024]{2,1,0:T(8,128)(2,1)}, f32[1,2048]{1,0:T(1,128)}, f32[5,1,2048]{2,1,0:T(1,128)}, f32[1,2048]{1,0:T(1,128)}) custom-call(bf16[1280,1024]{1,0:T(8,128)(2,1)} %all-gather.5.cloned.1.call-done.lead_ref, bf16[5006,1024]{1,0:T(8,128)(2,1)} %all-gather.7.cloned.1.call-done.table_ref.e_ref, ...), custom_call_target="tpu_custom_call" | custom-call | flops 3670016 | bytes 7340032 | tf_op jit(solution)/shard_map/pallas_call | solution.py:193
  369.9 23.9 %shard_map.293 = bf16[2048,512]{1,0:T(8,128)(2,1)} custom-call(bf16[1280,1024]{1,0:T(8,128)(2,1)} %all-gather.5.cloned.1.call-done.lead_ref, bf16[5006,1024]{1,0:T(8,128)(2,1)} %all-gather.7.cloned.1.call-done.table_ref.e_ref, bf16[6400,2048]{1,0:T(8,128)(2,1)} %get-tuple-element.107.q_ref, f32[5,1,2048]{2,1,0:T(1,128)} %get-tuple-element.104.fac_ref, ...), custom_call_target="tpu_custom_call" | custom-call | flops 26365394944 | bytes 51494912 | tf_op jit(solution)/shard_map/pallas_call | solution.py:1210
  393.7 23.8 %shard_map.294 = bf16[2048,512]{1,0:T(8,128)(2,1)} custom-call(bf16[1280,1024]{1,0:T(8,128)(2,1)} %all-gather.5.cloned.1.call-done.lead_ref, bf16[5006,1024]{1,0:T(8,128)(2,1)} %all-gather.7.cloned.1.call-done.table_ref.e_ref, bf16[6400,2048]{1,0:T(8,128)(2,1)} %get-tuple-element.107.q_ref, f32[5,1,2048]{2,1,0:T(1,128)} %get-tuple-element.104.fac_ref, ...), custom_call_target="tpu_custom_call" | custom-call | flops 26365394944 | bytes 51494912 | tf_op jit(solution)/shard_map/pallas_call | solution.py:1210
  418.3 34.1 %shard_map.295 = bf16[6286,1024]{1,0:T(8,128)(2,1)} custom-call(bf16[2048,1024]{1,0:T(8,128)(2,1)} %bitcast.114, bf16[6400,2048]{1,0:T(8,128)(2,1)} %get-tuple-element.107.q_ref, f32[5,1,2048]{2,1,0:T(1,128)} %get-tuple-element.104.fac_ref, f32[1,2048]{1,0:T(1,128)} %broadcast_select_fusion.2.w_ref, s32[1,2048]{1,0:T(1,128)} %sub.65.lab_ref), custom_call_target="tpu_custom_call" | custom-call | flops 26365394944 | bytes 51494912 | tf_op jit(solution)/shard_map/pallas_call | solution.py:1210
  452.5 37.4 %reduce-scatter.7.cloned.1.call-done = bf16[256,512]{1,0:T(8,128)(2,1)} async-done(((bf16[2048,512]{1,0:T(8,128)(2,1)}), bf16[256,512]{1,0:T(8,128)(2,1)}) %reduce-scatter.7.cloned.1.call-update) | async-done | bytes 262160 | tf_op jit(solution)/shard_map/reduce_scatter | solution.py:1835
  498.2 41.0 %shard_map.296 = (bf16[256,4384]{1,0:T(8,128)(2,1)}, f32[8,2304]{1,0:T(8,128)}, f32[8,128]{1,0:T(8,128)}, f32[1,2048]{1,0:T(1,128)}) custom-call(s32[1]{0:T(128)} %constant.74.clone.1.layer_ref, f32[256,2048]{1,0:T(8,128)} %fusion.10.dyn_ref, f32[256,2048]{1,0:T(8,128)} %get-tuple-element.109.y_ref, f32[256,4384]{1,0:T(8,128)} %fusion.9.proj_ref, ...), custom_call_target="tpu_custom_call" | custom-call | flops 524288 | bytes 1048576 | tf_op jit(solution)/shard_map/pallas_call | solution.py:193
  539.2 7.4 multiply_reduce_fusion.3
  552.0 37.5 %shard_map.297 = (bf16[256,4384]{1,0:T(8,128)(2,1)}, f32[8,2304]{1,0:T(8,128)}, f32[8,128]{1,0:T(8,128)}, f32[1,2048]{1,0:T(1,128)}) custom-call(s32[1]{0:T(128)} %constant.66.clone.1.layer_ref, f32[256,2048]{1,0:T(8,128)} %fusion.11.dyn_ref, f32[256,2048]{1,0:T(8,128)} %get-tuple-element.116.y_ref, f32[256,4384]{1,0:T(8,128)} %fusion.8.proj_ref, ...), custom_call_target="tpu_custom_call" | custom-call | flops 524288 | bytes 1048576 | tf_op jit(solution)/shard_map/pallas_call | solution.py:193
  589.5 8.0 multiply_reduce_fusion
  597.5 8.3 shard_map.298
  605.8 8.3 shard_map.299
  614.0 2.8 multiply_add_fusion.1.in_ref
  616.8 10.8 %shard_map.300 = bf16[4,256,256]{2,1,0:T(8,128)(2,1)} custom-call(f32[256,1024]{1,0:T(8,128)} %multiply_add_fusion.1.in_ref), custom_call_target="tpu_custom_call" | custom-call | flops 524288 | bytes 1048576 | tf_op jit(solution)/shard_map/pallas_call | solution.py:193
  629.2 220.1 %shard_map.301 = (f32[32,4384]{1,0:T(8,128)}, f32[64,1024]{1,0:T(8,128)}, f32[32,4384]{1,0:T(8,128)}, f32[64,1024]{1,0:T(8,128)}) custom-call(bf16[4,4,2,32,4384]{4,3,2,1,0:T(8,128)(2,1)} %bitcast.82, bf16[4,4,2,64,1024]{4,3,2,1,0:T(8,128)(2,1)} %bitcast.84, bf16[4,4,2,32,4384]{4,3,2,1,0:T(8,128)(2,1)} %bitcast.83, bf16[4,4,2,64,1024]{4,3,2,1,0:T(8,128)(2,1)} %bitcast.85), custom_call_target="tpu_custom_call" | custom-call | flops 26345472 | bytes 52690944 | tf_op jit(solution)/shard_map/pallas_call | solution.py:193
  854.0 14.1 %shard_map.302 = (f32[6286,256]{1,0:T(8,128)}, f32[8,256]{1,0:T(8,128)}) custom-call(s32[1]{0:T(128)} %bitcast.1.count_ref, s32[8192]{0:T(1024)} %get-tuple-element.183.row_ref, s32[8192]{0:T(1024)} %get-tuple-element.182.tok_ref, bf16[8192,256]{1,0:T(8,128)(2,1)} %bitcast.86, bf16[6286,256]{1,0:T(8,128)(2,1)} %reduce-scatter.11.cloned.1.call-done.base_ref), custom_call_target="tpu_custom_call" | custom-call | flops 7478276 | bytes 14956552 | tf_op jit(solution)/shard_map/pallas_call | solution.py:66
  874.0 23.0 %shard_map.303 = (f32[256,128]{1,0:T(8,128)}, f32[8,128]{1,0:T(8,128)}) custom-call(f32[256,128]{1,0:T(8,128)} %bitcast.88), custom_call_target="tpu_custom_call" | custom-call | flops 393216 | bytes 786432 | tf_op jit(solution)/shard_map/pallas_call | solution.py:193
  905.3 12.0 %fusion.4 = (bf16[6286,256]{1,0:T(8,128)(2,1)}, f32[6286,256]{1,0:T(8,128)S(1)}, f32[6286,256]{1,0:T(8,128)}) fusion(f32[6286,256]{1,0:T(8,128)} %table_ref.1, f32[6286,256]{1,0:T(8,128)} %get-tuple-element.149, f32[]{:T(128)} %bitcast.34, f32[6286,256]{1,0:T(8,128)} %param.19), kind=kLoop, calls=%fused_computation.75 | loop fusion | flops 12873728 | bytes 35402756 | tf_op jit(solution)/shard_map/convert_element_type | solution.py:1893
  917.4 2.7 copy-done
  920.1 6.4 add_multiply_fusion
  926.6 6.2 shard_map.304
  (149 shorter events, 48.4 us)
Async XLA Ops:
  8.0 173.9 %reduce-scatter.5.cloned.1.call-start = ((), (), s32[]{:S(2)}) async-start(), calls=%async_computation.4 | async-start | bytes 4718592 | tf_op jit(solution)/shard_map/reduce_scatter | solution.py:1781
  36.2 2.5 copy-start.11
  36.2 2.6 copy-start.6
  36.2 140.2 %copy-start.14 = (f32[30400]{0:T(1024)S(1)}, f32[30400]{0:T(1024)}, u32[]{:S(2)}) copy-start(f32[30400]{0:T(1024)} %param.27) | copy-start | bytes 364804
  36.2 140.3 %slice-start = ((f32[30400]{0:T(1024)}), f32[29376]{0:T(1024)S(1)}, s32[]{:S(2)}) async-start(f32[30400]{0:T(1024)} %param.27), calls=%async_computation.11 | async-start | bytes 237568 | tf_op jit(solution)/shard_map/slice | solution.py:1612
  36.2 243.5 %all-gather.5.cloned.1.call-start = ((), (), s32[]{:S(2)}) async-start(), calls=%async_computation.5 | async-start | bytes 3276800 | tf_op jit(solution)/shard_map/all_gather | solution.py:1760
  38.6 138.1 %copy-start.27 = (s32[2,4]{1,0:T(2,128)S(1)}, s32[2,4]{1,0:T(2,128)}, u32[]{:S(2)}) copy-start(s32[2,4]{1,0:T(2,128)} %param.17) | copy-start | bytes 100
  38.6 139.7 %copy-start.24 = (s32[2,1,1024]{2,1,0:T(1,128)S(1)}, s32[2,1,1024]{2,1,0:T(1,128)}, u32[]{:S(2)}) copy-start(s32[2,1,1024]{2,1,0:T(1,128)} %param.16) | copy-start | bytes 24580
  38.6 244.9 %all-gather.7.cloned.1.call-start = ((), (), s32[]{:S(2)}) async-start(), calls=%async_computation.6 | async-start | bytes 12820480 | tf_op jit(solution)/shard_map/all_gather | solution.py:1799
  176.4 276.1 %reduce-scatter.9.cloned.1.call-start = ((), (), s32[]{:S(2)}) async-start(), calls=%async_computation.8 | async-start | bytes 2359296 | tf_op jit(solution)/shard_map/reduce_scatter | solution.py:1835
  198.4 8.0 copy-start.9
  206.4 27.6 %copy-start.1 = (f32[256,1024]{1,0:T(8,128)S(1)}, f32[256,1024]{1,0:T(8,128)}, u32[]{:S(2)}) copy-start(f32[256,1024]{1,0:T(8,128)} %shard_map.288) | copy-start | bytes 3145732
  239.2 8.1 copy-start.10
  417.6 72.3 %reduce-scatter.7.cloned.1.call-start = ((), (), s32[]{:S(2)}) async-start(), calls=%async_computation.7 | async-start | bytes 2359296 | tf_op jit(solution)/shard_map/reduce_scatter | solution.py:1835
  418.3 435.6 %all-gather.9.cloned.1.call-start = ((), (), s32[]{:S(2)}) async-start(), calls=%async_computation.10 | async-start | bytes 4718592 | tf_op jit(solution)/shard_map/all_gather | solution.py:1861
  489.8 5.7 copy-start.29
  491.2 2.1 copy-start.2
  539.1 7.5 copy-start.3
  539.1 7.5 copy-start.5
  539.2 7.5 copy-start.8
  546.6 2.8 copy-start.28
  548.1 41.4 %copy-start.12 = (bf16[256,1024]{1,0:T(8,128)(2,1)}, bf16[256,1024]{1,0:T(8,128)(2,1)S(1)}, u32[]{:S(2)}) copy-start(bf16[256,1024]{1,0:T(8,128)(2,1)S(1)} %get-tuple-element.174.db_ref) | copy-start | bytes 1572868
  627.7 1.4 copy-start.19
  627.7 1.5 copy-start.20
  627.7 226.2 %reduce-scatter.11.cloned.1.call-start = ((), (), s32[]{:S(2)}) async-start(), calls=%async_computation.9 | async-start | bytes 16097280 | tf_op jit(solution)/shard_map/reduce_scatter | solution.py:1839
  849.3 23.3 %copy-start.21 = (f32[1,2048]{1,0:T(1,128)S(1)}, f32[1,2048]{1,0:T(1,128)}, u32[]{:S(2)}) copy-start(f32[1,2048]{1,0:T(1,128)} %get-tuple-element.128) | copy-start | bytes 24580
  849.4 23.3 %copy-start.22 = (f32[1,2048]{1,0:T(1,128)S(1)}, f32[1,2048]{1,0:T(1,128)}, u32[]{:S(2)}) copy-start(f32[1,2048]{1,0:T(1,128)} %get-tuple-element.125) | copy-start | bytes 24580
  851.1 51.3 %copy-start.15 = (f32[30400]{0:T(1024)S(1)}, f32[30400]{0:T(1024)}, u32[]{:S(2)}) copy-start(f32[30400]{0:T(1024)} %param.27) | copy-start | bytes 364804
  851.1 51.3 %copy-start.17 = (f32[30400]{0:T(1024)S(1)}, f32[30400]{0:T(1024)}, u32[]{:S(2)}) copy-start(f32[30400]{0:T(1024)} %param.28) | copy-start | bytes 364804
  853.1 51.5 %copy-start.18 = (f32[30400]{0:T(1024)S(1)}, f32[30400]{0:T(1024)}, u32[]{:S(2)}) copy-start(f32[30400]{0:T(1024)} %param.29) | copy-start | bytes 364804
  904.7 12.7 %copy-start.16 = (f32[30400]{0:T(1024)}, f32[30400]{0:T(1024)S(1)}, u32[]{:S(2)}) copy-start(f32[30400]{0:T(1024)S(1)} %get-tuple-element.165) | copy-start | bytes 364804
  917.4 2.8 copy-start
  (6 other events, 5.0 us)
Sparse Core Ops, SparseCore 0:
  36.3 83.5 reduce-scatter.4
  417.7 34.5 reduce-scatter.8
  455.2 34.6 reduce-scatter.6
  627.8 46.6 all-gather.8
Sparse Core Ops, SparseCore 1:
  39.1 62.9 all-gather.4
  176.5 107.1 all-gather.6
  631.4 221.6 reduce-scatter.10

commit v8 on v6

--- a/solution.py
+++ b/solution.py
@@ -330,9 +330,6 @@
 
 def bits_of(size):
     return [1 << b for b in range(size.bit_length() - 1)]
-
-
-TCHUNK = 512
 
 
 def stepped(weight, moment, average, grad, factor):
@@ -408,57 +405,6 @@
         (pltpu.VMEM, pltpu.VMEM),
         packed.size * 4 * 3,
     )
-
-
-def update_table_kernel(norm_ref, w_ref, m_ref, a_ref, g_ref, *outs):
-    new = stepped(w_ref[...], m_ref[...], a_ref[...], g_ref[...], norm_ref[1:2, 0:1])
-    for out, value in zip(outs, new + (new[0].astype(bf16),)):
-        out[...] = value
-
-
-def update_table(norms, weight, moment, average, grad):
-    rows, cols = weight.shape
-    block = pl.BlockSpec((TCHUNK, cols), lambda i: (i, 0))
-    return pl.pallas_call(
-        update_table_kernel,
-        name="update_table",
-        grid=(pl.cdiv(rows, TCHUNK),),
-        in_specs=[pl.BlockSpec((8, LANES), lambda i: (0, 0))] + [block] * 4,
-        out_specs=[block] * 4,
-        out_shape=[jax.ShapeDtypeStruct((rows, cols), kind) for kind in (f32, f32, f32, bf16)],
-        compiler_params=pltpu.CompilerParams(vmem_limit_bytes=VMEM_LIMIT),
-        cost_estimate=pl.CostEstimate(
-            flops=8 * weight.size, transcendentals=0, bytes_accessed=30 * weight.size
-        ),
-    )(norms, weight, moment, average, grad)
-
-
-def update_projections_kernel(norm_ref, *refs):
-    factor = norm_ref[1:2, 0:1]
-    sources = (refs[0:3], refs[3:6])
-    grads = refs[6 : 6 + 2 * LAYERS]
-    outs = refs[6 + 2 * LAYERS :]
-    for group in (0, 1):
-        for l in range(LAYERS):
-            grad = grads[2 * l + group]
-            step = min(grad.shape[0], 16)
-
-            def some(r, _, l=l, group=group, grad=grad, step=step):
-                rows = pl.ds(pl.multiple_of(r * step, step), step)
-                new = stepped(*(ref[l, rows, :] for ref in sources[group]), grad[rows, :], factor)
-                for i in range(3):
-                    outs[4 * group + i][l, rows, :] = new[i]
-                outs[4 * group + 3][l, rows, :] = new[0].astype(bf16)
-                return 0
-
-            lax.fori_loop(0, grad.shape[0] // step, some, 0)
-
-
-def update_projections(norms, projections, grads):
-    outs = []
-    for i in (0, 3):
-        outs += [(projections[i].shape, f32)] * 3 + [(projections[i].shape, bf16)]
-    return local_call(update_projections_kernel, (norms, *projections, *grads), tuple(outs))
 
 
 def snake(place, size):
@@ -971,7 +917,7 @@
         pre_ref[:, xs] = out
         return 0
 
-    lax.fori_loop(0, XBC // LANES, conv, 0)
+    lax.fori_loop(0, XBC // LANES, conv, 0, unroll=3)
     bm = silu(pre_ref[:, DI : DI + NSTATE]).astype(bf16)
     cm = silu(pre_ref[:, DI + NSTATE :]).astype(bf16)
     cb = dot_nt(cm, bm)
@@ -984,7 +930,7 @@
         st[xs, :] = dot_tn((tail * silu(pre_ref[:, xs])).astype(bf16), bm)
         return 0
 
-    lax.fori_loop(0, PAIRS, states, 0, unroll=2)
+    lax.fori_loop(0, PAIRS, states, 0, unroll=4)
     square[...] = jnp.zeros(square.shape, f32)
 
     def pair(p):
@@ -1021,7 +967,7 @@
         yn_ref[:, xs] = (g * scale * gg_ref[0:1, xs]).astype(bf16)
         return 0
 
-    lax.fori_loop(0, PAIRS, put, 0, unroll=2)
+    lax.fori_loop(0, PAIRS, put, 0, unroll=4)
 
     @pl.when(jnp.logical_not(final))
     def _():
@@ -1061,7 +1007,7 @@
         g = y_ref[:, xs] * silu(proj_ref[:, xs])
         return carry[0] + g * g, carry[1] + g * (dyn_ref[:, xs] * gg_ref[0:1, xs])
 
-    square, cross = lax.fori_loop(0, PAIRS, sums, (zero, zero))
+    square, cross = lax.fori_loop(0, PAIRS, sums, (zero, zero), unroll=4)
     scale = lax.rsqrt(jnp.sum(square, axis=1, keepdims=True) / DI + epsilon)
     mean = jnp.sum(cross, axis=1, keepdims=True) * scale / DI
 
@@ -1081,7 +1027,7 @@
         gst[xs, :] = dot_tn((jnp.exp(lcol[p]) * dy).astype(bf16), cm)
         return 0
 
-    lax.fori_loop(0, PAIRS, ungate, 0, unroll=2)
+    lax.fori_loop(0, PAIRS, ungate, 0, unroll=4)
     pad[0:8, :] = halo_ref[...]
     pad[8:, :] = proj_ref[:, DI : DI + XBC]
     grad[0:8, :] = jnp.zeros((8, XBC), f32)
@@ -1163,7 +1109,7 @@
         edge_ref[:, xs] = edge
         return 0
 
-    lax.fori_loop(0, XBC // LANES, edges, 0)
+    lax.fori_loop(0, XBC // LANES, edges, 0, unroll=9)
     edge = to_next(edge_ref, from_ref, edge_send, edge_recv, -1)
 
     @pl.when(jnp.logical_not(final))
@@ -1197,7 +1143,7 @@
         dx_ref[:, xs] = out
         return 0
 
-    lax.fori_loop(0, XBC // LANES, conv, 0)
+    lax.fori_loop(0, XBC // LANES, conv, 0, unroll=3)
 
     @pl.when(jnp.logical_not(first))
     def _():
@@ -1573,18 +1519,18 @@
 
 def weight_grads(normed, grad_proj, mixed, grad_branch):
     rows = normed.shape[0]
-    steps = D // LANES
+    steps = D // 256
     part = DI // steps
     return head_call(
         weight_grads_kernel,
         steps,
         [
-            pl.BlockSpec((rows, LANES), lambda i: (0, i)),
+            pl.BlockSpec((rows, 256), lambda i: (0, i)),
             pl.BlockSpec((rows, ZW), lambda i: (0, 0)),
             pl.BlockSpec((rows, part), lambda i: (0, i)),
             pl.BlockSpec((rows, D), lambda i: (0, 0)),
         ],
-        [pl.BlockSpec((LANES, ZW), lambda i: (i, 0)), pl.BlockSpec((part, D), lambda i: (i, 0))],
+        [pl.BlockSpec((256, ZW), lambda i: (i, 0)), pl.BlockSpec((part, D), lambda i: (i, 0))],
         [((D, ZW), bf16), ((DI, D), bf16)],
         (),
         (normed, grad_proj, mixed, grad_branch),
@@ -1841,19 +1787,19 @@
         grad_hidden, grad_in, grad_out, vec_parts[l] = layer_backward(
             grad_hidden, w_in[l], w_out[l], vecs, l, records[l]
         )
-        if l == 0:
-            sent = group_call(
-                to_columns_kernel,
-                9,
-                grad_hidden,
-                ((groups, rows, own_cols), bf16),
-                (pltpu.VMEM((groups, rows, own_cols), bf16),),
-            )
-            spread = lax.all_gather(sent, "fsdp", axis=0).reshape(every, own_cols)
         in_parts[l], out_parts[l] = grad_in, grad_out
     whole = []
     for l in range(LAYERS):
         whole += [in_parts[l], out_parts[l]]
+    sent = group_call(
+        to_columns_kernel,
+        9,
+        after(grad_hidden, whole),
+        ((groups, rows, own_cols), bf16),
+        (pltpu.VMEM((groups, rows, own_cols), bf16),),
+    )
+    whole = after(whole, sent)
+    spread = lax.all_gather(sent, "fsdp", axis=0).reshape(every, own_cols)
     summed_parts = reduce_layers(whole)
     spread = after(spread, summed_parts)
     table_total, table_squares = local_call(
@@ -1881,12 +1827,15 @@
         ]
     )
     packed, norms = total_of(packed.reshape(-1, LANES), small, used - 2)
-    updated = list(update_table(norms, embedding, embedding_mom, embedding_avg, table_total))
-    updated += update_projections(
-        norms,
-        (in_proj, in_proj_mom, in_proj_avg, out_proj, out_proj_mom, out_proj_avg),
-        summed_parts,
-    )
+    factor = norms[1, 0]
+    updated = []
+    for master, moment, average, grad in (
+        (embedding, embedding_mom, embedding_avg, table_total),
+        (in_proj, in_proj_mom, in_proj_avg, jnp.stack(summed_parts[0::2])),
+        (out_proj, out_proj_mom, out_proj_avg, jnp.stack(summed_parts[1::2])),
+    ):
+        new = stepped(master, moment, average, grad, factor)
+        updated += [*new, new[0].astype(bf16)]
     packed = packed.reshape(-1)
     vector_total = packed[:small]
     hidden_total = packed[small : small + D]
@@ -1894,7 +1843,7 @@
     mean_part = jnp.sum(hidden_total * column_total) * (0.1 / VOCAB)
     loss_value = (packed[used - 1] - mean_part) / total_count
     vector_new, vector_mom_new, vector_avg_new = stepped(
-        vector_params, vector_mom, vector_avg, vector_total, norms[1, 0]
+        vector_params, vector_mom, vector_avg, vector_total, factor
     )
     return (
         loss_value,

time: 884 us -> 892 us (level)
  Pallas kernels: 740 us -> 710 us
  other arithmetic: 30.2 us -> 58.5 us
  waiting for transfers between devices: 18.4 us -> 29.7 us
    pallas_call x1 -> x0, Pallas kernels: 21.1 us -> none  [update_table(): pl.pallas_call(update_table_kernel, name='update_table', grid=(pl.cdiv(ro...]
    convert_element_type x0 -> x3, other arithmetic: none -> 16 us  [whole_step(): updated += [*new, new[0].astype(bf16)]]
    add x1 -> x4, other arithmetic: 0.68 us -> 11.5 us  [stepped(): return (weight_new, moment_new, 0.5 * average + 0.5 * weight_new)]
    reduce_scatter x1, waiting for transfers between devices: 0.03 us -> 9.57 us  [whole_step(): lax.psum_scatter(table_grad, 'dp', scatter_dimension=1, tiled=True)]
    pallas_call x3 -> x2, Pallas kernels: 32.5 us -> 26.6 us  [local_call(): pl.pallas_call(kernel, out_shape=[jax.ShapeDtypeStruct(shape, kind) for s...]
  transfers between devices with their start and end apart: 6 -> 6, of which waited for: 2 -> 3; matrix products, arithmetic and copies ran while one was open for 5% -> 5% of each run, Pallas kernels for 53% -> 50%
where the time goes in v8:
time: 892 us; the launch traced here: 884 us
  Pallas kernels  710 us (80%)
  other arithmetic  58.5 us (7%)
  matrix products  45 us (5%)
  waiting for transfers between devices  29.7 us (3%)
  between operations  23 us (3%)
  local copies, waits for them, and re-layouts  17.5 us (2%)
    pallas_call x11, Pallas kernels, comm_call(): pl.pallas_call(kernel, out_shape=[jax.ShapeDtypeStruct(shape, kind) for s...  593 us
    pallas_call x4, Pallas kernels, head_call(): pl.pallas_call(kernel, grid=(grid,), in_specs=in_specs, out_specs=out_spe...  90.4 us
    pallas_call x2, Pallas kernels, local_call(): pl.pallas_call(kernel, out_shape=[jax.ShapeDtypeStruct(shape, kind) for s...  26.6 us
    dot_general x4, matrix products, dot_nt(): lax.dot_general(a, b, (((1,), (1,)), ((), ())), precision=precision, pref...  20.6 us
  transfers between devices with their start and end apart: 6, of which 3 were waited for; matrix products, arithmetic and copies ran while one was open for 5% of the time, Pallas kernels for 50%

profile of v8, /device:TPU:12, one launch (start us, length us, event | category | flops | bytes accessed | tf_op | source)
XLA Modules:
  0.0 883.8 jit_solution(9752104047242356931)
XLA Ops:
  9.4 6.0 shard_map.286
  16.3 6.2 sort.15
  23.7 12.5 %shard_map.287 = (bf16[8192,256]{1,0:T(8,128)(2,1)}, bf16[5006,256]{1,0:T(8,128)(2,1)}, f32[8,256]{1,0:T(8,128)}) custom-call(s32[1]{0:T(128)} %bitcast.1.count_ref, s32[8192]{0:T(1024)} %get-tuple-element.169.row_ref, s32[8192]{0:T(1024)} %get-tuple-element.168.tok_ref, f32[6286,256]{1,0:T(8,128)} %table_ref.1), custom_call_target="tpu_custom_call" | custom-call | flops 6502404 | bytes 13004808 | tf_op jit(solution)/shard_map/pallas_call | solution.py:66
  40.4 135.9 %shard_map.289 = (bf16[4,4,2,32,4384]{4,3,2,1,0:T(8,128)(2,1)}, bf16[4,4,2,64,1024]{4,3,2,1,0:T(8,128)(2,1)}, bf16[4,4,2,32,4384]{4,3,2,1,0:T(8,128)(2,1)}, bf16[4,4,2,64,1024]{4,3,2,1,0:T(8,128)(2,1)}) custom-call(bf16[32,4384]{1,0:T(8,128)(2,1)} %get-tuple-element.81.refs_0_, bf16[64,1024]{1,0:T(8,128)(2,1)} %get-tuple-element.82.refs_1_, ...), custom_call_target="tpu_custom_call" | custom-call | flops 19759104 | bytes 39518208 | tf_op jit(solution)/shard_map/pallas_call | solution.py:193
  181.9 13.7 %shard_map.288 = f32[256,1024]{1,0:T(8,128)} custom-call(bf16[4,256,256]{2,1,0:T(8,128)(2,1)} %bitcast.95), custom_call_target="tpu_custom_call" | custom-call | flops 524288 | bytes 1048576 | tf_op jit(solution)/shard_map/pallas_call | solution.py:193
  198.4 8.0 fusion.10.proj_ref
  206.4 26.3 %shard_map.290 = (f32[256,2304]{1,0:T(8,128)}, f32[256,2048]{1,0:T(8,128)}, bf16[256,2048]{1,0:T(8,128)(2,1)}, f32[256,128]{1,0:T(8,128)}, f32[256,128]{1,0:T(8,...) custom-call(s32[1]{0:T(128)} %constant.70.clone.1.layer_ref, f32[256,4384]{1,0:T(8,128)} %fusion.10.proj_ref, ...), custom_call_target="tpu_custom_call" | custom-call | flops 524288 | bytes 1048576 | tf_op jit(solution)/shard_map/pallas_call | solution.py:193
  232.7 4.1 multiply_reduce_fusion.8
  237.9 8.2 fusion.11.proj_ref
  246.2 25.3 %shard_map.291 = (f32[256,2304]{1,0:T(8,128)}, f32[256,2048]{1,0:T(8,128)}, bf16[256,2048]{1,0:T(8,128)(2,1)}, f32[256,128]{1,0:T(8,128)}, f32[256,128]{1,0:T(8,...) custom-call(s32[1]{0:T(128)} %constant.78.clone.1.layer_ref, f32[256,4384]{1,0:T(8,128)} %fusion.11.proj_ref, ...), custom_call_target="tpu_custom_call" | custom-call | flops 524288 | bytes 1048576 | tf_op jit(solution)/shard_map/pallas_call | solution.py:193
  271.5 4.1 multiply_reduce_fusion.7
  277.6 6.0 all-gather.7.cloned.1.call-done.table_ref.e_ref
  283.6 63.0 %shard_map.292 = (bf16[6400,2048]{1,0:T(8,128)(2,1)}, bf16[8,256,1024]{2,1,0:T(8,128)(2,1)}, f32[1,2048]{1,0:T(1,128)}, f32[5,1,2048]{2,1,0:T(1,128)}, f32[1,2048]{1,0:T(1,128)}) custom-call(bf16[1280,1024]{1,0:T(8,128)(2,1)} %all-gather.5.cloned.1.call-done.lead_ref, bf16[5006,1024]{1,0:T(8,128)(2,1)} %all-gather.7.cloned.1.call-done.table_ref.e_ref, ...), custom_call_target="tpu_custom_call" | custom-call | flops 3670016 | bytes 7340032 | tf_op jit(solution)/shard_map/pallas_call | solution.py:193
  346.6 40.0 %shard_map.293 = bf16[2048,1024]{1,0:T(8,128)(2,1)} custom-call(bf16[1280,1024]{1,0:T(8,128)(2,1)} %all-gather.5.cloned.1.call-done.lead_ref, bf16[5006,1024]{1,0:T(8,128)(2,1)} %all-gather.7.cloned.1.call-done.table_ref.e_ref, bf16[6400,2048]{1,0:T(8,128)(2,1)} %get-tuple-element.93.q_ref, f32[5,1,2048]{2,1,0:T(1,128)} %get-tuple-element.94.fac_ref, ...), custom_call_target="tpu_custom_call" | custom-call | flops 26365394944 | bytes 51494912 | tf_op jit(solution)/shard_map/pallas_call | solution.py:1177
  386.7 33.8 %shard_map.294 = bf16[6286,1024]{1,0:T(8,128)(2,1)} custom-call(bf16[2048,1024]{1,0:T(8,128)(2,1)} %bitcast.122, bf16[6400,2048]{1,0:T(8,128)(2,1)} %get-tuple-element.93.q_ref, f32[5,1,2048]{2,1,0:T(1,128)} %get-tuple-element.94.fac_ref, f32[1,2048]{1,0:T(1,128)} %broadcast_select_fusion.2.w_ref, s32[1,2048]{1,0:T(1,128)} %sub.71.lab_ref), custom_call_target="tpu_custom_call" | custom-call | flops 26365394944 | bytes 51494912 | tf_op jit(solution)/shard_map/pallas_call | solution.py:1177
  420.5 13.5 %reduce-scatter.6.cloned.1.call-done = bf16[256,1024]{1,0:T(8,128)(2,1)} async-done(((bf16[2048,1024]{1,0:T(8,128)(2,1)}), bf16[256,1024]{1,0:T(8,128)(2,1)}) %reduce-scatter.6.cloned.1.call-update) | async-done | bytes 524304 | tf_op jit(solution)/shard_map/reduce_scatter | solution.py:1776
  438.5 2.6 fusion.12.dyn_ref
  441.1 41.5 %shard_map.295 = (bf16[256,4384]{1,0:T(8,128)(2,1)}, f32[8,2304]{1,0:T(8,128)}, f32[8,128]{1,0:T(8,128)}, f32[1,2048]{1,0:T(1,128)}) custom-call(s32[1]{0:T(128)} %constant.78.clone.1.layer_ref, f32[256,2048]{1,0:T(8,128)} %fusion.12.dyn_ref, f32[256,2048]{1,0:T(8,128)} %get-tuple-element.97.y_ref, f32[256,4384]{1,0:T(8,128)} %fusion.11.proj_ref, ...), custom_call_target="tpu_custom_call" | custom-call | flops 524288 | bytes 1048576 | tf_op jit(solution)/shard_map/pallas_call | solution.py:193
  482.7 7.4 multiply_reduce_fusion.3
  492.9 2.6 fusion.13.dyn_ref
  495.5 37.3 %shard_map.296 = (bf16[256,4384]{1,0:T(8,128)(2,1)}, f32[8,2304]{1,0:T(8,128)}, f32[8,128]{1,0:T(8,128)}, f32[1,2048]{1,0:T(1,128)}) custom-call(s32[1]{0:T(128)} %constant.70.clone.1.layer_ref, f32[256,2048]{1,0:T(8,128)} %fusion.13.dyn_ref, f32[256,2048]{1,0:T(8,128)} %get-tuple-element.104.y_ref, f32[256,4384]{1,0:T(8,128)} %fusion.10.proj_ref, ...), custom_call_target="tpu_custom_call" | custom-call | flops 524288 | bytes 1048576 | tf_op jit(solution)/shard_map/pallas_call | solution.py:193
  532.8 7.9 multiply_reduce_fusion
  540.8 8.3 shard_map.297
  549.0 8.3 shard_map.298
  557.3 2.8 multiply_add_fusion.2.in_ref
  560.1 9.5 %shard_map.299 = bf16[4,256,256]{2,1,0:T(8,128)(2,1)} custom-call(f32[256,1024]{1,0:T(8,128)} %multiply_add_fusion.2.in_ref), custom_call_target="tpu_custom_call" | custom-call | flops 524288 | bytes 1048576 | tf_op jit(solution)/shard_map/pallas_call | solution.py:193
  571.2 208.4 %shard_map.300 = (f32[32,4384]{1,0:T(8,128)}, f32[64,1024]{1,0:T(8,128)}, f32[32,4384]{1,0:T(8,128)}, f32[64,1024]{1,0:T(8,128)}) custom-call(bf16[4,4,2,32,4384]{4,3,2,1,0:T(8,128)(2,1)} %bitcast.86, bf16[4,4,2,64,1024]{4,3,2,1,0:T(8,128)(2,1)} %bitcast.88, bf16[4,4,2,32,4384]{4,3,2,1,0:T(8,128)(2,1)} %bitcast.87, bf16[4,4,2,64,1024]{4,3,2,1,0:T(8,128)(2,1)} %bitcast.89), custom_call_target="tpu_custom_call" | custom-call | flops 26345472 | bytes 52690944 | tf_op jit(solution)/shard_map/pallas_call | solution.py:193
  784.2 9.6 %reduce-scatter.8.cloned.1.call-done.base_ref = bf16[6286,256]{1,0:T(8,128)(2,1)} async-done(((bf16[6286,1024]{1,0:T(8,128)(2,1)}), bf16[6286,256]{1,0:T(8,128)(2,1)}) %reduce-scatter.8.cloned.1.call-update) | async-done | bytes 3218448 | tf_op jit(solution)/shard_map/reduce_scatter | solution.py:1780
  793.7 14.1 %shard_map.301 = (f32[6286,256]{1,0:T(8,128)}, f32[8,256]{1,0:T(8,128)}) custom-call(s32[1]{0:T(128)} %bitcast.1.count_ref, s32[8192]{0:T(1024)} %get-tuple-element.169.row_ref, s32[8192]{0:T(1024)} %get-tuple-element.168.tok_ref, bf16[8192,256]{1,0:T(8,128)(2,1)} %bitcast.90, bf16[6286,256]{1,0:T(8,128)(2,1)} %reduce-scatter.8.cloned.1.call-done.base_ref), custom_call_target="tpu_custom_call" | custom-call | flops 7478276 | bytes 14956552 | tf_op jit(solution)/shard_map/pallas_call | solution.py:66
  813.9 25.7 %shard_map.302 = (f32[256,128]{1,0:T(8,128)}, f32[8,128]{1,0:T(8,128)}) custom-call(f32[256,128]{1,0:T(8,128)} %bitcast.96), custom_call_target="tpu_custom_call" | custom-call | flops 393216 | bytes 786432 | tf_op jit(solution)/shard_map/pallas_call | solution.py:193
  847.1 12.0 %fusion.6 = (bf16[6286,256]{1,0:T(8,128)(2,1)}, f32[6286,256]{1,0:T(8,128)S(1)}, f32[6286,256]{1,0:T(8,128)}) fusion(f32[6286,256]{1,0:T(8,128)} %table_ref.1, f32[6286,256]{1,0:T(8,128)} %get-tuple-element.137, f32[]{:T(128)} %bitcast.34, f32[6286,256]{1,0:T(8,128)} %param.19), kind=kLoop, calls=%fused_computation.84 | loop fusion | flops 12873728 | bytes 35402756 | tf_op jit(solution)/shard_map/convert_element_type | solution.py:1838
  859.2 8.8 add_multiply_fusion
  (172 shorter events, 47.1 us)
Async XLA Ops:
  8.0 173.8 %reduce-scatter.4.cloned.1.call-start = ((), (), s32[]{:S(2)}) async-start(), calls=%async_computation.3 | async-start | bytes 4718592 | tf_op jit(solution)/shard_map/reduce_scatter | solution.py:1727
  36.2 241.4 %all-gather.5.cloned.1.call-start = ((), (), s32[]{:S(2)}) async-start(), calls=%async_computation.4 | async-start | bytes 3276800 | tf_op jit(solution)/shard_map/all_gather | solution.py:1706
  38.6 137.8 %slice-start = ((f32[30400]{0:T(1024)}), f32[29376]{0:T(1024)S(1)}, s32[]{:S(2)}) async-start(f32[30400]{0:T(1024)} %param.27), calls=%async_computation.9 | async-start | bytes 237568 | tf_op jit(solution)/shard_map/slice | solution.py:1558
  38.6 138.1 %copy-start.27 = (f32[30400]{0:T(1024)S(1)}, f32[30400]{0:T(1024)}, u32[]{:S(2)}) copy-start(f32[30400]{0:T(1024)} %param.27) | copy-start | bytes 364804
  38.6 139.6 %copy-start.39 = (s32[2,4]{1,0:T(2,128)S(1)}, s32[2,4]{1,0:T(2,128)}, u32[]{:S(2)}) copy-start(s32[2,4]{1,0:T(2,128)} %param.17) | copy-start | bytes 100
  38.6 140.5 %copy-start.36 = (s32[2,1,1024]{2,1,0:T(1,128)S(1)}, s32[2,1,1024]{2,1,0:T(1,128)}, u32[]{:S(2)}) copy-start(s32[2,1,1024]{2,1,0:T(1,128)} %param.16) | copy-start | bytes 24580
  38.7 244.9 %all-gather.7.cloned.1.call-start = ((), (), s32[]{:S(2)}) async-start(), calls=%async_computation.5 | async-start | bytes 12820480 | tf_op jit(solution)/shard_map/all_gather | solution.py:1745
  176.4 257.6 %reduce-scatter.6.cloned.1.call-start = ((), (), s32[]{:S(2)}) async-start(), calls=%async_computation.6 | async-start | bytes 4718592 | tf_op jit(solution)/shard_map/reduce_scatter | solution.py:1776
  198.4 8.0 copy-start.14
  206.4 26.3 %copy-start.1 = (f32[256,1024]{1,0:T(8,128)S(1)}, f32[256,1024]{1,0:T(8,128)}, u32[]{:S(2)}) copy-start(f32[256,1024]{1,0:T(8,128)} %shard_map.288) | copy-start | bytes 3145732
  237.9 8.2 copy-start.15
  386.6 397.6 %all-gather.9.cloned.1.call-start = ((), (), s32[]{:S(2)}) async-start(), calls=%async_computation.8 | async-start | bytes 4718592 | tf_op jit(solution)/shard_map/all_gather | solution.py:1802
  420.5 16.9 %copy-start.5 = (f32[256,1024]{1,0:T(8,128)S(1)}, f32[256,1024]{1,0:T(8,128)}, u32[]{:S(2)}) copy-start(f32[256,1024]{1,0:T(8,128)} %copy-done.4) | copy-start | bytes 3145732
  434.0 4.5 copy-start.41
  482.7 7.5 copy-start.3
  482.7 7.5 copy-start.6
  482.7 7.5 copy-start.11
  491.6 41.2 %copy-start.24 = (bf16[256,1024]{1,0:T(8,128)(2,1)}, bf16[256,1024]{1,0:T(8,128)(2,1)S(1)}, u32[]{:S(2)}) copy-start(bf16[256,1024]{1,0:T(8,128)(2,1)S(1)} %get-tuple-element.160.db_ref) | copy-start | bytes 1572868
  569.7 224.0 %reduce-scatter.8.cloned.1.call-start = ((), (), s32[]{:S(2)}) async-start(), calls=%async_computation.7 | async-start | bytes 16097280 | tf_op jit(solution)/shard_map/reduce_scatter | solution.py:1780
  781.3 31.1 %copy-start.33 = (f32[1,2048]{1,0:T(1,128)S(1)}, f32[1,2048]{1,0:T(1,128)}, u32[]{:S(2)}) copy-start(f32[1,2048]{1,0:T(1,128)} %get-tuple-element.116) | copy-start | bytes 24580
  781.3 31.1 %copy-start.34 = (f32[1,2048]{1,0:T(1,128)S(1)}, f32[1,2048]{1,0:T(1,128)}, u32[]{:S(2)}) copy-start(f32[1,2048]{1,0:T(1,128)} %get-tuple-element.113) | copy-start | bytes 24580
  783.4 61.5 %copy-start.29 = (f32[30400]{0:T(1024)S(1)}, f32[30400]{0:T(1024)}, u32[]{:S(2)}) copy-start(f32[30400]{0:T(1024)} %param.28) | copy-start | bytes 364804
  847.1 27.0 %copy-start.28 = (f32[30400]{0:T(1024)}, f32[30400]{0:T(1024)S(1)}, u32[]{:S(2)}) copy-start(f32[30400]{0:T(1024)S(1)} %get-tuple-element.145) | copy-start | bytes 364804
  859.2 8.8 copy-start
  859.2 8.8 copy-start.8
  859.2 8.8 copy-start.12
  859.2 8.8 copy-start.13
  859.2 8.8 copy-start.19
  868.0 3.4 copy-start.18
  868.0 3.4 copy-start.21
  870.3 4.5 copy-start.9
  870.3 3.8 copy-start.30
  (17 other events, 31.8 us)
Sparse Core Ops, SparseCore 0:
  36.3 83.5 reduce-scatter.3
  386.7 47.2 reduce-scatter.5
  569.8 47.8 all-gather.8
Sparse Core Ops, SparseCore 1:
  39.1 62.9 all-gather.4
  176.5 107.1 all-gather.6
  573.3 220.4 reduce-scatter.7

commit v9 on v8

--- a/solution.py
+++ b/solution.py
@@ -339,47 +339,81 @@
     return weight_new, moment_new, 0.5 * average + 0.5 * weight_new
 
 
-def total_kernel(small, squares_at, packed_ref, total_ref, norm_ref, work, got, send, recv):
+def across(kind, bit):
     dp = lax.axis_index("dp")
     me = lax.axis_index("fsdp")
-    half = packed_ref.shape[0] // 2
-    core = me % MB
+    ids, other = (me, lambda v: (dp, v)) if kind == "f" else (dp, lambda v: (v, me))
+    return other(jnp.where((ids // bit) % 2 == 1, ids - bit, ids + bit))
+
+
+def total_partners():
     partners = [("f", b) for b in bits_of(lax.axis_size("fsdp")) if b > 1]
-    partners += [("d", b) for b in bits_of(lax.axis_size("dp"))]
-
-    def across(kind, bit):
-        ids, other = (me, lambda v: (dp, v)) if kind == "f" else (dp, lambda v: (v, me))
-        return other(jnp.where((ids // bit) % 2 == 1, ids - bit, ids + bit))
-
+    return partners + [("d", b) for b in bits_of(lax.axis_size("dp"))]
+
+
+def total_steps(in_ref, out_ref, work, got, send, recv):
+    half = in_ref.shape[0] // 2
+    core = lax.axis_index("fsdp") % MB
     mate = across("f", 1)
-    barrier = pltpu.get_barrier_semaphore()
-    for target in [mate] + [across(*p) for p in partners]:
-        pl.semaphore_signal(barrier, inc=1, device_id=target, device_id_type=MESH)
-    pl.semaphore_wait(barrier, 1 + len(partners))
-
     mine = pl.ds(pl.multiple_of(core * half, 8), half)
     theirs = pl.ds(pl.multiple_of((1 - core) * half, 8), half)
-    copy = remote(packed_ref.at[theirs], got.at[0], send.at[0], recv.at[0], *mate)
-    copy.start()
-    copy.wait()
-    work[0] = packed_ref[mine, :] + got[0]
+    partners = total_partners()
+    n = len(partners)
+    copies = [remote(in_ref.at[theirs], got.at[0], send.at[0], recv.at[0], *mate)]
     for i, p in enumerate(partners):
-        copy = remote(work.at[i], got.at[i + 1], send.at[i + 1], recv.at[i + 1], *across(*p))
-        copy.start()
-        copy.wait()
-        work[i + 1] = work[i] + got[i + 1]
-    n = len(partners)
-    copy = remote(work.at[n], got.at[n + 1], send.at[n + 1], recv.at[n + 1], *mate)
-    copy.start()
-    copy.wait()
-    total_ref[mine, :] = work[n]
-    total_ref[theirs, :] = got[n + 1]
-
-    total = total_ref[...]
-    index = lax.broadcasted_iota(jnp.int32, total.shape, 0) * LANES
-    index = index + lax.broadcasted_iota(jnp.int32, total.shape, 1)
-    parts = jnp.where(index < small, total * total, jnp.where(index == squares_at, total, 0.0))
-    square = jnp.sum(jnp.sum(parts, axis=0, keepdims=True), axis=1, keepdims=True)
+        copies.append(remote(work.at[i], got.at[i + 1], send.at[i + 1], recv.at[i + 1], *across(*p)))
+    copies.append(remote(work.at[n], got.at[n + 1], send.at[n + 1], recv.at[n + 1], *mate))
+    copies[0].start()
+    for i in range(n + 1):
+        yield
+        copies[i].wait()
+        work[i] = (in_ref[mine, :] if i == 0 else work[i - 1]) + got[i]
+        copies[i + 1].start()
+    yield
+    copies[n + 1].wait()
+    out_ref[mine, :] = work[n]
+    out_ref[theirs, :] = got[n + 1]
+
+
+def norm_kernel(small, square_ref, total_ref, norm_ref, inner, outer, send, recv, send2, recv2):
+    dp = lax.axis_index("dp")
+    me = lax.axis_index("fsdp")
+    shards = lax.axis_size("fsdp")
+    groups = lax.axis_size("dp")
+    near = [lax.rem(me + other, shards) for other in range(1, shards)]
+    far = [lax.rem(dp + other, groups) for other in range(1, groups)]
+    barrier = pltpu.get_barrier_semaphore()
+    for other in near:
+        pl.semaphore_signal(barrier, inc=1, device_id=(dp, other), device_id_type=MESH)
+    for other in far:
+        pl.semaphore_signal(barrier, inc=1, device_id=(other, me), device_id_type=MESH)
+    pl.semaphore_wait(barrier, shards + groups - 2)
+    for other in near:
+        remote(square_ref, inner.at[me], send.at[other], recv.at[me], dp, other).start()
+    inner[me] = square_ref[...]
+    for other in near:
+        copy = remote(square_ref, inner.at[other], send.at[other], recv.at[other], dp, other)
+        copy.wait_recv()
+        copy.wait_send()
+    total = inner[0]
+    for f in range(1, shards):
+        total = total + inner[f]
+    outer[dp] = total
+    for other in far:
+        remote(outer.at[dp], outer.at[dp], send2.at[other], recv2.at[dp], other, me).start()
+    for other in far:
+        copy = remote(outer.at[other], outer.at[other], send2.at[other], recv2.at[other], other, me)
+        copy.wait_recv()
+        copy.wait_send()
+    total = outer[0]
+    for d in range(1, groups):
+        total = total + outer[d]
+    vector = total_ref[...]
+    index = lax.broadcasted_iota(jnp.int32, vector.shape, 0) * LANES
+    index = index + lax.broadcasted_iota(jnp.int32, vector.shape, 1)
+    parts = jnp.sum(jnp.where(index < small, vector * vector, 0.0), axis=0, keepdims=True)
+    square = jnp.sum(parts, axis=1, keepdims=True)
+    square = square + jnp.sum(jnp.sum(total, axis=0, keepdims=True), axis=1, keepdims=True)
     norm = jnp.sqrt(square)
     factor = jnp.minimum(1.0, clip_limit / norm)
     norm_ref[0:1, :] = jnp.broadcast_to(norm, (1, LANES))
@@ -387,24 +421,25 @@
     norm_ref[2:8, :] = jnp.zeros((6, LANES), f32)
 
 
-def total_of(packed, small, squares_at):
-    steps = len(bits_of(lax.axis_size("fsdp"))) - 1 + len(bits_of(lax.axis_size("dp")))
-    rows = packed.shape[0]
+def norm_of(squares, vector_total, small):
+    shards, groups = lax.axis_size("fsdp"), lax.axis_size("dp")
     return comm_call(
-        functools.partial(total_kernel, small, squares_at),
+        functools.partial(norm_kernel, small),
         3,
-        (packed,),
-        ((packed.shape, f32), ((8, LANES), f32)),
+        (squares, vector_total),
+        (((8, LANES), f32),),
         (
-            pltpu.VMEM((steps + 1, rows // 2, LANES), f32),
-            pltpu.VMEM((steps + 2, rows // 2, LANES), f32),
-            pltpu.SemaphoreType.DMA((steps + 2,)),
-            pltpu.SemaphoreType.DMA((steps + 2,)),
+            pltpu.VMEM((shards, 8, LANES), f32),
+            pltpu.VMEM((groups, 8, LANES), f32),
+            pltpu.SemaphoreType.DMA((shards,)),
+            pltpu.SemaphoreType.DMA((shards,)),
+            pltpu.SemaphoreType.DMA((groups,)),
+            pltpu.SemaphoreType.DMA((groups,)),
         ),
+        (pltpu.VMEM, pltpu.VMEM),
         (pltpu.VMEM,),
-        (pltpu.VMEM, pltpu.VMEM),
-        packed.size * 4 * 3,
-    )
+        squares.size * 4 * 10,
+    )[0]
 
 
 def snake(place, size):
@@ -613,12 +648,15 @@
 
 def reduce_kernel(*refs):
     arrays = 2 * LAYERS
+    small_ref, *refs = refs
     grads = refs[:arrays]
+    total_ref, *refs = refs[arrays:]
+    refs = list(grads) + refs
     outs = refs[arrays : 2 * arrays]
     held, given, come, chained = (
         refs[(2 + i) * arrays : (3 + i) * arrays] for i in range(4)
     )
-    load_sem, mate_send, mate_recv, ring_send, ring_recv, z_send, z_recv = refs[6 * arrays :]
+    load_sem, mate_send, mate_recv, ring_send, ring_recv, z_send, z_recv, *rest = refs[6 * arrays :]
     dp = lax.axis_index("dp")
     me = lax.axis_index("fsdp")
     size = lax.axis_size("dp")
@@ -639,7 +677,8 @@
     for a in range(arrays):
         load(a).start()
     barrier = pltpu.get_barrier_semaphore()
-    for target in ((right, me), (left, me), (dp, mate)):
+    partners = [across(*p) for p in total_partners()]
+    for target in [(right, me), (left, me), (dp, mate)] + partners:
         pl.semaphore_signal(barrier, inc=1, device_id=target, device_id_type=MESH)
 
     @pl.when(has_up)
@@ -650,7 +689,10 @@
     def _():
         pl.semaphore_signal(barrier, inc=1, device_id=(dp, down), device_id_type=MESH)
 
-    pl.semaphore_wait(barrier, 3 + jnp.where(has_up, 1, 0) + jnp.where(has_down, 1, 0))
+    peers = 3 + len(partners)
+    pl.semaphore_wait(barrier, peers + jnp.where(has_up, 1, 0) + jnp.where(has_down, 1, 0))
+    small = total_steps(small_ref, total_ref, *rest)
+    next(small)
 
     def away(j, side):
         return snake(wrap(ring + j if side == 0 else ring - j, size), size)
@@ -713,14 +755,17 @@
         return jnp.where(i < uneven, k + long_side * (far_most - i), paired)
 
     add_mate(away(reach, 0))
+    next(small, None)
     for a in range(arrays):
         first_step(a, 0 if carried(a, 0) else 1).start()
     for s in range(1, reach):
         for side in (0, 1):
             add_mate(away(reach - s, side))
+            next(small, None)
         if s == 1:
             for a in range(arrays):
                 first_step(a, 0 if carried(a, 0) else 1).wait_recv()
+            next(small, None)
 
         def pass_on(i, _, s=s):
             z = chunk_at(i)
@@ -735,7 +780,10 @@
             return 0
 
         lax.fori_loop(0, count, pass_on, 0)
+        next(small, None)
     add_mate(dp)
+    for _ in small:
+        pass
 
     def along(a, side, z):
         return remote(
@@ -793,17 +841,19 @@
     lax.fori_loop(0, count, sent_along, 0)
 
 
-def reduce_layers(grads):
+def reduce_layers(small, grads):
     size, count = lax.axis_size("dp"), lax.axis_size("fsdp") // MB
     arrays = len(grads)
     reach = size // 2
     shards = [(g.shape[0] // (size * count * MB), g.shape[1]) for g in grads]
     blocks = [g.reshape((size, count, MB) + s) for g, s in zip(grads, shards)]
+    steps = len(total_partners())
+    half = small.shape[0] // 2
     return comm_call(
         reduce_kernel,
         5,
-        blocks,
-        tuple((s, f32) for s in shards),
+        (small, *blocks),
+        ((small.shape, f32),) + tuple((s, f32) for s in shards),
         tuple(pltpu.VMEM((size, count) + s, bf16) for s in shards) * 2
         + tuple(pltpu.VMEM((2, reach, count) + s, bf16) for s in shards)
         + tuple(pltpu.VMEM((2, count) + s, bf16) for s in shards)
@@ -815,9 +865,13 @@
             pltpu.SemaphoreType.DMA((arrays, 2, reach, count)),
             pltpu.SemaphoreType.DMA((arrays, count)),
             pltpu.SemaphoreType.DMA((arrays, 2, count)),
+            pltpu.VMEM((steps + 1, half, LANES), f32),
+            pltpu.VMEM((steps + 2, half, LANES), f32),
+            pltpu.SemaphoreType.DMA((steps + 2,)),
+            pltpu.SemaphoreType.DMA((steps + 2,)),
         ),
-        (pl.ANY,) * arrays,
-        (pltpu.VMEM,) * arrays,
+        (pltpu.VMEM,) + (pl.ANY,) * arrays,
+        (pltpu.VMEM,) * (1 + arrays),
         sum(g.size * 2 for g in grads),
     )
 
@@ -1425,7 +1479,7 @@
         acc[...] = jnp.zeros(acc.shape, f32)
 
     eid = lax.broadcasted_iota(jnp.int32, (VTILE, e_ref.shape[1]), 0)
-    part = jnp.where(step == 0, lead_ref[...].astype(f32), e_ref[...].astype(f32))
+    part = jnp.where(step == 0, lead_ref[...], e_ref[...]).astype(f32)
     et[...] = jnp.where(eid < vocab_rows - first, part, 0.0).T.astype(bf16)
 
     def chunk(j, _):
@@ -1800,7 +1854,14 @@
     )
     whole = after(whole, sent)
     spread = lax.all_gather(sent, "fsdp", axis=0).reshape(every, own_cols)
-    summed_parts = reduce_layers(whole)
+    small = vector_params.shape[0]
+    used = small + 2 * D + 1
+    padded = pl.cdiv(used, 16 * LANES) * 16 * LANES
+    packed = jnp.concatenate(
+        vec_parts
+        + [dfinal, hidden_sum, column_sum, loss_sum.reshape(1), jnp.zeros((padded - used,), f32)]
+    )
+    packed, *summed_parts = reduce_layers(packed.reshape(-1, LANES), whole)
     spread = after(spread, summed_parts)
     table_total, table_squares = local_call(
         spread_kernel,
@@ -1812,21 +1873,8 @@
     owner_squares = jnp.sum(table_squares)
     for part in summed_parts:
         owner_squares = owner_squares + jnp.sum(part * part)
-    small = vector_params.shape[0]
-    used = small + 2 * D + 2
-    padded = pl.cdiv(used, 16 * LANES) * 16 * LANES
-    packed = jnp.concatenate(
-        vec_parts
-        + [
-            dfinal,
-            hidden_sum,
-            column_sum,
-            owner_squares.reshape(1),
-            loss_sum.reshape(1),
-            jnp.zeros((padded - used,), f32),
-        ]
-    )
-    packed, norms = total_of(packed.reshape(-1, LANES), small, used - 2)
+    squares = jnp.pad(owner_squares.reshape(1, 1), ((0, 7), (0, LANES - 1)))
+    norms = norm_of(squares, packed, small)
     factor = norms[1, 0]
     updated = []
     for master, moment, average, grad in (

time: 892 us -> 888 us (level)
  waiting for transfers between devices: 29.7 us -> 20 us
    reduce_scatter x1, waiting for transfers between devices: 9.57 us -> 0.01 us  [whole_step(): lax.psum_scatter(table_grad, 'dp', scatter_dimension=1, tiled=True)]
  transfers between devices with their start and end apart: 6 -> 6, of which waited for: 3 -> 2; matrix products, arithmetic and copies ran while one was open for 5% -> 6% of each run, Pallas kernels for 50% -> 52%
where the time goes in v9:
time: 888 us; the launch traced here: 878 us
  Pallas kernels  710 us (80%)
  other arithmetic  60.8 us (7%)
  matrix products  45 us (5%)
  between operations  23.1 us (3%)
  waiting for transfers between devices  20 us (2%)
  local copies, waits for them, and re-layouts  18.1 us (2%)
    pallas_call x11, Pallas kernels, comm_call(): pl.pallas_call(kernel, out_shape=[jax.ShapeDtypeStruct(shape, kind) for s...  595 us
    pallas_call x4, Pallas kernels, head_call(): pl.pallas_call(kernel, grid=(grid,), in_specs=in_specs, out_specs=out_spe...  89.2 us
    pallas_call x2, Pallas kernels, local_call(): pl.pallas_call(kernel, out_shape=[jax.ShapeDtypeStruct(shape, kind) for s...  26.6 us
    dot_general x4, matrix products, dot_nt(): lax.dot_general(a, b, (((1,), (1,)), ((), ())), precision=precision, pref...  20.6 us
  transfers between devices with their start and end apart: 6, of which 2 were waited for; matrix products, arithmetic and copies ran while one was open for 6% of the time, Pallas kernels for 52%

profile of v9, /device:TPU:12, one launch (start us, length us, event | category | flops | bytes accessed | tf_op | source)
XLA Modules:
  0.0 877.6 jit_solution(12431998089640884066)
XLA Ops:
  9.4 6.0 shard_map.286
  16.3 6.2 sort.15
  23.7 12.5 %shard_map.287 = (bf16[8192,256]{1,0:T(8,128)(2,1)}, bf16[5006,256]{1,0:T(8,128)(2,1)}, f32[8,256]{1,0:T(8,128)}) custom-call(s32[1]{0:T(128)} %bitcast.1.count_ref, s32[8192]{0:T(1024)} %get-tuple-element.167.row_ref, s32[8192]{0:T(1024)} %get-tuple-element.166.tok_ref, f32[6286,256]{1,0:T(8,128)} %table_ref.1), custom_call_target="tpu_custom_call" | custom-call | flops 6502404 | bytes 13004808 | tf_op jit(solution)/shard_map/pallas_call | solution.py:66
  36.3 2.3 slice.144
  40.4 135.9 %shard_map.289 = (bf16[4,4,2,32,4384]{4,3,2,1,0:T(8,128)(2,1)}, bf16[4,4,2,64,1024]{4,3,2,1,0:T(8,128)(2,1)}, bf16[4,4,2,32,4384]{4,3,2,1,0:T(8,128)(2,1)}, bf16[4,4,2,64,1024]{4,3,2,1,0:T(8,128)(2,1)}) custom-call(bf16[32,4384]{1,0:T(8,128)(2,1)} %get-tuple-element.80.refs_0_, bf16[64,1024]{1,0:T(8,128)(2,1)} %get-tuple-element.81.refs_1_, ...), custom_call_target="tpu_custom_call" | custom-call | flops 19759104 | bytes 39518208 | tf_op jit(solution)/shard_map/pallas_call | solution.py:193
  181.9 13.7 %shard_map.288 = f32[256,1024]{1,0:T(8,128)} custom-call(bf16[4,256,256]{2,1,0:T(8,128)(2,1)} %bitcast.96), custom_call_target="tpu_custom_call" | custom-call | flops 524288 | bytes 1048576 | tf_op jit(solution)/shard_map/pallas_call | solution.py:193
  198.4 8.0 fusion.10.proj_ref
  206.4 26.3 %shard_map.290 = (f32[256,2304]{1,0:T(8,128)}, f32[256,2048]{1,0:T(8,128)}, bf16[256,2048]{1,0:T(8,128)(2,1)}, f32[256,128]{1,0:T(8,128)}, f32[256,128]{1,0:T(8,...) custom-call(s32[1]{0:T(128)} %constant.70.clone.1.layer_ref, f32[256,4384]{1,0:T(8,128)} %fusion.10.proj_ref, ...), custom_call_target="tpu_custom_call" | custom-call | flops 524288 | bytes 1048576 | tf_op jit(solution)/shard_map/pallas_call | solution.py:193
  232.7 4.1 multiply_reduce_fusion.8
  237.9 8.2 fusion.11.proj_ref
  246.2 25.3 %shard_map.291 = (f32[256,2304]{1,0:T(8,128)}, f32[256,2048]{1,0:T(8,128)}, bf16[256,2048]{1,0:T(8,128)(2,1)}, f32[256,128]{1,0:T(8,128)}, f32[256,128]{1,0:T(8,...) custom-call(s32[1]{0:T(128)} %constant.78.clone.1.layer_ref, f32[256,4384]{1,0:T(8,128)} %fusion.11.proj_ref, ...), custom_call_target="tpu_custom_call" | custom-call | flops 524288 | bytes 1048576 | tf_op jit(solution)/shard_map/pallas_call | solution.py:193
  271.5 4.1 multiply_reduce_fusion.7
  277.6 6.0 all-gather.7.cloned.1.call-done.table_ref.e_ref
  283.6 63.0 %shard_map.292 = (bf16[6400,2048]{1,0:T(8,128)(2,1)}, bf16[8,256,1024]{2,1,0:T(8,128)(2,1)}, f32[1,2048]{1,0:T(1,128)}, f32[5,1,2048]{2,1,0:T(1,128)}, f32[1,2048]{1,0:T(1,128)}) custom-call(bf16[1280,1024]{1,0:T(8,128)(2,1)} %all-gather.5.cloned.1.call-done.lead_ref, bf16[5006,1024]{1,0:T(8,128)(2,1)} %all-gather.7.cloned.1.call-done.table_ref.e_ref, ...), custom_call_target="tpu_custom_call" | custom-call | flops 3670016 | bytes 7340032 | tf_op jit(solution)/shard_map/pallas_call | solution.py:193
  346.6 38.8 %shard_map.293 = bf16[2048,1024]{1,0:T(8,128)(2,1)} custom-call(bf16[1280,1024]{1,0:T(8,128)(2,1)} %all-gather.5.cloned.1.call-done.lead_ref, bf16[5006,1024]{1,0:T(8,128)(2,1)} %all-gather.7.cloned.1.call-done.table_ref.e_ref, bf16[6400,2048]{1,0:T(8,128)(2,1)} %get-tuple-element.92.q_ref, f32[5,1,2048]{2,1,0:T(1,128)} %get-tuple-element.93.fac_ref, ...), custom_call_target="tpu_custom_call" | custom-call | flops 26365394944 | bytes 51494912 | tf_op jit(solution)/shard_map/pallas_call | solution.py:1231
  385.5 33.9 %shard_map.294 = bf16[6286,1024]{1,0:T(8,128)(2,1)} custom-call(bf16[2048,1024]{1,0:T(8,128)(2,1)} %bitcast.122, bf16[6400,2048]{1,0:T(8,128)(2,1)} %get-tuple-element.92.q_ref, f32[5,1,2048]{2,1,0:T(1,128)} %get-tuple-element.93.fac_ref, f32[1,2048]{1,0:T(1,128)} %broadcast_select_fusion.2.w_ref, s32[1,2048]{1,0:T(1,128)} %sub.71.lab_ref), custom_call_target="tpu_custom_call" | custom-call | flops 26365394944 | bytes 51494912 | tf_op jit(solution)/shard_map/pallas_call | solution.py:1231
  419.3 13.5 %reduce-scatter.6.cloned.1.call-done = bf16[256,1024]{1,0:T(8,128)(2,1)} async-done(((bf16[2048,1024]{1,0:T(8,128)(2,1)}), bf16[256,1024]{1,0:T(8,128)(2,1)}) %reduce-scatter.6.cloned.1.call-update) | async-done | bytes 524304 | tf_op jit(solution)/shard_map/reduce_scatter | solution.py:1830
  437.3 2.6 fusion.12.dyn_ref
  439.9 41.5 %shard_map.295 = (bf16[256,4384]{1,0:T(8,128)(2,1)}, f32[8,2304]{1,0:T(8,128)}, f32[8,128]{1,0:T(8,128)}, f32[1,2048]{1,0:T(1,128)}) custom-call(s32[1]{0:T(128)} %constant.78.clone.1.layer_ref, f32[256,2048]{1,0:T(8,128)} %fusion.12.dyn_ref, f32[256,2048]{1,0:T(8,128)} %get-tuple-element.96.y_ref, f32[256,4384]{1,0:T(8,128)} %fusion.11.proj_ref, ...), custom_call_target="tpu_custom_call" | custom-call | flops 524288 | bytes 1048576 | tf_op jit(solution)/shard_map/pallas_call | solution.py:193
  481.5 7.4 multiply_reduce_fusion.3
  491.7 2.6 fusion.13.dyn_ref
  494.3 37.3 %shard_map.296 = (bf16[256,4384]{1,0:T(8,128)(2,1)}, f32[8,2304]{1,0:T(8,128)}, f32[8,128]{1,0:T(8,128)}, f32[1,2048]{1,0:T(1,128)}) custom-call(s32[1]{0:T(128)} %constant.70.clone.1.layer_ref, f32[256,2048]{1,0:T(8,128)} %fusion.13.dyn_ref, f32[256,2048]{1,0:T(8,128)} %get-tuple-element.103.y_ref, f32[256,4384]{1,0:T(8,128)} %fusion.10.proj_ref, ...), custom_call_target="tpu_custom_call" | custom-call | flops 524288 | bytes 1048576 | tf_op jit(solution)/shard_map/pallas_call | solution.py:193
  531.6 8.0 multiply_reduce_fusion
  539.6 8.3 shard_map.297
  547.9 8.3 shard_map.298
  556.2 2.8 multiply_add_fusion.2.in_ref
  558.9 9.4 %shard_map.299 = bf16[4,256,256]{2,1,0:T(8,128)(2,1)} custom-call(f32[256,1024]{1,0:T(8,128)} %multiply_add_fusion.2.in_ref), custom_call_target="tpu_custom_call" | custom-call | flops 524288 | bytes 1048576 | tf_op jit(solution)/shard_map/pallas_call | solution.py:193
  572.2 219.4 %shard_map.300 = (f32[256,128]{1,0:T(8,128)}, f32[32,4384]{1,0:T(8,128)}, f32[64,1024]{1,0:T(8,128)}, f32[32,4384]{1,0:T(8,128)}, f32[64,1024]{1,0:T(8,128)}) custom-call(f32[256,128]{1,0:T(8,128)} %bitcast.95, bf16[4,4,2,32,4384]{4,3,2,1,0:T(8,128)(2,1)} %bitcast.86, bf16[4,4,2,64,1024]{4,3,2,1,0:T(8,128)(2,1)} %bitcast.88, ...), custom_call_target="tpu_custom_call" | custom-call | flops 26345472 | bytes 52690944 | tf_op jit(solution)/shard_map/pallas_call | solution.py:193
  802.5 14.1 %shard_map.301 = (f32[6286,256]{1,0:T(8,128)}, f32[8,256]{1,0:T(8,128)}) custom-call(s32[1]{0:T(128)} %bitcast.1.count_ref, s32[8192]{0:T(1024)} %get-tuple-element.167.row_ref, s32[8192]{0:T(1024)} %get-tuple-element.166.tok_ref, bf16[8192,256]{1,0:T(8,128)(2,1)} %bitcast.90, bf16[6286,256]{1,0:T(8,128)(2,1)} %reduce-scatter.8.cloned.1.call-done.base_ref), custom_call_target="tpu_custom_call" | custom-call | flops 7478276 | bytes 14956552 | tf_op jit(solution)/shard_map/pallas_call | solution.py:66
  821.9 16.5 %shard_map.302 = f32[8,128]{1,0:T(8,128)} custom-call(f32[8,128]{1,0:T(8,128)} %pad.9.square_ref, f32[256,128]{1,0:T(8,128)} %get-tuple-element.128.total_ref), custom_call_target="tpu_custom_call" | custom-call | flops 40960 | bytes 81920 | tf_op jit(solution)/shard_map/pallas_call | solution.py:193
  841.0 12.0 %fusion.6 = (bf16[6286,256]{1,0:T(8,128)(2,1)}, f32[6286,256]{1,0:T(8,128)S(1)}, f32[6286,256]{1,0:T(8,128)}) fusion(f32[6286,256]{1,0:T(8,128)} %table_ref.1, f32[6286,256]{1,0:T(8,128)} %get-tuple-element.135, f32[]{:T(128)} %bitcast.34, f32[6286,256]{1,0:T(8,128)} %param.19), kind=kLoop, calls=%fused_computation.84 | loop fusion | flops 12873728 | bytes 35402756 | tf_op jit(solution)/shard_map/convert_element_type | solution.py:1886
  853.0 8.8 add_multiply_fusion
  (177 shorter events, 47.7 us)
Async XLA Ops:
  8.0 173.9 %reduce-scatter.4.cloned.1.call-start = ((), (), s32[]{:S(2)}) async-start(), calls=%async_computation.3 | async-start | bytes 4718592 | tf_op jit(solution)/shard_map/reduce_scatter | solution.py:1781
  36.2 241.4 %all-gather.5.cloned.1.call-start = ((), (), s32[]{:S(2)}) async-start(), calls=%async_computation.4 | async-start | bytes 3276800 | tf_op jit(solution)/shard_map/all_gather | solution.py:1760
  38.6 137.8 %slice-start = ((f32[30400]{0:T(1024)}), f32[29376]{0:T(1024)S(1)}, s32[]{:S(2)}) async-start(f32[30400]{0:T(1024)} %param.27), calls=%async_computation.9 | async-start | bytes 237568 | tf_op jit(solution)/shard_map/slice | solution.py:1612
  38.6 138.1 %copy-start.28 = (f32[30400]{0:T(1024)S(1)}, f32[30400]{0:T(1024)}, u32[]{:S(2)}) copy-start(f32[30400]{0:T(1024)} %param.27) | copy-start | bytes 364804
  38.6 139.6 %copy-start.40 = (s32[2,4]{1,0:T(2,128)S(1)}, s32[2,4]{1,0:T(2,128)}, u32[]{:S(2)}) copy-start(s32[2,4]{1,0:T(2,128)} %param.17) | copy-start | bytes 100
  38.6 140.5 %copy-start.37 = (s32[2,1,1024]{2,1,0:T(1,128)S(1)}, s32[2,1,1024]{2,1,0:T(1,128)}, u32[]{:S(2)}) copy-start(s32[2,1,1024]{2,1,0:T(1,128)} %param.16) | copy-start | bytes 24580
  38.7 244.9 %all-gather.7.cloned.1.call-start = ((), (), s32[]{:S(2)}) async-start(), calls=%async_computation.5 | async-start | bytes 12820480 | tf_op jit(solution)/shard_map/all_gather | solution.py:1799
  176.4 256.4 %reduce-scatter.6.cloned.1.call-start = ((), (), s32[]{:S(2)}) async-start(), calls=%async_computation.6 | async-start | bytes 4718592 | tf_op jit(solution)/shard_map/reduce_scatter | solution.py:1830
  198.4 8.0 copy-start.14
  206.4 26.3 %copy-start.1 = (f32[256,1024]{1,0:T(8,128)S(1)}, f32[256,1024]{1,0:T(8,128)}, u32[]{:S(2)}) copy-start(f32[256,1024]{1,0:T(8,128)} %shard_map.288) | copy-start | bytes 3145732
  237.9 8.2 copy-start.15
  385.4 417.1 %all-gather.9.cloned.1.call-start = ((), (), s32[]{:S(2)}) async-start(), calls=%async_computation.8 | async-start | bytes 4718592 | tf_op jit(solution)/shard_map/all_gather | solution.py:1856
  419.3 16.9 %copy-start.5 = (f32[256,1024]{1,0:T(8,128)S(1)}, f32[256,1024]{1,0:T(8,128)}, u32[]{:S(2)}) copy-start(f32[256,1024]{1,0:T(8,128)} %copy-done.4) | copy-start | bytes 3145732
  432.8 4.5 copy-start.42
  481.4 7.5 copy-start.3
  481.5 7.5 copy-start.6
  481.5 7.5 copy-start.11
  490.4 41.2 %copy-start.24 = (bf16[256,1024]{1,0:T(8,128)(2,1)}, bf16[256,1024]{1,0:T(8,128)(2,1)S(1)}, u32[]{:S(2)}) copy-start(bf16[256,1024]{1,0:T(8,128)(2,1)S(1)} %get-tuple-element.158.db_ref) | copy-start | bytes 1572868
  568.5 234.0 %reduce-scatter.8.cloned.1.call-start = ((), (), s32[]{:S(2)}) async-start(), calls=%async_computation.7 | async-start | bytes 16097280 | tf_op jit(solution)/shard_map/reduce_scatter | solution.py:1834
  800.7 38.9 %copy-start.25 = (f32[256,128]{1,0:T(8,128)S(1)}, f32[256,128]{1,0:T(8,128)}, u32[]{:S(2)}) copy-start(f32[256,128]{1,0:T(8,128)} %get-tuple-element.128.total_ref) | copy-start | bytes 393220
  800.7 38.9 %copy-start.30 = (f32[30400]{0:T(1024)S(1)}, f32[30400]{0:T(1024)}, u32[]{:S(2)}) copy-start(f32[30400]{0:T(1024)} %param.28) | copy-start | bytes 364804
  841.0 27.0 %copy-start.29 = (f32[30400]{0:T(1024)}, f32[30400]{0:T(1024)S(1)}, u32[]{:S(2)}) copy-start(f32[30400]{0:T(1024)S(1)} %get-tuple-element.143) | copy-start | bytes 364804
  853.0 8.8 %copy-start = (f32[6286,256]{1,0:T(8,128)}, f32[6286,256]{1,0:T(8,128)S(1)}, u32[]{:S(2)}) copy-start(f32[6286,256]{1,0:T(8,128)S(1)} %get-tuple-element.152) | copy-start | bytes 19310596
  853.0 8.8 %copy-start.8 = (f32[2,32,4384]{2,1,0:T(8,128)S(1)}, f32[2,32,4384]{2,1,0:T(8,128)}, u32[]{:S(2)}) copy-start(f32[2,32,4384]{2,1,0:T(8,128)} %param.21) | copy-start | bytes 3366916
  853.0 8.8 %copy-start.12 = (f32[32,4384]{1,0:T(8,128)S(1)}, f32[32,4384]{1,0:T(8,128)}, u32[]{:S(2)}) copy-start(f32[32,4384]{1,0:T(8,128)} %get-tuple-element.129) | copy-start | bytes 1683460
  853.0 8.8 %copy-start.13 = (f32[32,4384]{1,0:T(8,128)S(1)}, f32[32,4384]{1,0:T(8,128)}, u32[]{:S(2)}) copy-start(f32[32,4384]{1,0:T(8,128)} %get-tuple-element.131) | copy-start | bytes 1683460
  853.0 8.8 %copy-start.19 = (f32[2,32,4384]{2,1,0:T(8,128)S(1)}, f32[2,32,4384]{2,1,0:T(8,128)}, u32[]{:S(2)}) copy-start(f32[2,32,4384]{2,1,0:T(8,128)} %param.22) | copy-start | bytes 3366916
  861.8 3.4 copy-start.18
  861.9 3.4 copy-start.21
  861.9 3.4 copy-start.22
  864.2 4.5 copy-start.9
  864.2 3.8 copy-start.31
  (18 other events, 33.0 us)
Sparse Core Ops, SparseCore 0:
  36.3 83.5 reduce-scatter.3
  385.5 47.2 reduce-scatter.5
  568.5 50.0 all-gather.8
Sparse Core Ops, SparseCore 1:
  39.1 62.9 all-gather.4
  176.5 107.1 all-gather.6
  572.1 224.8 reduce-scatter.7

commit v10 on v8

--- a/solution.py
+++ b/solution.py
@@ -1057,6 +1057,7 @@
         dy = dy_ref[:, xs]
         dyb = dy.astype(bf16)
         parts = []
+        pairs = []
         for j in range(2):
             h = 2 * p + j
             c = col[h]
@@ -1065,7 +1066,8 @@
             parts.append(dot_nn((w * cbt).astype(bf16), dyb))
             own = half if j == 0 else jnp.logical_not(half)
             q = dot_nt(jnp.where(own, xt, 0.0).astype(bf16), dyb)
-            dcb[...] += w * q
+            pairs.append(w * q)
+        dcb[...] += pairs[0] + pairs[1]
         lp = lcol[p]
         last = lp[rows - 1 : rows, :]
         tail = jnp.exp(last - lp)
@@ -1078,7 +1080,7 @@
         sk = sk_ref[pl.ds(p, 1), :]
         pick = jnp.where(lane_col == 2 * p + jnp.where(lane_row >= HDIM, 1, 0), 1.0, 0.0)
         dlog[...] += dot_nn(dy * (y_ref[:, xs] - sk * x) - xt * dxt, pick, highest)
-        dtx[...] += dot_nn(x * dxt, pick, highest)
+        dtx[...] += dot_nn((x * dxt).astype(bf16), pick.astype(bf16))
         held = dot_nt(ones, gin.astype(f32) * sin.astype(f32), highest)
         end = jnp.sum(xt * dst, axis=0, keepdims=True) + jnp.exp(last) * held[0:1, :]
         skip = jnp.sum(dy * x, axis=0, keepdims=True)
@@ -1425,7 +1427,7 @@
         acc[...] = jnp.zeros(acc.shape, f32)
 
     eid = lax.broadcasted_iota(jnp.int32, (VTILE, e_ref.shape[1]), 0)
-    part = jnp.where(step == 0, lead_ref[...].astype(f32), e_ref[...].astype(f32))
+    part = jnp.where(step == 0, lead_ref[...], e_ref[...]).astype(f32)
     et[...] = jnp.where(eid < vocab_rows - first, part, 0.0).T.astype(bf16)
 
     def chunk(j, _):

time: 892 us -> 886 us (level)
  transfers between devices with their start and end apart: 6 -> 6, of which waited for: 3 -> 3; matrix products, arithmetic and copies ran while one was open for 5% -> 5% of each run, Pallas kernels for 50% -> 51%
where the time goes in v10:
time: 886 us; the launch traced here: 878 us
  Pallas kernels  705 us (80%)
  other arithmetic  58.5 us (7%)
  matrix products  45 us (5%)
  waiting for transfers between devices  28.6 us (3%)
  between operations  23 us (3%)
  local copies, waits for them, and re-layouts  17.5 us (2%)
    pallas_call x11, Pallas kernels, comm_call(): pl.pallas_call(kernel, out_shape=[jax.ShapeDtypeStruct(shape, kind) for s...  589 us
    pallas_call x4, Pallas kernels, head_call(): pl.pallas_call(kernel, grid=(grid,), in_specs=in_specs, out_specs=out_spe...  89.2 us
    pallas_call x2, Pallas kernels, local_call(): pl.pallas_call(kernel, out_shape=[jax.ShapeDtypeStruct(shape, kind) for s...  26.6 us
    dot_general x4, matrix products, dot_nt(): lax.dot_general(a, b, (((1,), (1,)), ((), ())), precision=precision, pref...  20.6 us
  transfers between devices with their start and end apart: 6, of which 3 were waited for; matrix products, arithmetic and copies ran while one was open for 5% of the time, Pallas kernels for 51%

profile of v10, /device:TPU:12, one launch (start us, length us, event | category | flops | bytes accessed | tf_op | source)
XLA Modules:
  0.0 877.6 jit_solution(6745639807104730328)
XLA Ops:
  9.4 6.0 shard_map.286
  16.3 6.2 sort.15
  23.7 12.5 %shard_map.287 = (bf16[8192,256]{1,0:T(8,128)(2,1)}, bf16[5006,256]{1,0:T(8,128)(2,1)}, f32[8,256]{1,0:T(8,128)}) custom-call(s32[1]{0:T(128)} %bitcast.1.count_ref, s32[8192]{0:T(1024)} %get-tuple-element.169.row_ref, s32[8192]{0:T(1024)} %get-tuple-element.168.tok_ref, f32[6286,256]{1,0:T(8,128)} %table_ref.1), custom_call_target="tpu_custom_call" | custom-call | flops 6502404 | bytes 13004808 | tf_op jit(solution)/shard_map/pallas_call | solution.py:66
  40.4 135.9 %shard_map.289 = (bf16[4,4,2,32,4384]{4,3,2,1,0:T(8,128)(2,1)}, bf16[4,4,2,64,1024]{4,3,2,1,0:T(8,128)(2,1)}, bf16[4,4,2,32,4384]{4,3,2,1,0:T(8,128)(2,1)}, bf16[4,4,2,64,1024]{4,3,2,1,0:T(8,128)(2,1)}) custom-call(bf16[32,4384]{1,0:T(8,128)(2,1)} %get-tuple-element.81.refs_0_, bf16[64,1024]{1,0:T(8,128)(2,1)} %get-tuple-element.82.refs_1_, ...), custom_call_target="tpu_custom_call" | custom-call | flops 19759104 | bytes 39518208 | tf_op jit(solution)/shard_map/pallas_call | solution.py:193
  181.9 13.7 %shard_map.288 = f32[256,1024]{1,0:T(8,128)} custom-call(bf16[4,256,256]{2,1,0:T(8,128)(2,1)} %bitcast.95), custom_call_target="tpu_custom_call" | custom-call | flops 524288 | bytes 1048576 | tf_op jit(solution)/shard_map/pallas_call | solution.py:193
  198.4 8.0 fusion.10.proj_ref
  206.4 26.3 %shard_map.290 = (f32[256,2304]{1,0:T(8,128)}, f32[256,2048]{1,0:T(8,128)}, bf16[256,2048]{1,0:T(8,128)(2,1)}, f32[256,128]{1,0:T(8,128)}, f32[256,128]{1,0:T(8,...) custom-call(s32[1]{0:T(128)} %constant.70.clone.1.layer_ref, f32[256,4384]{1,0:T(8,128)} %fusion.10.proj_ref, ...), custom_call_target="tpu_custom_call" | custom-call | flops 524288 | bytes 1048576 | tf_op jit(solution)/shard_map/pallas_call | solution.py:193
  232.7 4.1 multiply_reduce_fusion.8
  237.9 8.2 fusion.11.proj_ref
  246.2 25.3 %shard_map.291 = (f32[256,2304]{1,0:T(8,128)}, f32[256,2048]{1,0:T(8,128)}, bf16[256,2048]{1,0:T(8,128)(2,1)}, f32[256,128]{1,0:T(8,128)}, f32[256,128]{1,0:T(8,...) custom-call(s32[1]{0:T(128)} %constant.78.clone.1.layer_ref, f32[256,4384]{1,0:T(8,128)} %fusion.11.proj_ref, ...), custom_call_target="tpu_custom_call" | custom-call | flops 524288 | bytes 1048576 | tf_op jit(solution)/shard_map/pallas_call | solution.py:193
  271.5 4.1 multiply_reduce_fusion.7
  277.6 6.0 all-gather.7.cloned.1.call-done.table_ref.e_ref
  283.6 63.0 %shard_map.292 = (bf16[6400,2048]{1,0:T(8,128)(2,1)}, bf16[8,256,1024]{2,1,0:T(8,128)(2,1)}, f32[1,2048]{1,0:T(1,128)}, f32[5,1,2048]{2,1,0:T(1,128)}, f32[1,2048]{1,0:T(1,128)}) custom-call(bf16[1280,1024]{1,0:T(8,128)(2,1)} %all-gather.5.cloned.1.call-done.lead_ref, bf16[5006,1024]{1,0:T(8,128)(2,1)} %all-gather.7.cloned.1.call-done.table_ref.e_ref, ...), custom_call_target="tpu_custom_call" | custom-call | flops 3670016 | bytes 7340032 | tf_op jit(solution)/shard_map/pallas_call | solution.py:193
  346.6 38.8 %shard_map.293 = bf16[2048,1024]{1,0:T(8,128)(2,1)} custom-call(bf16[1280,1024]{1,0:T(8,128)(2,1)} %all-gather.5.cloned.1.call-done.lead_ref, bf16[5006,1024]{1,0:T(8,128)(2,1)} %all-gather.7.cloned.1.call-done.table_ref.e_ref, bf16[6400,2048]{1,0:T(8,128)(2,1)} %get-tuple-element.93.q_ref, f32[5,1,2048]{2,1,0:T(1,128)} %get-tuple-element.94.fac_ref, ...), custom_call_target="tpu_custom_call" | custom-call | flops 26365394944 | bytes 51494912 | tf_op jit(solution)/shard_map/pallas_call | solution.py:1179
  385.4 33.8 %shard_map.294 = bf16[6286,1024]{1,0:T(8,128)(2,1)} custom-call(bf16[2048,1024]{1,0:T(8,128)(2,1)} %bitcast.122, bf16[6400,2048]{1,0:T(8,128)(2,1)} %get-tuple-element.93.q_ref, f32[5,1,2048]{2,1,0:T(1,128)} %get-tuple-element.94.fac_ref, f32[1,2048]{1,0:T(1,128)} %broadcast_select_fusion.2.w_ref, s32[1,2048]{1,0:T(1,128)} %sub.71.lab_ref), custom_call_target="tpu_custom_call" | custom-call | flops 26365394944 | bytes 51494912 | tf_op jit(solution)/shard_map/pallas_call | solution.py:1179
  419.3 13.5 %reduce-scatter.6.cloned.1.call-done = bf16[256,1024]{1,0:T(8,128)(2,1)} async-done(((bf16[2048,1024]{1,0:T(8,128)(2,1)}), bf16[256,1024]{1,0:T(8,128)(2,1)}) %reduce-scatter.6.cloned.1.call-update) | async-done | bytes 524304 | tf_op jit(solution)/shard_map/reduce_scatter | solution.py:1778
  437.3 2.6 fusion.12.dyn_ref
  439.9 39.3 %shard_map.295 = (bf16[256,4384]{1,0:T(8,128)(2,1)}, f32[8,2304]{1,0:T(8,128)}, f32[8,128]{1,0:T(8,128)}, f32[1,2048]{1,0:T(1,128)}) custom-call(s32[1]{0:T(128)} %constant.78.clone.1.layer_ref, f32[256,2048]{1,0:T(8,128)} %fusion.12.dyn_ref, f32[256,2048]{1,0:T(8,128)} %get-tuple-element.97.y_ref, f32[256,4384]{1,0:T(8,128)} %fusion.11.proj_ref, ...), custom_call_target="tpu_custom_call" | custom-call | flops 524288 | bytes 1048576 | tf_op jit(solution)/shard_map/pallas_call | solution.py:193
  479.2 7.4 multiply_reduce_fusion.3
  489.4 2.6 fusion.13.dyn_ref
  492.0 35.3 %shard_map.296 = (bf16[256,4384]{1,0:T(8,128)(2,1)}, f32[8,2304]{1,0:T(8,128)}, f32[8,128]{1,0:T(8,128)}, f32[1,2048]{1,0:T(1,128)}) custom-call(s32[1]{0:T(128)} %constant.70.clone.1.layer_ref, f32[256,2048]{1,0:T(8,128)} %fusion.13.dyn_ref, f32[256,2048]{1,0:T(8,128)} %get-tuple-element.104.y_ref, f32[256,4384]{1,0:T(8,128)} %fusion.10.proj_ref, ...), custom_call_target="tpu_custom_call" | custom-call | flops 524288 | bytes 1048576 | tf_op jit(solution)/shard_map/pallas_call | solution.py:193
  527.3 8.0 multiply_reduce_fusion
  535.2 8.3 shard_map.297
  543.5 8.3 shard_map.298
  551.8 2.8 multiply_add_fusion.2.in_ref
  554.6 9.4 %shard_map.299 = bf16[4,256,256]{2,1,0:T(8,128)(2,1)} custom-call(f32[256,1024]{1,0:T(8,128)} %multiply_add_fusion.2.in_ref), custom_call_target="tpu_custom_call" | custom-call | flops 524288 | bytes 1048576 | tf_op jit(solution)/shard_map/pallas_call | solution.py:193
  565.6 209.4 %shard_map.300 = (f32[32,4384]{1,0:T(8,128)}, f32[64,1024]{1,0:T(8,128)}, f32[32,4384]{1,0:T(8,128)}, f32[64,1024]{1,0:T(8,128)}) custom-call(bf16[4,4,2,32,4384]{4,3,2,1,0:T(8,128)(2,1)} %bitcast.86, bf16[4,4,2,64,1024]{4,3,2,1,0:T(8,128)(2,1)} %bitcast.88, bf16[4,4,2,32,4384]{4,3,2,1,0:T(8,128)(2,1)} %bitcast.87, bf16[4,4,2,64,1024]{4,3,2,1,0:T(8,128)(2,1)} %bitcast.89), custom_call_target="tpu_custom_call" | custom-call | flops 26345472 | bytes 52690944 | tf_op jit(solution)/shard_map/pallas_call | solution.py:193
  779.6 8.5 reduce-scatter.8.cloned.1.call-done.base_ref
  788.0 14.1 %shard_map.301 = (f32[6286,256]{1,0:T(8,128)}, f32[8,256]{1,0:T(8,128)}) custom-call(s32[1]{0:T(128)} %bitcast.1.count_ref, s32[8192]{0:T(1024)} %get-tuple-element.169.row_ref, s32[8192]{0:T(1024)} %get-tuple-element.168.tok_ref, bf16[8192,256]{1,0:T(8,128)(2,1)} %bitcast.90, bf16[6286,256]{1,0:T(8,128)(2,1)} %reduce-scatter.8.cloned.1.call-done.base_ref), custom_call_target="tpu_custom_call" | custom-call | flops 7478276 | bytes 14956552 | tf_op jit(solution)/shard_map/pallas_call | solution.py:66
  808.2 25.2 %shard_map.302 = (f32[256,128]{1,0:T(8,128)}, f32[8,128]{1,0:T(8,128)}) custom-call(f32[256,128]{1,0:T(8,128)} %bitcast.96), custom_call_target="tpu_custom_call" | custom-call | flops 393216 | bytes 786432 | tf_op jit(solution)/shard_map/pallas_call | solution.py:193
  840.9 12.0 %fusion.6 = (bf16[6286,256]{1,0:T(8,128)(2,1)}, f32[6286,256]{1,0:T(8,128)S(1)}, f32[6286,256]{1,0:T(8,128)}) fusion(f32[6286,256]{1,0:T(8,128)} %table_ref.1, f32[6286,256]{1,0:T(8,128)} %get-tuple-element.137, f32[]{:T(128)} %bitcast.34, f32[6286,256]{1,0:T(8,128)} %param.19), kind=kLoop, calls=%fused_computation.84 | loop fusion | flops 12873728 | bytes 35402756 | tf_op jit(solution)/shard_map/convert_element_type | solution.py:1840
  853.0 8.8 add_multiply_fusion
  (172 shorter events, 47.1 us)
Async XLA Ops:
  8.0 173.8 %reduce-scatter.4.cloned.1.call-start = ((), (), s32[]{:S(2)}) async-start(), calls=%async_computation.3 | async-start | bytes 4718592 | tf_op jit(solution)/shard_map/reduce_scatter | solution.py:1729
  36.2 241.4 %all-gather.5.cloned.1.call-start = ((), (), s32[]{:S(2)}) async-start(), calls=%async_computation.4 | async-start | bytes 3276800 | tf_op jit(solution)/shard_map/all_gather | solution.py:1708
  38.6 137.8 %slice-start = ((f32[30400]{0:T(1024)}), f32[29376]{0:T(1024)S(1)}, s32[]{:S(2)}) async-start(f32[30400]{0:T(1024)} %param.27), calls=%async_computation.9 | async-start | bytes 237568 | tf_op jit(solution)/shard_map/slice | solution.py:1560
  38.6 138.1 %copy-start.27 = (f32[30400]{0:T(1024)S(1)}, f32[30400]{0:T(1024)}, u32[]{:S(2)}) copy-start(f32[30400]{0:T(1024)} %param.27) | copy-start | bytes 364804
  38.6 139.6 %copy-start.39 = (s32[2,4]{1,0:T(2,128)S(1)}, s32[2,4]{1,0:T(2,128)}, u32[]{:S(2)}) copy-start(s32[2,4]{1,0:T(2,128)} %param.17) | copy-start | bytes 100
  38.6 140.5 %copy-start.36 = (s32[2,1,1024]{2,1,0:T(1,128)S(1)}, s32[2,1,1024]{2,1,0:T(1,128)}, u32[]{:S(2)}) copy-start(s32[2,1,1024]{2,1,0:T(1,128)} %param.16) | copy-start | bytes 24580
  38.7 244.9 %all-gather.7.cloned.1.call-start = ((), (), s32[]{:S(2)}) async-start(), calls=%async_computation.5 | async-start | bytes 12820480 | tf_op jit(solution)/shard_map/all_gather | solution.py:1747
  176.4 256.4 %reduce-scatter.6.cloned.1.call-start = ((), (), s32[]{:S(2)}) async-start(), calls=%async_computation.6 | async-start | bytes 4718592 | tf_op jit(solution)/shard_map/reduce_scatter | solution.py:1778
  198.4 8.0 copy-start.14
  206.4 26.3 %copy-start.1 = (f32[256,1024]{1,0:T(8,128)S(1)}, f32[256,1024]{1,0:T(8,128)}, u32[]{:S(2)}) copy-start(f32[256,1024]{1,0:T(8,128)} %shard_map.288) | copy-start | bytes 3145732
  237.9 8.2 copy-start.15
  385.4 394.1 %all-gather.9.cloned.1.call-start = ((), (), s32[]{:S(2)}) async-start(), calls=%async_computation.8 | async-start | bytes 4718592 | tf_op jit(solution)/shard_map/all_gather | solution.py:1804
  419.3 16.9 %copy-start.5 = (f32[256,1024]{1,0:T(8,128)S(1)}, f32[256,1024]{1,0:T(8,128)}, u32[]{:S(2)}) copy-start(f32[256,1024]{1,0:T(8,128)} %copy-done.4) | copy-start | bytes 3145732
  432.8 4.5 copy-start.41
  479.2 7.5 copy-start.3
  479.2 7.5 copy-start.6
  479.2 7.5 copy-start.11
  488.1 39.1 %copy-start.24 = (bf16[256,1024]{1,0:T(8,128)(2,1)}, bf16[256,1024]{1,0:T(8,128)(2,1)S(1)}, u32[]{:S(2)}) copy-start(bf16[256,1024]{1,0:T(8,128)(2,1)S(1)} %get-tuple-element.160.db_ref) | copy-start | bytes 1572868
  564.1 224.0 %reduce-scatter.8.cloned.1.call-start = ((), (), s32[]{:S(2)}) async-start(), calls=%async_computation.7 | async-start | bytes 16097280 | tf_op jit(solution)/shard_map/reduce_scatter | solution.py:1782
  776.7 30.0 %copy-start.33 = (f32[1,2048]{1,0:T(1,128)S(1)}, f32[1,2048]{1,0:T(1,128)}, u32[]{:S(2)}) copy-start(f32[1,2048]{1,0:T(1,128)} %get-tuple-element.116) | copy-start | bytes 24580
  776.7 30.0 %copy-start.34 = (f32[1,2048]{1,0:T(1,128)S(1)}, f32[1,2048]{1,0:T(1,128)}, u32[]{:S(2)}) copy-start(f32[1,2048]{1,0:T(1,128)} %get-tuple-element.113) | copy-start | bytes 24580
  778.7 59.9 %copy-start.29 = (f32[30400]{0:T(1024)S(1)}, f32[30400]{0:T(1024)}, u32[]{:S(2)}) copy-start(f32[30400]{0:T(1024)} %param.28) | copy-start | bytes 364804
  840.9 27.0 %copy-start.28 = (f32[30400]{0:T(1024)}, f32[30400]{0:T(1024)S(1)}, u32[]{:S(2)}) copy-start(f32[30400]{0:T(1024)S(1)} %get-tuple-element.145) | copy-start | bytes 364804
  853.0 8.8 %copy-start = (f32[6286,256]{1,0:T(8,128)}, f32[6286,256]{1,0:T(8,128)S(1)}, u32[]{:S(2)}) copy-start(f32[6286,256]{1,0:T(8,128)S(1)} %get-tuple-element.154) | copy-start | bytes 19310596
  853.0 8.8 %copy-start.8 = (f32[2,32,4384]{2,1,0:T(8,128)S(1)}, f32[2,32,4384]{2,1,0:T(8,128)}, u32[]{:S(2)}) copy-start(f32[2,32,4384]{2,1,0:T(8,128)} %param.21) | copy-start | bytes 3366916
  853.0 8.8 %copy-start.12 = (f32[32,4384]{1,0:T(8,128)S(1)}, f32[32,4384]{1,0:T(8,128)}, u32[]{:S(2)}) copy-start(f32[32,4384]{1,0:T(8,128)} %get-tuple-element.127) | copy-start | bytes 1683460
  853.0 8.8 %copy-start.13 = (f32[32,4384]{1,0:T(8,128)S(1)}, f32[32,4384]{1,0:T(8,128)}, u32[]{:S(2)}) copy-start(f32[32,4384]{1,0:T(8,128)} %get-tuple-element.129) | copy-start | bytes 1683460
  853.0 8.8 %copy-start.19 = (f32[2,32,4384]{2,1,0:T(8,128)S(1)}, f32[2,32,4384]{2,1,0:T(8,128)}, u32[]{:S(2)}) copy-start(f32[2,32,4384]{2,1,0:T(8,128)} %param.22) | copy-start | bytes 3366916
  861.8 3.4 copy-start.18
  861.8 3.4 copy-start.21
  864.1 4.5 copy-start.9
  864.1 3.8 copy-start.30
  (17 other events, 31.8 us)
Sparse Core Ops, SparseCore 0:
  36.3 83.5 reduce-scatter.3
  385.5 47.2 reduce-scatter.5
  564.2 47.4 all-gather.8
Sparse Core Ops, SparseCore 1:
  39.1 62.9 all-gather.4
  176.5 107.1 all-gather.6
  567.7 220.3 reduce-scatter.7
